TPU v7x, 8 devices: a whole 2x2x1 slice. The times are simulated.
8 devices in a mesh: dp: 2 (over z, y), tp: 4 (over x, core).
Axes of the slice: x: 2, y: 2, z: 1, core: 2. Of those that a mesh axis runs over, the one named last changes fastest.
Arguments:
- ids: int32 [4, 256], P('dp'), parts along dimension 0
- E: bfloat16 [32768, 2304], P('tp')
- g: bfloat16 [2304], replicated
- W: bfloat16 [2304, 4096], P(None, 'tp')
- du: bfloat16 [4, 256, 4096], P('dp', None, 'tp'), parts along dimension 0
- dres: bfloat16 [4, 256, 2304], P('dp', 'tp'), parts along dimension 0
Outputs:
- output 1: bfloat16 [4, 256, 4096], P('dp', None, 'tp'), parts along dimension 0
- output 2: bfloat16 [4, 256, 2304], P('dp', 'tp'), parts along dimension 0
- output 3: float32 [65536, 2304], P(('dp', 'tp')), parts along dimension 0
- output 4: float32 [4608, 4096], P('dp', 'tp'), parts along dimension 0
- output 5: float32 [4608], P('dp'), parts along dimension 0
There are 2 independent parts. A program takes and returns all parts, laid end to end along the dimension named above; an argument that names none is the same for every part.
All inputs are finite; a program needn't handle non-finite values.
Results may differ from a plain program's by a relative error of at most 0.00682878.
Values are sent between devices in bfloat16 or wider.
A program may use at most 1 GiB of HBM per device.

v0:
```python
import jax
import jax.numpy as jnp
from jax import lax
from jax.sharding import PartitionSpec as P

EPS = 1e-6


def solution(mesh):
    ntp = mesh.shape["tp"]

    def body(ids, E, g, W, du, dres):
        vs, d = E.shape
        nk, t = ids.shape
        ts = t // ntp
        me = lax.axis_index("tp")
        lo = me * vs
        gf = g.astype(jnp.float32)
        rows = lax.broadcasted_iota(jnp.int32, (vs, t), 0)
        c0 = (((0,), (0,)), ((), ()))
        c1 = (((1,), (1,)), ((), ()))
        dE = None
        dW = None
        dg = jnp.zeros((d,), jnp.float32)
        us = []
        xs = []
        for k in range(nk):
            oh = (rows == (ids[k] - lo)[None, :]).astype(jnp.bfloat16)
            xp = lax.dot_general(oh, E, c0, preferred_element_type=jnp.float32).astype(jnp.bfloat16)
            x = lax.psum(xp, "tp")
            xf = x.astype(jnp.float32)
            rs = lax.rsqrt(jnp.mean(xf * xf, axis=-1, keepdims=True) + EPS)
            nh = xf * rs
            n = (nh * gf).astype(jnp.bfloat16)
            us.append(jnp.dot(n, W, preferred_element_type=jnp.float32).astype(jnp.bfloat16))
            xs.append(lax.dynamic_slice_in_dim(x, me * ts, ts, 0))
            p = lax.dot_general(du[k], W, c1, preferred_element_type=jnp.float32).astype(jnp.bfloat16)
            got = lax.all_to_all(p.reshape(ntp, ts, d), "tp", 0, 0, tiled=True)
            dn = jnp.sum(got.astype(jnp.float32), axis=0)
            nhl = lax.dynamic_slice_in_dim(nh, me * ts, ts, 0)
            rsl = lax.dynamic_slice_in_dim(rs, me * ts, ts, 0)
            gdn = gf * dn
            dx = dres[k].astype(jnp.float32) + rsl * (gdn - nhl * jnp.mean(nhl * gdn, axis=-1, keepdims=True))
            dg = dg + jnp.sum(dn * nhl, axis=0)
            dxa = lax.all_gather(dx.astype(jnp.bfloat16), "tp", axis=0, tiled=True)
            de = jnp.dot(oh, dxa, preferred_element_type=jnp.float32)
            dE = de if dE is None else dE + de
            dw = lax.dot_general(n, du[k], c0, preferred_element_type=jnp.float32)
            dW = dw if dW is None else dW + dw
        dg = lax.psum(dg, "tp")
        return jnp.stack(us), jnp.stack(xs), dE, dW, dg

    return jax.shard_map(
        body,
        mesh=mesh,
        in_specs=(P("dp", None), P("tp", None), P(None), P(None, "tp"), P("dp", None, "tp"), P("dp", "tp", None)),
        out_specs=(P("dp", None, "tp"), P("dp", "tp", None), P(("dp", "tp"), None), P("dp", "tp"), P("dp")),
        check_vma=False,
    )
```

profile of v0, /device:TPU:0, one launch (start us, length us, event | category | flops | bytes accessed | tf_op | source)
XLA Modules:
  0.0 237.1 jit_solution(4982524144997860831)
XLA Ops:
  7.2 5.0 %convolution_convert_fusion = bf16[256,2304]{1,0:T(8,128)(2,1)} fusion(bf16[2304,1024]{1,0:T(8,128)(2,1)} %param.9, bf16[2,256,1024]{2,1,0:T(8,128)(2,1)} %param.10), kind=kOutput, calls=%fused_computation.11 | convolution fusion | flops 1208549376 | bytes 6422528 | tf_op jit(solution)/shard_map/dot_general | solution.py:37
  12.1 4.7 %all-to-all-start.1 = ((bf16[4,64,2304]{2,1,0:T(8,128)(2,1)}), bf16[4,64,2304]{2,1,0:T(8,128)(2,1)S(1)}, u32[]{:S(2)}, u32[]{:S(2)}) async-start(bf16[4,64,2304]{2,1,0:T(8,128)(2,1)} %bitcast.11), calls=%async_computation.1 | async-start | bytes 2359296 | tf_op jit(solution)/shard_map/all_to_all | solution.py:38
  16.9 17.5 %fusion.7 = bf16[256,2304]{1,0:T(8,128)(2,1)} fusion(bf16[8192,2304]{1,0:T(8,128)(2,1)} %param.7, s32[256]{0:T(256)S(1)} %bitcast.38), kind=kOutput, calls=%fused_computation.13 | convolution fusion | flops 9666363392 | bytes 38929408 | tf_op jit(solution)/shard_map/dot_general | solution.py:29
  34.4 17.5 %fusion.8 = bf16[256,2304]{1,0:T(8,128)(2,1)} fusion(bf16[8192,2304]{1,0:T(8,128)(2,1)} %param.7, s32[256]{0:T(256)S(1)} %bitcast.36), kind=kOutput, calls=%fused_computation.14 | convolution fusion | flops 9666363392 | bytes 38929408 | tf_op jit(solution)/shard_map/dot_general | solution.py:29
  52.0 1.2 copy-done.2
  53.2 4.8 %convolution_convert_fusion.1 = bf16[256,2304]{1,0:T(8,128)(2,1)} fusion(bf16[2304,1024]{1,0:T(8,128)(2,1)} %param.9, bf16[2,256,1024]{2,1,0:T(8,128)(2,1)S(1)} %copy-done.2), kind=kOutput, calls=%fused_computation.12 | convolution fusion | flops 1208549376 | bytes 6422528 | tf_op jit(solution)/shard_map/dot_general | solution.py:37
  58.0 3.7 %all-to-all-start = ((bf16[4,64,2304]{2,1,0:T(8,128)(2,1)}), bf16[4,64,2304]{2,1,0:T(8,128)(2,1)S(1)}, u32[]{:S(2)}, u32[]{:S(2)}) async-start(bf16[4,64,2304]{2,1,0:T(8,128)(2,1)} %bitcast.8), calls=%async_computation | async-start | bytes 2359296 | tf_op jit(solution)/shard_map/all_to_all | solution.py:38
  61.7 0.2 all-gather.3.cloned.1.call-start
  61.9 0.2 convert_reduce_fusion
  62.1 28.2 %all-to-all-done = bf16[4,64,2304]{2,1,0:T(8,128)(2,1)S(1)} async-done(((bf16[4,64,2304]{2,1,0:T(8,128)(2,1)}), bf16[4,64,2304]{2,1,0:T(8,128)(2,1)S(1)}, u32[]{:S(2)}, u32[]{:S(2)}) %all-to-all-start) | async-done | bytes 1179680 | tf_op jit(solution)/shard_map/all_to_all | solution.py:38
  90.2 0.2 convert_reduce_fusion.1
  90.4 26.5 %all-reduce.3.cloned.1.call-done = (bf16[256,2304]{1,0:T(8,128)(2,1)}, bf16[256,2304]{1,0:T(8,128)(2,1)}) async-done(((bf16[256,2304]{1,0:T(8,128)(2,1)}, bf16[256,2304]{1,0:T(8,128)(2,1)}), (bf16[256,2304]{1,0:T(8,128)(2,1)}, bf16[256,2304]{1,0:T(8,128)(2,1)})) %all-reduce.3.cloned.1.call-update) | async-done | bytes 2359312 | tf_op jit(solution)/shard_map/psum | solution.py:30
  117.0 1.7 fusion.10
  118.7 1.6 fusion.9
  120.4 0.4 convert_multiply_fusion
  120.7 0.1 dynamic-slice.6
  120.8 0.1 dynamic-slice.7
  120.9 0.0 copy-done.8
  120.9 4.6 %fusion.11 = bf16[1,256,1024]{2,1,0:T(8,128)(2,1)} fusion(bf16[2304,1024]{1,0:T(8,128)(2,1)} %param.9, f32[2304]{0:T(1024)S(1)} %convert_element_type.61, bf16[256,2304]{1,0:T(8,128)(2,1)S(1)} %copy-done, f32[256]{0:T(256)S(1)} %add_rsqrt_fusion.1), kind=kOutput, calls=%fused_computation.27 | convolution fusion | flops 1210580992 | bytes 6432768 | tf_op jit(solution)/shard_map/dot_general | solution.py:35
  125.5 0.9 multiply_reduce_fusion
  126.4 0.2 copy-done.4
  126.6 1.2 fusion.13
  127.8 0.0 all-gather.5.cloned.1.call-start
  127.9 0.7 add.62
  128.6 11.3 %psum.23 = f32[2304]{0:T(1024)} all-reduce(f32[2304]{0:T(1024)S(1)} %add.62), channel_id=1, replica_groups=mesh['dp'=2,'tp'=4] {'tp'}, use_global_device_ids=true, to_apply=%region_10.0 | all-reduce | flops 2304 | bytes 18432 | tf_op jit(solution)/shard_map/psum | solution.py:50
  139.9 3.9 %fusion.12 = bf16[1,256,1024]{2,1,0:T(8,128)(2,1)S(1)} fusion(bf16[2304,1024]{1,0:T(8,128)(2,1)} %param.9, f32[2304]{0:T(1024)S(1)} %convert_element_type.61, bf16[256,2304]{1,0:T(8,128)(2,1)S(1)} %copy-done.1, f32[256]{0:T(256)} %copy-done.10), kind=kOutput, calls=%fused_computation.28 | convolution fusion | flops 1210580992 | bytes 6432768 | tf_op jit(solution)/shard_map/dot_general | solution.py:35
  143.8 1.5 fusion.17
  145.4 5.4 %convolution_add_fusion.1 = f32[2304,1024]{1,0:T(8,128)} fusion(f32[2304,1024]{1,0:T(8,128)S(1)} %fusion.17, bf16[2,256,1024]{2,1,0:T(8,128)(2,1)S(1)} %copy-done.3, f32[2304]{0:T(1024)S(1)} %convert_element_type.61, bf16[256,2304]{1,0:T(8,128)(2,1)S(1)} %copy-done.1, f32[256]{0:T(256)S(1)} %copy-done.11), kind=kOutput, calls=%fused_computation.6 | convolution fusion | flops 1212678144 | bytes 20591616 | tf_op jit(solution)/shard_map/dot_general | solution.py:48
  150.8 0.9 pad_maximum_fusion.1
  151.7 1.1 pad_maximum_fusion
  152.8 29.5 %fusion.1 = f32[8192,2304]{1,0:T(8,128)} fusion(bf16[256,2304]{1,0:T(8,128)(2,1)} %all-gather.3.cloned.1.call-done, s32[256]{0:T(256)S(1)} %bitcast.39), kind=kOutput, calls=%fused_computation.4 | convolution fusion | flops 9665773568 | bytes 76678144 | tf_op jit(solution)/shard_map/dot_general | solution.py:46
  182.3 48.3 %convolution_add_fusion = f32[8192,2304]{1,0:T(8,128)} fusion(f32[8192,2304]{1,0:T(8,128)} %fusion.1, bf16[256,2304]{1,0:T(8,128)(2,1)} %all-gather.5.cloned.1.call-done, s32[256]{0:T(256)S(1)} %bitcast.37), kind=kOutput, calls=%fused_computation | convolution fusion | flops 9684647936 | bytes 152175616 | tf_op jit(solution)/shard_map/dot_general | solution.py:46
  (39 shorter events, 0.2 us)
Async XLA Ops:
  12.1 4.8 %copy-start.13 = (s32[2,256]{1,0:T(2,128)S(1)}, s32[2,256]{1,0:T(2,128)}, u32[]{:S(2)}) copy-start(s32[2,256]{1,0:T(2,128)} %param.6) | copy-start | bytes 6148
  12.1 45.8 %all-to-all-start.1 = ((bf16[4,64,2304]{2,1,0:T(8,128)(2,1)}), bf16[4,64,2304]{2,1,0:T(8,128)(2,1)S(1)}, u32[]{:S(2)}, u32[]{:S(2)}) async-start(bf16[4,64,2304]{2,1,0:T(8,128)(2,1)} %bitcast.11), calls=%async_computation.1 | async-start | bytes 2359296 | tf_op jit(solution)/shard_map/all_to_all | solution.py:38
  16.9 100.1 %all-reduce.3.cloned.1.call-start = ((), (), s32[]{:S(2)}) async-start(), calls=%async_computation.4 | async-start | bytes 4718592 | tf_op jit(solution)/shard_map/psum | solution.py:30
  16.9 17.5 %copy-start.6 = (s32[1,256]{1,0:T(1,128)}, s32[1,256]{1,0:T(1,128)S(1)}, u32[]{:S(2)}) copy-start(s32[1,256]{1,0:T(1,128)S(1)} %get-tuple-element.15) | copy-start | bytes 3076
  51.9 1.2 copy-start.2
  58.0 3.9 %copy-start.12 = (bf16[2304]{0:T(1024)(128)(2,1)S(1)}, bf16[2304]{0:T(1024)(128)(2,1)}, u32[]{:S(2)}) copy-start(bf16[2304]{0:T(1024)(128)(2,1)} %param.8) | copy-start | bytes 13828
  58.0 32.3 %all-to-all-start = ((bf16[4,64,2304]{2,1,0:T(8,128)(2,1)}), bf16[4,64,2304]{2,1,0:T(8,128)(2,1)S(1)}, u32[]{:S(2)}, u32[]{:S(2)}) async-start(bf16[4,64,2304]{2,1,0:T(8,128)(2,1)} %bitcast.8), calls=%async_computation | async-start | bytes 2359296 | tf_op jit(solution)/shard_map/all_to_all | solution.py:38
  61.7 91.1 %all-gather.3.cloned.1.call-start = ((), (), s32[]{:S(2)}) async-start(), calls=%async_computation.2 | async-start | bytes 1474560 | tf_op jit(solution)/shard_map/all_gather | solution.py:45
  117.0 3.4 %copy-start = (bf16[256,2304]{1,0:T(8,128)(2,1)S(1)}, bf16[256,2304]{1,0:T(8,128)(2,1)}, u32[]{:S(2)}) copy-start(bf16[256,2304]{1,0:T(8,128)(2,1)} %get-tuple-element.10) | copy-start | bytes 3538948
  117.0 3.4 %copy-start.1 = (bf16[256,2304]{1,0:T(8,128)(2,1)S(1)}, bf16[256,2304]{1,0:T(8,128)(2,1)}, u32[]{:S(2)}) copy-start(bf16[256,2304]{1,0:T(8,128)(2,1)} %get-tuple-element.9) | copy-start | bytes 3538948
  118.7 2.1 copy-start.10
  120.3 0.6 copy-start.8
  125.5 1.1 copy-start.4
  127.8 54.5 %all-gather.5.cloned.1.call-start = ((), (), s32[]{:S(2)}) async-start(), calls=%async_computation.3 | async-start | bytes 1474560 | tf_op jit(solution)/shard_map/all_gather | solution.py:45
  139.9 3.9 %copy-start.3 = (bf16[2,256,1024]{2,1,0:T(8,128)(2,1)S(1)}, bf16[2,256,1024]{2,1,0:T(8,128)(2,1)}, u32[]{:S(2)}) copy-start(bf16[2,256,1024]{2,1,0:T(8,128)(2,1)} %param.10) | copy-start | bytes 3145732
  139.9 3.9 %copy-start.9 = (f32[256]{0:T(256)S(1)}, f32[256]{0:T(256)}, u32[]{:S(2)}) copy-start(f32[256]{0:T(256)} %copy-done.8) | copy-start | bytes 3076
  143.8 1.5 copy-start.11
  145.4 6.3 %copy-start.5 = (bf16[1,256,1024]{2,1,0:T(8,128)(2,1)S(1)}, bf16[1,256,1024]{2,1,0:T(8,128)(2,1)}, u32[]{:S(2)}) copy-start(bf16[1,256,1024]{2,1,0:T(8,128)(2,1)} %fusion.11) | copy-start | bytes 1572868
  150.8 2.0 copy-start.7
Sparse Core Ops, SparseCore 0:
  52.1 64.8 all-reduce.2
  127.9 14.6 all-gather.2
  151.0 14.8 all-gather.4
where the time goes:
time: 238 us; the launch traced here: 237 us
  matrix products  138 us (58%)
  waiting for transfers between devices  54.8 us (23%)
  between operations  13.9 us (6%)
  blocking collectives  11.3 us (5%)
  other arithmetic  8.78 us (4%)
  starting transfers between devices  8.68 us (4%)
    dot_general x2, matrix products, body(): de = jnp.dot(oh, dxa, preferred_element_type=jnp.float32)  77.8 us
    dot_general x2, matrix products, body(): lax.dot_general(oh, E, c0, preferred_element_type=jnp.float32)  35 us
    all_to_all x2, waiting for transfers between devices, body(): got = lax.all_to_all(p.reshape(ntp, ts, d), 'tp', 0, 0, tiled=True)  28.2 us
    psum x1, waiting for transfers between devices, body(): x = lax.psum(xp, 'tp')  26.5 us
    psum x1, blocking collectives, body(): dg = lax.psum(dg, 'tp')  11.3 us
    dot_general x2, matrix products, body(): lax.dot_general(du[k], W, c1, preferred_element_type=jnp.float32)  9.76 us
    dot_general x2, matrix products, body(): jnp.dot(n, W, preferred_element_type=jnp.float32).astype(jnp.bfloat16)  8.49 us
    all_to_all x2, starting transfers between devices, body(): got = lax.all_to_all(p.reshape(ntp, ts, d), 'tp', 0, 0, tiled=True)  8.47 us
  transfers between devices with their start and end apart: 5, of which 2 were waited for; matrix products, arithmetic and copies ran while one was open for 35% of the time, Pallas kernels for 0%

commit v1 on v0

v1 whole, which is shorter than its diff:
```python
import functools

import jax
import jax.numpy as jnp
from jax import lax
from jax.experimental import pallas as pl
from jax.experimental.pallas import tpu as pltpu
from jax.sharding import PartitionSpec as P


EPS = 1e-6
C = 64
G = 16
CB = 256
ZR = 128
Z1, Z2 = 24, 20
TB = 64

F32 = jnp.float32
BF16 = jnp.bfloat16
VMEM = pltpu.VMEM


def _sm():
    return pl.BlockSpec(memory_space=pltpu.SMEM)


def _vm():
    return pl.BlockSpec(memory_space=pltpu.VMEM)


def _any():
    return pl.BlockSpec(memory_space=pl.ANY)


def _params(mb):
    return pltpu.CompilerParams(vmem_limit_bytes=mb << 20)


def _cost(us):
    return pl.CostEstimate(flops=int(us * 4_000_000_000), bytes_accessed=1_000_000, transcendentals=0)


def _iota(shape, dim):
    return lax.broadcasted_iota(jnp.int32, shape, dim).astype(F32)


def _me():
    return lax.axis_index("tp").astype(jnp.int32)


def _index_kernel(vs, ntp, first, *refs):
    if first:
        ids_ref, e_ref, tab_ref, pos_ref, srow_ref, list_ref, cnt_ref, buf, glv, gls, gsem, sem = refs
        base = 0.0
    else:
        c_ref, ids_ref, e_ref, tab_ref, pos_ref, srow_ref, list_ref, cnt_ref, buf, glv, gls, gsem, sem = refs
        base = (c_ref[0] * C).astype(F32)
    mei = _me()
    me = mei.astype(F32)
    lo = me * vs
    nk, t = ids_ref.shape
    ntok = nk * t
    nb = ntok // TB
    idsf = ids_ref[...].astype(F32)
    idr = jnp.concatenate([idsf[k:k + 1] for k in range(nk)], axis=1)

    def column(row, b):
        w = (b * TB) // 128 * 128
        part = jnp.broadcast_to(row[:, w:w + 128], (TB, 128))
        hit = _iota((TB, 128), 1) == _iota((TB, 128), 0) + float(b * TB - w)
        return jnp.sum(jnp.where(hit, part, 0.0), axis=1, keepdims=True)

    def fold(a):
        return sum(a[8 * q:8 * q + 8] for q in range(1, TB // 8)) + a[:8]

    lane = _iota((TB, ntok), 1)
    thr = _iota((TB, 128), 1) * float(vs)
    rank8 = jnp.zeros((8, ntok), F32)
    below8 = jnp.zeros((8, 128), F32)
    idcs = []
    for b in range(nb):
        idc = column(idr, b)
        idcs.append(idc)
        idb = jnp.broadcast_to(idc, (TB, ntok))
        dup = (idb == idr) & (lane < _iota((TB, ntok), 0) + float(b * TB))
        seen = jnp.max(jnp.where(dup, 1.0, 0.0), axis=1, keepdims=True)
        key = jnp.where(seen > 0.5, float(vs * ntp), idc)
        rank8 = rank8 + fold(jnp.where(jnp.broadcast_to(key, (TB, ntok)) < idr, 1.0, 0.0))
        below8 = below8 + fold(jnp.where(jnp.broadcast_to(key, (TB, 128)) < thr, 1.0, 0.0))
    rank = jnp.sum(rank8, axis=0, keepdims=True)
    below = jnp.sum(below8, axis=0, keepdims=True)
    own_r = jnp.floor(idr * (1.0 / vs))
    start = jnp.zeros_like(rank)
    mine0 = jnp.zeros((1, 1), F32)
    cnt = jnp.zeros((1, 1), F32)
    mx = jnp.zeros((1, 1), F32)
    for d in range(ntp):
        ld = below[:, d:d + 1]
        nd = below[:, d + 1:d + 2] - ld
        start = jnp.where(own_r == float(d), ld, start)
        cnt = jnp.where(me == float(d), nd, cnt)
        mx = jnp.maximum(mx, nd)
    slot_r = rank - start
    my_r = jnp.where(own_r == me, slot_r, -1.0)

    slot_l = _iota((TB, 128), 1) + base
    acc = jnp.zeros((TB, 128), F32)
    mys = []
    for b in range(nb):
        my_c = column(my_r, b)
        mys.append(my_c)
        acc = jnp.maximum(acc, jnp.where(my_c == slot_l, idcs[b] - lo, 0.0))
    glv[...] = jnp.broadcast_to(jnp.max(acc, axis=0, keepdims=True), (8, 128)).astype(jnp.int32)
    cp = pltpu.make_async_copy(glv, gls, gsem)
    cp.start()
    cp.wait()

    def fetch(j, carry):
        g = pl.multiple_of((gls[0, j] // G) * G, G)
        pltpu.make_async_copy(e_ref.at[pl.ds(g, G)], buf.at[pl.ds(pl.multiple_of(j * G, G), G)], sem).start()
        return carry

    lax.fori_loop(0, C, fetch, 0, unroll=8)

    srow_ref[...] = my_r
    full = jnp.zeros((8, ntok), F32)
    lane8 = _iota((8, ntok), 1)
    for b in range(nb):
        for q in range(TB // 8):
            s = slice(8 * q, 8 * q + 8)
            full = jnp.maximum(full, jnp.where(mys[b][s] == lane8, idcs[b][s] - lo, 0.0))
    list_ref[...] = jnp.max(full, axis=0, keepdims=True).astype(jnp.int32)
    rel = (own_r.astype(jnp.int32) ^ mei).astype(F32)
    pos = jnp.where((slot_r >= base) & (slot_r < base + C), rel * C + slot_r - base, -1.0)
    for b in range(nb):
        pos_ref[b * TB:(b + 1) * TB, :] = column(pos, b)
    lane1 = lax.broadcasted_iota(jnp.int32, (1, 128), 1)
    cnt_ref[...] = jnp.where(lane1 == 0, mx, cnt).astype(jnp.int32)
    want = jnp.max(jnp.where(my_r == _iota((C, ntok), 0) + base, idr - lo, 0.0), axis=1, keepdims=True)
    want = want - jnp.floor(want * (1.0 / G)) * G + _iota((C, 1), 0) * G
    sel = jnp.where(_iota((C, C * G), 1) == want, 1.0, 0.0).astype(BF16)
    pltpu.make_async_copy(e_ref.at[pl.ds(0, C * G)], buf, sem).wait()
    for c in range(tab_ref.shape[1] // CB):
        s = slice(c * CB, (c + 1) * CB)
        tab_ref[:, s] = jnp.dot(sel, buf[:, s], preferred_element_type=F32).astype(BF16)


def _index_call(chunk, ids, E, ntp):
    vs, d = E.shape
    ntok = ids.shape[0] * ids.shape[1]
    first = chunk is None
    return pl.pallas_call(
        functools.partial(_index_kernel, vs, ntp, first),
        out_shape=(
            jax.ShapeDtypeStruct((C, d), BF16),
            jax.ShapeDtypeStruct((ntok, 1), F32),
            jax.ShapeDtypeStruct((1, ntok), F32),
            jax.ShapeDtypeStruct((1, ntok), jnp.int32),
            jax.ShapeDtypeStruct((1, 128), jnp.int32),
        ),
        in_specs=([] if first else [_sm()]) + [_vm(), pl.BlockSpec(memory_space=pltpu.HBM)],
        out_specs=(_vm(),) * 5,
        scratch_shapes=[
            VMEM((C * G, d), BF16),
            VMEM((8, 128), jnp.int32),
            pltpu.SMEM((8, 128), jnp.int32),
            pltpu.SemaphoreType.DMA,
            pltpu.SemaphoreType.DMA,
        ],
        compiler_params=_params(14),
        cost_estimate=_cost(5),
        name="index_gather",
    )(*([] if first else [chunk.reshape(1)]), ids, E)


def _expand_kernel(ts, acc, *refs):
    if acc:
        x_in, pos, t0, t1, t2, t3, x_out, xl_out = refs
    else:
        pos, t0, t1, t2, t3, x_out, xl_out = refs
    oh = jnp.where(pos[...] == _iota((pos.shape[0], 4 * C), 1), 1.0, 0.0).astype(BF16)
    for c in range(x_out.shape[1] // CB):
        s = slice(c * CB, (c + 1) * CB)
        tab = jnp.concatenate([t[:, s] for t in (t0, t1, t2, t3)], axis=0)
        tot = jnp.dot(oh, tab, preferred_element_type=F32)
        if acc:
            tot = tot + x_in[:, s].astype(F32)
        x_out[:, s] = tot.astype(BF16)
    t = 4 * ts
    for k in range(x_out.shape[0] // t):
        at = pl.multiple_of(k * t + _me() * ts, ts)
        xl_out[k] = x_out[pl.ds(at, ts), :]


def _expand(pos, tabs, ts, x=None):
    ntok, d = pos.shape[0], tabs[0].shape[1]
    ins = ([x] if x is not None else []) + [pos, *tabs]
    return pl.pallas_call(
        functools.partial(_expand_kernel, ts, x is not None),
        out_shape=(jax.ShapeDtypeStruct((ntok, d), BF16), jax.ShapeDtypeStruct((ntok // (4 * ts), ts, d), BF16)),
        in_specs=[_vm()] * len(ins),
        out_specs=(_vm(), _vm()),
        compiler_params=_params(12),
        cost_estimate=_cost(3),
        name="expand",
    )(*ins)


def _p_kernel(ts, du_ref, w_ref, *refs):
    outs, dur = refs[:-1], refs[-1]
    nk = du_ref.shape[0]

    @pl.when(pl.program_id(0) == 0)
    def _():
        for k in range(nk):
            for r in range(4):
                at = pl.multiple_of((_me() ^ r) * ts, ts)
                dur[pl.ds((k * 4 + r) * ts, ts), :] = du_ref[k, pl.ds(at, ts), :]

    out = lax.dot_general(dur[...], w_ref[...], (((1,), (1,)), ((), ())), preferred_element_type=F32)
    for i, o in enumerate(outs):
        o[...] = out[i * ts:(i + 1) * ts].astype(BF16)


def _p_terms(du, W, ts):
    nk, t, f = du.shape
    d = W.shape[0]
    cb = 3 * CB
    out = pl.pallas_call(
        functools.partial(_p_kernel, ts),
        out_shape=(jax.ShapeDtypeStruct((ts, d), BF16),) * (4 * nk),
        grid=(d // cb,),
        in_specs=[pl.BlockSpec((nk, t, f), lambda i: (0, 0, 0)), pl.BlockSpec((cb, f), lambda i: (i, 0))],
        out_specs=(pl.BlockSpec((ts, cb), lambda i: (0, i)),) * (4 * nk),
        scratch_shapes=[VMEM((nk * t, f), BF16)],
        compiler_params=_params(20),
        cost_estimate=_cost(5),
        name="p_terms",
    )(du, W)
    return [out[4 * k:4 * k + 4] for k in range(nk)]


def _fill(z, o, sems, lo, hi, wait):
    for i in range(lo, hi):
        c = pltpu.make_async_copy(z, o.at[pl.ds(i * ZR, ZR)], sems.at[i - lo])
        c.wait() if wait else c.start()


def _zero_kernel(lo, hi, de_in, o, z, sems):
    z[...] = jnp.zeros_like(z)
    _fill(z, o, sems, lo, hi, False)
    _fill(z, o, sems, lo, hi, True)


def _zeros(de, lo, hi):
    vs, d = de.shape
    return pl.pallas_call(
        functools.partial(_zero_kernel, lo, hi),
        out_shape=jax.ShapeDtypeStruct((vs, d), F32),
        in_specs=[_any()],
        out_specs=_any(),
        scratch_shapes=[VMEM((ZR, d), F32), pltpu.SemaphoreType.DMA((hi - lo,))],
        input_output_aliases={0: 0},
        compiler_params=_params(4),
        cost_estimate=_cost((hi - lo) * 0.375),
        name="zero_fill",
    )(de)


def _dx_kernel(x, p0, p1, p2, p3, dres, g, *refs):
    prev, (dx, dg) = refs[:-2], refs[-2:]
    xf = x[...].astype(F32)
    rs = lax.rsqrt(jnp.mean(xf * xf, axis=-1, keepdims=True) + EPS)
    nh = xf * rs
    dn = (p0[...].astype(F32) + p1[...].astype(F32)) + (p2[...].astype(F32) + p3[...].astype(F32))
    gdn = g[...].astype(F32) * dn
    out = dres[...].astype(F32) + rs * (gdn - nh * jnp.mean(nh * gdn, axis=-1, keepdims=True))
    dx[...] = out.astype(BF16)
    part = jnp.sum(dn * nh, axis=0, keepdims=True)
    dg[...] = part + prev[0][...] if prev else part


def _dx(x, ps, dres, g, k, prev):
    _, m, d = x.shape
    row = pl.BlockSpec((pl.Squeezed(), m, d), lambda i: (k, 0, 0))
    whole = lambda a: pl.BlockSpec(a.shape, lambda i: (0,) * a.ndim)
    return pl.pallas_call(
        _dx_kernel,
        out_shape=(jax.ShapeDtypeStruct((m, d), BF16), jax.ShapeDtypeStruct((1, d), F32)),
        grid=(1,),
        in_specs=[row, *map(whole, ps), row, whole(g), *map(whole, prev)],
        out_specs=(pl.BlockSpec((m, d), lambda i: (0, 0)), pl.BlockSpec((1, d), lambda i: (0, 0))),
        compiler_params=_params(12),
        cost_estimate=_cost(2),
        name="dx_form",
    )(x, *ps, dres, g, *prev)


def _u_kernel(zn, x_ref, g_ref, w_ref, *refs):
    u_ref, n_ref, de, z, sems = refs[-5:]
    z[...] = jnp.zeros_like(z)
    _fill(z, de, sems, 0, zn, False)
    rows = 64
    for b in range(n_ref.shape[0] // rows):
        s = slice(b * rows, (b + 1) * rows)
        xf = x_ref[s].astype(F32)
        rs = lax.rsqrt(jnp.mean(xf * xf, axis=-1, keepdims=True) + EPS)
        n_ref[s] = (xf * rs * g_ref[...].astype(F32)).astype(BF16)
    nk, t, f = u_ref.shape
    for c in range(f // CB):
        s = slice(c * CB, (c + 1) * CB)
        out = jnp.dot(n_ref[...], w_ref[:, s], preferred_element_type=F32).astype(BF16)
        for k in range(nk):
            u_ref[k, :, s] = out[k * t:(k + 1) * t]
    _fill(z, de, sems, 0, zn, True)


def _u(x, g, W, vs, nk, de):
    ntok, d = x.shape
    f = W.shape[1]
    return pl.pallas_call(
        functools.partial(_u_kernel, Z1),
        out_shape=(
            jax.ShapeDtypeStruct((nk, ntok // nk, f), BF16),
            jax.ShapeDtypeStruct((ntok, d), BF16),
            jax.ShapeDtypeStruct((vs, d), F32),
        ),
        in_specs=[_vm(), _vm(), _vm()] + [_any()] * len(de),
        out_specs=(_vm(), _vm(), _any()),
        scratch_shapes=[VMEM((ZR, d), F32), pltpu.SemaphoreType.DMA((Z1,))],
        input_output_aliases={3: 2} if de else {},
        compiler_params=_params(20),
        cost_estimate=_cost(10),
        name="u_terms",
    )(x, g, W, *de)


def _dw_kernel(lo, hi, n_ref, du_ref, de_in, dw_ref, de, z, sems):
    i = pl.program_id(0)
    nk, t, f = du_ref.shape

    @pl.when(i == 0)
    def _():
        z[...] = jnp.zeros_like(z)
        _fill(z, de, sems, lo, hi, False)

    dw_ref[...] = lax.dot_general(
        n_ref[...], du_ref[...].reshape(nk * t, f), (((0,), (0,)), ((), ())), preferred_element_type=F32
    )

    @pl.when(i == pl.num_programs(0) - 1)
    def _():
        _fill(z, de, sems, lo, hi, True)


def _dw(n, du, de, lo, hi):
    nk, t, f = du.shape
    ntok, d = n.shape
    return pl.pallas_call(
        functools.partial(_dw_kernel, lo, hi),
        out_shape=(jax.ShapeDtypeStruct((d, f), F32), jax.ShapeDtypeStruct(de.shape, F32)),
        grid=(d // CB,),
        in_specs=[
            pl.BlockSpec((ntok, CB), lambda i: (0, i)),
            pl.BlockSpec((nk, t, f), lambda i: (0, 0, 0)),
            _any(),
        ],
        out_specs=(pl.BlockSpec((CB, f), lambda i: (i, 0)), _any()),
        scratch_shapes=[VMEM((ZR, d), F32), pltpu.SemaphoreType.DMA((hi - lo,))],
        input_output_aliases={2: 1},
        compiler_params=_params(20),
        cost_estimate=_cost(10),
        name="dw_terms",
    )(n, du, de)


def _scatter_kernel(ts, nk, cnt_ref, list_ref, srow_ref, *refs):
    pieces, (de_in, de, dx, acc, sem) = refs[:-5], refs[-5:]
    ntok = nk * 4 * ts
    for k in range(nk):
        for r in range(4):
            at = pl.multiple_of(k * 4 * ts + (_me() ^ r) * ts, ts)
            dx[pl.ds(at, ts), :] = pieces[k * 4 + r][...]
    cnt = cnt_ref[0, 1]

    def chunk(i, carry):
        base = i * C
        slot = (lax.broadcasted_iota(jnp.int32, (C, ntok), 0) + base).astype(F32)
        oh = jnp.where(slot == srow_ref[...], 1.0, 0.0).astype(BF16)
        for c in range(acc.shape[1] // CB):
            s = slice(c * CB, (c + 1) * CB)
            acc[:, s] = jnp.dot(oh, dx[:, s], preferred_element_type=F32)
        here = jnp.minimum(cnt - base, C)

        def put(j, c2):
            row = list_ref[0, base + j]
            pltpu.make_async_copy(acc.at[pl.ds(j, 1)], de.at[pl.ds(row, 1)], sem).start()
            return c2

        def done(j, c2):
            pltpu.make_async_copy(acc.at[pl.ds(j, 1)], de.at[pl.ds(0, 1)], sem).wait()
            return c2

        lax.fori_loop(0, here, put, 0)
        lax.fori_loop(0, here, done, 0)
        return carry

    lax.fori_loop(0, (cnt + C - 1) // C, chunk, 0)


def _scatter(cnts, rows, srow, pieces, de, ts, nk):
    vs, d = de.shape
    ntok = srow.shape[1]
    return pl.pallas_call(
        functools.partial(_scatter_kernel, ts, nk),
        out_shape=jax.ShapeDtypeStruct((vs, d), F32),
        in_specs=[_sm(), _sm(), _vm()] + [_vm()] * len(pieces) + [_any()],
        out_specs=_any(),
        scratch_shapes=[VMEM((ntok, d), BF16), VMEM((C, d), F32), pltpu.SemaphoreType.DMA],
        input_output_aliases={3 + len(pieces): 0},
        compiler_params=_params(16),
        cost_estimate=_cost(3),
        name="scatter_rows",
    )(cnts, rows, srow, *pieces, de)


def solution(mesh):
    ntp = mesh.shape["tp"]
    ndp = mesh.shape["dp"]

    def swap(a, bit):
        return lax.ppermute(a, "tp", [(i, i ^ bit) for i in range(ntp)])

    def share(t):
        t2 = swap(t, 2)
        t1 = swap(t, 1)
        return t, t1, t2, swap(t2, 1)

    def p_terms(du, W, ts):
        ps = _p_terms(du, W, ts)
        return [(q[0], swap(q[1], 1), swap(q[2], 2), swap(q[3], 3)) for q in ps]

    def finish(x, xl, ps, g2, W, du, dres, cnts, rows, srow, vs, de):
        nk, ts, d = xl.shape
        nz = vs // ZR
        u, n, de = _u(x, g2, W, vs, nk, de)
        dx0, dg0 = _dx(xl, ps[0], dres, g2, 0, ())
        de = _zeros(de, Z1, Z1 + Z2)
        dx1, dgp = _dx(xl, ps[1], dres, g2, 1, (dg0,))
        pieces = share(dx0) + share(dx1)
        dW, de = _dw(n, du, de, Z1 + Z2, nz)
        dg = ((dgp + swap(dgp, 1)) + (swap(dgp, 2) + swap(dgp, 3))).reshape(d)
        dE = _scatter(cnts, rows, srow, pieces, de, ts, nk)
        return u, xl, dE, dW, dg

    def body(ids, E, g, W, du, dres):
        vs, d = E.shape
        ts = ids.shape[1] // ntp
        g2 = g.reshape(1, d)

        tab, pos, srow, rows, cnts = _index_call(None, ids, E, ntp)
        tabs = share(tab)
        ps = p_terms(du, W, ts)
        other = lax.ppermute(cnts, "dp", [(i, (i + 1) % ndp) for i in range(ndp)])
        x, xl = _expand(pos, tabs, ts)
        outs = finish(x, xl, ps, g2, W, du, dres, cnts, rows, srow, vs, ())
        rounds = (jnp.maximum(cnts[0, 0], other[0, 0]) + C - 1) // C

        inputs = ids, E, W, du, dres, g2

        def again(c):
            once, (_, _, de, _, _) = c
            ids, E, W, du, dres, g2, once = lax.optimization_barrier((*inputs, once))

            def more(q):
                i, x, _ = q
                tab, pos, _, _, _ = _index_call(i, ids, E, ntp)
                return i + 1, *_expand(pos, share(tab), ts, x)

            zeros = jnp.zeros(x.shape, BF16), jnp.zeros(xl.shape, BF16)
            _, xa, xla = lax.while_loop(lambda q: q[0] < rounds, more, (jnp.int32(0), *zeros))
            _, _, srow, rows, cnts = _index_call(once - 1, ids, E, ntp)
            return rounds, finish(xa, xla, p_terms(du, W, ts), g2, W, du, dres, cnts, rows, srow, vs, (de,))

        _, outs = lax.while_loop(lambda c: c[0] < rounds, again, (jnp.int32(1), outs))
        return outs

    return jax.shard_map(
        body,
        mesh=mesh,
        in_specs=(P("dp", None), P("tp", None), P(None), P(None, "tp"), P("dp", None, "tp"), P("dp", "tp", None)),
        out_specs=(P("dp", None, "tp"), P("dp", "tp", None), P(("dp", "tp"), None), P("dp", "tp"), P("dp")),
        check_vma=False,
    )
```

time: 238 us -> 99.9 us (0.42)
  matrix products: 138 us -> 0 us
  Pallas kernels: 0 us -> 52.8 us
  waiting for transfers between devices: 54.8 us -> 26.2 us
  between operations: 13.9 us -> 1.06 us
  blocking collectives: 11.3 us -> 0 us
  other arithmetic: 8.78 us -> 0.64 us
  starting transfers between devices: 8.68 us -> 14.3 us
  local copies, waits for them, and re-layouts: 1.66 us -> 4.4 us
    dot_general x10 -> x0, matrix products: 138 us -> none  [the longest x2 77.8 us: body(): de = jnp.dot(oh, dxa, preferred_element_type=jnp.float32)]
    pallas_call x0 -> x9, Pallas kernels: none -> 52.8 us  [the longest x1 15.5 us: _dw(): pl.pallas_call(functools.partial(_dw_kernel, lo, hi), out_shape=(jax.Shap...]
    all_to_all x2 -> x0, waiting for transfers between devices: 28.2 us -> none  [body(): got = lax.all_to_all(p.reshape(ntp, ts, d), 'tp', 0, 0, tiled=True)]
    psum x1 -> x0, waiting for transfers between devices: 26.5 us -> none  [body(): x = lax.psum(xp, 'tp')]
    ppermute x0 -> x19, waiting for transfers between devices: none -> 26.2 us  [the longest x18 26.2 us: swap(): return lax.ppermute(a, 'tp', [(i, i ^ bit) for i in range(ntp)])]
    ppermute x0 -> x19, starting transfers between devices: none -> 14.3 us  [the longest x18 12.8 us: swap(): return lax.ppermute(a, 'tp', [(i, i ^ bit) for i in range(ntp)])]
    psum x1 -> x0, blocking collectives: 11.3 us -> none  [body(): dg = lax.psum(dg, 'tp')]
    all_to_all x2 -> x0, starting transfers between devices: 8.47 us -> none  [body(): got = lax.all_to_all(p.reshape(ntp, ts, d), 'tp', 0, 0, tiled=True)]
  transfers between devices with their start and end apart: 5 -> 19, of which waited for: 2 -> 5; matrix products, arithmetic and copies ran while one was open for 35% -> 2% of each run, Pallas kernels for 0% -> 44%
where the time goes in v1:
time: 99.9 us; the launch traced here: 99.7 us
  Pallas kernels  52.8 us (53%)
  waiting for transfers between devices  26.2 us (26%)
  starting transfers between devices  14.3 us (14%)
  local copies, waits for them, and re-layouts  4.4 us (4%)
  between operations  1.06 us (1%)
    ppermute x18, waiting for transfers between devices, swap(): return lax.ppermute(a, 'tp', [(i, i ^ bit) for i in range(ntp)])  26.2 us
    pallas_call x1, Pallas kernels, _dw(): pl.pallas_call(functools.partial(_dw_kernel, lo, hi), out_shape=(jax.Shap...  15.5 us
    pallas_call x1, Pallas kernels, _u(): pl.pallas_call(functools.partial(_u_kernel, Z1), out_shape=(jax.ShapeDtyp...  13.6 us
    ppermute x18, starting transfers between devices, swap(): return lax.ppermute(a, 'tp', [(i, i ^ bit) for i in range(ntp)])  12.8 us
    pallas_call x1, Pallas kernels, _zeros(): pl.pallas_call(functools.partial(_zero_kernel, lo, hi), out_shape=jax.Sha...  8.14 us
    pallas_call x1, Pallas kernels, _index_call(): pl.pallas_call(functools.partial(_index_kernel, vs, ntp, first), out_shap...  6.68 us
    pallas_call x1, Pallas kernels, _p_terms(): pl.pallas_call(functools.partial(_p_kernel, ts), out_shape=(jax.ShapeDtyp...  4.59 us
    unnamed x26, local copies, waits for them, and re-layouts  3.11 us
  transfers between devices with their start and end apart: 19, of which 5 were waited for; matrix products, arithmetic and copies ran while one was open for 2% of the time, Pallas kernels for 44%

profile of v1, /device:TPU:0, one launch (start us, length us, event | category | flops | bytes accessed | tf_op | source)
XLA Modules:
  0.0 99.7 jit_solution(7350941316118166330)
XLA Ops:
  0.6 6.7 %index_gather.6 = (bf16[64,2304]{1,0:T(8,128)(2,1)S(1)}, f32[512,1]{1,0:T(8,128)S(1)}, f32[1,512]{1,0:T(1,128)S(1)}, s32[1,512]{1,0:T(1,128)S(1)}, s32[1,128]{1,0:T(1,128)S(1)}) custom-call(s32[2,256]{1,0:T(2,128)} %refs_0_.1, bf16[8192,2304]{1,0:T(8,128)(2,1)} %refs_1_.1), custom_call_target="tpu_custom_call" | custom-call | flops 20000000000 | bytes 1000000 | tf_op jit(solution)/shard_map/index_gather/pallas_call | solution.py:153
  7.3 0.7 copy-done.4
  8.0 3.0 %collective-permute-start.19 = (bf16[64,2304]{1,0:T(8,128)(2,1)S(1)}, bf16[64,2304]{1,0:T(8,128)(2,1)S(1)}, u32[]{:S(2)}, u32[]{:S(2)}) collective-permute-start(bf16[64,2304]{1,0:T(8,128)(2,1)S(1)} %get-tuple-element.250.refs_1_), channel_id=1, source_target_pairs={{0,2},{1,3},{2,0},{3,1},{4,6},{5,7},{6,4},{7,5}} | collective-permute-start | bytes 884744 | tf_op jit(solution)/shard_map/ppermute | solution.py:433
  11.0 1.6 %collective-permute-start.36 = (s32[1,128]{1,0:T(1,128)S(1)}, s32[1,128]{1,0:T(1,128)S(1)}, u32[]{:S(2)}, u32[]{:S(2)}) collective-permute-start(s32[1,128]{1,0:T(1,128)S(1)} %get-tuple-element.254.cnt_ref), channel_id=1, source_target_pairs={{0,4},{4,0},{1,5},{5,1},{2,6},{6,2},{3,7},{7,3}} | collective-permute-start | bytes 1544 | tf_op jit(solution)/shard_map/ppermute | solution.py:465
  12.6 5.6 %collective-permute-done.19.refs_3_ = bf16[64,2304]{1,0:T(8,128)(2,1)S(1)} collective-permute-done((bf16[64,2304]{1,0:T(8,128)(2,1)S(1)}, bf16[64,2304]{1,0:T(8,128)(2,1)S(1)}, u32[]{:S(2)}, u32[]{:S(2)}) %collective-permute-start.19) | collective-permute-done | bytes 294944 | tf_op jit(solution)/shard_map/ppermute | solution.py:433
  18.2 4.6 %p_terms.5 = (bf16[64,2304]{1,0:T(8,128)(2,1)S(1)}, bf16[64,2304]{1,0:T(8,128)(2,1)S(1)}, bf16[64,2304]{1,0:T(8,128)(2,1)S(1)}, bf16[64,2304]{1,0:T(8,128)(2,1)S...) custom-call(bf16[2,256,1024]{2,1,0:T(8,128)(2,1)} %du_ref.3, ...), custom_call_target="tpu_custom_call" | custom-call | flops 20000000000 | bytes 1000000 | tf_op jit(solution)/shard_map/p_terms/pallas_call | solution.py:230
  22.8 0.7 copy-done
  23.5 0.7 copy-done.2
  24.2 0.5 collective-permute-start.21
  24.8 1.3 %reshape.31.g_ref.g = bf16[1,2304]{1,0:T(2,128)(2,1)} reshape(bf16[2304]{0:T(1024)(128)(2,1)} %param.12) | data formatting | bytes 9216 | tf_op jit(solution)/shard_map/reshape | solution.py:460
  26.0 1.8 %collective-permute-start.22 = (bf16[64,2304]{1,0:T(8,128)(2,1)S(1)}, bf16[64,2304]{1,0:T(8,128)(2,1)S(1)}, u32[]{:S(2)}, u32[]{:S(2)}) collective-permute-start(bf16[64,2304]{1,0:T(8,128)(2,1)S(1)} %get-tuple-element.259), channel_id=1, source_target_pairs={{0,2},{1,3},{2,0},{3,1},{4,6},{5,7},{6,4},{7,5}} | collective-permute-start | bytes 884744 | tf_op jit(solution)/shard_map/ppermute | solution.py:433
  27.9 0.4 collective-permute-start.27
  28.3 0.9 copy-done.5
  29.2 0.9 expand.2
  30.2 1.8 %collective-permute-start.28 = (bf16[64,2304]{1,0:T(8,128)(2,1)S(1)}, bf16[64,2304]{1,0:T(8,128)(2,1)S(1)}, u32[]{:S(2)}, u32[]{:S(2)}) collective-permute-start(bf16[64,2304]{1,0:T(8,128)(2,1)S(1)} %get-tuple-element.264), channel_id=1, source_target_pairs={{0,2},{1,3},{2,0},{3,1},{4,6},{5,7},{6,4},{7,5}} | collective-permute-start | bytes 884744 | tf_op jit(solution)/shard_map/ppermute | solution.py:433
  32.0 4.0 %collective-permute-done.22.p2 = bf16[64,2304]{1,0:T(8,128)(2,1)S(1)} collective-permute-done((bf16[64,2304]{1,0:T(8,128)(2,1)S(1)}, bf16[64,2304]{1,0:T(8,128)(2,1)S(1)}, u32[]{:S(2)}, u32[]{:S(2)}) %collective-permute-start.22) | collective-permute-done | bytes 294944 | tf_op jit(solution)/shard_map/ppermute | solution.py:433
  35.9 5.6 %collective-permute-done.23.p3 = bf16[64,2304]{1,0:T(8,128)(2,1)S(1)} collective-permute-done((bf16[64,2304]{1,0:T(8,128)(2,1)S(1)}, bf16[64,2304]{1,0:T(8,128)(2,1)S(1)}, u32[]{:S(2)}, u32[]{:S(2)}) %collective-permute-start.23) | collective-permute-done | bytes 294944 | tf_op jit(solution)/shard_map/ppermute | solution.py:433
  41.6 0.6 dx_form.10
  42.2 6.4 %collective-permute-done.28.p2 = bf16[64,2304]{1,0:T(8,128)(2,1)S(1)} collective-permute-done((bf16[64,2304]{1,0:T(8,128)(2,1)S(1)}, bf16[64,2304]{1,0:T(8,128)(2,1)S(1)}, u32[]{:S(2)}, u32[]{:S(2)}) %collective-permute-start.28) | collective-permute-done | bytes 294944 | tf_op jit(solution)/shard_map/ppermute | solution.py:433
  48.6 4.6 %collective-permute-done.29.p3 = bf16[64,2304]{1,0:T(8,128)(2,1)S(1)} collective-permute-done((bf16[64,2304]{1,0:T(8,128)(2,1)S(1)}, bf16[64,2304]{1,0:T(8,128)(2,1)S(1)}, u32[]{:S(2)}, u32[]{:S(2)}) %collective-permute-start.29) | collective-permute-done | bytes 294944 | tf_op jit(solution)/shard_map/ppermute | solution.py:433
  53.2 0.6 dx_form.11
  53.8 1.9 %collective-permute-start.35 = (f32[1,2304]{1,0:T(1,128)S(1)}, f32[1,2304]{1,0:T(1,128)S(1)}, u32[]{:S(2)}, u32[]{:S(2)}) collective-permute-start(f32[1,2304]{1,0:T(1,128)S(1)} %get-tuple-element.272), channel_id=1, source_target_pairs={{0,3},{1,2},{2,1},{3,0},{4,7},{5,6},{6,5},{7,4}} | collective-permute-start | bytes 27656 | tf_op jit(solution)/shard_map/ppermute | solution.py:433
  55.8 0.3 collective-permute-start.34
  56.0 1.7 %collective-permute-start.25 = (bf16[64,2304]{1,0:T(8,128)(2,1)S(1)}, bf16[64,2304]{1,0:T(8,128)(2,1)S(1)}, u32[]{:S(2)}, u32[]{:S(2)}) collective-permute-start(bf16[64,2304]{1,0:T(8,128)(2,1)S(1)} %get-tuple-element.261.refs_0_), channel_id=1, source_target_pairs={{0,2},{1,3},{2,0},{3,1},{4,6},{5,7},{6,4},{7,5}} | collective-permute-start | bytes 884744 | tf_op jit(solution)/shard_map/ppermute | solution.py:433
  57.8 0.3 collective-permute-start.31
  58.1 13.6 %u_terms.5 = (bf16[2,256,1024]{2,1,0:T(8,128)(2,1)}, bf16[512,2304]{1,0:T(8,128)(2,1)S(1)}, f32[8192,2304]{1,0:T(8,128)}) custom-call(bf16[512,2304]{1,0:T(8,128)(2,1)S(1)} %get-tuple-element.251.x_ref, bf16[1,2304]{1,0:T(2,128)(2,1)S(1)} %copy-done.6, bf16[2304,1024]{1,0:T(8,128)(2,1)S(1)} %bitcast.11), custom_call_target="tpu_custom_call" | custom-call | flops 40000000000 | bytes 1000000 | tf_op jit(solution)/shard_map/u_terms/pallas_call | solution.py:322
  71.7 8.1 %zero_fill.2.de_in = f32[8192,2304]{1,0:T(8,128)} custom-call(f32[8192,2304]{1,0:T(8,128)} %get-tuple-element.269.de_in), custom_call_target="tpu_custom_call", output_to_operand_aliasing={{}: (0, {})} | custom-call | flops 30000001024 | bytes 1000000 | tf_op jit(solution)/shard_map/zero_fill/pallas_call | solution.py:258
  79.9 0.5 collective-permute-start.33
  80.4 0.5 collective-permute-start.26
  80.9 15.5 %dw_terms.5 = (f32[2304,1024]{1,0:T(8,128)}, f32[8192,2304]{1,0:T(8,128)}) custom-call(bf16[512,2304]{1,0:T(8,128)(2,1)S(1)} %get-tuple-element.268.n_ref, bf16[2,256,1024]{2,1,0:T(8,128)(2,1)} %du_ref.3, f32[8192,2304]{1,0:T(8,128)} %zero_fill.2.de_in), custom_call_target="tpu_custom_call", output_to_operand_aliasing={{1}: (2, {})} | custom-call | flops 40000000000 | bytes 1000000 | tf_op jit(solution)/shard_map/dw_terms/pallas_call | solution.py:360
  96.5 0.6 add_reduce_fusion.1
  97.2 2.1 %scatter_rows.5 = f32[8192,2304]{1,0:T(8,128)} custom-call(s32[1,128]{1,0:T(1,128)S(1)} %get-tuple-element.254.cnt_ref, s32[1,512]{1,0:T(1,128)S(1)} %get-tuple-element.255.list_ref, f32[1,512]{1,0:T(1,128)S(1)} %get-tuple-element.256.srow_ref, bf16[64,2304]{1,0:T(8,128)(2,1)S(1)} %get-tuple-element.261.refs_0_, ...), custom_call_target="tpu_custom_call", output_to_operand_aliasing={{}: (11, {})} | custom-call | flops 12000000000 | bytes 1000000 | tf_op jit(solution)/shard_map/scatter_rows/pallas_call | solution.py:415
  (45 shorter events, 0.4 us)
Async XLA Ops:
  0.6 17.6 %copy-start.8 = (bf16[2304,1024]{1,0:T(8,128)(2,1)S(1)}, bf16[2304,1024]{1,0:T(8,128)(2,1)}, u32[]{:S(2)}) copy-start(bf16[2304,1024]{1,0:T(8,128)(2,1)} %w_ref.3) | copy-start | bytes 14155780
  7.3 0.7 copy-start.4
  8.0 10.2 %collective-permute-start.19 = (bf16[64,2304]{1,0:T(8,128)(2,1)S(1)}, bf16[64,2304]{1,0:T(8,128)(2,1)S(1)}, u32[]{:S(2)}, u32[]{:S(2)}) collective-permute-start(bf16[64,2304]{1,0:T(8,128)(2,1)S(1)} %get-tuple-element.250.refs_1_), channel_id=1, source_target_pairs={{0,2},{1,3},{2,0},{3,1},{4,6},{5,7},{6,4},{7,5}} | collective-permute-start | bytes 884744 | tf_op jit(solution)/shard_map/ppermute | solution.py:433
  11.0 16.9 %collective-permute-start.18 = (bf16[64,2304]{1,0:T(8,128)(2,1)S(1)}, bf16[64,2304]{1,0:T(8,128)(2,1)S(1)}, u32[]{:S(2)}, u32[]{:S(2)}) collective-permute-start(bf16[64,2304]{1,0:T(8,128)(2,1)S(1)} %get-tuple-element.250.refs_1_), channel_id=1, source_target_pairs={{0,1},{1,0},{2,3},{3,2},{4,5},{5,4},{6,7},{7,6}} | collective-permute-start | bytes 884744 | tf_op jit(solution)/shard_map/ppermute | solution.py:433
  11.0 16.8 %collective-permute-start.36 = (s32[1,128]{1,0:T(1,128)S(1)}, s32[1,128]{1,0:T(1,128)S(1)}, u32[]{:S(2)}, u32[]{:S(2)}) collective-permute-start(s32[1,128]{1,0:T(1,128)S(1)} %get-tuple-element.254.cnt_ref), channel_id=1, source_target_pairs={{0,4},{4,0},{1,5},{5,1},{2,6},{6,2},{3,7},{7,3}} | collective-permute-start | bytes 1544 | tf_op jit(solution)/shard_map/ppermute | solution.py:465
  18.2 10.1 %collective-permute-start.20 = (bf16[64,2304]{1,0:T(8,128)(2,1)S(1)}, bf16[64,2304]{1,0:T(8,128)(2,1)S(1)}, u32[]{:S(2)}, u32[]{:S(2)}) collective-permute-start(bf16[64,2304]{1,0:T(8,128)(2,1)S(1)} %collective-permute-done.19.refs_3_), channel_id=1, source_target_pairs={{0,1},{1,0},{2,3},{3,2},{4,5},{5,4},{6,7},{7,6}} | collective-permute-start | bytes 884744 | tf_op jit(solution)/shard_map/ppermute | solution.py:433
  22.8 0.7 copy-start
  23.5 0.7 copy-start.2
  24.2 7.7 %collective-permute-start.21 = (bf16[64,2304]{1,0:T(8,128)(2,1)S(1)}, bf16[64,2304]{1,0:T(8,128)(2,1)S(1)}, u32[]{:S(2)}, u32[]{:S(2)}) collective-permute-start(bf16[64,2304]{1,0:T(8,128)(2,1)S(1)} %get-tuple-element.258), channel_id=1, source_target_pairs={{0,1},{1,0},{2,3},{3,2},{4,5},{5,4},{6,7},{7,6}} | collective-permute-start | bytes 884744 | tf_op jit(solution)/shard_map/ppermute | solution.py:433
  26.0 9.9 %collective-permute-start.22 = (bf16[64,2304]{1,0:T(8,128)(2,1)S(1)}, bf16[64,2304]{1,0:T(8,128)(2,1)S(1)}, u32[]{:S(2)}, u32[]{:S(2)}) collective-permute-start(bf16[64,2304]{1,0:T(8,128)(2,1)S(1)} %get-tuple-element.259), channel_id=1, source_target_pairs={{0,2},{1,3},{2,0},{3,1},{4,6},{5,7},{6,4},{7,5}} | collective-permute-start | bytes 884744 | tf_op jit(solution)/shard_map/ppermute | solution.py:433
  27.9 13.7 %collective-permute-start.23 = (bf16[64,2304]{1,0:T(8,128)(2,1)S(1)}, bf16[64,2304]{1,0:T(8,128)(2,1)S(1)}, u32[]{:S(2)}, u32[]{:S(2)}) collective-permute-start(bf16[64,2304]{1,0:T(8,128)(2,1)S(1)} %get-tuple-element.260), channel_id=1, source_target_pairs={{0,3},{1,2},{2,1},{3,0},{4,7},{5,6},{6,5},{7,4}} | collective-permute-start | bytes 884744 | tf_op jit(solution)/shard_map/ppermute | solution.py:433
  27.9 14.3 %collective-permute-start.27 = (bf16[64,2304]{1,0:T(8,128)(2,1)S(1)}, bf16[64,2304]{1,0:T(8,128)(2,1)S(1)}, u32[]{:S(2)}, u32[]{:S(2)}) collective-permute-start(bf16[64,2304]{1,0:T(8,128)(2,1)S(1)} %get-tuple-element.263), channel_id=1, source_target_pairs={{0,1},{1,0},{2,3},{3,2},{4,5},{5,4},{6,7},{7,6}} | collective-permute-start | bytes 884744 | tf_op jit(solution)/shard_map/ppermute | solution.py:433
  28.3 1.0 copy-start.5
  29.2 12.3 %copy-start.3 = (bf16[64,2304]{1,0:T(8,128)(2,1)S(1)}, bf16[64,2304]{1,0:T(8,128)(2,1)}, u32[]{:S(2)}) copy-start(bf16[64,2304]{1,0:T(8,128)(2,1)} %copy-done.2) | copy-start | bytes 884740
  29.2 12.3 %copy-start.6 = (bf16[1,2304]{1,0:T(2,128)(2,1)S(1)}, bf16[1,2304]{1,0:T(2,128)(2,1)}, u32[]{:S(2)}) copy-start(bf16[1,2304]{1,0:T(2,128)(2,1)} %reshape.31.g_ref.g) | copy-start | bytes 13828
  29.2 12.3 %copy-start.9 = (bf16[2,64,2304]{2,1,0:T(8,128)(2,1)S(1)}, bf16[2,64,2304]{2,1,0:T(8,128)(2,1)}, u32[]{:S(2)}) copy-start(bf16[2,64,2304]{2,1,0:T(8,128)(2,1)} %dres.3) | copy-start | bytes 1769476
  30.2 23.0 %copy-start.12 = (bf16[2,64,2304]{2,1,0:T(8,128)(2,1)}, bf16[2,64,2304]{2,1,0:T(8,128)(2,1)S(1)}, u32[]{:S(2)}) copy-start(bf16[2,64,2304]{2,1,0:T(8,128)(2,1)S(1)} %get-tuple-element.526.x) | copy-start | bytes 1769476
  30.2 18.4 %collective-permute-start.28 = (bf16[64,2304]{1,0:T(8,128)(2,1)S(1)}, bf16[64,2304]{1,0:T(8,128)(2,1)S(1)}, u32[]{:S(2)}, u32[]{:S(2)}) collective-permute-start(bf16[64,2304]{1,0:T(8,128)(2,1)S(1)} %get-tuple-element.264), channel_id=1, source_target_pairs={{0,2},{1,3},{2,0},{3,1},{4,6},{5,7},{6,4},{7,5}} | collective-permute-start | bytes 884744 | tf_op jit(solution)/shard_map/ppermute | solution.py:433
  32.0 21.2 %collective-permute-start.29 = (bf16[64,2304]{1,0:T(8,128)(2,1)S(1)}, bf16[64,2304]{1,0:T(8,128)(2,1)S(1)}, u32[]{:S(2)}, u32[]{:S(2)}) collective-permute-start(bf16[64,2304]{1,0:T(8,128)(2,1)S(1)} %get-tuple-element.265), channel_id=1, source_target_pairs={{0,3},{1,2},{2,1},{3,0},{4,7},{5,6},{6,5},{7,4}} | collective-permute-start | bytes 884744 | tf_op jit(solution)/shard_map/ppermute | solution.py:433
  41.5 11.7 %copy-start.1 = (bf16[64,2304]{1,0:T(8,128)(2,1)S(1)}, bf16[64,2304]{1,0:T(8,128)(2,1)}, u32[]{:S(2)}) copy-start(bf16[64,2304]{1,0:T(8,128)(2,1)} %copy-done) | copy-start | bytes 884740
  41.5 16.5 %slice-start = ((s8[4718592]{0:T(1024)(128)(4,1)}), s8[4194304]{0:T(1024)(128)(4,1)S(1)}, s32[]{:S(2)}) async-start(s8[4718592]{0:T(1024)(128)(4,1)} %bitcast.10), calls=%async_computation | async-start | bytes 8388608
  53.2 4.9 %slice-start.1 = ((s8[4718592]{0:T(1024)(128)(4,1)}), s8[524288]{0:T(1024)(128)(4,1)S(1)}, s32[]{:S(2)}) async-start(s8[4718592]{0:T(1024)(128)(4,1)} %bitcast.10), calls=%async_computation.1 | async-start | bytes 1048576
  53.8 26.0 %collective-permute-start.35 = (f32[1,2304]{1,0:T(1,128)S(1)}, f32[1,2304]{1,0:T(1,128)S(1)}, u32[]{:S(2)}, u32[]{:S(2)}) collective-permute-start(f32[1,2304]{1,0:T(1,128)S(1)} %get-tuple-element.272), channel_id=1, source_target_pairs={{0,3},{1,2},{2,1},{3,0},{4,7},{5,6},{6,5},{7,4}} | collective-permute-start | bytes 27656 | tf_op jit(solution)/shard_map/ppermute | solution.py:433
  55.8 24.6 %collective-permute-start.34 = (f32[1,2304]{1,0:T(1,128)S(1)}, f32[1,2304]{1,0:T(1,128)S(1)}, u32[]{:S(2)}, u32[]{:S(2)}) collective-permute-start(f32[1,2304]{1,0:T(1,128)S(1)} %get-tuple-element.272), channel_id=1, source_target_pairs={{0,2},{1,3},{2,0},{3,1},{4,6},{5,7},{6,4},{7,5}} | collective-permute-start | bytes 27656 | tf_op jit(solution)/shard_map/ppermute | solution.py:433
  56.0 24.4 %collective-permute-start.25 = (bf16[64,2304]{1,0:T(8,128)(2,1)S(1)}, bf16[64,2304]{1,0:T(8,128)(2,1)S(1)}, u32[]{:S(2)}, u32[]{:S(2)}) collective-permute-start(bf16[64,2304]{1,0:T(8,128)(2,1)S(1)} %get-tuple-element.261.refs_0_), channel_id=1, source_target_pairs={{0,2},{1,3},{2,0},{3,1},{4,6},{5,7},{6,4},{7,5}} | collective-permute-start | bytes 884744 | tf_op jit(solution)/shard_map/ppermute | solution.py:433
  57.8 23.1 %collective-permute-start.31 = (bf16[64,2304]{1,0:T(8,128)(2,1)S(1)}, bf16[64,2304]{1,0:T(8,128)(2,1)S(1)}, u32[]{:S(2)}, u32[]{:S(2)}) collective-permute-start(bf16[64,2304]{1,0:T(8,128)(2,1)S(1)} %get-tuple-element.267.refs_4_), channel_id=1, source_target_pairs={{0,2},{1,3},{2,0},{3,1},{4,6},{5,7},{6,4},{7,5}} | collective-permute-start | bytes 884744 | tf_op jit(solution)/shard_map/ppermute | solution.py:433
  79.8 17.3 %collective-permute-start.24 = (bf16[64,2304]{1,0:T(8,128)(2,1)S(1)}, bf16[64,2304]{1,0:T(8,128)(2,1)S(1)}, u32[]{:S(2)}, u32[]{:S(2)}) collective-permute-start(bf16[64,2304]{1,0:T(8,128)(2,1)S(1)} %get-tuple-element.261.refs_0_), channel_id=1, source_target_pairs={{0,1},{1,0},{2,3},{3,2},{4,5},{5,4},{6,7},{7,6}} | collective-permute-start | bytes 884744 | tf_op jit(solution)/shard_map/ppermute | solution.py:433
  79.9 16.6 %collective-permute-start.33 = (f32[1,2304]{1,0:T(1,128)S(1)}, f32[1,2304]{1,0:T(1,128)S(1)}, u32[]{:S(2)}, u32[]{:S(2)}) collective-permute-start(f32[1,2304]{1,0:T(1,128)S(1)} %get-tuple-element.272), channel_id=1, source_target_pairs={{0,1},{1,0},{2,3},{3,2},{4,5},{5,4},{6,7},{7,6}} | collective-permute-start | bytes 27656 | tf_op jit(solution)/shard_map/ppermute | solution.py:433
  80.4 16.8 %collective-permute-start.30 = (bf16[64,2304]{1,0:T(8,128)(2,1)S(1)}, bf16[64,2304]{1,0:T(8,128)(2,1)S(1)}, u32[]{:S(2)}, u32[]{:S(2)}) collective-permute-start(bf16[64,2304]{1,0:T(8,128)(2,1)S(1)} %get-tuple-element.267.refs_4_), channel_id=1, source_target_pairs={{0,1},{1,0},{2,3},{3,2},{4,5},{5,4},{6,7},{7,6}} | collective-permute-start | bytes 884744 | tf_op jit(solution)/shard_map/ppermute | solution.py:433
  80.4 16.7 %collective-permute-start.26 = (bf16[64,2304]{1,0:T(8,128)(2,1)S(1)}, bf16[64,2304]{1,0:T(8,128)(2,1)S(1)}, u32[]{:S(2)}, u32[]{:S(2)}) collective-permute-start(bf16[64,2304]{1,0:T(8,128)(2,1)S(1)} %collective-permute-done.25.refs_2_), channel_id=1, source_target_pairs={{0,1},{1,0},{2,3},{3,2},{4,5},{5,4},{6,7},{7,6}} | collective-permute-start | bytes 884744 | tf_op jit(solution)/shard_map/ppermute | solution.py:433
  80.9 16.3 %collective-permute-start.32 = (bf16[64,2304]{1,0:T(8,128)(2,1)S(1)}, bf16[64,2304]{1,0:T(8,128)(2,1)S(1)}, u32[]{:S(2)}, u32[]{:S(2)}) collective-permute-start(bf16[64,2304]{1,0:T(8,128)(2,1)S(1)} %collective-permute-done.31.refs_6_), channel_id=1, source_target_pairs={{0,1},{1,0},{2,3},{3,2},{4,5},{5,4},{6,7},{7,6}} | collective-permute-start | bytes 884744 | tf_op jit(solution)/shard_map/ppermute | solution.py:433
  97.1 2.2 %copy-start.11 = (s32[2,256]{1,0:T(2,128)S(1)}, s32[2,256]{1,0:T(2,128)}, u32[]{:S(2)}) copy-start(s32[2,256]{1,0:T(2,128)} %refs_0_.1) | copy-start | bytes 6148

commit v2 on v1

--- a/solution.py
+++ b/solution.py
@@ -11,9 +11,10 @@
 EPS = 1e-6
 C = 64
 G = 16
+GS = 16
 CB = 256
 ZR = 128
-Z1, Z2 = 24, 20
+ZP, ZU, ZZ = 8, 16, 24
 TB = 64
 
 F32 = jnp.float32
@@ -51,10 +52,10 @@
 
 def _index_kernel(vs, ntp, first, *refs):
     if first:
-        ids_ref, e_ref, tab_ref, pos_ref, srow_ref, list_ref, cnt_ref, buf, glv, gls, gsem, sem = refs
+        ids_ref, e_ref, tab_ref, pos_ref, srow_ref, list_ref, cnt_ref, buf, glv, gls, gsem, sems = refs
         base = 0.0
     else:
-        c_ref, ids_ref, e_ref, tab_ref, pos_ref, srow_ref, list_ref, cnt_ref, buf, glv, gls, gsem, sem = refs
+        c_ref, ids_ref, e_ref, tab_ref, pos_ref, srow_ref, list_ref, cnt_ref, buf, glv, gls, gsem, sems = refs
         base = (c_ref[0] * C).astype(F32)
     mei = _me()
     me = mei.astype(F32)
@@ -116,12 +117,15 @@
     cp.start()
     cp.wait()
 
-    def fetch(j, carry):
-        g = pl.multiple_of((gls[0, j] // G) * G, G)
-        pltpu.make_async_copy(e_ref.at[pl.ds(g, G)], buf.at[pl.ds(pl.multiple_of(j * G, G), G)], sem).start()
+    def fetch(q, j, carry):
+        j = q * GS + j
+        g = pl.multiple_of((gls[0, j] >> 4) << 4, G)
+        at = pl.multiple_of(j * G, G)
+        pltpu.make_async_copy(e_ref.at[pl.ds(g, G)], buf.at[pl.ds(at, G)], sems.at[q]).start()
         return carry
 
-    lax.fori_loop(0, C, fetch, 0, unroll=8)
+    for q in range(C // GS):
+        lax.fori_loop(0, GS, functools.partial(fetch, q), 0, unroll=8)
 
     srow_ref[...] = my_r
     full = jnp.zeros((8, ntok), F32)
@@ -137,13 +141,15 @@
         pos_ref[b * TB:(b + 1) * TB, :] = column(pos, b)
     lane1 = lax.broadcasted_iota(jnp.int32, (1, 128), 1)
     cnt_ref[...] = jnp.where(lane1 == 0, mx, cnt).astype(jnp.int32)
-    want = jnp.max(jnp.where(my_r == _iota((C, ntok), 0) + base, idr - lo, 0.0), axis=1, keepdims=True)
-    want = want - jnp.floor(want * (1.0 / G)) * G + _iota((C, 1), 0) * G
-    sel = jnp.where(_iota((C, C * G), 1) == want, 1.0, 0.0).astype(BF16)
-    pltpu.make_async_copy(e_ref.at[pl.ds(0, C * G)], buf, sem).wait()
-    for c in range(tab_ref.shape[1] // CB):
-        s = slice(c * CB, (c + 1) * CB)
-        tab_ref[:, s] = jnp.dot(sel, buf[:, s], preferred_element_type=F32).astype(BF16)
+    hit = jnp.where(my_r == _iota((C, ntok), 0) + base, idr - lo, 0.0)
+    want = jnp.max(hit, axis=1, keepdims=True)
+    want = want - jnp.floor(want * (1.0 / G)) * G
+    for q in range(C // GS):
+        r = slice(q * GS * G, (q + 1) * GS * G)
+        mine = want[q * GS:(q + 1) * GS] + _iota((GS, 1), 0) * G
+        sel = jnp.where(_iota((GS, GS * G), 1) == mine, 1.0, 0.0).astype(BF16)
+        pltpu.make_async_copy(e_ref.at[pl.ds(0, GS * G)], buf.at[r], sems.at[q]).wait()
+        tab_ref[q * GS:(q + 1) * GS, :] = jnp.dot(sel, buf[r, :], preferred_element_type=F32).astype(BF16)
 
 
 def _index_call(chunk, ids, E, ntp):
@@ -166,7 +172,7 @@
             VMEM((8, 128), jnp.int32),
             pltpu.SMEM((8, 128), jnp.int32),
             pltpu.SemaphoreType.DMA,
-            pltpu.SemaphoreType.DMA,
+            pltpu.SemaphoreType.DMA((C // GS,)),
         ],
         compiler_params=_params(14),
         cost_estimate=_cost(5),
@@ -207,63 +213,77 @@
     )(*ins)
 
 
+def _fill(z, o, sems, lo, first, n, wait):
+    def step(i, carry):
+        at = pl.multiple_of((lo + i) * ZR, ZR)
+        c = pltpu.make_async_copy(z, o.at[pl.ds(at, ZR)], sems.at[i])
+        c.wait() if wait else c.start()
+        return carry
+
+    lax.fori_loop(first, first + n, step, 0)
+
+
+def _zscratch(d, n):
+    return [VMEM((ZR, d), F32), pltpu.SemaphoreType.DMA((n,))]
+
+
 def _p_kernel(ts, du_ref, w_ref, *refs):
-    outs, dur = refs[:-1], refs[-1]
+    outs, (de, dur, z, sems) = refs[:-4], refs[-4:]
     nk = du_ref.shape[0]
 
     @pl.when(pl.program_id(0) == 0)
     def _():
+        z[...] = jnp.zeros_like(z)
         for k in range(nk):
             for r in range(4):
                 at = pl.multiple_of((_me() ^ r) * ts, ts)
                 dur[pl.ds((k * 4 + r) * ts, ts), :] = du_ref[k, pl.ds(at, ts), :]
+        _fill(z, de, sems, 0, 0, ZP, False)
 
     out = lax.dot_general(dur[...], w_ref[...], (((1,), (1,)), ((), ())), preferred_element_type=F32)
     for i, o in enumerate(outs):
         o[...] = out[i * ts:(i + 1) * ts].astype(BF16)
 
-
-def _p_terms(du, W, ts):
+    @pl.when(pl.program_id(0) == pl.num_programs(0) - 1)
+    def _():
+        _fill(z, de, sems, 0, 0, ZP, True)
+
+
+def _p_terms(du, W, ts, vs):
     nk, t, f = du.shape
     d = W.shape[0]
     cb = 3 * CB
     out = pl.pallas_call(
         functools.partial(_p_kernel, ts),
-        out_shape=(jax.ShapeDtypeStruct((ts, d), BF16),) * (4 * nk),
+        out_shape=(jax.ShapeDtypeStruct((ts, d), BF16),) * (4 * nk) + (jax.ShapeDtypeStruct((vs, d), F32),),
         grid=(d // cb,),
         in_specs=[pl.BlockSpec((nk, t, f), lambda i: (0, 0, 0)), pl.BlockSpec((cb, f), lambda i: (i, 0))],
-        out_specs=(pl.BlockSpec((ts, cb), lambda i: (0, i)),) * (4 * nk),
-        scratch_shapes=[VMEM((nk * t, f), BF16)],
+        out_specs=(pl.BlockSpec((ts, cb), lambda i: (0, i)),) * (4 * nk) + (_any(),),
+        scratch_shapes=[VMEM((nk * t, f), BF16)] + _zscratch(d, ZP),
         compiler_params=_params(20),
         cost_estimate=_cost(5),
         name="p_terms",
     )(du, W)
-    return [out[4 * k:4 * k + 4] for k in range(nk)]
-
-
-def _fill(z, o, sems, lo, hi, wait):
-    for i in range(lo, hi):
-        c = pltpu.make_async_copy(z, o.at[pl.ds(i * ZR, ZR)], sems.at[i - lo])
-        c.wait() if wait else c.start()
-
-
-def _zero_kernel(lo, hi, de_in, o, z, sems):
+    return [out[4 * k:4 * k + 4] for k in range(nk)], out[-1]
+
+
+def _zero_kernel(lo, n, de_in, o, z, sems):
     z[...] = jnp.zeros_like(z)
-    _fill(z, o, sems, lo, hi, False)
-    _fill(z, o, sems, lo, hi, True)
-
-
-def _zeros(de, lo, hi):
+    _fill(z, o, sems, lo, 0, n, False)
+    _fill(z, o, sems, lo, 0, n, True)
+
+
+def _zeros(de, lo, n):
     vs, d = de.shape
     return pl.pallas_call(
-        functools.partial(_zero_kernel, lo, hi),
+        functools.partial(_zero_kernel, lo, n),
         out_shape=jax.ShapeDtypeStruct((vs, d), F32),
         in_specs=[_any()],
         out_specs=_any(),
-        scratch_shapes=[VMEM((ZR, d), F32), pltpu.SemaphoreType.DMA((hi - lo,))],
+        scratch_shapes=_zscratch(d, n),
         input_output_aliases={0: 0},
         compiler_params=_params(4),
-        cost_estimate=_cost((hi - lo) * 0.375),
+        cost_estimate=_cost(n * 0.375),
         name="zero_fill",
     )(de)
 
@@ -297,10 +317,9 @@
     )(x, *ps, dres, g, *prev)
 
 
-def _u_kernel(zn, x_ref, g_ref, w_ref, *refs):
-    u_ref, n_ref, de, z, sems = refs[-5:]
+def _u_kernel(x_ref, g_ref, w_ref, de_in, u_ref, n_ref, de, z, sems):
     z[...] = jnp.zeros_like(z)
-    _fill(z, de, sems, 0, zn, False)
+    _fill(z, de, sems, ZP, 0, ZU, False)
     rows = 64
     for b in range(n_ref.shape[0] // rows):
         s = slice(b * rows, (b + 1) * rows)
@@ -313,61 +332,62 @@
         out = jnp.dot(n_ref[...], w_ref[:, s], preferred_element_type=F32).astype(BF16)
         for k in range(nk):
             u_ref[k, :, s] = out[k * t:(k + 1) * t]
-    _fill(z, de, sems, 0, zn, True)
-
-
-def _u(x, g, W, vs, nk, de):
+    _fill(z, de, sems, ZP, 0, ZU, True)
+
+
+def _u(x, g, W, nk, de):
     ntok, d = x.shape
     f = W.shape[1]
     return pl.pallas_call(
-        functools.partial(_u_kernel, Z1),
+        _u_kernel,
         out_shape=(
             jax.ShapeDtypeStruct((nk, ntok // nk, f), BF16),
             jax.ShapeDtypeStruct((ntok, d), BF16),
-            jax.ShapeDtypeStruct((vs, d), F32),
+            jax.ShapeDtypeStruct(de.shape, F32),
         ),
-        in_specs=[_vm(), _vm(), _vm()] + [_any()] * len(de),
+        in_specs=[_vm(), _vm(), _vm(), _any()],
         out_specs=(_vm(), _vm(), _any()),
-        scratch_shapes=[VMEM((ZR, d), F32), pltpu.SemaphoreType.DMA((Z1,))],
-        input_output_aliases={3: 2} if de else {},
+        scratch_shapes=_zscratch(d, ZU),
+        input_output_aliases={3: 2},
         compiler_params=_params(20),
         cost_estimate=_cost(10),
         name="u_terms",
-    )(x, g, W, *de)
-
-
-def _dw_kernel(lo, hi, n_ref, du_ref, de_in, dw_ref, de, z, sems):
+    )(x, g, W, de)
+
+
+def _dw_kernel(lo, n, per, n_ref, du_ref, de_in, dw_ref, de, z, sems):
     i = pl.program_id(0)
     nk, t, f = du_ref.shape
 
     @pl.when(i == 0)
     def _():
         z[...] = jnp.zeros_like(z)
-        _fill(z, de, sems, lo, hi, False)
-
+
+    _fill(z, de, sems, lo, i * per, jnp.minimum(per, n - i * per), False)
     dw_ref[...] = lax.dot_general(
         n_ref[...], du_ref[...].reshape(nk * t, f), (((0,), (0,)), ((), ())), preferred_element_type=F32
     )
 
     @pl.when(i == pl.num_programs(0) - 1)
     def _():
-        _fill(z, de, sems, lo, hi, True)
-
-
-def _dw(n, du, de, lo, hi):
+        _fill(z, de, sems, lo, 0, n, True)
+
+
+def _dw(n, du, de, lo, nz):
     nk, t, f = du.shape
     ntok, d = n.shape
-    return pl.pallas_call(
-        functools.partial(_dw_kernel, lo, hi),
+    steps = d // CB
+    return pl.pallas_call(
+        functools.partial(_dw_kernel, lo, nz, -(-nz // steps)),
         out_shape=(jax.ShapeDtypeStruct((d, f), F32), jax.ShapeDtypeStruct(de.shape, F32)),
-        grid=(d // CB,),
+        grid=(steps,),
         in_specs=[
             pl.BlockSpec((ntok, CB), lambda i: (0, i)),
             pl.BlockSpec((nk, t, f), lambda i: (0, 0, 0)),
             _any(),
         ],
         out_specs=(pl.BlockSpec((CB, f), lambda i: (i, 0)), _any()),
-        scratch_shapes=[VMEM((ZR, d), F32), pltpu.SemaphoreType.DMA((hi - lo,))],
+        scratch_shapes=_zscratch(d, nz),
         input_output_aliases={2: 1},
         compiler_params=_params(20),
         cost_estimate=_cost(10),
@@ -437,19 +457,20 @@
         t1 = swap(t, 1)
         return t, t1, t2, swap(t2, 1)
 
-    def p_terms(du, W, ts):
-        ps = _p_terms(du, W, ts)
-        return [(q[0], swap(q[1], 1), swap(q[2], 2), swap(q[3], 3)) for q in ps]
-
-    def finish(x, xl, ps, g2, W, du, dres, cnts, rows, srow, vs, de):
+    def p_terms(du, W, ts, vs):
+        ps, de = _p_terms(du, W, ts, vs)
+        return de, [(q[0], swap(q[1], 1), swap(q[2], 2), swap(q[3], 3)) for q in ps]
+
+    def finish(x, xl, de_ps, g2, W, du, dres, cnts, rows, srow):
         nk, ts, d = xl.shape
-        nz = vs // ZR
-        u, n, de = _u(x, g2, W, vs, nk, de)
+        de, ps = de_ps
+        u, n, de = _u(x, g2, W, nk, de)
         dx0, dg0 = _dx(xl, ps[0], dres, g2, 0, ())
-        de = _zeros(de, Z1, Z1 + Z2)
+        de = _zeros(de, ZP + ZU, ZZ)
         dx1, dgp = _dx(xl, ps[1], dres, g2, 1, (dg0,))
         pieces = share(dx0) + share(dx1)
-        dW, de = _dw(n, du, de, Z1 + Z2, nz)
+        done = ZP + ZU + ZZ
+        dW, de = _dw(n, du, de, done, de.shape[0] // ZR - done)
         dg = ((dgp + swap(dgp, 1)) + (swap(dgp, 2) + swap(dgp, 3))).reshape(d)
         dE = _scatter(cnts, rows, srow, pieces, de, ts, nk)
         return u, xl, dE, dW, dg
@@ -461,16 +482,16 @@
 
         tab, pos, srow, rows, cnts = _index_call(None, ids, E, ntp)
         tabs = share(tab)
-        ps = p_terms(du, W, ts)
+        de_ps = p_terms(du, W, ts, vs)
         other = lax.ppermute(cnts, "dp", [(i, (i + 1) % ndp) for i in range(ndp)])
         x, xl = _expand(pos, tabs, ts)
-        outs = finish(x, xl, ps, g2, W, du, dres, cnts, rows, srow, vs, ())
+        outs = finish(x, xl, de_ps, g2, W, du, dres, cnts, rows, srow)
         rounds = (jnp.maximum(cnts[0, 0], other[0, 0]) + C - 1) // C
 
         inputs = ids, E, W, du, dres, g2
 
         def again(c):
-            once, (_, _, de, _, _) = c
+            once, _ = c
             ids, E, W, du, dres, g2, once = lax.optimization_barrier((*inputs, once))
 
             def more(q):
@@ -481,7 +502,7 @@
             zeros = jnp.zeros(x.shape, BF16), jnp.zeros(xl.shape, BF16)
             _, xa, xla = lax.while_loop(lambda q: q[0] < rounds, more, (jnp.int32(0), *zeros))
             _, _, srow, rows, cnts = _index_call(once - 1, ids, E, ntp)
-            return rounds, finish(xa, xla, p_terms(du, W, ts), g2, W, du, dres, cnts, rows, srow, vs, (de,))
+            return rounds, finish(xa, xla, p_terms(du, W, ts, vs), g2, W, du, dres, cnts, rows, srow)
 
         _, outs = lax.while_loop(lambda c: c[0] < rounds, again, (jnp.int32(1), outs))
         return outs

time: 99.9 us -> 90.9 us (0.910)
  Pallas kernels: 52.8 us -> 43.8 us
    pallas_call x3, Pallas kernels: 37.3 us -> 28.4 us  [the longest x1 11.1 us: _dw(): pl.pallas_call(functools.partial(_dw_kernel, lo, nz, -(-nz // steps)), ou...]
  transfers between devices with their start and end apart: 19 -> 19, of which waited for: 5 -> 5; matrix products, arithmetic and copies ran while one was open for 2% -> 2% of each run, Pallas kernels for 44% -> 39%
where the time goes in v2:
time: 90.9 us; the launch traced here: 90.6 us
  Pallas kernels  43.8 us (48%)
  waiting for transfers between devices  26.2 us (29%)
  starting transfers between devices  14.3 us (16%)
  local copies, waits for them, and re-layouts  4.4 us (5%)
  between operations  1.06 us (1%)
    ppermute x18, waiting for transfers between devices, swap(): return lax.ppermute(a, 'tp', [(i, i ^ bit) for i in range(ntp)])  26.2 us
    ppermute x18, starting transfers between devices, swap(): return lax.ppermute(a, 'tp', [(i, i ^ bit) for i in range(ntp)])  12.7 us
    pallas_call x1, Pallas kernels, _dw(): pl.pallas_call(functools.partial(_dw_kernel, lo, nz, -(-nz // steps)), ou...  11.1 us
    pallas_call x1, Pallas kernels, _zeros(): pl.pallas_call(functools.partial(_zero_kernel, lo, n), out_shape=jax.Shap...  9.6 us
    pallas_call x1, Pallas kernels, _u(): pl.pallas_call(_u_kernel, out_shape=(jax.ShapeDtypeStruct((nk, ntok // nk...  7.65 us
    pallas_call x1, Pallas kernels, _index_call(): pl.pallas_call(functools.partial(_index_kernel, vs, ntp, first), out_shap...  6.03 us
    pallas_call x1, Pallas kernels, _p_terms(): pl.pallas_call(functools.partial(_p_kernel, ts), out_shape=(jax.ShapeDtyp...  5.16 us
    unnamed x26, local copies, waits for them, and re-layouts  3.11 us
  transfers between devices with their start and end apart: 19, of which 5 were waited for; matrix products, arithmetic and copies ran while one was open for 2% of the time, Pallas kernels for 39%

profile of v2, /device:TPU:0, one launch (start us, length us, event | category | flops | bytes accessed | tf_op | source)
XLA Modules:
  0.0 90.6 jit_solution(9543091442884174882)
XLA Ops:
  0.6 6.0 %index_gather.6 = (bf16[64,2304]{1,0:T(8,128)(2,1)S(1)}, f32[512,1]{1,0:T(8,128)S(1)}, f32[1,512]{1,0:T(1,128)S(1)}, s32[1,512]{1,0:T(1,128)S(1)}, s32[1,128]{1,0:T(1,128)S(1)}) custom-call(s32[2,256]{1,0:T(2,128)} %refs_0_.1, bf16[8192,2304]{1,0:T(8,128)(2,1)} %refs_1_.1), custom_call_target="tpu_custom_call" | custom-call | flops 20000000000 | bytes 1000000 | tf_op jit(solution)/shard_map/index_gather/pallas_call | solution.py:159
  6.7 0.7 copy-done.4
  7.4 3.0 %collective-permute-start.19 = (bf16[64,2304]{1,0:T(8,128)(2,1)S(1)}, bf16[64,2304]{1,0:T(8,128)(2,1)S(1)}, u32[]{:S(2)}, u32[]{:S(2)}) collective-permute-start(bf16[64,2304]{1,0:T(8,128)(2,1)S(1)} %get-tuple-element.250.refs_1_), channel_id=1, source_target_pairs={{0,2},{1,3},{2,0},{3,1},{4,6},{5,7},{6,4},{7,5}} | collective-permute-start | bytes 884744 | tf_op jit(solution)/shard_map/ppermute | solution.py:453
  10.4 1.6 %collective-permute-start.36 = (s32[1,128]{1,0:T(1,128)S(1)}, s32[1,128]{1,0:T(1,128)S(1)}, u32[]{:S(2)}, u32[]{:S(2)}) collective-permute-start(s32[1,128]{1,0:T(1,128)S(1)} %get-tuple-element.255.cnt_ref), channel_id=1, source_target_pairs={{0,4},{4,0},{1,5},{5,1},{2,6},{6,2},{3,7},{7,3}} | collective-permute-start | bytes 1544 | tf_op jit(solution)/shard_map/ppermute | solution.py:486
  12.0 5.6 %collective-permute-done.19.refs_3_ = bf16[64,2304]{1,0:T(8,128)(2,1)S(1)} collective-permute-done((bf16[64,2304]{1,0:T(8,128)(2,1)S(1)}, bf16[64,2304]{1,0:T(8,128)(2,1)S(1)}, u32[]{:S(2)}, u32[]{:S(2)}) %collective-permute-start.19) | collective-permute-done | bytes 294944 | tf_op jit(solution)/shard_map/ppermute | solution.py:453
  17.5 5.2 %p_terms.5 = (bf16[64,2304]{1,0:T(8,128)(2,1)S(1)}, bf16[64,2304]{1,0:T(8,128)(2,1)S(1)}, bf16[64,2304]{1,0:T(8,128)(2,1)S(1)}, bf16[64,2304]{1,0:T(8,128)(2,1)S...) custom-call(bf16[2,256,1024]{2,1,0:T(8,128)(2,1)} %du_ref.3, ...), custom_call_target="tpu_custom_call" | custom-call | flops 20000000000 | bytes 1000000 | tf_op jit(solution)/shard_map/p_terms/pallas_call | solution.py:256
  22.7 0.7 copy-done
  23.4 0.7 copy-done.2
  24.1 0.5 collective-permute-start.21
  24.6 1.3 %reshape.31.g_ref.g = bf16[1,2304]{1,0:T(2,128)(2,1)} reshape(bf16[2304]{0:T(1024)(128)(2,1)} %param.12) | data formatting | bytes 9216 | tf_op jit(solution)/shard_map/reshape | solution.py:481
  25.9 1.7 %collective-permute-start.22 = (bf16[64,2304]{1,0:T(8,128)(2,1)S(1)}, bf16[64,2304]{1,0:T(8,128)(2,1)S(1)}, u32[]{:S(2)}, u32[]{:S(2)}) collective-permute-start(bf16[64,2304]{1,0:T(8,128)(2,1)S(1)} %get-tuple-element.260), channel_id=1, source_target_pairs={{0,2},{1,3},{2,0},{3,1},{4,6},{5,7},{6,4},{7,5}} | collective-permute-start | bytes 884744 | tf_op jit(solution)/shard_map/ppermute | solution.py:453
  27.8 0.4 collective-permute-start.27
  28.2 0.9 %copy-done.5 = f32[512,1]{1,0:T(8,128)S(1)} copy-done((f32[512,1]{1,0:T(8,128)S(1)}, f32[512,1]{1,0:T(8,128)}, u32[]{:S(2)}) %copy-start.5) | copy-done | bytes 2072
  29.1 0.9 %expand.2 = (bf16[512,2304]{1,0:T(8,128)(2,1)S(1)}, bf16[2,64,2304]{2,1,0:T(8,128)(2,1)S(1)}) custom-call(f32[512,1]{1,0:T(8,128)S(1)} %copy-done.5, bf16[64,2304]{1,0:T(8,128)(2,1)S(1)} %get-tuple-element.250.refs_1_, bf16[64,2304]{1,0:T(8,128)(2,1)S(1)} %collective-permute-done.18.refs_2_, bf16[64,2304]{1,0:T(8,128)(2,1)S(1)} %collective-permute-done.19.refs_3_, ...), custom_call_target="tpu_custom_call" | custom-call | flops 12000000000 | bytes 1000000 | tf_op jit(solution)/shard_map/expand/pallas_call | solution.py:205
  30.1 1.8 %collective-permute-start.28 = (bf16[64,2304]{1,0:T(8,128)(2,1)S(1)}, bf16[64,2304]{1,0:T(8,128)(2,1)S(1)}, u32[]{:S(2)}, u32[]{:S(2)}) collective-permute-start(bf16[64,2304]{1,0:T(8,128)(2,1)S(1)} %get-tuple-element.265), channel_id=1, source_target_pairs={{0,2},{1,3},{2,0},{3,1},{4,6},{5,7},{6,4},{7,5}} | collective-permute-start | bytes 884744 | tf_op jit(solution)/shard_map/ppermute | solution.py:453
  31.8 4.0 %collective-permute-done.22.p2 = bf16[64,2304]{1,0:T(8,128)(2,1)S(1)} collective-permute-done((bf16[64,2304]{1,0:T(8,128)(2,1)S(1)}, bf16[64,2304]{1,0:T(8,128)(2,1)S(1)}, u32[]{:S(2)}, u32[]{:S(2)}) %collective-permute-start.22) | collective-permute-done | bytes 294944 | tf_op jit(solution)/shard_map/ppermute | solution.py:453
  35.8 5.6 %collective-permute-done.23.p3 = bf16[64,2304]{1,0:T(8,128)(2,1)S(1)} collective-permute-done((bf16[64,2304]{1,0:T(8,128)(2,1)S(1)}, bf16[64,2304]{1,0:T(8,128)(2,1)S(1)}, u32[]{:S(2)}, u32[]{:S(2)}) %collective-permute-start.23) | collective-permute-done | bytes 294944 | tf_op jit(solution)/shard_map/ppermute | solution.py:453
  41.4 0.6 dx_form.10
  42.1 6.4 %collective-permute-done.28.p2 = bf16[64,2304]{1,0:T(8,128)(2,1)S(1)} collective-permute-done((bf16[64,2304]{1,0:T(8,128)(2,1)S(1)}, bf16[64,2304]{1,0:T(8,128)(2,1)S(1)}, u32[]{:S(2)}, u32[]{:S(2)}) %collective-permute-start.28) | collective-permute-done | bytes 294944 | tf_op jit(solution)/shard_map/ppermute | solution.py:453
  48.5 4.6 %collective-permute-done.29.p3 = bf16[64,2304]{1,0:T(8,128)(2,1)S(1)} collective-permute-done((bf16[64,2304]{1,0:T(8,128)(2,1)S(1)}, bf16[64,2304]{1,0:T(8,128)(2,1)S(1)}, u32[]{:S(2)}, u32[]{:S(2)}) %collective-permute-start.29) | collective-permute-done | bytes 294944 | tf_op jit(solution)/shard_map/ppermute | solution.py:453
  53.1 0.6 dx_form.11
  53.7 1.9 %collective-permute-start.35 = (f32[1,2304]{1,0:T(1,128)S(1)}, f32[1,2304]{1,0:T(1,128)S(1)}, u32[]{:S(2)}, u32[]{:S(2)}) collective-permute-start(f32[1,2304]{1,0:T(1,128)S(1)} %get-tuple-element.273), channel_id=1, source_target_pairs={{0,3},{1,2},{2,1},{3,0},{4,7},{5,6},{6,5},{7,4}} | collective-permute-start | bytes 27656 | tf_op jit(solution)/shard_map/ppermute | solution.py:453
  55.6 0.3 collective-permute-start.34
  55.9 1.7 %collective-permute-start.25 = (bf16[64,2304]{1,0:T(8,128)(2,1)S(1)}, bf16[64,2304]{1,0:T(8,128)(2,1)S(1)}, u32[]{:S(2)}, u32[]{:S(2)}) collective-permute-start(bf16[64,2304]{1,0:T(8,128)(2,1)S(1)} %get-tuple-element.262.refs_0_), channel_id=1, source_target_pairs={{0,2},{1,3},{2,0},{3,1},{4,6},{5,7},{6,4},{7,5}} | collective-permute-start | bytes 884744 | tf_op jit(solution)/shard_map/ppermute | solution.py:453
  57.7 0.3 collective-permute-start.31
  58.0 7.7 %u_terms.5 = (bf16[2,256,1024]{2,1,0:T(8,128)(2,1)}, bf16[512,2304]{1,0:T(8,128)(2,1)S(1)}, f32[8192,2304]{1,0:T(8,128)}) custom-call(bf16[512,2304]{1,0:T(8,128)(2,1)S(1)} %get-tuple-element.251.x_ref, bf16[1,2304]{1,0:T(2,128)(2,1)S(1)} %copy-done.6, bf16[2304,1024]{1,0:T(8,128)(2,1)S(1)} %bitcast.11, ...), custom_call_target="tpu_custom_call", output_to_operand_aliasing={{2}: (3, {})} | custom-call | flops 40000000000 | bytes 1000000 | tf_op jit(solution)/shard_map/u_terms/pallas_call | solution.py:341
  65.6 9.6 %zero_fill.2.de_in = f32[8192,2304]{1,0:T(8,128)} custom-call(f32[8192,2304]{1,0:T(8,128)} %get-tuple-element.270.de_in), custom_call_target="tpu_custom_call", output_to_operand_aliasing={{}: (0, {})} | custom-call | flops 35999997952 | bytes 1000000 | tf_op jit(solution)/shard_map/zero_fill/pallas_call | solution.py:278
  75.3 0.5 collective-permute-start.33
  75.8 0.5 collective-permute-start.26
  76.3 11.1 %dw_terms.5 = (f32[2304,1024]{1,0:T(8,128)}, f32[8192,2304]{1,0:T(8,128)}) custom-call(bf16[512,2304]{1,0:T(8,128)(2,1)S(1)} %get-tuple-element.269.n_ref, bf16[2,256,1024]{2,1,0:T(8,128)(2,1)} %du_ref.3, f32[8192,2304]{1,0:T(8,128)} %zero_fill.2.de_in), custom_call_target="tpu_custom_call", output_to_operand_aliasing={{1}: (2, {})} | custom-call | flops 40000000000 | bytes 1000000 | tf_op jit(solution)/shard_map/dw_terms/pallas_call | solution.py:380
  87.5 0.6 add_reduce_fusion.1
  88.1 2.1 %scatter_rows.5 = f32[8192,2304]{1,0:T(8,128)} custom-call(s32[1,128]{1,0:T(1,128)S(1)} %get-tuple-element.255.cnt_ref, s32[1,512]{1,0:T(1,128)S(1)} %get-tuple-element.256.list_ref, f32[1,512]{1,0:T(1,128)S(1)} %get-tuple-element.257.srow_ref, bf16[64,2304]{1,0:T(8,128)(2,1)S(1)} %get-tuple-element.262.refs_0_, ...), custom_call_target="tpu_custom_call", output_to_operand_aliasing={{}: (11, {})} | custom-call | flops 12000000000 | bytes 1000000 | tf_op jit(solution)/shard_map/scatter_rows/pallas_call | solution.py:435
  (45 shorter events, 0.4 us)
Async XLA Ops:
  0.6 16.9 %copy-start.8 = (bf16[2304,1024]{1,0:T(8,128)(2,1)S(1)}, bf16[2304,1024]{1,0:T(8,128)(2,1)}, u32[]{:S(2)}) copy-start(bf16[2304,1024]{1,0:T(8,128)(2,1)} %w_ref.3) | copy-start | bytes 14155780
  6.7 0.7 copy-start.4
  7.4 10.2 %collective-permute-start.19 = (bf16[64,2304]{1,0:T(8,128)(2,1)S(1)}, bf16[64,2304]{1,0:T(8,128)(2,1)S(1)}, u32[]{:S(2)}, u32[]{:S(2)}) collective-permute-start(bf16[64,2304]{1,0:T(8,128)(2,1)S(1)} %get-tuple-element.250.refs_1_), channel_id=1, source_target_pairs={{0,2},{1,3},{2,0},{3,1},{4,6},{5,7},{6,4},{7,5}} | collective-permute-start | bytes 884744 | tf_op jit(solution)/shard_map/ppermute | solution.py:453
  10.4 17.4 %collective-permute-start.18 = (bf16[64,2304]{1,0:T(8,128)(2,1)S(1)}, bf16[64,2304]{1,0:T(8,128)(2,1)S(1)}, u32[]{:S(2)}, u32[]{:S(2)}) collective-permute-start(bf16[64,2304]{1,0:T(8,128)(2,1)S(1)} %get-tuple-element.250.refs_1_), channel_id=1, source_target_pairs={{0,1},{1,0},{2,3},{3,2},{4,5},{5,4},{6,7},{7,6}} | collective-permute-start | bytes 884744 | tf_op jit(solution)/shard_map/ppermute | solution.py:453
  10.4 17.3 %collective-permute-start.36 = (s32[1,128]{1,0:T(1,128)S(1)}, s32[1,128]{1,0:T(1,128)S(1)}, u32[]{:S(2)}, u32[]{:S(2)}) collective-permute-start(s32[1,128]{1,0:T(1,128)S(1)} %get-tuple-element.255.cnt_ref), channel_id=1, source_target_pairs={{0,4},{4,0},{1,5},{5,1},{2,6},{6,2},{3,7},{7,3}} | collective-permute-start | bytes 1544 | tf_op jit(solution)/shard_map/ppermute | solution.py:486
  17.5 10.6 %collective-permute-start.20 = (bf16[64,2304]{1,0:T(8,128)(2,1)S(1)}, bf16[64,2304]{1,0:T(8,128)(2,1)S(1)}, u32[]{:S(2)}, u32[]{:S(2)}) collective-permute-start(bf16[64,2304]{1,0:T(8,128)(2,1)S(1)} %collective-permute-done.19.refs_3_), channel_id=1, source_target_pairs={{0,1},{1,0},{2,3},{3,2},{4,5},{5,4},{6,7},{7,6}} | collective-permute-start | bytes 884744 | tf_op jit(solution)/shard_map/ppermute | solution.py:453
  22.7 0.7 copy-start
  23.4 0.7 copy-start.2
  24.1 7.7 %collective-permute-start.21 = (bf16[64,2304]{1,0:T(8,128)(2,1)S(1)}, bf16[64,2304]{1,0:T(8,128)(2,1)S(1)}, u32[]{:S(2)}, u32[]{:S(2)}) collective-permute-start(bf16[64,2304]{1,0:T(8,128)(2,1)S(1)} %get-tuple-element.259), channel_id=1, source_target_pairs={{0,1},{1,0},{2,3},{3,2},{4,5},{5,4},{6,7},{7,6}} | collective-permute-start | bytes 884744 | tf_op jit(solution)/shard_map/ppermute | solution.py:453
  25.9 9.9 %collective-permute-start.22 = (bf16[64,2304]{1,0:T(8,128)(2,1)S(1)}, bf16[64,2304]{1,0:T(8,128)(2,1)S(1)}, u32[]{:S(2)}, u32[]{:S(2)}) collective-permute-start(bf16[64,2304]{1,0:T(8,128)(2,1)S(1)} %get-tuple-element.260), channel_id=1, source_target_pairs={{0,2},{1,3},{2,0},{3,1},{4,6},{5,7},{6,4},{7,5}} | collective-permute-start | bytes 884744 | tf_op jit(solution)/shard_map/ppermute | solution.py:453
  27.8 13.7 %collective-permute-start.23 = (bf16[64,2304]{1,0:T(8,128)(2,1)S(1)}, bf16[64,2304]{1,0:T(8,128)(2,1)S(1)}, u32[]{:S(2)}, u32[]{:S(2)}) collective-permute-start(bf16[64,2304]{1,0:T(8,128)(2,1)S(1)} %get-tuple-element.261), channel_id=1, source_target_pairs={{0,3},{1,2},{2,1},{3,0},{4,7},{5,6},{6,5},{7,4}} | collective-permute-start | bytes 884744 | tf_op jit(solution)/shard_map/ppermute | solution.py:453
  27.8 14.3 %collective-permute-start.27 = (bf16[64,2304]{1,0:T(8,128)(2,1)S(1)}, bf16[64,2304]{1,0:T(8,128)(2,1)S(1)}, u32[]{:S(2)}, u32[]{:S(2)}) collective-permute-start(bf16[64,2304]{1,0:T(8,128)(2,1)S(1)} %get-tuple-element.264), channel_id=1, source_target_pairs={{0,1},{1,0},{2,3},{3,2},{4,5},{5,4},{6,7},{7,6}} | collective-permute-start | bytes 884744 | tf_op jit(solution)/shard_map/ppermute | solution.py:453
  28.2 1.0 %copy-start.5 = (f32[512,1]{1,0:T(8,128)S(1)}, f32[512,1]{1,0:T(8,128)}, u32[]{:S(2)}) copy-start(f32[512,1]{1,0:T(8,128)} %copy-done.4) | copy-start | bytes 6148
  29.1 12.3 %copy-start.3 = (bf16[64,2304]{1,0:T(8,128)(2,1)S(1)}, bf16[64,2304]{1,0:T(8,128)(2,1)}, u32[]{:S(2)}) copy-start(bf16[64,2304]{1,0:T(8,128)(2,1)} %copy-done.2) | copy-start | bytes 884740
  29.1 12.3 %copy-start.6 = (bf16[1,2304]{1,0:T(2,128)(2,1)S(1)}, bf16[1,2304]{1,0:T(2,128)(2,1)}, u32[]{:S(2)}) copy-start(bf16[1,2304]{1,0:T(2,128)(2,1)} %reshape.31.g_ref.g) | copy-start | bytes 13828
  29.1 12.3 %copy-start.9 = (bf16[2,64,2304]{2,1,0:T(8,128)(2,1)S(1)}, bf16[2,64,2304]{2,1,0:T(8,128)(2,1)}, u32[]{:S(2)}) copy-start(bf16[2,64,2304]{2,1,0:T(8,128)(2,1)} %dres.3) | copy-start | bytes 1769476
  30.1 23.0 %copy-start.12 = (bf16[2,64,2304]{2,1,0:T(8,128)(2,1)}, bf16[2,64,2304]{2,1,0:T(8,128)(2,1)S(1)}, u32[]{:S(2)}) copy-start(bf16[2,64,2304]{2,1,0:T(8,128)(2,1)S(1)} %get-tuple-element.527.x) | copy-start | bytes 1769476
  30.1 18.4 %collective-permute-start.28 = (bf16[64,2304]{1,0:T(8,128)(2,1)S(1)}, bf16[64,2304]{1,0:T(8,128)(2,1)S(1)}, u32[]{:S(2)}, u32[]{:S(2)}) collective-permute-start(bf16[64,2304]{1,0:T(8,128)(2,1)S(1)} %get-tuple-element.265), channel_id=1, source_target_pairs={{0,2},{1,3},{2,0},{3,1},{4,6},{5,7},{6,4},{7,5}} | collective-permute-start | bytes 884744 | tf_op jit(solution)/shard_map/ppermute | solution.py:453
  31.8 21.2 %collective-permute-start.29 = (bf16[64,2304]{1,0:T(8,128)(2,1)S(1)}, bf16[64,2304]{1,0:T(8,128)(2,1)S(1)}, u32[]{:S(2)}, u32[]{:S(2)}) collective-permute-start(bf16[64,2304]{1,0:T(8,128)(2,1)S(1)} %get-tuple-element.266), channel_id=1, source_target_pairs={{0,3},{1,2},{2,1},{3,0},{4,7},{5,6},{6,5},{7,4}} | collective-permute-start | bytes 884744 | tf_op jit(solution)/shard_map/ppermute | solution.py:453
  41.4 11.7 %copy-start.1 = (bf16[64,2304]{1,0:T(8,128)(2,1)S(1)}, bf16[64,2304]{1,0:T(8,128)(2,1)}, u32[]{:S(2)}) copy-start(bf16[64,2304]{1,0:T(8,128)(2,1)} %copy-done) | copy-start | bytes 884740
  41.4 16.5 %slice-start = ((s8[4718592]{0:T(1024)(128)(4,1)}), s8[4194304]{0:T(1024)(128)(4,1)S(1)}, s32[]{:S(2)}) async-start(s8[4718592]{0:T(1024)(128)(4,1)} %bitcast.10), calls=%async_computation | async-start | bytes 8388608
  53.1 4.9 %slice-start.1 = ((s8[4718592]{0:T(1024)(128)(4,1)}), s8[524288]{0:T(1024)(128)(4,1)S(1)}, s32[]{:S(2)}) async-start(s8[4718592]{0:T(1024)(128)(4,1)} %bitcast.10), calls=%async_computation.1 | async-start | bytes 1048576
  53.7 21.6 %collective-permute-start.35 = (f32[1,2304]{1,0:T(1,128)S(1)}, f32[1,2304]{1,0:T(1,128)S(1)}, u32[]{:S(2)}, u32[]{:S(2)}) collective-permute-start(f32[1,2304]{1,0:T(1,128)S(1)} %get-tuple-element.273), channel_id=1, source_target_pairs={{0,3},{1,2},{2,1},{3,0},{4,7},{5,6},{6,5},{7,4}} | collective-permute-start | bytes 27656 | tf_op jit(solution)/shard_map/ppermute | solution.py:453
  55.6 20.1 %collective-permute-start.34 = (f32[1,2304]{1,0:T(1,128)S(1)}, f32[1,2304]{1,0:T(1,128)S(1)}, u32[]{:S(2)}, u32[]{:S(2)}) collective-permute-start(f32[1,2304]{1,0:T(1,128)S(1)} %get-tuple-element.273), channel_id=1, source_target_pairs={{0,2},{1,3},{2,0},{3,1},{4,6},{5,7},{6,4},{7,5}} | collective-permute-start | bytes 27656 | tf_op jit(solution)/shard_map/ppermute | solution.py:453
  55.9 19.9 %collective-permute-start.25 = (bf16[64,2304]{1,0:T(8,128)(2,1)S(1)}, bf16[64,2304]{1,0:T(8,128)(2,1)S(1)}, u32[]{:S(2)}, u32[]{:S(2)}) collective-permute-start(bf16[64,2304]{1,0:T(8,128)(2,1)S(1)} %get-tuple-element.262.refs_0_), channel_id=1, source_target_pairs={{0,2},{1,3},{2,0},{3,1},{4,6},{5,7},{6,4},{7,5}} | collective-permute-start | bytes 884744 | tf_op jit(solution)/shard_map/ppermute | solution.py:453
  57.7 18.6 %collective-permute-start.31 = (bf16[64,2304]{1,0:T(8,128)(2,1)S(1)}, bf16[64,2304]{1,0:T(8,128)(2,1)S(1)}, u32[]{:S(2)}, u32[]{:S(2)}) collective-permute-start(bf16[64,2304]{1,0:T(8,128)(2,1)S(1)} %get-tuple-element.268.refs_4_), channel_id=1, source_target_pairs={{0,2},{1,3},{2,0},{3,1},{4,6},{5,7},{6,4},{7,5}} | collective-permute-start | bytes 884744 | tf_op jit(solution)/shard_map/ppermute | solution.py:453
  75.2 12.9 %collective-permute-start.24 = (bf16[64,2304]{1,0:T(8,128)(2,1)S(1)}, bf16[64,2304]{1,0:T(8,128)(2,1)S(1)}, u32[]{:S(2)}, u32[]{:S(2)}) collective-permute-start(bf16[64,2304]{1,0:T(8,128)(2,1)S(1)} %get-tuple-element.262.refs_0_), channel_id=1, source_target_pairs={{0,1},{1,0},{2,3},{3,2},{4,5},{5,4},{6,7},{7,6}} | collective-permute-start | bytes 884744 | tf_op jit(solution)/shard_map/ppermute | solution.py:453
  75.3 12.2 %collective-permute-start.33 = (f32[1,2304]{1,0:T(1,128)S(1)}, f32[1,2304]{1,0:T(1,128)S(1)}, u32[]{:S(2)}, u32[]{:S(2)}) collective-permute-start(f32[1,2304]{1,0:T(1,128)S(1)} %get-tuple-element.273), channel_id=1, source_target_pairs={{0,1},{1,0},{2,3},{3,2},{4,5},{5,4},{6,7},{7,6}} | collective-permute-start | bytes 27656 | tf_op jit(solution)/shard_map/ppermute | solution.py:453
  75.8 12.3 %collective-permute-start.30 = (bf16[64,2304]{1,0:T(8,128)(2,1)S(1)}, bf16[64,2304]{1,0:T(8,128)(2,1)S(1)}, u32[]{:S(2)}, u32[]{:S(2)}) collective-permute-start(bf16[64,2304]{1,0:T(8,128)(2,1)S(1)} %get-tuple-element.268.refs_4_), channel_id=1, source_target_pairs={{0,1},{1,0},{2,3},{3,2},{4,5},{5,4},{6,7},{7,6}} | collective-permute-start | bytes 884744 | tf_op jit(solution)/shard_map/ppermute | solution.py:453
  75.8 12.3 %collective-permute-start.26 = (bf16[64,2304]{1,0:T(8,128)(2,1)S(1)}, bf16[64,2304]{1,0:T(8,128)(2,1)S(1)}, u32[]{:S(2)}, u32[]{:S(2)}) collective-permute-start(bf16[64,2304]{1,0:T(8,128)(2,1)S(1)} %collective-permute-done.25.refs_2_), channel_id=1, source_target_pairs={{0,1},{1,0},{2,3},{3,2},{4,5},{5,4},{6,7},{7,6}} | collective-permute-start | bytes 884744 | tf_op jit(solution)/shard_map/ppermute | solution.py:453
  76.3 11.8 %collective-permute-start.32 = (bf16[64,2304]{1,0:T(8,128)(2,1)S(1)}, bf16[64,2304]{1,0:T(8,128)(2,1)S(1)}, u32[]{:S(2)}, u32[]{:S(2)}) collective-permute-start(bf16[64,2304]{1,0:T(8,128)(2,1)S(1)} %collective-permute-done.31.refs_6_), channel_id=1, source_target_pairs={{0,1},{1,0},{2,3},{3,2},{4,5},{5,4},{6,7},{7,6}} | collective-permute-start | bytes 884744 | tf_op jit(solution)/shard_map/ppermute | solution.py:453
  88.1 2.2 %copy-start.11 = (s32[2,256]{1,0:T(2,128)S(1)}, s32[2,256]{1,0:T(2,128)}, u32[]{:S(2)}) copy-start(s32[2,256]{1,0:T(2,128)} %refs_0_.1) | copy-start | bytes 6148

commit v3 on v2

--- a/solution.py
+++ b/solution.py
@@ -12,9 +12,10 @@
 C = 64
 G = 16
 GS = 16
+C2 = 32
 CB = 256
 ZR = 128
-ZP, ZU, ZZ = 8, 16, 24
+ZP, ZU, ZW = 8, 14, 22
 TB = 64
 
 F32 = jnp.float32
@@ -52,10 +53,10 @@
 
 def _index_kernel(vs, ntp, first, *refs):
     if first:
-        ids_ref, e_ref, tab_ref, pos_ref, srow_ref, list_ref, cnt_ref, buf, glv, gls, gsem, sems = refs
+        ids_ref, e_ref, tab_ref, pos_ref, srow_ref, list_ref, cnt_ref, slot_ref, map_ref, buf, glv, gls, gsem, sems = refs
         base = 0.0
     else:
-        c_ref, ids_ref, e_ref, tab_ref, pos_ref, srow_ref, list_ref, cnt_ref, buf, glv, gls, gsem, sems = refs
+        c_ref, ids_ref, e_ref, tab_ref, pos_ref, srow_ref, list_ref, cnt_ref, slot_ref, map_ref, buf, glv, gls, gsem, sems = refs
         base = (c_ref[0] * C).astype(F32)
     mei = _me()
     me = mei.astype(F32)
@@ -76,9 +77,14 @@
         return sum(a[8 * q:8 * q + 8] for q in range(1, TB // 8)) + a[:8]
 
     lane = _iota((TB, ntok), 1)
+    ts = t // ntp
+    part = lax.broadcasted_iota(jnp.int32, (1, ntok), 1) // ts % ntp
+    chips = [jnp.where(part // 2 == c, 1.0, 0.0) for c in range(ntp // 2)]
     thr = _iota((TB, 128), 1) * float(vs)
     rank8 = jnp.zeros((8, ntok), F32)
     below8 = jnp.zeros((8, 128), F32)
+    rank28 = jnp.zeros((8, ntok), F32)
+    below28 = [jnp.zeros((8, 128), F32) for _ in chips]
     idcs = []
     for b in range(nb):
         idc = column(idr, b)
@@ -89,11 +95,15 @@
         key = jnp.where(seen > 0.5, float(vs * ntp), idc)
         rank8 = rank8 + fold(jnp.where(jnp.broadcast_to(key, (TB, ntok)) < idr, 1.0, 0.0))
         below8 = below8 + fold(jnp.where(jnp.broadcast_to(key, (TB, 128)) < thr, 1.0, 0.0))
+        c = b * TB // ts % ntp // 2
+        seen = jnp.max(jnp.where(dup, chips[c], 0.0), axis=1, keepdims=True)
+        key = jnp.where(seen > 0.5, float(vs * ntp), idc)
+        rank28 = rank28 + fold(jnp.where(jnp.broadcast_to(key, (TB, ntok)) < idr, chips[c], 0.0))
+        below28[c] = below28[c] + fold(jnp.where(jnp.broadcast_to(key, (TB, 128)) < thr, 1.0, 0.0))
     rank = jnp.sum(rank8, axis=0, keepdims=True)
     below = jnp.sum(below8, axis=0, keepdims=True)
     own_r = jnp.floor(idr * (1.0 / vs))
     start = jnp.zeros_like(rank)
-    mine0 = jnp.zeros((1, 1), F32)
     cnt = jnp.zeros((1, 1), F32)
     mx = jnp.zeros((1, 1), F32)
     for d in range(ntp):
@@ -103,6 +113,20 @@
         cnt = jnp.where(me == float(d), nd, cnt)
         mx = jnp.maximum(mx, nd)
     slot_r = rank - start
+    rank2 = jnp.sum(rank28, axis=0, keepdims=True)
+    below2 = [jnp.sum(b8, axis=0, keepdims=True) for b8 in below28]
+    start2 = jnp.zeros_like(rank)
+    cnt2 = jnp.zeros((1, 1), F32)
+    mx2 = jnp.zeros((1, 1), F32)
+    for c, chip in enumerate(chips):
+        for d in range(ntp):
+            ld = below2[c][:, d:d + 1]
+            nd = below2[c][:, d + 1:d + 2] - ld
+            start2 = jnp.where((own_r == float(d)) & (chip > 0.5), ld, start2)
+            if d // 2 != c:
+                cnt2 = jnp.where(me == float(d), nd, cnt2)
+                mx2 = jnp.maximum(mx2, nd)
+    slot2_r = rank2 - start2
     my_r = jnp.where(own_r == me, slot_r, -1.0)
 
     slot_l = _iota((TB, 128), 1) + base
@@ -140,7 +164,30 @@
     for b in range(nb):
         pos_ref[b * TB:(b + 1) * TB, :] = column(pos, b)
     lane1 = lax.broadcasted_iota(jnp.int32, (1, 128), 1)
-    cnt_ref[...] = jnp.where(lane1 == 0, mx, cnt).astype(jnp.int32)
+    over = jnp.where((mx > C) | (mx2 > C2 - 1), 1.0, 0.0)
+    cnts = jnp.where(lane1 == 0, mx, jnp.where(lane1 == 1, cnt, jnp.where(lane1 == 2, over, cnt2)))
+    cnt_ref[...] = cnts.astype(jnp.int32)
+    facing = (mei ^ 2).astype(F32)
+    sums_r = jnp.where(own_r == facing, slot2_r, -1.0)
+    rows = [jnp.zeros((1, nk * ts), F32)] * 4
+    for q in range(ntp):
+        at = [slice(k * t + q * ts, k * t + (q + 1) * ts) for k in range(nk)]
+        mine = jnp.concatenate([my_r[:, w] for w in at], axis=1)
+        sums = jnp.concatenate([sums_r[:, w] for w in at], axis=1)
+        own, sib = me == float(q), me == float(q ^ 1)
+        rows = [
+            jnp.where(own, mine, rows[0]), jnp.where(sib, mine, rows[1]),
+            jnp.where(own, sums, rows[2]), jnp.where(sib, sums, rows[3]),
+        ]
+    for j, r in enumerate(rows):
+        slot_ref[j:j + 1, :] = r
+    far = (part // 2).astype(F32) != jnp.floor(me * 0.5)
+    got_r = jnp.where(far & (own_r == me), slot2_r, -1.0)
+    acc2 = jnp.zeros((TB, 128), F32)
+    slot_j = _iota((TB, 128), 1)
+    for b in range(nb):
+        acc2 = jnp.maximum(acc2, jnp.where(column(got_r, b) == slot_j, mys[b], 0.0))
+    map_ref[...] = jnp.minimum(jnp.max(acc2, axis=0, keepdims=True), C - 1.0).astype(jnp.int32)
     hit = jnp.where(my_r == _iota((C, ntok), 0) + base, idr - lo, 0.0)
     want = jnp.max(hit, axis=1, keepdims=True)
     want = want - jnp.floor(want * (1.0 / G)) * G
@@ -164,9 +211,11 @@
             jax.ShapeDtypeStruct((1, ntok), F32),
             jax.ShapeDtypeStruct((1, ntok), jnp.int32),
             jax.ShapeDtypeStruct((1, 128), jnp.int32),
+            jax.ShapeDtypeStruct((4, ntok // ntp), F32),
+            jax.ShapeDtypeStruct((1, 128), jnp.int32),
         ),
         in_specs=([] if first else [_sm()]) + [_vm(), pl.BlockSpec(memory_space=pltpu.HBM)],
-        out_specs=(_vm(),) * 5,
+        out_specs=(_vm(),) * 7,
         scratch_shapes=[
             VMEM((C * G, d), BF16),
             VMEM((8, 128), jnp.int32),
@@ -237,12 +286,12 @@
         for k in range(nk):
             for r in range(4):
                 at = pl.multiple_of((_me() ^ r) * ts, ts)
-                dur[pl.ds((k * 4 + r) * ts, ts), :] = du_ref[k, pl.ds(at, ts), :]
+                dur[pl.ds((r * nk + k) * ts, ts), :] = du_ref[k, pl.ds(at, ts), :]
         _fill(z, de, sems, 0, 0, ZP, False)
 
     out = lax.dot_general(dur[...], w_ref[...], (((1,), (1,)), ((), ())), preferred_element_type=F32)
     for i, o in enumerate(outs):
-        o[...] = out[i * ts:(i + 1) * ts].astype(BF16)
+        o[...] = out[i * nk * ts:(i + 1) * nk * ts].astype(BF16)
 
     @pl.when(pl.program_id(0) == pl.num_programs(0) - 1)
     def _():
@@ -255,16 +304,16 @@
     cb = 3 * CB
     out = pl.pallas_call(
         functools.partial(_p_kernel, ts),
-        out_shape=(jax.ShapeDtypeStruct((ts, d), BF16),) * (4 * nk) + (jax.ShapeDtypeStruct((vs, d), F32),),
+        out_shape=(jax.ShapeDtypeStruct((nk * ts, d), BF16),) * 4 + (jax.ShapeDtypeStruct((vs, d), F32),),
         grid=(d // cb,),
         in_specs=[pl.BlockSpec((nk, t, f), lambda i: (0, 0, 0)), pl.BlockSpec((cb, f), lambda i: (i, 0))],
-        out_specs=(pl.BlockSpec((ts, cb), lambda i: (0, i)),) * (4 * nk) + (_any(),),
+        out_specs=(pl.BlockSpec((nk * ts, cb), lambda i: (0, i)),) * 4 + (_any(),),
         scratch_shapes=[VMEM((nk * t, f), BF16)] + _zscratch(d, ZP),
         compiler_params=_params(20),
         cost_estimate=_cost(5),
         name="p_terms",
     )(du, W)
-    return [out[4 * k:4 * k + 4] for k in range(nk)], out[-1]
+    return out[:4], out[4]
 
 
 def _zero_kernel(lo, n, de_in, o, z, sems):
@@ -288,33 +337,58 @@
     )(de)
 
 
-def _dx_kernel(x, p0, p1, p2, p3, dres, g, *refs):
-    prev, (dx, dg) = refs[:-2], refs[-2:]
-    xf = x[...].astype(F32)
-    rs = lax.rsqrt(jnp.mean(xf * xf, axis=-1, keepdims=True) + EPS)
-    nh = xf * rs
-    dn = (p0[...].astype(F32) + p1[...].astype(F32)) + (p2[...].astype(F32) + p3[...].astype(F32))
-    gdn = g[...].astype(F32) * dn
-    out = dres[...].astype(F32) + rs * (gdn - nh * jnp.mean(nh * gdn, axis=-1, keepdims=True))
-    dx[...] = out.astype(BF16)
-    part = jnp.sum(dn * nh, axis=0, keepdims=True)
-    dg[...] = part + prev[0][...] if prev else part
-
-
-def _dx(x, ps, dres, g, k, prev):
-    _, m, d = x.shape
-    row = pl.BlockSpec((pl.Squeezed(), m, d), lambda i: (k, 0, 0))
-    whole = lambda a: pl.BlockSpec(a.shape, lambda i: (0,) * a.ndim)
+def _dx_kernel(x, p0, p1, p2, p3, dres, g, dx, dg):
+    rows = 32
+    tot = None
+    for b in range(dx.shape[0] // rows):
+        s = slice(b * rows, (b + 1) * rows)
+        xf = x[s].astype(F32)
+        rs = lax.rsqrt(jnp.mean(xf * xf, axis=-1, keepdims=True) + EPS)
+        nh = xf * rs
+        dn = (p0[s].astype(F32) + p1[s].astype(F32)) + (p2[s].astype(F32) + p3[s].astype(F32))
+        gdn = g[...].astype(F32) * dn
+        out = dres[s].astype(F32) + rs * (gdn - nh * jnp.mean(nh * gdn, axis=-1, keepdims=True))
+        dx[s] = out.astype(BF16)
+        part = jnp.sum(dn * nh, axis=0, keepdims=True)
+        tot = part if tot is None else tot + part
+    dg[...] = tot
+
+
+def _dx(x, ps, dres, g):
+    m, d = x.shape
     return pl.pallas_call(
         _dx_kernel,
         out_shape=(jax.ShapeDtypeStruct((m, d), BF16), jax.ShapeDtypeStruct((1, d), F32)),
-        grid=(1,),
-        in_specs=[row, *map(whole, ps), row, whole(g), *map(whole, prev)],
-        out_specs=(pl.BlockSpec((m, d), lambda i: (0, 0)), pl.BlockSpec((1, d), lambda i: (0, 0))),
+        in_specs=[_vm()] * 7,
+        out_specs=(_vm(), _vm()),
         compiler_params=_params(12),
         cost_estimate=_cost(2),
         name="dx_form",
-    )(x, *ps, dres, g, *prev)
+    )(x, *ps, dres, g)
+
+
+def _sums_kernel(slot_ref, dx0, dx1, dg0, dg1, out):
+    m = dx0.shape[0]
+    j = _iota((C2, m), 0)
+    ohs = [jnp.where(slot_ref[i:i + 1, :] == j, 1.0, 0.0).astype(BF16) for i in (2, 3)]
+    last = lax.broadcasted_iota(jnp.int32, (C2, CB), 0) == C2 - 1
+    for c in range(out.shape[1] // CB):
+        s = slice(c * CB, (c + 1) * CB)
+        tot = jnp.dot(ohs[0], dx0[:, s], preferred_element_type=F32)
+        tot = tot + jnp.dot(ohs[1], dx1[:, s], preferred_element_type=F32)
+        out[:, s] = jnp.where(last, dg0[:, s] + dg1[:, s], tot)
+
+
+def _sums(slots, dx0, dx1, dg0, dg1):
+    return pl.pallas_call(
+        _sums_kernel,
+        out_shape=jax.ShapeDtypeStruct((C2, dx0.shape[1]), F32),
+        in_specs=[_vm()] * 5,
+        out_specs=_vm(),
+        compiler_params=_params(6),
+        cost_estimate=_cost(1),
+        name="dx_sums",
+    )(slots, dx0, dx1, dg0, dg1)
 
 
 def _u_kernel(x_ref, g_ref, w_ref, de_in, u_ref, n_ref, de, z, sems):
@@ -376,17 +450,18 @@
 def _dw(n, du, de, lo, nz):
     nk, t, f = du.shape
     ntok, d = n.shape
-    steps = d // CB
+    cb = d // 6
+    steps = d // cb
     return pl.pallas_call(
         functools.partial(_dw_kernel, lo, nz, -(-nz // steps)),
         out_shape=(jax.ShapeDtypeStruct((d, f), F32), jax.ShapeDtypeStruct(de.shape, F32)),
         grid=(steps,),
         in_specs=[
-            pl.BlockSpec((ntok, CB), lambda i: (0, i)),
+            pl.BlockSpec((ntok, cb), lambda i: (0, i)),
             pl.BlockSpec((nk, t, f), lambda i: (0, 0, 0)),
             _any(),
         ],
-        out_specs=(pl.BlockSpec((CB, f), lambda i: (i, 0)), _any()),
+        out_specs=(pl.BlockSpec((cb, f), lambda i: (i, 0)), _any()),
         scratch_shapes=_zscratch(d, nz),
         input_output_aliases={2: 1},
         compiler_params=_params(20),
@@ -401,7 +476,7 @@
     for k in range(nk):
         for r in range(4):
             at = pl.multiple_of(k * 4 * ts + (_me() ^ r) * ts, ts)
-            dx[pl.ds(at, ts), :] = pieces[k * 4 + r][...]
+            dx[pl.ds(at, ts), :] = pieces[r][k * ts:(k + 1) * ts, :]
     cnt = cnt_ref[0, 1]
 
     def chunk(i, carry):
@@ -445,6 +520,51 @@
     )(cnts, rows, srow, *pieces, de)
 
 
+def _write_kernel(cnt_ref, list_ref, map_ref, slot_ref, dx0, dx1, dg_ref, mine_ref, got_ref, de_in, de, dg_out, acc, sem):
+    m = dx0.shape[0]
+    j = _iota((C, m), 0)
+    ohs = [jnp.where(slot_ref[i:i + 1, :] == j, 1.0, 0.0).astype(BF16) for i in (0, 1)]
+    for c in range(acc.shape[1] // CB):
+        s = slice(c * CB, (c + 1) * CB)
+        tot = jnp.dot(ohs[0], dx0[:, s], preferred_element_type=F32)
+        acc[:, s] = tot + jnp.dot(ohs[1], dx1[:, s], preferred_element_type=F32)
+
+    def add(j, carry):
+        at = pl.ds(map_ref[0, j], 1)
+        acc[at, :] = acc[at, :] + got_ref[pl.ds(j, 1), :]
+        return carry
+
+    lax.fori_loop(0, jnp.minimum(cnt_ref[0, 3], C2 - 1), add, 0)
+    here = jnp.minimum(cnt_ref[0, 1], C)
+
+    def put(j, carry):
+        pltpu.make_async_copy(acc.at[pl.ds(j, 1)], de.at[pl.ds(list_ref[0, j], 1)], sem).start()
+        return carry
+
+    def done(j, carry):
+        pltpu.make_async_copy(acc.at[pl.ds(j, 1)], de.at[pl.ds(0, 1)], sem).wait()
+        return carry
+
+    lax.fori_loop(0, here, put, 0)
+    dg_out[...] = mine_ref[C2 - 1:C2, :] + got_ref[C2 - 1:C2, :]
+    lax.fori_loop(0, here, done, 0)
+
+
+def _write(cnts, rows, where, slots, dx0, dx1, dgp, mine, got, de):
+    vs, d = de.shape
+    return pl.pallas_call(
+        _write_kernel,
+        out_shape=(jax.ShapeDtypeStruct((vs, d), F32), jax.ShapeDtypeStruct((1, d), F32)),
+        in_specs=[_sm(), _sm(), _sm()] + [_vm()] * 6 + [_any()],
+        out_specs=(_any(), _vm()),
+        scratch_shapes=[VMEM((C, d), F32), pltpu.SemaphoreType.DMA],
+        input_output_aliases={9: 0},
+        compiler_params=_params(8),
+        cost_estimate=_cost(3),
+        name="write_rows",
+    )(cnts, rows, where, slots, dx0, dx1, dgp, mine, got, de)
+
+
 def solution(mesh):
     ntp = mesh.shape["tp"]
     ndp = mesh.shape["dp"]
@@ -458,53 +578,62 @@
         return t, t1, t2, swap(t2, 1)
 
     def p_terms(du, W, ts, vs):
-        ps, de = _p_terms(du, W, ts, vs)
-        return de, [(q[0], swap(q[1], 1), swap(q[2], 2), swap(q[3], 3)) for q in ps]
-
-    def finish(x, xl, de_ps, g2, W, du, dres, cnts, rows, srow):
-        nk, ts, d = xl.shape
-        de, ps = de_ps
-        u, n, de = _u(x, g2, W, nk, de)
-        dx0, dg0 = _dx(xl, ps[0], dres, g2, 0, ())
-        de = _zeros(de, ZP + ZU, ZZ)
-        dx1, dgp = _dx(xl, ps[1], dres, g2, 1, (dg0,))
-        pieces = share(dx0) + share(dx1)
-        done = ZP + ZU + ZZ
-        dW, de = _dw(n, du, de, done, de.shape[0] // ZR - done)
-        dg = ((dgp + swap(dgp, 1)) + (swap(dgp, 2) + swap(dgp, 3))).reshape(d)
-        dE = _scatter(cnts, rows, srow, pieces, de, ts, nk)
-        return u, xl, dE, dW, dg
+        q, de = _p_terms(du, W, ts, vs)
+        return de, (q[0], swap(q[1], 1), swap(q[2], 2), swap(q[3], 3))
+
+    def fill_rest(de):
+        n = ZP + ZU + ZW
+        return _zeros(de, n, de.shape[0] // ZR - n)
 
     def body(ids, E, g, W, du, dres):
         vs, d = E.shape
-        ts = ids.shape[1] // ntp
+        nk, t = ids.shape
+        ts = t // ntp
+        m = nk * ts
         g2 = g.reshape(1, d)
 
-        tab, pos, srow, rows, cnts = _index_call(None, ids, E, ntp)
+        tab, pos, _, rows, cnts, slots, where = _index_call(None, ids, E, ntp)
         tabs = share(tab)
-        de_ps = p_terms(du, W, ts, vs)
+        de, ps = p_terms(du, W, ts, vs)
+        x, xl = _expand(pos, tabs, ts)
+        u, n, de = _u(x, g2, W, nk, de)
+        dW, de = _dw(n, du, de, ZP + ZU, ZW)
+        dx, dg = _dx(xl.reshape(m, d), ps, dres.reshape(m, d), g2)
+        dx1, dg1 = swap(dx, 1), swap(dg, 1)
+        mine = _sums(slots, dx, dx1, dg, dg1)
+        got = swap(mine, 2)
         other = lax.ppermute(cnts, "dp", [(i, (i + 1) % ndp) for i in range(ndp)])
-        x, xl = _expand(pos, tabs, ts)
-        outs = finish(x, xl, de_ps, g2, W, du, dres, cnts, rows, srow)
-        rounds = (jnp.maximum(cnts[0, 0], other[0, 0]) + C - 1) // C
+        de = fill_rest(de)
+        dE, dg = _write(cnts, rows, where, slots, dx, dx1, dg, mine, got, de)
+        outs = u, xl, dE, dW, dg.reshape(d)
+        over = jnp.maximum(cnts[0, 2], other[0, 2])
 
         inputs = ids, E, W, du, dres, g2
 
         def again(c):
-            once, _ = c
-            ids, E, W, du, dres, g2, once = lax.optimization_barrier((*inputs, once))
+            i0, _ = c
+            ids, E, W, du, dres, g2, i0 = lax.optimization_barrier((*inputs, c[0]))
+            top = lax.ppermute(cnts, "dp", [(i, (i + 1) % ndp) for i in range(ndp)])
+            rounds = (jnp.maximum(cnts[0, 0], top[0, 0]) + C - 1) // C
 
             def more(q):
                 i, x, _ = q
-                tab, pos, _, _, _ = _index_call(i, ids, E, ntp)
+                tab, pos, *_ = _index_call(i, ids, E, ntp)
                 return i + 1, *_expand(pos, share(tab), ts, x)
 
-            zeros = jnp.zeros(x.shape, BF16), jnp.zeros(xl.shape, BF16)
-            _, xa, xla = lax.while_loop(lambda q: q[0] < rounds, more, (jnp.int32(0), *zeros))
-            _, _, srow, rows, cnts = _index_call(once - 1, ids, E, ntp)
-            return rounds, finish(xa, xla, p_terms(du, W, ts, vs), g2, W, du, dres, cnts, rows, srow)
-
-        _, outs = lax.while_loop(lambda c: c[0] < rounds, again, (jnp.int32(1), outs))
+            zeros = jnp.zeros((nk * t, d), BF16), jnp.zeros((nk, ts, d), BF16)
+            _, x, xl = lax.while_loop(lambda q: q[0] < rounds, more, (i0, *zeros))
+            _, _, srow, rows, cs, _, _ = _index_call(i0, ids, E, ntp)
+            de, ps = p_terms(du, W, ts, vs)
+            u, n, de = _u(x, g2, W, nk, de)
+            dW, de = _dw(n, du, de, ZP + ZU, ZW)
+            dx, dg = _dx(xl.reshape(m, d), ps, dres.reshape(m, d), g2)
+            dg2 = dg + swap(dg, 1)
+            dg = (dg2 + swap(dg2, 2)).reshape(d)
+            dE = _scatter(cs, rows, srow, share(dx), fill_rest(de), ts, nk)
+            return i0 + 1, (u, xl, dE, dW, dg)
+
+        _, outs = lax.while_loop(lambda c: c[0] < over, again, (jnp.int32(0), outs))
         return outs
 
     return jax.shard_map(

time: 90.9 us -> 89.8 us (0.988)
  starting transfers between devices: 14.3 us -> 9.26 us
  Pallas kernels: 43.8 us -> 48.5 us
  between operations: 1.06 us -> 3.47 us
  local copies, waits for them, and re-layouts: 4.4 us -> 2.08 us
    ppermute x18 -> x9, starting transfers between devices: 12.7 us -> 7.68 us  [swap(): return lax.ppermute(a, 'tp', [(i, i ^ bit) for i in range(ntp)])]
    pallas_call x1, Pallas kernels: 11.1 us -> 13.7 us  [_dw(): pl.pallas_call(functools.partial(_dw_kernel, lo, nz, -(-nz // steps)), ou...]
    unnamed x26 -> x16, local copies, waits for them, and re-layouts: 3.11 us -> 0.85 us
    pallas_call x1, Pallas kernels: 7.65 us -> 9.26 us  [_u(): pl.pallas_call(_u_kernel, out_shape=(jax.ShapeDtypeStruct((nk, ntok // nk...]
    pallas_call x1, Pallas kernels: 9.6 us -> 8.14 us  [_zeros(): pl.pallas_call(functools.partial(_zero_kernel, lo, n), out_shape=jax.Shap...]
    reshape x1, local copies, waits for them, and re-layouts: 1.29 us -> 0.01 us  [body(): g2 = g.reshape(1, d)]
    pallas_call x1, Pallas kernels: 0.92 us -> 2.18 us  [_expand(): pl.pallas_call(functools.partial(_expand_kernel, ts, x is not None), out_...]
    slice x0 -> x2, local copies, waits for them, and re-layouts: none -> 1.23 us  [again(): rounds = (jnp.maximum(cnts[0, 0], top[0, 0]) + C - 1) // C]
  transfers between devices with their start and end apart: 19 -> 10, of which waited for: 5 -> 3; matrix products, arithmetic and copies ran while one was open for 2% -> 1% of each run, Pallas kernels for 39% -> 43%
where the time goes in v3:
time: 89.8 us; the launch traced here: 89.5 us
  Pallas kernels  48.5 us (54%)
  waiting for transfers between devices  25.5 us (28%)
  starting transfers between devices  9.26 us (10%)
  between operations  3.47 us (4%)
  local copies, waits for them, and re-layouts  2.08 us (2%)
    ppermute x9, waiting for transfers between devices, swap(): return lax.ppermute(a, 'tp', [(i, i ^ bit) for i in range(ntp)])  25.5 us
    pallas_call x1, Pallas kernels, _dw(): pl.pallas_call(functools.partial(_dw_kernel, lo, nz, -(-nz // steps)), ou...  13.7 us
    pallas_call x1, Pallas kernels, _u(): pl.pallas_call(_u_kernel, out_shape=(jax.ShapeDtypeStruct((nk, ntok // nk...  9.26 us
    pallas_call x1, Pallas kernels, _zeros(): pl.pallas_call(functools.partial(_zero_kernel, lo, n), out_shape=jax.Shap...  8.14 us
    ppermute x9, starting transfers between devices, swap(): return lax.ppermute(a, 'tp', [(i, i ^ bit) for i in range(ntp)])  7.68 us
    pallas_call x1, Pallas kernels, _index_call(): pl.pallas_call(functools.partial(_index_kernel, vs, ntp, first), out_shap...  6.71 us
    pallas_call x1, Pallas kernels, _p_terms(): pl.pallas_call(functools.partial(_p_kernel, ts), out_shape=(jax.ShapeDtyp...  5.14 us
    pallas_call x1, Pallas kernels, _expand(): pl.pallas_call(functools.partial(_expand_kernel, ts, x is not None), out_...  2.18 us
  transfers between devices with their start and end apart: 10, of which 3 were waited for; matrix products, arithmetic and copies ran while one was open for 1% of the time, Pallas kernels for 43%

profile of v3, /device:TPU:0, one launch (start us, length us, event | category | flops | bytes accessed | tf_op | source)
XLA Modules:
  0.0 89.5 jit_solution(700861172362479387)
XLA Ops:
  0.6 0.0 copy-start.5
  0.6 6.7 %index_gather.6 = (bf16[64,2304]{1,0:T(8,128)(2,1)S(1)}, f32[512,1]{1,0:T(8,128)S(1)}, f32[1,512]{1,0:T(1,128)}, s32[1,512]{1,0:T(1,128)S(1)}, s32[1,128]{1,0:T(...) custom-call(s32[2,256]{1,0:T(2,128)} %refs_0_.1, bf16[8192,2304]{1,0:T(8,128)(2,1)} %refs_1_.1), custom_call_target="tpu_custom_call" | custom-call | flops 20000000000 | bytes 1000000 | tf_op jit(solution)/shard_map/index_gather/pallas_call | solution.py:206
  7.4 3.0 %collective-permute-start.12 = (bf16[64,2304]{1,0:T(8,128)(2,1)S(1)}, bf16[64,2304]{1,0:T(8,128)(2,1)}, u32[]{:S(2)}, u32[]{:S(2)}) collective-permute-start(bf16[64,2304]{1,0:T(8,128)(2,1)S(1)} %get-tuple-element.344.refs_1_), channel_id=1, source_target_pairs={{0,2},{1,3},{2,0},{3,1},{4,6},{5,7},{6,4},{7,5}} | collective-permute-start | bytes 884744 | tf_op jit(solution)/shard_map/ppermute | solution.py:573
  10.4 0.0 collective-permute-start.11
  10.4 1.6 %collective-permute-start.20 = (s32[1,128]{1,0:T(1,128)S(1)}, s32[1,128]{1,0:T(1,128)S(1)}, u32[]{:S(2)}, u32[]{:S(2)}) collective-permute-start(s32[1,128]{1,0:T(1,128)S(1)} %get-tuple-element.349.cnt_ref), channel_id=1, source_target_pairs={{0,4},{4,0},{1,5},{5,1},{2,6},{6,2},{3,7},{7,3}} | collective-permute-start | bytes 1544 | tf_op jit(solution)/shard_map/ppermute | solution.py:605
  12.0 5.7 %collective-permute-done.12.refs_3_ = bf16[64,2304]{1,0:T(8,128)(2,1)} collective-permute-done((bf16[64,2304]{1,0:T(8,128)(2,1)S(1)}, bf16[64,2304]{1,0:T(8,128)(2,1)}, u32[]{:S(2)}, u32[]{:S(2)}) %collective-permute-start.12) | collective-permute-done | bytes 294944 | tf_op jit(solution)/shard_map/ppermute | solution.py:573
  17.6 5.1 %p_terms.5 = (bf16[128,2304]{1,0:T(8,128)(2,1)S(1)}, bf16[128,2304]{1,0:T(8,128)(2,1)S(1)}, bf16[128,2304]{1,0:T(8,128)(2,1)S(1)}, bf16[128,2304]{1,0:T(8,128)(2,1)S(1)}, f32[8192,2304]{1,0:T(8,128)}) custom-call(bf16[2,256,1024]{2,1,0:T(8,128)(2,1)} %du_ref.3, bf16[2304,1024]{1,0:T(8,128)(2,1)S(1)} %copy-done.5), custom_call_target="tpu_custom_call" | custom-call | flops 20000000000 | bytes 1000000 | tf_op jit(solution)/shard_map/p_terms/pallas_call | solution.py:305
  22.8 0.0 copy-start
  22.8 0.8 copy-done
  23.6 0.5 collective-permute-start.14
  24.1 0.6 fusion.1
  24.7 1.8 %collective-permute-start.15 = (bf16[128,2304]{1,0:T(8,128)(2,1)S(1)}, bf16[128,2304]{1,0:T(8,128)(2,1)S(1)}, u32[]{:S(2)}, u32[]{:S(2)}) collective-permute-start(bf16[128,2304]{1,0:T(8,128)(2,1)S(1)} %get-tuple-element.355), channel_id=1, source_target_pairs={{0,2},{1,3},{2,0},{3,1},{4,6},{5,7},{6,4},{7,5}} | collective-permute-start | bytes 1769480 | tf_op jit(solution)/shard_map/ppermute | solution.py:573
  26.5 0.6 fusion
  29.8 0.0 collective-permute-start.16
  29.8 0.0 collective-permute-done.11.refs_2_
  29.8 0.0 copy-start.1
  29.8 0.0 copy-start.6
  29.9 2.2 %expand.2 = (bf16[512,2304]{1,0:T(8,128)(2,1)S(1)}, bf16[2,64,2304]{2,1,0:T(8,128)(2,1)S(1)}) custom-call(f32[512,1]{1,0:T(8,128)S(1)} %get-tuple-element.343.refs_0_, bf16[64,2304]{1,0:T(8,128)(2,1)S(1)} %get-tuple-element.344.refs_1_, bf16[64,2304]{1,0:T(8,128)(2,1)} %collective-permute-done.11.refs_2_, bf16[64,2304]{1,0:T(8,128)(2,1)} %collective-permute-done.12.refs_3_, ...), custom_call_target="tpu_custom_call" | custom-call | flops 12000000000 | bytes 1000000 | tf_op jit(solution)/shard_map/expand/pallas_call | solution.py:254
  32.0 0.0 copy-start.9
  32.1 8.9 %collective-permute-done.15.p2 = bf16[128,2304]{1,0:T(8,128)(2,1)S(1)} collective-permute-done((bf16[128,2304]{1,0:T(8,128)(2,1)S(1)}, bf16[128,2304]{1,0:T(8,128)(2,1)S(1)}, u32[]{:S(2)}, u32[]{:S(2)}) %collective-permute-start.15) | collective-permute-done | bytes 589856 | tf_op jit(solution)/shard_map/ppermute | solution.py:573
  40.9 10.9 %collective-permute-done.16.p3 = bf16[128,2304]{1,0:T(8,128)(2,1)S(1)} collective-permute-done((bf16[128,2304]{1,0:T(8,128)(2,1)S(1)}, bf16[128,2304]{1,0:T(8,128)(2,1)S(1)}, u32[]{:S(2)}, u32[]{:S(2)}) %collective-permute-start.16) | collective-permute-done | bytes 589856 | tf_op jit(solution)/shard_map/ppermute | solution.py:573
  51.9 1.2 %dx_form.5 = (bf16[128,2304]{1,0:T(8,128)(2,1)S(1)}, f32[1,2304]{1,0:T(1,128)S(1)}) custom-call(bf16[128,2304]{1,0:T(8,128)(2,1)S(1)} %bitcast.20, bf16[128,2304]{1,0:T(8,128)(2,1)S(1)} %copy-done.1, bf16[128,2304]{1,0:T(8,128)(2,1)S(1)} %collective-permute-done.14.p1, bf16[128,2304]{1,0:T(8,128)(2,1)S(1)} %collective-permute-done.15.p2, ...), custom_call_target="tpu_custom_call" | custom-call | flops 8000000000 | bytes 1000000 | tf_op jit(solution)/shard_map/dx_form/pallas_call | solution.py:359
  53.1 0.6 collective-permute-start.18
  53.7 0.0 collective-permute-start.17
  53.7 9.3 %u_terms.5 = (bf16[2,256,1024]{2,1,0:T(8,128)(2,1)}, bf16[512,2304]{1,0:T(8,128)(2,1)S(1)}, f32[8192,2304]{1,0:T(8,128)}) custom-call(bf16[512,2304]{1,0:T(8,128)(2,1)S(1)} %get-tuple-element.345.x_ref, bf16[1,2304]{1,0:T(2,128)(2,1)S(1)} %reshape.44.g_ref.g, bf16[2304,1024]{1,0:T(8,128)(2,1)} %w_ref.3, ...), custom_call_target="tpu_custom_call", output_to_operand_aliasing={{2}: (3, {})} | custom-call | flops 40000000000 | bytes 1000000 | tf_op jit(solution)/shard_map/u_terms/pallas_call | solution.py:415
  63.0 13.7 %dw_terms.5 = (f32[2304,1024]{1,0:T(8,128)}, f32[8192,2304]{1,0:T(8,128)}) custom-call(bf16[512,2304]{1,0:T(8,128)(2,1)S(1)} %get-tuple-element.359.n_ref, bf16[2,256,1024]{2,1,0:T(8,128)(2,1)} %du_ref.3, f32[8192,2304]{1,0:T(8,128)} %get-tuple-element.360.de_in), custom_call_target="tpu_custom_call", output_to_operand_aliasing={{1}: (2, {})} | custom-call | flops 40000000000 | bytes 1000000 | tf_op jit(solution)/shard_map/dw_terms/pallas_call | solution.py:455
  76.7 0.3 dx_sums.1.mine_ref
  77.0 1.7 %collective-permute-start.19 = (f32[32,2304]{1,0:T(8,128)S(1)}, f32[32,2304]{1,0:T(8,128)S(1)}, u32[]{:S(2)}, u32[]{:S(2)}) collective-permute-start(f32[32,2304]{1,0:T(8,128)S(1)} %dx_sums.1.mine_ref), channel_id=1, source_target_pairs={{0,2},{1,3},{2,0},{3,1},{4,6},{5,7},{6,4},{7,5}} | collective-permute-start | bytes 884744 | tf_op jit(solution)/shard_map/ppermute | solution.py:573
  78.7 8.1 %zero_fill.2.de_in = f32[8192,2304]{1,0:T(8,128)} custom-call(f32[8192,2304]{1,0:T(8,128)} %get-tuple-element.361.de_in), custom_call_target="tpu_custom_call", output_to_operand_aliasing={{}: (0, {})} | custom-call | flops 30000001024 | bytes 1000000 | tf_op jit(solution)/shard_map/zero_fill/pallas_call | solution.py:327
  86.9 0.0 copy-start.8
  86.9 1.9 %write_rows.1 = (f32[8192,2304]{1,0:T(8,128)}, f32[1,2304]{1,0:T(1,128)S(1)}) custom-call(s32[1,128]{1,0:T(1,128)S(1)} %get-tuple-element.349.cnt_ref, s32[1,512]{1,0:T(1,128)S(1)} %get-tuple-element.350.list_ref, s32[1,128]{1,0:T(1,128)S(1)} %get-tuple-element.351.map_ref, ...), custom_call_target="tpu_custom_call", output_to_operand_aliasing={{0}: (9, {})} | custom-call | flops 12000000000 | bytes 1000000 | tf_op jit(solution)/shard_map/write_rows/pallas_call | solution.py:555
  88.9 0.6 reduce.1
  (18 shorter events, 0.0 us)
Async XLA Ops:
  0.6 17.0 %copy-start.5 = (bf16[2304,1024]{1,0:T(8,128)(2,1)S(1)}, bf16[2304,1024]{1,0:T(8,128)(2,1)}, u32[]{:S(2)}) copy-start(bf16[2304,1024]{1,0:T(8,128)(2,1)} %w_ref.3) | copy-start | bytes 14155780
  7.4 10.3 %collective-permute-start.12 = (bf16[64,2304]{1,0:T(8,128)(2,1)S(1)}, bf16[64,2304]{1,0:T(8,128)(2,1)}, u32[]{:S(2)}, u32[]{:S(2)}) collective-permute-start(bf16[64,2304]{1,0:T(8,128)(2,1)S(1)} %get-tuple-element.344.refs_1_), channel_id=1, source_target_pairs={{0,2},{1,3},{2,0},{3,1},{4,6},{5,7},{6,4},{7,5}} | collective-permute-start | bytes 884744 | tf_op jit(solution)/shard_map/ppermute | solution.py:573
  10.4 19.4 %collective-permute-start.11 = (bf16[64,2304]{1,0:T(8,128)(2,1)S(1)}, bf16[64,2304]{1,0:T(8,128)(2,1)}, u32[]{:S(2)}, u32[]{:S(2)}) collective-permute-start(bf16[64,2304]{1,0:T(8,128)(2,1)S(1)} %get-tuple-element.344.refs_1_), channel_id=1, source_target_pairs={{0,1},{1,0},{2,3},{3,2},{4,5},{5,4},{6,7},{7,6}} | collective-permute-start | bytes 884744 | tf_op jit(solution)/shard_map/ppermute | solution.py:573
  10.4 14.3 %copy-start.4 = (bf16[2304]{0:T(1024)(128)(2,1)S(1)}, bf16[2304]{0:T(1024)(128)(2,1)}, u32[]{:S(2)}) copy-start(bf16[2304]{0:T(1024)(128)(2,1)} %param.12) | copy-start | bytes 13828
  10.4 16.1 %collective-permute-start.20 = (s32[1,128]{1,0:T(1,128)S(1)}, s32[1,128]{1,0:T(1,128)S(1)}, u32[]{:S(2)}, u32[]{:S(2)}) collective-permute-start(s32[1,128]{1,0:T(1,128)S(1)} %get-tuple-element.349.cnt_ref), channel_id=1, source_target_pairs={{0,4},{4,0},{1,5},{5,1},{2,6},{6,2},{3,7},{7,3}} | collective-permute-start | bytes 1544 | tf_op jit(solution)/shard_map/ppermute | solution.py:605
  17.6 12.2 %collective-permute-start.13 = (bf16[64,2304]{1,0:T(8,128)(2,1)}, bf16[64,2304]{1,0:T(8,128)(2,1)}, u32[]{:S(2)}, u32[]{:S(2)}) collective-permute-start(bf16[64,2304]{1,0:T(8,128)(2,1)} %collective-permute-done.12.refs_3_), channel_id=1, source_target_pairs={{0,1},{1,0},{2,3},{3,2},{4,5},{5,4},{6,7},{7,6}} | collective-permute-start | bytes 884744 | tf_op jit(solution)/shard_map/ppermute | solution.py:573
  22.8 0.8 copy-start
  23.6 8.4 %collective-permute-start.14 = (bf16[128,2304]{1,0:T(8,128)(2,1)S(1)}, bf16[128,2304]{1,0:T(8,128)(2,1)S(1)}, u32[]{:S(2)}, u32[]{:S(2)}) collective-permute-start(bf16[128,2304]{1,0:T(8,128)(2,1)S(1)} %get-tuple-element.354), channel_id=1, source_target_pairs={{0,1},{1,0},{2,3},{3,2},{4,5},{5,4},{6,7},{7,6}} | collective-permute-start | bytes 1769480 | tf_op jit(solution)/shard_map/ppermute | solution.py:573
  24.7 29.0 %copy-start.2 = (bf16[1,2304]{1,0:T(2,128)(2,1)}, bf16[1,2304]{1,0:T(2,128)(2,1)S(1)}, u32[]{:S(2)}) copy-start(bf16[1,2304]{1,0:T(2,128)(2,1)S(1)} %reshape.44.g_ref.g) | copy-start | bytes 13828
  24.7 16.2 %collective-permute-start.15 = (bf16[128,2304]{1,0:T(8,128)(2,1)S(1)}, bf16[128,2304]{1,0:T(8,128)(2,1)S(1)}, u32[]{:S(2)}, u32[]{:S(2)}) collective-permute-start(bf16[128,2304]{1,0:T(8,128)(2,1)S(1)} %get-tuple-element.355), channel_id=1, source_target_pairs={{0,2},{1,3},{2,0},{3,1},{4,6},{5,7},{6,4},{7,5}} | collective-permute-start | bytes 1769480 | tf_op jit(solution)/shard_map/ppermute | solution.py:573
  29.8 22.1 %collective-permute-start.16 = (bf16[128,2304]{1,0:T(8,128)(2,1)S(1)}, bf16[128,2304]{1,0:T(8,128)(2,1)S(1)}, u32[]{:S(2)}, u32[]{:S(2)}) collective-permute-start(bf16[128,2304]{1,0:T(8,128)(2,1)S(1)} %get-tuple-element.356), channel_id=1, source_target_pairs={{0,3},{1,2},{2,1},{3,0},{4,7},{5,6},{6,5},{7,4}} | collective-permute-start | bytes 1769480 | tf_op jit(solution)/shard_map/ppermute | solution.py:573
  29.8 22.1 %copy-start.1 = (bf16[128,2304]{1,0:T(8,128)(2,1)S(1)}, bf16[128,2304]{1,0:T(8,128)(2,1)}, u32[]{:S(2)}) copy-start(bf16[128,2304]{1,0:T(8,128)(2,1)} %copy-done) | copy-start | bytes 1769476
  29.8 22.0 %copy-start.6 = (bf16[2,64,2304]{2,1,0:T(8,128)(2,1)S(1)}, bf16[2,64,2304]{2,1,0:T(8,128)(2,1)}, u32[]{:S(2)}) copy-start(bf16[2,64,2304]{2,1,0:T(8,128)(2,1)} %param.15) | copy-start | bytes 1769476
  32.0 21.1 %copy-start.9 = (bf16[2,64,2304]{2,1,0:T(8,128)(2,1)}, bf16[2,64,2304]{2,1,0:T(8,128)(2,1)S(1)}, u32[]{:S(2)}) copy-start(bf16[2,64,2304]{2,1,0:T(8,128)(2,1)S(1)} %get-tuple-element.617) | copy-start | bytes 1769476
  53.1 23.6 %collective-permute-start.18 = (f32[1,2304]{1,0:T(1,128)S(1)}, f32[1,2304]{1,0:T(1,128)S(1)}, u32[]{:S(2)}, u32[]{:S(2)}) collective-permute-start(f32[1,2304]{1,0:T(1,128)S(1)} %get-tuple-element.358.dg0.dg_ref), channel_id=1, source_target_pairs={{0,1},{1,0},{2,3},{3,2},{4,5},{5,4},{6,7},{7,6}} | collective-permute-start | bytes 27656 | tf_op jit(solution)/shard_map/ppermute | solution.py:573
  53.7 23.0 %collective-permute-start.17 = (bf16[128,2304]{1,0:T(8,128)(2,1)S(1)}, bf16[128,2304]{1,0:T(8,128)(2,1)S(1)}, u32[]{:S(2)}, u32[]{:S(2)}) collective-permute-start(bf16[128,2304]{1,0:T(8,128)(2,1)S(1)} %get-tuple-element.357.dx0), channel_id=1, source_target_pairs={{0,1},{1,0},{2,3},{3,2},{4,5},{5,4},{6,7},{7,6}} | collective-permute-start | bytes 1769480 | tf_op jit(solution)/shard_map/ppermute | solution.py:573
  77.0 9.9 %collective-permute-start.19 = (f32[32,2304]{1,0:T(8,128)S(1)}, f32[32,2304]{1,0:T(8,128)S(1)}, u32[]{:S(2)}, u32[]{:S(2)}) collective-permute-start(f32[32,2304]{1,0:T(8,128)S(1)} %dx_sums.1.mine_ref), channel_id=1, source_target_pairs={{0,2},{1,3},{2,0},{3,1},{4,6},{5,7},{6,4},{7,5}} | collective-permute-start | bytes 884744 | tf_op jit(solution)/shard_map/ppermute | solution.py:573
  86.9 2.6 %copy-start.8 = (s32[2,256]{1,0:T(2,128)S(1)}, s32[2,256]{1,0:T(2,128)}, u32[]{:S(2)}) copy-start(s32[2,256]{1,0:T(2,128)} %refs_0_.1) | copy-start | bytes 6148

commit v4 on v3

--- a/solution.py
+++ b/solution.py
@@ -10,8 +10,8 @@
 
 EPS = 1e-6
 C = 64
-G = 16
-GS = 16
+G = 2
+GS = 64
 C2 = 32
 CB = 256
 ZR = 128
@@ -143,7 +143,7 @@
 
     def fetch(q, j, carry):
         j = q * GS + j
-        g = pl.multiple_of((gls[0, j] >> 4) << 4, G)
+        g = pl.multiple_of((gls[0, j] >> 1) << 1, G)
         at = pl.multiple_of(j * G, G)
         pltpu.make_async_copy(e_ref.at[pl.ds(g, G)], buf.at[pl.ds(at, G)], sems.at[q]).start()
         return carry
@@ -165,7 +165,8 @@
         pos_ref[b * TB:(b + 1) * TB, :] = column(pos, b)
     lane1 = lax.broadcasted_iota(jnp.int32, (1, 128), 1)
     over = jnp.where((mx > C) | (mx2 > C2 - 1), 1.0, 0.0)
-    cnts = jnp.where(lane1 == 0, mx, jnp.where(lane1 == 1, cnt, jnp.where(lane1 == 2, over, cnt2)))
+    rounds = jnp.floor((mx + C - 1.0) * (1.0 / C))
+    cnts = jnp.where(lane1 == 0, rounds, jnp.where(lane1 == 1, cnt, jnp.where(lane1 == 2, over, cnt2)))
     cnt_ref[...] = cnts.astype(jnp.int32)
     facing = (mei ^ 2).astype(F32)
     sums_r = jnp.where(own_r == facing, slot2_r, -1.0)
@@ -520,7 +521,11 @@
     )(cnts, rows, srow, *pieces, de)
 
 
-def _write_kernel(cnt_ref, list_ref, map_ref, slot_ref, dx0, dx1, dg_ref, mine_ref, got_ref, de_in, de, dg_out, acc, sem):
+def _acc_kernel(lo, n, cnt_ref, oth_ref, slot_ref, dx0, dx1, de_in, de, acc, flag, z, sems):
+    z[...] = jnp.zeros_like(z)
+    _fill(z, de, sems, lo, 0, n, False)
+    for i in (0, 2):
+        flag[0, i] = jnp.maximum(cnt_ref[0, i], oth_ref[0, i])
     m = dx0.shape[0]
     j = _iota((C, m), 0)
     ohs = [jnp.where(slot_ref[i:i + 1, :] == j, 1.0, 0.0).astype(BF16) for i in (0, 1)]
@@ -528,6 +533,31 @@
         s = slice(c * CB, (c + 1) * CB)
         tot = jnp.dot(ohs[0], dx0[:, s], preferred_element_type=F32)
         acc[:, s] = tot + jnp.dot(ohs[1], dx1[:, s], preferred_element_type=F32)
+    _fill(z, de, sems, lo, 0, n, True)
+
+
+def _acc(cnts, other, slots, dx0, dx1, de, lo):
+    vs, d = de.shape
+    n = vs // ZR - lo
+    return pl.pallas_call(
+        functools.partial(_acc_kernel, lo, n),
+        out_shape=(
+            jax.ShapeDtypeStruct((vs, d), F32),
+            jax.ShapeDtypeStruct((C, d), F32),
+            jax.ShapeDtypeStruct((1, 4), jnp.int32),
+        ),
+        in_specs=[_sm(), _sm()] + [_vm()] * 3 + [_any()],
+        out_specs=(_any(), _vm(), _sm()),
+        scratch_shapes=_zscratch(d, n),
+        input_output_aliases={5: 0},
+        compiler_params=_params(8),
+        cost_estimate=_cost(n * 0.375),
+        name="fill_acc",
+    )(cnts, other, slots, dx0, dx1, de)
+
+
+def _write_kernel(cnt_ref, list_ref, map_ref, acc_in, mine_ref, got_ref, de_in, de, dg_out, acc, sem):
+    acc[...] = acc_in[...]
 
     def add(j, carry):
         at = pl.ds(map_ref[0, j], 1)
@@ -546,23 +576,24 @@
         return carry
 
     lax.fori_loop(0, here, put, 0)
-    dg_out[...] = mine_ref[C2 - 1:C2, :] + got_ref[C2 - 1:C2, :]
+    dg = mine_ref[C2 - 1:C2, :] + got_ref[C2 - 1:C2, :]
+    dg_out[...] = dg.reshape(dg_out.shape)
     lax.fori_loop(0, here, done, 0)
 
 
-def _write(cnts, rows, where, slots, dx0, dx1, dgp, mine, got, de):
+def _write(cnts, rows, where, acc, mine, got, de):
     vs, d = de.shape
     return pl.pallas_call(
         _write_kernel,
-        out_shape=(jax.ShapeDtypeStruct((vs, d), F32), jax.ShapeDtypeStruct((1, d), F32)),
-        in_specs=[_sm(), _sm(), _sm()] + [_vm()] * 6 + [_any()],
+        out_shape=(jax.ShapeDtypeStruct((vs, d), F32), jax.ShapeDtypeStruct((d,), F32)),
+        in_specs=[_sm(), _sm(), _sm()] + [_vm()] * 3 + [_any()],
         out_specs=(_any(), _vm()),
         scratch_shapes=[VMEM((C, d), F32), pltpu.SemaphoreType.DMA],
-        input_output_aliases={9: 0},
-        compiler_params=_params(8),
+        input_output_aliases={6: 0},
+        compiler_params=_params(6),
         cost_estimate=_cost(3),
         name="write_rows",
-    )(cnts, rows, where, slots, dx0, dx1, dgp, mine, got, de)
+    )(cnts, rows, where, acc, mine, got, de)
 
 
 def solution(mesh):
@@ -603,18 +634,16 @@
         mine = _sums(slots, dx, dx1, dg, dg1)
         got = swap(mine, 2)
         other = lax.ppermute(cnts, "dp", [(i, (i + 1) % ndp) for i in range(ndp)])
-        de = fill_rest(de)
-        dE, dg = _write(cnts, rows, where, slots, dx, dx1, dg, mine, got, de)
-        outs = u, xl, dE, dW, dg.reshape(d)
-        over = jnp.maximum(cnts[0, 2], other[0, 2])
-
-        inputs = ids, E, W, du, dres, g2
+        de, acc, flags = _acc(cnts, other, slots, dx, dx1, de, ZP + ZU + ZW)
+        dE, dg = _write(cnts, rows, where, acc, mine, got, de)
+        outs = u, xl, dE, dW, dg
+
+        inputs = ids, E, W, du, dres, g2, flags
 
         def again(c):
-            i0, _ = c
-            ids, E, W, du, dres, g2, i0 = lax.optimization_barrier((*inputs, c[0]))
-            top = lax.ppermute(cnts, "dp", [(i, (i + 1) % ndp) for i in range(ndp)])
-            rounds = (jnp.maximum(cnts[0, 0], top[0, 0]) + C - 1) // C
+            ids, E, W, du, dres, g2, fl, left = lax.optimization_barrier((*inputs, c[0]))
+            rounds = fl[0, 0]
+            i0 = left - left
 
             def more(q):
                 i, x, _ = q
@@ -631,9 +660,9 @@
             dg2 = dg + swap(dg, 1)
             dg = (dg2 + swap(dg2, 2)).reshape(d)
             dE = _scatter(cs, rows, srow, share(dx), fill_rest(de), ts, nk)
-            return i0 + 1, (u, xl, dE, dW, dg)
-
-        _, outs = lax.while_loop(lambda c: c[0] < over, again, (jnp.int32(0), outs))
+            return i0, (u, xl, dE, dW, dg)
+
+        _, outs = lax.while_loop(lambda c: c[0] > 0, again, (flags[0, 2], outs))
         return outs
 
     return jax.shard_map(

time: 89.8 us -> 84.4 us (0.940)
  Pallas kernels: 48.5 us -> 42.5 us
  waiting for transfers between devices: 25.5 us -> 30 us
  between operations: 3.47 us -> 0.95 us
  local copies, waits for them, and re-layouts: 2.08 us -> 0.6 us
    ppermute x9, waiting for transfers between devices: 25.5 us -> 30 us  [swap(): return lax.ppermute(a, 'tp', [(i, i ^ bit) for i in range(ntp)])]
    pallas_call x1, Pallas kernels: 9.26 us -> 6.93 us  [_u(): pl.pallas_call(_u_kernel, out_shape=(jax.ShapeDtypeStruct((nk, ntok // nk...]
    pallas_call x1, Pallas kernels: 6.71 us -> 5.24 us  [_index_call(): pl.pallas_call(functools.partial(_index_kernel, vs, ntp, first), out_shap...]
    pallas_call x1, Pallas kernels: 2.18 us -> 0.92 us  [_expand(): pl.pallas_call(functools.partial(_expand_kernel, ts, x is not None), out_...]
    pallas_call x1, Pallas kernels: 5.14 us -> 3.94 us  [_p_terms(): pl.pallas_call(functools.partial(_p_kernel, ts), out_shape=(jax.ShapeDtyp...]
    pallas_call x1, Pallas kernels: 13.7 us -> 12.5 us  [_dw(): pl.pallas_call(functools.partial(_dw_kernel, lo, nz, -(-nz // steps)), ou...]
    pallas_call x1, Pallas kernels: 8.14 us -> 9.28 us  [_acc(): pl.pallas_call(functools.partial(_acc_kernel, lo, n), out_shape=(jax.Shap...]
  transfers between devices with their start and end apart: 10 -> 10, of which waited for: 3 -> 3; matrix products, arithmetic and copies ran while one was open for 1% -> 1% of each run, Pallas kernels for 43% -> 42%
where the time goes in v4:
time: 84.4 us; the launch traced here: 84.2 us
  Pallas kernels  42.5 us (50%)
  waiting for transfers between devices  30 us (36%)
  starting transfers between devices  9.37 us (11%)
  between operations  0.95 us (1%)
    ppermute x9, waiting for transfers between devices, swap(): return lax.ppermute(a, 'tp', [(i, i ^ bit) for i in range(ntp)])  30 us
    pallas_call x1, Pallas kernels, _dw(): pl.pallas_call(functools.partial(_dw_kernel, lo, nz, -(-nz // steps)), ou...  12.5 us
    pallas_call x1, Pallas kernels, _acc(): pl.pallas_call(functools.partial(_acc_kernel, lo, n), out_shape=(jax.Shap...  9.28 us
    ppermute x9, starting transfers between devices, swap(): return lax.ppermute(a, 'tp', [(i, i ^ bit) for i in range(ntp)])  7.8 us
    pallas_call x1, Pallas kernels, _u(): pl.pallas_call(_u_kernel, out_shape=(jax.ShapeDtypeStruct((nk, ntok // nk...  6.93 us
    pallas_call x1, Pallas kernels, _index_call(): pl.pallas_call(functools.partial(_index_kernel, vs, ntp, first), out_shap...  5.24 us
    pallas_call x1, Pallas kernels, _p_terms(): pl.pallas_call(functools.partial(_p_kernel, ts), out_shape=(jax.ShapeDtyp...  3.94 us
    pallas_call x1, Pallas kernels, _write(): pl.pallas_call(_write_kernel, out_shape=(jax.ShapeDtypeStruct((vs, d), F3...  2.26 us
  transfers between devices with their start and end apart: 10, of which 3 were waited for; matrix products, arithmetic and copies ran while one was open for 1% of the time, Pallas kernels for 42%

profile of v4, /device:TPU:0, one launch (start us, length us, event | category | flops | bytes accessed | tf_op | source)
XLA Modules:
  0.0 84.2 jit_solution(5764811887802941067)
XLA Ops:
  0.6 0.0 copy-start.4
  0.6 0.0 copy-start.3
  0.7 5.2 %index_gather.4 = (bf16[64,2304]{1,0:T(8,128)(2,1)S(1)}, f32[512,1]{1,0:T(8,128)S(1)}, f32[1,512]{1,0:T(1,128)}, s32[1,512]{1,0:T(1,128)S(1)}, s32[1,128]{1,0:T(...) custom-call(s32[2,256]{1,0:T(2,128)} %refs_0_.1, bf16[8192,2304]{1,0:T(8,128)(2,1)} %refs_1_.1), custom_call_target="tpu_custom_call" | custom-call | flops 20000000000 | bytes 1000000 | tf_op jit(solution)/shard_map/index_gather/pallas_call | solution.py:207
  5.9 3.2 %collective-permute-start.13 = (bf16[64,2304]{1,0:T(8,128)(2,1)S(1)}, bf16[64,2304]{1,0:T(8,128)(2,1)S(1)}, u32[]{:S(2)}, u32[]{:S(2)}) collective-permute-start(bf16[64,2304]{1,0:T(8,128)(2,1)S(1)} %get-tuple-element.157.refs_1_), channel_id=1, source_target_pairs={{0,2},{1,3},{2,0},{3,1},{4,6},{5,7},{6,4},{7,5}} | collective-permute-start | bytes 884744 | tf_op jit(solution)/shard_map/ppermute | solution.py:604
  9.1 0.0 collective-permute-start.12
  9.1 1.6 %collective-permute-start.11 = (s32[1,128]{1,0:T(1,128)S(1)}, s32[1,128]{1,0:T(1,128)S(1)}, u32[]{:S(2)}, u32[]{:S(2)}) collective-permute-start(s32[1,128]{1,0:T(1,128)S(1)} %get-tuple-element.154.cnt_ref), channel_id=1, source_target_pairs={{0,4},{4,0},{1,5},{5,1},{2,6},{6,2},{3,7},{7,3}} | collective-permute-start | bytes 1544 | tf_op jit(solution)/shard_map/ppermute | solution.py:636
  10.6 5.5 %collective-permute-done.13.refs_3_ = bf16[64,2304]{1,0:T(8,128)(2,1)S(1)} collective-permute-done((bf16[64,2304]{1,0:T(8,128)(2,1)S(1)}, bf16[64,2304]{1,0:T(8,128)(2,1)S(1)}, u32[]{:S(2)}, u32[]{:S(2)}) %collective-permute-start.13) | collective-permute-done | bytes 294944 | tf_op jit(solution)/shard_map/ppermute | solution.py:604
  16.2 0.0 collective-permute-start.14
  16.2 3.9 %p_terms.3 = (bf16[128,2304]{1,0:T(8,128)(2,1)S(1)}, bf16[128,2304]{1,0:T(8,128)(2,1)S(1)}, bf16[128,2304]{1,0:T(8,128)(2,1)S(1)}, bf16[128,2304]{1,0:T(8,128)(2,1)S(1)}, f32[8192,2304]{1,0:T(8,128)}) custom-call(bf16[2,256,1024]{2,1,0:T(8,128)(2,1)S(1)} %copy-done.4, bf16[2304,1024]{1,0:T(8,128)(2,1)S(1)} %copy-done.3), custom_call_target="tpu_custom_call" | custom-call | flops 20000000000 | bytes 1000000 | tf_op jit(solution)/shard_map/p_terms/pallas_call | solution.py:306
  20.1 0.5 collective-permute-start.15
  20.6 1.8 %collective-permute-start.16 = (bf16[128,2304]{1,0:T(8,128)(2,1)S(1)}, bf16[128,2304]{1,0:T(8,128)(2,1)S(1)}, u32[]{:S(2)}, u32[]{:S(2)}) collective-permute-start(bf16[128,2304]{1,0:T(8,128)(2,1)S(1)} %get-tuple-element.161), channel_id=1, source_target_pairs={{0,2},{1,3},{2,0},{3,1},{4,6},{5,7},{6,4},{7,5}} | collective-permute-start | bytes 1769480 | tf_op jit(solution)/shard_map/ppermute | solution.py:604
  22.4 0.0 collective-permute-done.12.refs_2_
  22.4 0.0 collective-permute-start.17
  22.4 0.0 copy-start.6
  22.4 0.9 %expand.2 = (bf16[512,2304]{1,0:T(8,128)(2,1)S(1)}, bf16[2,64,2304]{2,1,0:T(8,128)(2,1)S(1)}) custom-call(f32[512,1]{1,0:T(8,128)S(1)} %get-tuple-element.156.refs_0_, bf16[64,2304]{1,0:T(8,128)(2,1)S(1)} %get-tuple-element.157.refs_1_, bf16[64,2304]{1,0:T(8,128)(2,1)S(1)} %collective-permute-done.12.refs_2_, ...), custom_call_target="tpu_custom_call" | custom-call | flops 12000000000 | bytes 1000000 | tf_op jit(solution)/shard_map/expand/pallas_call | solution.py:255
  23.3 0.0 copy-start.9
  23.4 0.0 collective-permute-done.15.p1
  23.4 13.5 %collective-permute-done.16.p2 = bf16[128,2304]{1,0:T(8,128)(2,1)S(1)} collective-permute-done((bf16[128,2304]{1,0:T(8,128)(2,1)S(1)}, bf16[128,2304]{1,0:T(8,128)(2,1)S(1)}, u32[]{:S(2)}, u32[]{:S(2)}) %collective-permute-start.16) | collective-permute-done | bytes 589856 | tf_op jit(solution)/shard_map/ppermute | solution.py:604
  36.9 11.0 %collective-permute-done.17.p3 = bf16[128,2304]{1,0:T(8,128)(2,1)S(1)} collective-permute-done((bf16[128,2304]{1,0:T(8,128)(2,1)S(1)}, bf16[128,2304]{1,0:T(8,128)(2,1)S(1)}, u32[]{:S(2)}, u32[]{:S(2)}) %collective-permute-start.17) | collective-permute-done | bytes 589856 | tf_op jit(solution)/shard_map/ppermute | solution.py:604
  47.8 1.2 %dx_form.3 = (bf16[128,2304]{1,0:T(8,128)(2,1)S(1)}, f32[1,2304]{1,0:T(1,128)S(1)}) custom-call(bf16[128,2304]{1,0:T(8,128)(2,1)S(1)} %bitcast.14, bf16[128,2304]{1,0:T(8,128)(2,1)S(1)} %get-tuple-element.159.p0, bf16[128,2304]{1,0:T(8,128)(2,1)S(1)} %collective-permute-done.15.p1, bf16[128,2304]{1,0:T(8,128)(2,1)S(1)} %collective-permute-done.16.p2, ...), custom_call_target="tpu_custom_call" | custom-call | flops 8000000000 | bytes 1000000 | tf_op jit(solution)/shard_map/dx_form/pallas_call | solution.py:360
  49.0 0.6 collective-permute-start.19
  49.6 0.0 collective-permute-start.18
  49.6 6.9 %u_terms.3 = (bf16[2,256,1024]{2,1,0:T(8,128)(2,1)}, bf16[512,2304]{1,0:T(8,128)(2,1)S(1)}, f32[8192,2304]{1,0:T(8,128)}) custom-call(bf16[512,2304]{1,0:T(8,128)(2,1)S(1)} %get-tuple-element.164.x_ref, bf16[1,2304]{1,0:T(2,128)(2,1)S(1)} %reshape.33.g.g_ref, bf16[2304,1024]{1,0:T(8,128)(2,1)S(1)} %copy-done.3, ...), custom_call_target="tpu_custom_call", output_to_operand_aliasing={{2}: (3, {})} | custom-call | flops 40000000000 | bytes 1000000 | tf_op jit(solution)/shard_map/u_terms/pallas_call | solution.py:416
  56.6 12.5 %dw_terms.3 = (f32[2304,1024]{1,0:T(8,128)}, f32[8192,2304]{1,0:T(8,128)}) custom-call(bf16[512,2304]{1,0:T(8,128)(2,1)S(1)} %get-tuple-element.166.n_ref, bf16[2,256,1024]{2,1,0:T(8,128)(2,1)S(1)} %copy-done.4, f32[8192,2304]{1,0:T(8,128)} %get-tuple-element.167.de_in), custom_call_target="tpu_custom_call", output_to_operand_aliasing={{1}: (2, {})} | custom-call | flops 40000000000 | bytes 1000000 | tf_op jit(solution)/shard_map/dw_terms/pallas_call | solution.py:456
  69.1 0.0 collective-permute-done.19.dg1
  69.1 0.3 dx_sums.1.mine_ref
  69.4 1.7 %collective-permute-start.20 = (f32[32,2304]{1,0:T(8,128)S(1)}, f32[32,2304]{1,0:T(8,128)S(1)}, u32[]{:S(2)}, u32[]{:S(2)}) collective-permute-start(f32[32,2304]{1,0:T(8,128)S(1)} %dx_sums.1.mine_ref), channel_id=1, source_target_pairs={{0,2},{1,3},{2,0},{3,1},{4,6},{5,7},{6,4},{7,5}} | collective-permute-start | bytes 884744 | tf_op jit(solution)/shard_map/ppermute | solution.py:604
  71.1 0.0 collective-permute-done.11.oth_ref
  71.1 9.3 %fill_acc.1 = (f32[8192,2304]{1,0:T(8,128)}, f32[64,2304]{1,0:T(8,128)S(1)}, s32[1,4]{1,0:T(1,128)S(1)}) custom-call(s32[1,128]{1,0:T(1,128)S(1)} %get-tuple-element.154.cnt_ref, s32[1,128]{1,0:T(1,128)S(1)} %collective-permute-done.11.oth_ref, f32[4,128]{1,0:T(4,128)S(1)} %get-tuple-element.155.slot_ref, ...), custom_call_target="tpu_custom_call", output_to_operand_aliasing={{0}: (5, {})} | custom-call | flops 30000001024 | bytes 1000000 | tf_op jit(solution)/shard_map/fill_acc/pallas_call | solution.py:542
  80.4 0.6 slice.6
  81.0 2.3 %write_rows.1 = (f32[8192,2304]{1,0:T(8,128)}, f32[2304]{0:T(1024)}) custom-call(s32[1,128]{1,0:T(1,128)S(1)} %get-tuple-element.154.cnt_ref, s32[1,512]{1,0:T(1,128)S(1)} %get-tuple-element.171.list_ref, s32[1,128]{1,0:T(1,128)S(1)} %get-tuple-element.172.map_ref, f32[64,2304]{1,0:T(8,128)S(1)} %get-tuple-element.173.acc_in, ...), custom_call_target="tpu_custom_call", output_to_operand_aliasing={{0}: (6, {})} | custom-call | flops 12000000000 | bytes 1000000 | tf_op jit(solution)/shard_map/write_rows/pallas_call | solution.py:586
  83.3 0.7 while.28
  (14 shorter events, 0.0 us)
Async XLA Ops:
  0.6 15.5 %copy-start.4 = (bf16[2,256,1024]{2,1,0:T(8,128)(2,1)S(1)}, bf16[2,256,1024]{2,1,0:T(8,128)(2,1)}, u32[]{:S(2)}) copy-start(bf16[2,256,1024]{2,1,0:T(8,128)(2,1)} %du_ref.3) | copy-start | bytes 3145732
  0.6 15.5 %copy-start.3 = (bf16[2304,1024]{1,0:T(8,128)(2,1)S(1)}, bf16[2304,1024]{1,0:T(8,128)(2,1)}, u32[]{:S(2)}) copy-start(bf16[2304,1024]{1,0:T(8,128)(2,1)} %w_ref.3) | copy-start | bytes 14155780
  5.9 10.3 %collective-permute-start.13 = (bf16[64,2304]{1,0:T(8,128)(2,1)S(1)}, bf16[64,2304]{1,0:T(8,128)(2,1)S(1)}, u32[]{:S(2)}, u32[]{:S(2)}) collective-permute-start(bf16[64,2304]{1,0:T(8,128)(2,1)S(1)} %get-tuple-element.157.refs_1_), channel_id=1, source_target_pairs={{0,2},{1,3},{2,0},{3,1},{4,6},{5,7},{6,4},{7,5}} | collective-permute-start | bytes 884744 | tf_op jit(solution)/shard_map/ppermute | solution.py:604
  9.1 13.3 %collective-permute-start.12 = (bf16[64,2304]{1,0:T(8,128)(2,1)S(1)}, bf16[64,2304]{1,0:T(8,128)(2,1)S(1)}, u32[]{:S(2)}, u32[]{:S(2)}) collective-permute-start(bf16[64,2304]{1,0:T(8,128)(2,1)S(1)} %get-tuple-element.157.refs_1_), channel_id=1, source_target_pairs={{0,1},{1,0},{2,3},{3,2},{4,5},{5,4},{6,7},{7,6}} | collective-permute-start | bytes 884744 | tf_op jit(solution)/shard_map/ppermute | solution.py:604
  9.1 11.5 %copy-start.2 = (bf16[2304]{0:T(1024)(128)(2,1)S(1)}, bf16[2304]{0:T(1024)(128)(2,1)}, u32[]{:S(2)}) copy-start(bf16[2304]{0:T(1024)(128)(2,1)} %param.12) | copy-start | bytes 13828
  9.1 62.1 %collective-permute-start.11 = (s32[1,128]{1,0:T(1,128)S(1)}, s32[1,128]{1,0:T(1,128)S(1)}, u32[]{:S(2)}, u32[]{:S(2)}) collective-permute-start(s32[1,128]{1,0:T(1,128)S(1)} %get-tuple-element.154.cnt_ref), channel_id=1, source_target_pairs={{0,4},{4,0},{1,5},{5,1},{2,6},{6,2},{3,7},{7,3}} | collective-permute-start | bytes 1544 | tf_op jit(solution)/shard_map/ppermute | solution.py:636
  16.2 6.3 %collective-permute-start.14 = (bf16[64,2304]{1,0:T(8,128)(2,1)S(1)}, bf16[64,2304]{1,0:T(8,128)(2,1)S(1)}, u32[]{:S(2)}, u32[]{:S(2)}) collective-permute-start(bf16[64,2304]{1,0:T(8,128)(2,1)S(1)} %collective-permute-done.13.refs_3_), channel_id=1, source_target_pairs={{0,1},{1,0},{2,3},{3,2},{4,5},{5,4},{6,7},{7,6}} | collective-permute-start | bytes 884744 | tf_op jit(solution)/shard_map/ppermute | solution.py:604
  20.1 3.2 %collective-permute-start.15 = (bf16[128,2304]{1,0:T(8,128)(2,1)S(1)}, bf16[128,2304]{1,0:T(8,128)(2,1)S(1)}, u32[]{:S(2)}, u32[]{:S(2)}) collective-permute-start(bf16[128,2304]{1,0:T(8,128)(2,1)S(1)} %get-tuple-element.160), channel_id=1, source_target_pairs={{0,1},{1,0},{2,3},{3,2},{4,5},{5,4},{6,7},{7,6}} | collective-permute-start | bytes 1769480 | tf_op jit(solution)/shard_map/ppermute | solution.py:604
  20.6 29.0 %copy-start = (bf16[1,2304]{1,0:T(2,128)(2,1)}, bf16[1,2304]{1,0:T(2,128)(2,1)S(1)}, u32[]{:S(2)}) copy-start(bf16[1,2304]{1,0:T(2,128)(2,1)S(1)} %reshape.33.g.g_ref) | copy-start | bytes 13828
  20.6 16.2 %collective-permute-start.16 = (bf16[128,2304]{1,0:T(8,128)(2,1)S(1)}, bf16[128,2304]{1,0:T(8,128)(2,1)S(1)}, u32[]{:S(2)}, u32[]{:S(2)}) collective-permute-start(bf16[128,2304]{1,0:T(8,128)(2,1)S(1)} %get-tuple-element.161), channel_id=1, source_target_pairs={{0,2},{1,3},{2,0},{3,1},{4,6},{5,7},{6,4},{7,5}} | collective-permute-start | bytes 1769480 | tf_op jit(solution)/shard_map/ppermute | solution.py:604
  22.4 25.4 %collective-permute-start.17 = (bf16[128,2304]{1,0:T(8,128)(2,1)S(1)}, bf16[128,2304]{1,0:T(8,128)(2,1)S(1)}, u32[]{:S(2)}, u32[]{:S(2)}) collective-permute-start(bf16[128,2304]{1,0:T(8,128)(2,1)S(1)} %get-tuple-element.162), channel_id=1, source_target_pairs={{0,3},{1,2},{2,1},{3,0},{4,7},{5,6},{6,5},{7,4}} | collective-permute-start | bytes 1769480 | tf_op jit(solution)/shard_map/ppermute | solution.py:604
  22.4 25.4 %copy-start.6 = (bf16[2,64,2304]{2,1,0:T(8,128)(2,1)S(1)}, bf16[2,64,2304]{2,1,0:T(8,128)(2,1)}, u32[]{:S(2)}) copy-start(bf16[2,64,2304]{2,1,0:T(8,128)(2,1)} %param.15) | copy-start | bytes 1769476
  23.3 25.7 %copy-start.9 = (bf16[2,64,2304]{2,1,0:T(8,128)(2,1)}, bf16[2,64,2304]{2,1,0:T(8,128)(2,1)S(1)}, u32[]{:S(2)}) copy-start(bf16[2,64,2304]{2,1,0:T(8,128)(2,1)S(1)} %get-tuple-element.302) | copy-start | bytes 1769476
  49.0 20.1 %collective-permute-start.19 = (f32[1,2304]{1,0:T(1,128)S(1)}, f32[1,2304]{1,0:T(1,128)S(1)}, u32[]{:S(2)}, u32[]{:S(2)}) collective-permute-start(f32[1,2304]{1,0:T(1,128)S(1)} %get-tuple-element.174.dg0), channel_id=1, source_target_pairs={{0,1},{1,0},{2,3},{3,2},{4,5},{5,4},{6,7},{7,6}} | collective-permute-start | bytes 27656 | tf_op jit(solution)/shard_map/ppermute | solution.py:604
  49.6 19.5 %collective-permute-start.18 = (bf16[128,2304]{1,0:T(8,128)(2,1)S(1)}, bf16[128,2304]{1,0:T(8,128)(2,1)S(1)}, u32[]{:S(2)}, u32[]{:S(2)}) collective-permute-start(bf16[128,2304]{1,0:T(8,128)(2,1)S(1)} %get-tuple-element.163.dx0), channel_id=1, source_target_pairs={{0,1},{1,0},{2,3},{3,2},{4,5},{5,4},{6,7},{7,6}} | collective-permute-start | bytes 1769480 | tf_op jit(solution)/shard_map/ppermute | solution.py:604
  69.4 11.6 %collective-permute-start.20 = (f32[32,2304]{1,0:T(8,128)S(1)}, f32[32,2304]{1,0:T(8,128)S(1)}, u32[]{:S(2)}, u32[]{:S(2)}) collective-permute-start(f32[32,2304]{1,0:T(8,128)S(1)} %dx_sums.1.mine_ref), channel_id=1, source_target_pairs={{0,2},{1,3},{2,0},{3,1},{4,6},{5,7},{6,4},{7,5}} | collective-permute-start | bytes 884744 | tf_op jit(solution)/shard_map/ppermute | solution.py:604
  81.0 2.3 %copy-start.8 = (s32[2,256]{1,0:T(2,128)S(1)}, s32[2,256]{1,0:T(2,128)}, u32[]{:S(2)}) copy-start(s32[2,256]{1,0:T(2,128)} %refs_0_.1) | copy-start | bytes 6148

commit v5 on v4

--- a/solution.py
+++ b/solution.py
@@ -15,7 +15,8 @@
 C2 = 32
 CB = 256
 ZR = 128
-ZP, ZU, ZW = 8, 14, 22
+ZI, ZP, ZU, ZW, ZD = 6, 9, 15, 18, 3
+AT_P, AT_U, AT_W, AT_D, AT_R = ZI, ZI + ZP, ZI + ZP + ZU, ZI + ZP + ZU + ZW, ZI + ZP + ZU + ZW + ZD
 TB = 64
 
 F32 = jnp.float32
@@ -51,10 +52,27 @@
     return lax.axis_index("tp").astype(jnp.int32)
 
 
+def _fill(z, o, sems, lo, first, n, wait):
+    def step(i, carry):
+        at = pl.multiple_of((lo + i) * ZR, ZR)
+        c = pltpu.make_async_copy(z, o.at[pl.ds(at, ZR)], sems.at[i])
+        c.wait() if wait else c.start()
+        return carry
+
+    lax.fori_loop(first, first + n, step, 0)
+
+
+def _zscratch(d, n):
+    return [VMEM((ZR, d), F32), pltpu.SemaphoreType.DMA((n,))]
+
+
 def _index_kernel(vs, ntp, first, *refs):
     if first:
-        ids_ref, e_ref, tab_ref, pos_ref, srow_ref, list_ref, cnt_ref, slot_ref, map_ref, buf, glv, gls, gsem, sems = refs
+        refs, (de, z, zsems) = refs[:-2], (refs[9], *refs[-2:])
+        ids_ref, e_ref, tab_ref, pos_ref, srow_ref, list_ref, cnt_ref, slot_ref, map_ref, _, buf, glv, gls, gsem, sems = refs
         base = 0.0
+        z[...] = jnp.zeros_like(z)
+        _fill(z, de, zsems, 0, 0, ZI, False)
     else:
         c_ref, ids_ref, e_ref, tab_ref, pos_ref, srow_ref, list_ref, cnt_ref, slot_ref, map_ref, buf, glv, gls, gsem, sems = refs
         base = (c_ref[0] * C).astype(F32)
@@ -77,14 +95,9 @@
         return sum(a[8 * q:8 * q + 8] for q in range(1, TB // 8)) + a[:8]
 
     lane = _iota((TB, ntok), 1)
-    ts = t // ntp
-    part = lax.broadcasted_iota(jnp.int32, (1, ntok), 1) // ts % ntp
-    chips = [jnp.where(part // 2 == c, 1.0, 0.0) for c in range(ntp // 2)]
     thr = _iota((TB, 128), 1) * float(vs)
     rank8 = jnp.zeros((8, ntok), F32)
     below8 = jnp.zeros((8, 128), F32)
-    rank28 = jnp.zeros((8, ntok), F32)
-    below28 = [jnp.zeros((8, 128), F32) for _ in chips]
     idcs = []
     for b in range(nb):
         idc = column(idr, b)
@@ -95,11 +108,6 @@
         key = jnp.where(seen > 0.5, float(vs * ntp), idc)
         rank8 = rank8 + fold(jnp.where(jnp.broadcast_to(key, (TB, ntok)) < idr, 1.0, 0.0))
         below8 = below8 + fold(jnp.where(jnp.broadcast_to(key, (TB, 128)) < thr, 1.0, 0.0))
-        c = b * TB // ts % ntp // 2
-        seen = jnp.max(jnp.where(dup, chips[c], 0.0), axis=1, keepdims=True)
-        key = jnp.where(seen > 0.5, float(vs * ntp), idc)
-        rank28 = rank28 + fold(jnp.where(jnp.broadcast_to(key, (TB, ntok)) < idr, chips[c], 0.0))
-        below28[c] = below28[c] + fold(jnp.where(jnp.broadcast_to(key, (TB, 128)) < thr, 1.0, 0.0))
     rank = jnp.sum(rank8, axis=0, keepdims=True)
     below = jnp.sum(below8, axis=0, keepdims=True)
     own_r = jnp.floor(idr * (1.0 / vs))
@@ -113,6 +121,43 @@
         cnt = jnp.where(me == float(d), nd, cnt)
         mx = jnp.maximum(mx, nd)
     slot_r = rank - start
+    my_r = jnp.where(own_r == me, slot_r, -1.0)
+
+    slot_l = _iota((TB, 128), 1) + base
+    acc = jnp.zeros((TB, 128), F32)
+    mys = []
+    for b in range(nb):
+        my_c = column(my_r, b)
+        mys.append(my_c)
+        acc = jnp.maximum(acc, jnp.where(my_c == slot_l, idcs[b] - lo, 0.0))
+    glv[...] = jnp.broadcast_to(jnp.max(acc, axis=0, keepdims=True), (8, 128)).astype(jnp.int32)
+    cp = pltpu.make_async_copy(glv, gls, gsem)
+    cp.start()
+    cp.wait()
+
+    def fetch(q, j, carry):
+        j = q * GS + j
+        g = pl.multiple_of((gls[0, j] >> 1) << 1, G)
+        at = pl.multiple_of(j * G, G)
+        pltpu.make_async_copy(e_ref.at[pl.ds(g, G)], buf.at[pl.ds(at, G)], sems.at[q]).start()
+        return carry
+
+    for q in range(C // GS):
+        lax.fori_loop(0, GS, functools.partial(fetch, q), 0, unroll=8)
+
+    ts = t // ntp
+    part = lax.broadcasted_iota(jnp.int32, (1, ntok), 1) // ts % ntp
+    chips = [jnp.where(part // 2 == c, 1.0, 0.0) for c in range(ntp // 2)]
+    rank28 = jnp.zeros((8, ntok), F32)
+    below28 = [jnp.zeros((8, 128), F32) for _ in chips]
+    for b in range(nb):
+        idc = idcs[b]
+        dup = (jnp.broadcast_to(idc, (TB, ntok)) == idr) & (lane < _iota((TB, ntok), 0) + float(b * TB))
+        c = b * TB // ts % ntp // 2
+        seen = jnp.max(jnp.where(dup, chips[c], 0.0), axis=1, keepdims=True)
+        key = jnp.where(seen > 0.5, float(vs * ntp), idc)
+        rank28 = rank28 + fold(jnp.where(jnp.broadcast_to(key, (TB, ntok)) < idr, chips[c], 0.0))
+        below28[c] = below28[c] + fold(jnp.where(jnp.broadcast_to(key, (TB, 128)) < thr, 1.0, 0.0))
     rank2 = jnp.sum(rank28, axis=0, keepdims=True)
     below2 = [jnp.sum(b8, axis=0, keepdims=True) for b8 in below28]
     start2 = jnp.zeros_like(rank)
@@ -127,30 +172,6 @@
                 cnt2 = jnp.where(me == float(d), nd, cnt2)
                 mx2 = jnp.maximum(mx2, nd)
     slot2_r = rank2 - start2
-    my_r = jnp.where(own_r == me, slot_r, -1.0)
-
-    slot_l = _iota((TB, 128), 1) + base
-    acc = jnp.zeros((TB, 128), F32)
-    mys = []
-    for b in range(nb):
-        my_c = column(my_r, b)
-        mys.append(my_c)
-        acc = jnp.maximum(acc, jnp.where(my_c == slot_l, idcs[b] - lo, 0.0))
-    glv[...] = jnp.broadcast_to(jnp.max(acc, axis=0, keepdims=True), (8, 128)).astype(jnp.int32)
-    cp = pltpu.make_async_copy(glv, gls, gsem)
-    cp.start()
-    cp.wait()
-
-    def fetch(q, j, carry):
-        j = q * GS + j
-        g = pl.multiple_of((gls[0, j] >> 1) << 1, G)
-        at = pl.multiple_of(j * G, G)
-        pltpu.make_async_copy(e_ref.at[pl.ds(g, G)], buf.at[pl.ds(at, G)], sems.at[q]).start()
-        return carry
-
-    for q in range(C // GS):
-        lax.fori_loop(0, GS, functools.partial(fetch, q), 0, unroll=8)
-
     srow_ref[...] = my_r
     full = jnp.zeros((8, ntok), F32)
     lane8 = _iota((8, ntok), 1)
@@ -198,6 +219,8 @@
         sel = jnp.where(_iota((GS, GS * G), 1) == mine, 1.0, 0.0).astype(BF16)
         pltpu.make_async_copy(e_ref.at[pl.ds(0, GS * G)], buf.at[r], sems.at[q]).wait()
         tab_ref[q * GS:(q + 1) * GS, :] = jnp.dot(sel, buf[r, :], preferred_element_type=F32).astype(BF16)
+    if first:
+        _fill(z, de, zsems, 0, 0, ZI, True)
 
 
 def _index_call(chunk, ids, E, ntp):
@@ -214,17 +237,17 @@
             jax.ShapeDtypeStruct((1, 128), jnp.int32),
             jax.ShapeDtypeStruct((4, ntok // ntp), F32),
             jax.ShapeDtypeStruct((1, 128), jnp.int32),
-        ),
+        ) + ((jax.ShapeDtypeStruct((vs, d), F32),) if first else ()),
         in_specs=([] if first else [_sm()]) + [_vm(), pl.BlockSpec(memory_space=pltpu.HBM)],
-        out_specs=(_vm(),) * 7,
+        out_specs=(_vm(),) * 7 + ((_any(),) if first else ()),
         scratch_shapes=[
             VMEM((C * G, d), BF16),
             VMEM((8, 128), jnp.int32),
             pltpu.SMEM((8, 128), jnp.int32),
             pltpu.SemaphoreType.DMA,
             pltpu.SemaphoreType.DMA((C // GS,)),
-        ],
-        compiler_params=_params(14),
+        ] + (_zscratch(d, ZI) if first else []),
+        compiler_params=_params(8),
         cost_estimate=_cost(5),
         name="index_gather",
     )(*([] if first else [chunk.reshape(1)]), ids, E)
@@ -263,21 +286,7 @@
     )(*ins)
 
 
-def _fill(z, o, sems, lo, first, n, wait):
-    def step(i, carry):
-        at = pl.multiple_of((lo + i) * ZR, ZR)
-        c = pltpu.make_async_copy(z, o.at[pl.ds(at, ZR)], sems.at[i])
-        c.wait() if wait else c.start()
-        return carry
-
-    lax.fori_loop(first, first + n, step, 0)
-
-
-def _zscratch(d, n):
-    return [VMEM((ZR, d), F32), pltpu.SemaphoreType.DMA((n,))]
-
-
-def _p_kernel(ts, du_ref, w_ref, *refs):
+def _p_kernel(ts, du_ref, w_ref, de_in, *refs):
     outs, (de, dur, z, sems) = refs[:-4], refs[-4:]
     nk = du_ref.shape[0]
 
@@ -288,7 +297,7 @@
             for r in range(4):
                 at = pl.multiple_of((_me() ^ r) * ts, ts)
                 dur[pl.ds((r * nk + k) * ts, ts), :] = du_ref[k, pl.ds(at, ts), :]
-        _fill(z, de, sems, 0, 0, ZP, False)
+        _fill(z, de, sems, AT_P, 0, ZP, False)
 
     out = lax.dot_general(dur[...], w_ref[...], (((1,), (1,)), ((), ())), preferred_element_type=F32)
     for i, o in enumerate(outs):
@@ -296,24 +305,25 @@
 
     @pl.when(pl.program_id(0) == pl.num_programs(0) - 1)
     def _():
-        _fill(z, de, sems, 0, 0, ZP, True)
-
-
-def _p_terms(du, W, ts, vs):
+        _fill(z, de, sems, AT_P, 0, ZP, True)
+
+
+def _p_terms(du, W, ts, de):
     nk, t, f = du.shape
     d = W.shape[0]
     cb = 3 * CB
     out = pl.pallas_call(
         functools.partial(_p_kernel, ts),
-        out_shape=(jax.ShapeDtypeStruct((nk * ts, d), BF16),) * 4 + (jax.ShapeDtypeStruct((vs, d), F32),),
+        out_shape=(jax.ShapeDtypeStruct((nk * ts, d), BF16),) * 4 + (jax.ShapeDtypeStruct(de.shape, F32),),
         grid=(d // cb,),
-        in_specs=[pl.BlockSpec((nk, t, f), lambda i: (0, 0, 0)), pl.BlockSpec((cb, f), lambda i: (i, 0))],
+        in_specs=[pl.BlockSpec((nk, t, f), lambda i: (0, 0, 0)), pl.BlockSpec((cb, f), lambda i: (i, 0)), _any()],
         out_specs=(pl.BlockSpec((nk * ts, cb), lambda i: (0, i)),) * 4 + (_any(),),
         scratch_shapes=[VMEM((nk * t, f), BF16)] + _zscratch(d, ZP),
+        input_output_aliases={2: 4},
         compiler_params=_params(20),
         cost_estimate=_cost(5),
         name="p_terms",
-    )(du, W)
+    )(du, W, de)
     return out[:4], out[4]
 
 
@@ -338,7 +348,9 @@
     )(de)
 
 
-def _dx_kernel(x, p0, p1, p2, p3, dres, g, dx, dg):
+def _dx_kernel(x, p0, p1, p2, p3, dres, g, de_in, dx, dg, de, z, sems):
+    z[...] = jnp.zeros_like(z)
+    _fill(z, de, sems, AT_D, 0, ZD, False)
     rows = 32
     tot = None
     for b in range(dx.shape[0] // rows):
@@ -353,19 +365,26 @@
         part = jnp.sum(dn * nh, axis=0, keepdims=True)
         tot = part if tot is None else tot + part
     dg[...] = tot
-
-
-def _dx(x, ps, dres, g):
+    _fill(z, de, sems, AT_D, 0, ZD, True)
+
+
+def _dx(x, ps, dres, g, de):
     m, d = x.shape
     return pl.pallas_call(
         _dx_kernel,
-        out_shape=(jax.ShapeDtypeStruct((m, d), BF16), jax.ShapeDtypeStruct((1, d), F32)),
-        in_specs=[_vm()] * 7,
-        out_specs=(_vm(), _vm()),
+        out_shape=(
+            jax.ShapeDtypeStruct((m, d), BF16),
+            jax.ShapeDtypeStruct((1, d), F32),
+            jax.ShapeDtypeStruct(de.shape, F32),
+        ),
+        in_specs=[_vm()] * 7 + [_any()],
+        out_specs=(_vm(), _vm(), _any()),
+        scratch_shapes=_zscratch(d, ZD),
+        input_output_aliases={7: 2},
         compiler_params=_params(12),
         cost_estimate=_cost(2),
         name="dx_form",
-    )(x, *ps, dres, g)
+    )(x, *ps, dres, g, de)
 
 
 def _sums_kernel(slot_ref, dx0, dx1, dg0, dg1, out):
@@ -394,7 +413,7 @@
 
 def _u_kernel(x_ref, g_ref, w_ref, de_in, u_ref, n_ref, de, z, sems):
     z[...] = jnp.zeros_like(z)
-    _fill(z, de, sems, ZP, 0, ZU, False)
+    _fill(z, de, sems, AT_U, 0, ZU, False)
     rows = 64
     for b in range(n_ref.shape[0] // rows):
         s = slice(b * rows, (b + 1) * rows)
@@ -407,7 +426,7 @@
         out = jnp.dot(n_ref[...], w_ref[:, s], preferred_element_type=F32).astype(BF16)
         for k in range(nk):
             u_ref[k, :, s] = out[k * t:(k + 1) * t]
-    _fill(z, de, sems, ZP, 0, ZU, True)
+    _fill(z, de, sems, AT_U, 0, ZU, True)
 
 
 def _u(x, g, W, nk, de):
@@ -608,13 +627,9 @@
         t1 = swap(t, 1)
         return t, t1, t2, swap(t2, 1)
 
-    def p_terms(du, W, ts, vs):
-        q, de = _p_terms(du, W, ts, vs)
+    def p_terms(du, W, ts, de):
+        q, de = _p_terms(du, W, ts, de)
         return de, (q[0], swap(q[1], 1), swap(q[2], 2), swap(q[3], 3))
-
-    def fill_rest(de):
-        n = ZP + ZU + ZW
-        return _zeros(de, n, de.shape[0] // ZR - n)
 
     def body(ids, E, g, W, du, dres):
         vs, d = E.shape
@@ -623,18 +638,18 @@
         m = nk * ts
         g2 = g.reshape(1, d)
 
-        tab, pos, _, rows, cnts, slots, where = _index_call(None, ids, E, ntp)
+        tab, pos, _, rows, cnts, slots, where, de = _index_call(None, ids, E, ntp)
         tabs = share(tab)
-        de, ps = p_terms(du, W, ts, vs)
+        de, ps = p_terms(du, W, ts, de)
         x, xl = _expand(pos, tabs, ts)
         u, n, de = _u(x, g2, W, nk, de)
-        dW, de = _dw(n, du, de, ZP + ZU, ZW)
-        dx, dg = _dx(xl.reshape(m, d), ps, dres.reshape(m, d), g2)
+        dW, de = _dw(n, du, de, AT_W, ZW)
+        dx, dg, de = _dx(xl.reshape(m, d), ps, dres.reshape(m, d), g2, de)
         dx1, dg1 = swap(dx, 1), swap(dg, 1)
         mine = _sums(slots, dx, dx1, dg, dg1)
         got = swap(mine, 2)
         other = lax.ppermute(cnts, "dp", [(i, (i + 1) % ndp) for i in range(ndp)])
-        de, acc, flags = _acc(cnts, other, slots, dx, dx1, de, ZP + ZU + ZW)
+        de, acc, flags = _acc(cnts, other, slots, dx, dx1, de, AT_R)
         dE, dg = _write(cnts, rows, where, acc, mine, got, de)
         outs = u, xl, dE, dW, dg
 
@@ -653,16 +668,16 @@
             zeros = jnp.zeros((nk * t, d), BF16), jnp.zeros((nk, ts, d), BF16)
             _, x, xl = lax.while_loop(lambda q: q[0] < rounds, more, (i0, *zeros))
             _, _, srow, rows, cs, _, _ = _index_call(i0, ids, E, ntp)
-            de, ps = p_terms(du, W, ts, vs)
+            de, ps = p_terms(du, W, ts, _zeros(c[1][2], 0, ZI))
             u, n, de = _u(x, g2, W, nk, de)
-            dW, de = _dw(n, du, de, ZP + ZU, ZW)
-            dx, dg = _dx(xl.reshape(m, d), ps, dres.reshape(m, d), g2)
+            dW, de = _dw(n, du, de, AT_W, ZW)
+            dx, dg, de = _dx(xl.reshape(m, d), ps, dres.reshape(m, d), g2, de)
             dg2 = dg + swap(dg, 1)
             dg = (dg2 + swap(dg2, 2)).reshape(d)
-            dE = _scatter(cs, rows, srow, share(dx), fill_rest(de), ts, nk)
+            dE = _scatter(cs, rows, srow, share(dx), _zeros(de, AT_R, vs // ZR - AT_R), ts, nk)
             return i0, (u, xl, dE, dW, dg)
 
-        _, outs = lax.while_loop(lambda c: c[0] > 0, again, (flags[0, 2], outs))
+        _, outs = lax.while_loop(lambda c: c[0] > 0, again, (jnp.minimum(flags[0, 2], 1), outs))
         return outs
 
     return jax.shard_map(

time: 84.4 us -> 66.6 us (0.79)
  waiting for transfers between devices: 30 us -> 13 us
  Pallas kernels: 42.5 us -> 41.3 us
    ppermute x9, waiting for transfers between devices: 30 us -> 13 us  [swap(): return lax.ppermute(a, 'tp', [(i, i ^ bit) for i in range(ntp)])]
    pallas_call x1, Pallas kernels: 9.28 us -> 6.73 us  [_acc(): pl.pallas_call(functools.partial(_acc_kernel, lo, n), out_shape=(jax.Shap...]
    pallas_call x1, Pallas kernels: 3.94 us -> 5.5 us  [_p_terms(): pl.pallas_call(functools.partial(_p_kernel, ts), out_shape=(jax.ShapeDtyp...]
    pallas_call x1, Pallas kernels: 12.5 us -> 11.1 us  [_dw(): pl.pallas_call(functools.partial(_dw_kernel, lo, nz, -(-nz // steps)), ou...]
  transfers between devices with their start and end apart: 10 -> 10, of which waited for: 3 -> 2; matrix products, arithmetic and copies ran while one was open for 1% -> 1% of each run, Pallas kernels for 42% -> 48%
where the time goes in v5:
time: 66.6 us; the launch traced here: 66.4 us
  Pallas kernels  41.3 us (62%)
  waiting for transfers between devices  13 us (20%)
  starting transfers between devices  9.57 us (14%)
  between operations  1.66 us (2%)
    ppermute x9, waiting for transfers between devices, swap(): return lax.ppermute(a, 'tp', [(i, i ^ bit) for i in range(ntp)])  13 us
    pallas_call x1, Pallas kernels, _dw(): pl.pallas_call(functools.partial(_dw_kernel, lo, nz, -(-nz // steps)), ou...  11.1 us
    ppermute x9, starting transfers between devices, swap(): return lax.ppermute(a, 'tp', [(i, i ^ bit) for i in range(ntp)])  7.69 us
    pallas_call x1, Pallas kernels, _u(): pl.pallas_call(_u_kernel, out_shape=(jax.ShapeDtypeStruct((nk, ntok // nk...  7.3 us
    pallas_call x1, Pallas kernels, _acc(): pl.pallas_call(functools.partial(_acc_kernel, lo, n), out_shape=(jax.Shap...  6.73 us
    pallas_call x1, Pallas kernels, _p_terms(): pl.pallas_call(functools.partial(_p_kernel, ts), out_shape=(jax.ShapeDtyp...  5.5 us
    pallas_call x1, Pallas kernels, _index_call(): pl.pallas_call(functools.partial(_index_kernel, vs, ntp, first), out_shap...  5.34 us
    pallas_call x1, Pallas kernels, _write(): pl.pallas_call(_write_kernel, out_shape=(jax.ShapeDtypeStruct((vs, d), F3...  2.27 us
  transfers between devices with their start and end apart: 10, of which 2 were waited for; matrix products, arithmetic and copies ran while one was open for 1% of the time, Pallas kernels for 48%

profile of v5, /device:TPU:0, one launch (start us, length us, event | category | flops | bytes accessed | tf_op | source)
XLA Modules:
  0.0 66.4 jit_solution(1997580203375963448)
XLA Ops:
  0.6 0.0 copy-start
  0.7 5.3 %index_gather.4 = (bf16[64,2304]{1,0:T(8,128)(2,1)S(1)}, f32[512,1]{1,0:T(8,128)S(1)}, f32[1,512]{1,0:T(1,128)}, s32[1,512]{1,0:T(1,128)S(1)}, s32[1,128]{1,0:T(...) custom-call(s32[2,256]{1,0:T(2,128)} %refs_0_.1, bf16[8192,2304]{1,0:T(8,128)(2,1)} %refs_1_.1), custom_call_target="tpu_custom_call" | custom-call | flops 20000000000 | bytes 1000000 | tf_op jit(solution)/shard_map/index_gather/pallas_call | solution.py:230
  6.0 3.3 %collective-permute-start.13 = (bf16[64,2304]{1,0:T(8,128)(2,1)S(1)}, bf16[64,2304]{1,0:T(8,128)(2,1)S(1)}, u32[]{:S(2)}, u32[]{:S(2)}) collective-permute-start(bf16[64,2304]{1,0:T(8,128)(2,1)S(1)} %get-tuple-element.161.refs_1_), channel_id=1, source_target_pairs={{0,2},{1,3},{2,0},{3,1},{4,6},{5,7},{6,4},{7,5}} | collective-permute-start | bytes 884744 | tf_op jit(solution)/shard_map/ppermute | solution.py:623
  9.3 0.0 collective-permute-start.12
  9.3 7.0 %collective-permute-done.13.refs_3_ = bf16[64,2304]{1,0:T(8,128)(2,1)S(1)} collective-permute-done((bf16[64,2304]{1,0:T(8,128)(2,1)S(1)}, bf16[64,2304]{1,0:T(8,128)(2,1)S(1)}, u32[]{:S(2)}, u32[]{:S(2)}) %collective-permute-start.13) | collective-permute-done | bytes 294944 | tf_op jit(solution)/shard_map/ppermute | solution.py:623
  16.3 0.0 collective-permute-start.14
  16.3 5.5 %p_terms.3 = (bf16[128,2304]{1,0:T(8,128)(2,1)S(1)}, bf16[128,2304]{1,0:T(8,128)(2,1)S(1)}, bf16[128,2304]{1,0:T(8,128)(2,1)S(1)}, bf16[128,2304]{1,0:T(8,128)(2,1)S(1)}, f32[8192,2304]{1,0:T(8,128)}) custom-call(bf16[2,256,1024]{2,1,0:T(8,128)(2,1)} %du_ref.3, bf16[2304,1024]{1,0:T(8,128)(2,1)S(1)} %copy-done, ...), custom_call_target="tpu_custom_call", output_to_operand_aliasing={{4}: (2, {})} | custom-call | flops 20000000000 | bytes 1000000 | tf_op jit(solution)/shard_map/p_terms/pallas_call | solution.py:315
  21.8 0.5 collective-permute-start.15
  22.3 1.7 %collective-permute-start.16 = (bf16[128,2304]{1,0:T(8,128)(2,1)S(1)}, bf16[128,2304]{1,0:T(8,128)(2,1)S(1)}, u32[]{:S(2)}, u32[]{:S(2)}) collective-permute-start(bf16[128,2304]{1,0:T(8,128)(2,1)S(1)} %get-tuple-element.166), channel_id=1, source_target_pairs={{0,2},{1,3},{2,0},{3,1},{4,6},{5,7},{6,4},{7,5}} | collective-permute-start | bytes 1769480 | tf_op jit(solution)/shard_map/ppermute | solution.py:623
  24.1 0.0 collective-permute-start.17
  24.1 0.0 collective-permute-done.12.refs_2_
  24.2 0.0 collective-permute-done.14.refs_4_
  24.2 0.9 %expand.2 = (bf16[512,2304]{1,0:T(8,128)(2,1)S(1)}, bf16[2,64,2304]{2,1,0:T(8,128)(2,1)S(1)}) custom-call(f32[512,1]{1,0:T(8,128)S(1)} %get-tuple-element.160.refs_0_, bf16[64,2304]{1,0:T(8,128)(2,1)S(1)} %get-tuple-element.161.refs_1_, bf16[64,2304]{1,0:T(8,128)(2,1)S(1)} %collective-permute-done.12.refs_2_, ...), custom_call_target="tpu_custom_call" | custom-call | flops 12000000000 | bytes 1000000 | tf_op jit(solution)/shard_map/expand/pallas_call | solution.py:278
  25.1 0.0 copy-start.7
  25.1 0.0 copy-start.2
  25.1 7.3 %u_terms.3 = (bf16[2,256,1024]{2,1,0:T(8,128)(2,1)}, bf16[512,2304]{1,0:T(8,128)(2,1)S(1)}, f32[8192,2304]{1,0:T(8,128)}) custom-call(bf16[512,2304]{1,0:T(8,128)(2,1)S(1)} %get-tuple-element.168.x_ref, bf16[1,2304]{1,0:T(2,128)(2,1)S(1)} %reshape.35.g_ref.g, bf16[2304,1024]{1,0:T(8,128)(2,1)S(1)} %copy-done, ...), custom_call_target="tpu_custom_call", output_to_operand_aliasing={{2}: (3, {})} | custom-call | flops 40000000000 | bytes 1000000 | tf_op jit(solution)/shard_map/u_terms/pallas_call | solution.py:435
  32.4 0.0 copy-start.5
  32.4 11.1 %dw_terms.3 = (f32[2304,1024]{1,0:T(8,128)}, f32[8192,2304]{1,0:T(8,128)}) custom-call(bf16[512,2304]{1,0:T(8,128)(2,1)S(1)} %get-tuple-element.170.n_ref, bf16[2,256,1024]{2,1,0:T(8,128)(2,1)S(1)} %copy-done.2, f32[8192,2304]{1,0:T(8,128)} %get-tuple-element.171.de_in), custom_call_target="tpu_custom_call", output_to_operand_aliasing={{1}: (2, {})} | custom-call | flops 40000000000 | bytes 1000000 | tf_op jit(solution)/shard_map/dw_terms/pallas_call | solution.py:475
  43.5 0.0 collective-permute-done.15.p1
  43.5 0.0 collective-permute-done.16.p2
  43.5 6.0 %collective-permute-done.17.p3 = bf16[128,2304]{1,0:T(8,128)(2,1)S(1)} collective-permute-done((bf16[128,2304]{1,0:T(8,128)(2,1)S(1)}, bf16[128,2304]{1,0:T(8,128)(2,1)S(1)}, u32[]{:S(2)}, u32[]{:S(2)}) %collective-permute-start.17) | collective-permute-done | bytes 589856 | tf_op jit(solution)/shard_map/ppermute | solution.py:623
  49.5 1.9 %dx_form.3 = (bf16[128,2304]{1,0:T(8,128)(2,1)S(1)}, f32[1,2304]{1,0:T(1,128)S(1)}, f32[8192,2304]{1,0:T(8,128)}) custom-call(bf16[128,2304]{1,0:T(8,128)(2,1)S(1)} %bitcast.12, bf16[128,2304]{1,0:T(8,128)(2,1)S(1)} %get-tuple-element.164.p0, bf16[128,2304]{1,0:T(8,128)(2,1)S(1)} %collective-permute-done.15.p1, ...), custom_call_target="tpu_custom_call", output_to_operand_aliasing={{2}: (7, {})} | custom-call | flops 8000000000 | bytes 1000000 | tf_op jit(solution)/shard_map/dx_form/pallas_call | solution.py:373
  51.4 0.6 collective-permute-start.18
  52.0 0.0 collective-permute-start.19
  52.1 1.9 %collective-permute-start.11 = (s32[1,128]{1,0:T(1,128)S(1)}, s32[1,128]{1,0:T(1,128)S(1)}, u32[]{:S(2)}, u32[]{:S(2)}) collective-permute-start(s32[1,128]{1,0:T(1,128)S(1)} %get-tuple-element.158.cnt_ref), channel_id=1, source_target_pairs={{0,4},{4,0},{1,5},{5,1},{2,6},{6,2},{3,7},{7,3}} | collective-permute-start | bytes 1544 | tf_op jit(solution)/shard_map/ppermute | solution.py:651
  53.9 0.0 collective-permute-done.19.dg1
  53.9 0.3 dx_sums.1.mine_ref
  54.2 1.5 %collective-permute-start.20 = (f32[32,2304]{1,0:T(8,128)S(1)}, f32[32,2304]{1,0:T(8,128)S(1)}, u32[]{:S(2)}, u32[]{:S(2)}) collective-permute-start(f32[32,2304]{1,0:T(8,128)S(1)} %dx_sums.1.mine_ref), channel_id=1, source_target_pairs={{0,2},{1,3},{2,0},{3,1},{4,6},{5,7},{6,4},{7,5}} | collective-permute-start | bytes 884744 | tf_op jit(solution)/shard_map/ppermute | solution.py:623
  55.7 6.7 %fill_acc.1 = (f32[8192,2304]{1,0:T(8,128)}, f32[64,2304]{1,0:T(8,128)S(1)}, s32[1,4]{1,0:T(1,128)S(1)}) custom-call(s32[1,128]{1,0:T(1,128)S(1)} %get-tuple-element.158.cnt_ref, s32[1,128]{1,0:T(1,128)S(1)} %collective-permute-done.11.oth_ref, f32[4,128]{1,0:T(4,128)S(1)} %get-tuple-element.159.slot_ref, ...), custom_call_target="tpu_custom_call", output_to_operand_aliasing={{0}: (5, {})} | custom-call | flops 19499999232 | bytes 1000000 | tf_op jit(solution)/shard_map/fill_acc/pallas_call | solution.py:561
  62.5 0.6 slice.6
  63.7 2.3 %write_rows.1 = (f32[8192,2304]{1,0:T(8,128)}, f32[2304]{0:T(1024)}) custom-call(s32[1,128]{1,0:T(1,128)S(1)} %get-tuple-element.158.cnt_ref, s32[1,512]{1,0:T(1,128)S(1)} %get-tuple-element.177.list_ref, s32[1,128]{1,0:T(1,128)S(1)} %get-tuple-element.178.map_ref, f32[64,2304]{1,0:T(8,128)S(1)} %get-tuple-element.179.acc_in, ...), custom_call_target="tpu_custom_call", output_to_operand_aliasing={{0}: (6, {})} | custom-call | flops 12000000000 | bytes 1000000 | tf_op jit(solution)/shard_map/write_rows/pallas_call | solution.py:605
  66.0 0.2 while.28
  (18 shorter events, 0.0 us)
Async XLA Ops:
  0.6 15.7 %copy-start = (bf16[2304,1024]{1,0:T(8,128)(2,1)S(1)}, bf16[2304,1024]{1,0:T(8,128)(2,1)}, u32[]{:S(2)}) copy-start(bf16[2304,1024]{1,0:T(8,128)(2,1)} %w_ref.3) | copy-start | bytes 14155780
  0.6 23.4 %copy-start.11 = (bf16[2304]{0:T(1024)(128)(2,1)S(1)}, bf16[2304]{0:T(1024)(128)(2,1)}, u32[]{:S(2)}) copy-start(bf16[2304]{0:T(1024)(128)(2,1)} %param.12) | copy-start | bytes 13828
  6.0 10.3 %collective-permute-start.13 = (bf16[64,2304]{1,0:T(8,128)(2,1)S(1)}, bf16[64,2304]{1,0:T(8,128)(2,1)S(1)}, u32[]{:S(2)}, u32[]{:S(2)}) collective-permute-start(bf16[64,2304]{1,0:T(8,128)(2,1)S(1)} %get-tuple-element.161.refs_1_), channel_id=1, source_target_pairs={{0,2},{1,3},{2,0},{3,1},{4,6},{5,7},{6,4},{7,5}} | collective-permute-start | bytes 884744 | tf_op jit(solution)/shard_map/ppermute | solution.py:623
  9.3 14.9 %collective-permute-start.12 = (bf16[64,2304]{1,0:T(8,128)(2,1)S(1)}, bf16[64,2304]{1,0:T(8,128)(2,1)S(1)}, u32[]{:S(2)}, u32[]{:S(2)}) collective-permute-start(bf16[64,2304]{1,0:T(8,128)(2,1)S(1)} %get-tuple-element.161.refs_1_), channel_id=1, source_target_pairs={{0,1},{1,0},{2,3},{3,2},{4,5},{5,4},{6,7},{7,6}} | collective-permute-start | bytes 884744 | tf_op jit(solution)/shard_map/ppermute | solution.py:623
  16.3 7.9 %collective-permute-start.14 = (bf16[64,2304]{1,0:T(8,128)(2,1)S(1)}, bf16[64,2304]{1,0:T(8,128)(2,1)S(1)}, u32[]{:S(2)}, u32[]{:S(2)}) collective-permute-start(bf16[64,2304]{1,0:T(8,128)(2,1)S(1)} %collective-permute-done.13.refs_3_), channel_id=1, source_target_pairs={{0,1},{1,0},{2,3},{3,2},{4,5},{5,4},{6,7},{7,6}} | collective-permute-start | bytes 884744 | tf_op jit(solution)/shard_map/ppermute | solution.py:623
  21.8 21.7 %collective-permute-start.15 = (bf16[128,2304]{1,0:T(8,128)(2,1)S(1)}, bf16[128,2304]{1,0:T(8,128)(2,1)S(1)}, u32[]{:S(2)}, u32[]{:S(2)}) collective-permute-start(bf16[128,2304]{1,0:T(8,128)(2,1)S(1)} %get-tuple-element.165), channel_id=1, source_target_pairs={{0,1},{1,0},{2,3},{3,2},{4,5},{5,4},{6,7},{7,6}} | collective-permute-start | bytes 1769480 | tf_op jit(solution)/shard_map/ppermute | solution.py:623
  22.3 21.2 %collective-permute-start.16 = (bf16[128,2304]{1,0:T(8,128)(2,1)S(1)}, bf16[128,2304]{1,0:T(8,128)(2,1)S(1)}, u32[]{:S(2)}, u32[]{:S(2)}) collective-permute-start(bf16[128,2304]{1,0:T(8,128)(2,1)S(1)} %get-tuple-element.166), channel_id=1, source_target_pairs={{0,2},{1,3},{2,0},{3,1},{4,6},{5,7},{6,4},{7,5}} | collective-permute-start | bytes 1769480 | tf_op jit(solution)/shard_map/ppermute | solution.py:623
  24.1 25.4 %copy-start.9 = (bf16[1,2304]{1,0:T(2,128)(2,1)}, bf16[1,2304]{1,0:T(2,128)(2,1)S(1)}, u32[]{:S(2)}) copy-start(bf16[1,2304]{1,0:T(2,128)(2,1)S(1)} %reshape.35.g_ref.g) | copy-start | bytes 13828
  24.1 25.4 %collective-permute-start.17 = (bf16[128,2304]{1,0:T(8,128)(2,1)S(1)}, bf16[128,2304]{1,0:T(8,128)(2,1)S(1)}, u32[]{:S(2)}, u32[]{:S(2)}) collective-permute-start(bf16[128,2304]{1,0:T(8,128)(2,1)S(1)} %get-tuple-element.167), channel_id=1, source_target_pairs={{0,3},{1,2},{2,1},{3,0},{4,7},{5,6},{6,5},{7,4}} | collective-permute-start | bytes 1769480 | tf_op jit(solution)/shard_map/ppermute | solution.py:623
  25.1 24.4 %copy-start.7 = (bf16[2,64,2304]{2,1,0:T(8,128)(2,1)}, bf16[2,64,2304]{2,1,0:T(8,128)(2,1)S(1)}, u32[]{:S(2)}) copy-start(bf16[2,64,2304]{2,1,0:T(8,128)(2,1)S(1)} %get-tuple-element.308) | copy-start | bytes 1769476
  25.1 7.3 %copy-start.2 = (bf16[2,256,1024]{2,1,0:T(8,128)(2,1)S(1)}, bf16[2,256,1024]{2,1,0:T(8,128)(2,1)}, u32[]{:S(2)}) copy-start(bf16[2,256,1024]{2,1,0:T(8,128)(2,1)} %du_ref.3) | copy-start | bytes 3145732
  32.4 17.1 %copy-start.5 = (bf16[2,64,2304]{2,1,0:T(8,128)(2,1)S(1)}, bf16[2,64,2304]{2,1,0:T(8,128)(2,1)}, u32[]{:S(2)}) copy-start(bf16[2,64,2304]{2,1,0:T(8,128)(2,1)} %param.15) | copy-start | bytes 1769476
  51.4 2.5 %collective-permute-start.18 = (bf16[128,2304]{1,0:T(8,128)(2,1)S(1)}, bf16[128,2304]{1,0:T(8,128)(2,1)S(1)}, u32[]{:S(2)}, u32[]{:S(2)}) collective-permute-start(bf16[128,2304]{1,0:T(8,128)(2,1)S(1)} %get-tuple-element.173.dx0), channel_id=1, source_target_pairs={{0,1},{1,0},{2,3},{3,2},{4,5},{5,4},{6,7},{7,6}} | collective-permute-start | bytes 1769480 | tf_op jit(solution)/shard_map/ppermute | solution.py:623
  52.0 1.9 %collective-permute-start.19 = (f32[1,2304]{1,0:T(1,128)S(1)}, f32[1,2304]{1,0:T(1,128)S(1)}, u32[]{:S(2)}, u32[]{:S(2)}) collective-permute-start(f32[1,2304]{1,0:T(1,128)S(1)} %get-tuple-element.180.dg0), channel_id=1, source_target_pairs={{0,1},{1,0},{2,3},{3,2},{4,5},{5,4},{6,7},{7,6}} | collective-permute-start | bytes 27656 | tf_op jit(solution)/shard_map/ppermute | solution.py:623
  52.1 3.6 %collective-permute-start.11 = (s32[1,128]{1,0:T(1,128)S(1)}, s32[1,128]{1,0:T(1,128)S(1)}, u32[]{:S(2)}, u32[]{:S(2)}) collective-permute-start(s32[1,128]{1,0:T(1,128)S(1)} %get-tuple-element.158.cnt_ref), channel_id=1, source_target_pairs={{0,4},{4,0},{1,5},{5,1},{2,6},{6,2},{3,7},{7,3}} | collective-permute-start | bytes 1544 | tf_op jit(solution)/shard_map/ppermute | solution.py:651
  54.2 9.5 %collective-permute-start.20 = (f32[32,2304]{1,0:T(8,128)S(1)}, f32[32,2304]{1,0:T(8,128)S(1)}, u32[]{:S(2)}, u32[]{:S(2)}) collective-permute-start(f32[32,2304]{1,0:T(8,128)S(1)} %dx_sums.1.mine_ref), channel_id=1, source_target_pairs={{0,2},{1,3},{2,0},{3,1},{4,6},{5,7},{6,4},{7,5}} | collective-permute-start | bytes 884744 | tf_op jit(solution)/shard_map/ppermute | solution.py:623
  55.7 10.3 %copy-start.3 = (bf16[2,256,1024]{2,1,0:T(8,128)(2,1)S(1)}, bf16[2,256,1024]{2,1,0:T(8,128)(2,1)}, u32[]{:S(2)}) copy-start(bf16[2,256,1024]{2,1,0:T(8,128)(2,1)} %du_ref.3) | copy-start | bytes 3145732
  55.7 10.3 %copy-start.12 = (s32[2,256]{1,0:T(2,128)S(1)}, s32[2,256]{1,0:T(2,128)}, u32[]{:S(2)}) copy-start(s32[2,256]{1,0:T(2,128)} %refs_0_.1) | copy-start | bytes 6148
  62.4 3.5 %copy-start.13 = (s32[1,4]{1,0:T(1,128)}, s32[1,4]{1,0:T(1,128)S(1)}, u32[]{:S(2)}) copy-start(s32[1,4]{1,0:T(1,128)S(1)} %get-tuple-element.318) | copy-start | bytes 52

commit v6 on v5

--- a/solution.py
+++ b/solution.py
@@ -15,8 +15,8 @@
 C2 = 32
 CB = 256
 ZR = 128
-ZI, ZP, ZU, ZW, ZD = 6, 9, 15, 18, 3
-AT_P, AT_U, AT_W, AT_D, AT_R = ZI, ZI + ZP, ZI + ZP + ZU, ZI + ZP + ZU + ZW, ZI + ZP + ZU + ZW + ZD
+ZP, ZU, ZW = 8, 15, 24
+AT_U, AT_W, AT_R = ZP, ZP + ZU, ZP + ZU + ZW
 TB = 64
 
 F32 = jnp.float32
@@ -68,11 +68,8 @@
 
 def _index_kernel(vs, ntp, first, *refs):
     if first:
-        refs, (de, z, zsems) = refs[:-2], (refs[9], *refs[-2:])
-        ids_ref, e_ref, tab_ref, pos_ref, srow_ref, list_ref, cnt_ref, slot_ref, map_ref, _, buf, glv, gls, gsem, sems = refs
+        ids_ref, e_ref, tab_ref, pos_ref, srow_ref, list_ref, cnt_ref, slot_ref, map_ref, buf, glv, gls, gsem, sems = refs
         base = 0.0
-        z[...] = jnp.zeros_like(z)
-        _fill(z, de, zsems, 0, 0, ZI, False)
     else:
         c_ref, ids_ref, e_ref, tab_ref, pos_ref, srow_ref, list_ref, cnt_ref, slot_ref, map_ref, buf, glv, gls, gsem, sems = refs
         base = (c_ref[0] * C).astype(F32)
@@ -206,10 +203,16 @@
     far = (part // 2).astype(F32) != jnp.floor(me * 0.5)
     got_r = jnp.where(far & (own_r == me), slot2_r, -1.0)
     acc2 = jnp.zeros((TB, 128), F32)
+    acc3 = jnp.zeros((TB, 128), F32)
     slot_j = _iota((TB, 128), 1)
     for b in range(nb):
-        acc2 = jnp.maximum(acc2, jnp.where(column(got_r, b) == slot_j, mys[b], 0.0))
-    map_ref[...] = jnp.minimum(jnp.max(acc2, axis=0, keepdims=True), C - 1.0).astype(jnp.int32)
+        hit = column(got_r, b) == slot_j
+        acc2 = jnp.maximum(acc2, jnp.where(hit, mys[b], 0.0))
+        acc3 = jnp.maximum(acc3, jnp.where(hit, idcs[b] - lo, 0.0))
+    slots = jnp.minimum(jnp.max(acc2, axis=0, keepdims=True), C - 1.0)
+    local = jnp.max(acc3, axis=0, keepdims=True)
+    many = jnp.where(lane1 == 127, cnt2, slots)
+    map_ref[...] = jnp.concatenate([many, local], axis=1).astype(jnp.int32)
     hit = jnp.where(my_r == _iota((C, ntok), 0) + base, idr - lo, 0.0)
     want = jnp.max(hit, axis=1, keepdims=True)
     want = want - jnp.floor(want * (1.0 / G)) * G
@@ -219,8 +222,6 @@
         sel = jnp.where(_iota((GS, GS * G), 1) == mine, 1.0, 0.0).astype(BF16)
         pltpu.make_async_copy(e_ref.at[pl.ds(0, GS * G)], buf.at[r], sems.at[q]).wait()
         tab_ref[q * GS:(q + 1) * GS, :] = jnp.dot(sel, buf[r, :], preferred_element_type=F32).astype(BF16)
-    if first:
-        _fill(z, de, zsems, 0, 0, ZI, True)
 
 
 def _index_call(chunk, ids, E, ntp):
@@ -236,19 +237,19 @@
             jax.ShapeDtypeStruct((1, ntok), jnp.int32),
             jax.ShapeDtypeStruct((1, 128), jnp.int32),
             jax.ShapeDtypeStruct((4, ntok // ntp), F32),
-            jax.ShapeDtypeStruct((1, 128), jnp.int32),
-        ) + ((jax.ShapeDtypeStruct((vs, d), F32),) if first else ()),
+            jax.ShapeDtypeStruct((1, 256), jnp.int32),
+        ),
         in_specs=([] if first else [_sm()]) + [_vm(), pl.BlockSpec(memory_space=pltpu.HBM)],
-        out_specs=(_vm(),) * 7 + ((_any(),) if first else ()),
+        out_specs=(_vm(),) * 7,
         scratch_shapes=[
             VMEM((C * G, d), BF16),
             VMEM((8, 128), jnp.int32),
             pltpu.SMEM((8, 128), jnp.int32),
             pltpu.SemaphoreType.DMA,
             pltpu.SemaphoreType.DMA((C // GS,)),
-        ] + (_zscratch(d, ZI) if first else []),
+        ],
         compiler_params=_params(8),
-        cost_estimate=_cost(5),
+        cost_estimate=_cost(12),
         name="index_gather",
     )(*([] if first else [chunk.reshape(1)]), ids, E)
 
@@ -286,7 +287,7 @@
     )(*ins)
 
 
-def _p_kernel(ts, du_ref, w_ref, de_in, *refs):
+def _p_kernel(ts, du_ref, w_ref, *refs):
     outs, (de, dur, z, sems) = refs[:-4], refs[-4:]
     nk = du_ref.shape[0]
 
@@ -297,7 +298,7 @@
             for r in range(4):
                 at = pl.multiple_of((_me() ^ r) * ts, ts)
                 dur[pl.ds((r * nk + k) * ts, ts), :] = du_ref[k, pl.ds(at, ts), :]
-        _fill(z, de, sems, AT_P, 0, ZP, False)
+        _fill(z, de, sems, 0, 0, ZP, False)
 
     out = lax.dot_general(dur[...], w_ref[...], (((1,), (1,)), ((), ())), preferred_element_type=F32)
     for i, o in enumerate(outs):
@@ -305,25 +306,24 @@
 
     @pl.when(pl.program_id(0) == pl.num_programs(0) - 1)
     def _():
-        _fill(z, de, sems, AT_P, 0, ZP, True)
-
-
-def _p_terms(du, W, ts, de):
+        _fill(z, de, sems, 0, 0, ZP, True)
+
+
+def _p_terms(du, W, ts, vs):
     nk, t, f = du.shape
     d = W.shape[0]
     cb = 3 * CB
     out = pl.pallas_call(
         functools.partial(_p_kernel, ts),
-        out_shape=(jax.ShapeDtypeStruct((nk * ts, d), BF16),) * 4 + (jax.ShapeDtypeStruct(de.shape, F32),),
+        out_shape=(jax.ShapeDtypeStruct((nk * ts, d), BF16),) * 4 + (jax.ShapeDtypeStruct((vs, d), F32),),
         grid=(d // cb,),
-        in_specs=[pl.BlockSpec((nk, t, f), lambda i: (0, 0, 0)), pl.BlockSpec((cb, f), lambda i: (i, 0)), _any()],
+        in_specs=[pl.BlockSpec((nk, t, f), lambda i: (0, 0, 0)), pl.BlockSpec((cb, f), lambda i: (i, 0))],
         out_specs=(pl.BlockSpec((nk * ts, cb), lambda i: (0, i)),) * 4 + (_any(),),
         scratch_shapes=[VMEM((nk * t, f), BF16)] + _zscratch(d, ZP),
-        input_output_aliases={2: 4},
         compiler_params=_params(20),
         cost_estimate=_cost(5),
         name="p_terms",
-    )(du, W, de)
+    )(du, W)
     return out[:4], out[4]
 
 
@@ -348,9 +348,7 @@
     )(de)
 
 
-def _dx_kernel(x, p0, p1, p2, p3, dres, g, de_in, dx, dg, de, z, sems):
-    z[...] = jnp.zeros_like(z)
-    _fill(z, de, sems, AT_D, 0, ZD, False)
+def _dx_kernel(x, p0, p1, p2, p3, dres, g, dx, dg):
     rows = 32
     tot = None
     for b in range(dx.shape[0] // rows):
@@ -365,26 +363,22 @@
         part = jnp.sum(dn * nh, axis=0, keepdims=True)
         tot = part if tot is None else tot + part
     dg[...] = tot
-    _fill(z, de, sems, AT_D, 0, ZD, True)
-
-
-def _dx(x, ps, dres, g, de):
+
+
+def _dx(x, ps, dres, g):
     m, d = x.shape
     return pl.pallas_call(
         _dx_kernel,
         out_shape=(
             jax.ShapeDtypeStruct((m, d), BF16),
             jax.ShapeDtypeStruct((1, d), F32),
-            jax.ShapeDtypeStruct(de.shape, F32),
         ),
-        in_specs=[_vm()] * 7 + [_any()],
-        out_specs=(_vm(), _vm(), _any()),
-        scratch_shapes=_zscratch(d, ZD),
-        input_output_aliases={7: 2},
+        in_specs=[_vm()] * 7,
+        out_specs=(_vm(), _vm()),
         compiler_params=_params(12),
         cost_estimate=_cost(2),
         name="dx_form",
-    )(x, *ps, dres, g, de)
+    )(x, *ps, dres, g)
 
 
 def _sums_kernel(slot_ref, dx0, dx1, dg0, dg1, out):
@@ -540,7 +534,7 @@
     )(cnts, rows, srow, *pieces, de)
 
 
-def _acc_kernel(lo, n, cnt_ref, oth_ref, slot_ref, dx0, dx1, de_in, de, acc, flag, z, sems):
+def _acc_kernel(lo, n, cnt_ref, oth_ref, list_ref, slot_ref, dx0, dx1, de_in, de, acc, flag, z, sems, sem):
     z[...] = jnp.zeros_like(z)
     _fill(z, de, sems, lo, 0, n, False)
     for i in (0, 2):
@@ -553,9 +547,21 @@
         tot = jnp.dot(ohs[0], dx0[:, s], preferred_element_type=F32)
         acc[:, s] = tot + jnp.dot(ohs[1], dx1[:, s], preferred_element_type=F32)
     _fill(z, de, sems, lo, 0, n, True)
-
-
-def _acc(cnts, other, slots, dx0, dx1, de, lo):
+    here = jnp.minimum(cnt_ref[0, 1], C)
+
+    def put(j, carry):
+        pltpu.make_async_copy(acc.at[pl.ds(j, 1)], de.at[pl.ds(list_ref[0, j], 1)], sem).start()
+        return carry
+
+    def done(j, carry):
+        pltpu.make_async_copy(acc.at[pl.ds(j, 1)], de.at[pl.ds(0, 1)], sem).wait()
+        return carry
+
+    lax.fori_loop(0, here, put, 0)
+    lax.fori_loop(0, here, done, 0)
+
+
+def _acc(cnts, other, rows, slots, dx0, dx1, de, lo):
     vs, d = de.shape
     n = vs // ZR - lo
     return pl.pallas_call(
@@ -565,54 +571,47 @@
             jax.ShapeDtypeStruct((C, d), F32),
             jax.ShapeDtypeStruct((1, 4), jnp.int32),
         ),
-        in_specs=[_sm(), _sm()] + [_vm()] * 3 + [_any()],
+        in_specs=[_sm(), _sm(), _sm()] + [_vm()] * 3 + [_any()],
         out_specs=(_any(), _vm(), _sm()),
-        scratch_shapes=_zscratch(d, n),
-        input_output_aliases={5: 0},
+        scratch_shapes=_zscratch(d, n) + [pltpu.SemaphoreType.DMA],
+        input_output_aliases={6: 0},
         compiler_params=_params(8),
         cost_estimate=_cost(n * 0.375),
         name="fill_acc",
-    )(cnts, other, slots, dx0, dx1, de)
-
-
-def _write_kernel(cnt_ref, list_ref, map_ref, acc_in, mine_ref, got_ref, de_in, de, dg_out, acc, sem):
-    acc[...] = acc_in[...]
-
-    def add(j, carry):
-        at = pl.ds(map_ref[0, j], 1)
-        acc[at, :] = acc[at, :] + got_ref[pl.ds(j, 1), :]
+    )(cnts, other, rows, slots, dx0, dx1, de)
+
+
+def _write_kernel(map_ref, acc, mine_ref, got_ref, de_in, de, dg_out, out, sem):
+    n = jnp.minimum(map_ref[0, 127], C2 - 1)
+
+    def put(j, carry):
+        out[pl.ds(j, 1), :] = acc[pl.ds(map_ref[0, j], 1), :] + got_ref[pl.ds(j, 1), :]
+        pltpu.make_async_copy(out.at[pl.ds(j, 1)], de.at[pl.ds(map_ref[0, 128 + j], 1)], sem).start()
         return carry
 
-    lax.fori_loop(0, jnp.minimum(cnt_ref[0, 3], C2 - 1), add, 0)
-    here = jnp.minimum(cnt_ref[0, 1], C)
-
-    def put(j, carry):
-        pltpu.make_async_copy(acc.at[pl.ds(j, 1)], de.at[pl.ds(list_ref[0, j], 1)], sem).start()
+    def done(j, carry):
+        pltpu.make_async_copy(out.at[pl.ds(j, 1)], de.at[pl.ds(0, 1)], sem).wait()
         return carry
 
-    def done(j, carry):
-        pltpu.make_async_copy(acc.at[pl.ds(j, 1)], de.at[pl.ds(0, 1)], sem).wait()
-        return carry
-
-    lax.fori_loop(0, here, put, 0)
+    lax.fori_loop(0, n, put, 0)
     dg = mine_ref[C2 - 1:C2, :] + got_ref[C2 - 1:C2, :]
     dg_out[...] = dg.reshape(dg_out.shape)
-    lax.fori_loop(0, here, done, 0)
-
-
-def _write(cnts, rows, where, acc, mine, got, de):
+    lax.fori_loop(0, n, done, 0)
+
+
+def _write(where, acc, mine, got, de):
     vs, d = de.shape
     return pl.pallas_call(
         _write_kernel,
         out_shape=(jax.ShapeDtypeStruct((vs, d), F32), jax.ShapeDtypeStruct((d,), F32)),
-        in_specs=[_sm(), _sm(), _sm()] + [_vm()] * 3 + [_any()],
+        in_specs=[_sm()] + [_vm()] * 3 + [_any()],
         out_specs=(_any(), _vm()),
-        scratch_shapes=[VMEM((C, d), F32), pltpu.SemaphoreType.DMA],
-        input_output_aliases={6: 0},
+        scratch_shapes=[VMEM((C2, d), F32), pltpu.SemaphoreType.DMA],
+        input_output_aliases={4: 0},
         compiler_params=_params(6),
         cost_estimate=_cost(3),
         name="write_rows",
-    )(cnts, rows, where, acc, mine, got, de)
+    )(where, acc, mine, got, de)
 
 
 def solution(mesh):
@@ -627,8 +626,8 @@
         t1 = swap(t, 1)
         return t, t1, t2, swap(t2, 1)
 
-    def p_terms(du, W, ts, de):
-        q, de = _p_terms(du, W, ts, de)
+    def p_terms(du, W, ts, vs):
+        q, de = _p_terms(du, W, ts, vs)
         return de, (q[0], swap(q[1], 1), swap(q[2], 2), swap(q[3], 3))
 
     def body(ids, E, g, W, du, dres):
@@ -638,19 +637,19 @@
         m = nk * ts
         g2 = g.reshape(1, d)
 
-        tab, pos, _, rows, cnts, slots, where, de = _index_call(None, ids, E, ntp)
+        tab, pos, _, rows, cnts, slots, where = _index_call(None, ids, E, ntp)
         tabs = share(tab)
-        de, ps = p_terms(du, W, ts, de)
+        de, ps = p_terms(du, W, ts, vs)
         x, xl = _expand(pos, tabs, ts)
         u, n, de = _u(x, g2, W, nk, de)
         dW, de = _dw(n, du, de, AT_W, ZW)
-        dx, dg, de = _dx(xl.reshape(m, d), ps, dres.reshape(m, d), g2, de)
+        dx, dg = _dx(xl.reshape(m, d), ps, dres.reshape(m, d), g2)
         dx1, dg1 = swap(dx, 1), swap(dg, 1)
         mine = _sums(slots, dx, dx1, dg, dg1)
         got = swap(mine, 2)
         other = lax.ppermute(cnts, "dp", [(i, (i + 1) % ndp) for i in range(ndp)])
-        de, acc, flags = _acc(cnts, other, slots, dx, dx1, de, AT_R)
-        dE, dg = _write(cnts, rows, where, acc, mine, got, de)
+        de, acc, flags = _acc(cnts, other, rows, slots, dx, dx1, de, AT_R)
+        dE, dg = _write(where, acc, mine, got, de)
         outs = u, xl, dE, dW, dg
 
         inputs = ids, E, W, du, dres, g2, flags
@@ -668,10 +667,10 @@
             zeros = jnp.zeros((nk * t, d), BF16), jnp.zeros((nk, ts, d), BF16)
             _, x, xl = lax.while_loop(lambda q: q[0] < rounds, more, (i0, *zeros))
             _, _, srow, rows, cs, _, _ = _index_call(i0, ids, E, ntp)
-            de, ps = p_terms(du, W, ts, _zeros(c[1][2], 0, ZI))
+            de, ps = p_terms(du, W, ts, vs)
             u, n, de = _u(x, g2, W, nk, de)
             dW, de = _dw(n, du, de, AT_W, ZW)
-            dx, dg, de = _dx(xl.reshape(m, d), ps, dres.reshape(m, d), g2, de)
+            dx, dg = _dx(xl.reshape(m, d), ps, dres.reshape(m, d), g2)
             dg2 = dg + swap(dg, 1)
             dg = (dg2 + swap(dg2, 2)).reshape(d)
             dE = _scatter(cs, rows, srow, share(dx), _zeros(de, AT_R, vs // ZR - AT_R), ts, nk)

time: 66.6 us -> 84.8 us (1.27)
  waiting for transfers between devices: 13 us -> 30 us
  Pallas kernels: 41.3 us -> 42.7 us
    ppermute x9, waiting for transfers between devices: 13 us -> 30 us  [swap(): return lax.ppermute(a, 'tp', [(i, i ^ bit) for i in range(ntp)])]
    pallas_call x1, Pallas kernels: 6.73 us -> 8.96 us  [_acc(): pl.pallas_call(functools.partial(_acc_kernel, lo, n), out_shape=(jax.Shap...]
    pallas_call x1, Pallas kernels: 11.1 us -> 13.2 us  [_dw(): pl.pallas_call(functools.partial(_dw_kernel, lo, nz, -(-nz // steps)), ou...]
    pallas_call x1, Pallas kernels: 5.5 us -> 3.94 us  [_p_terms(): pl.pallas_call(functools.partial(_p_kernel, ts), out_shape=(jax.ShapeDtyp...]
  transfers between devices with their start and end apart: 10 -> 10, of which waited for: 2 -> 3; matrix products, arithmetic and copies ran while one was open for 1% -> 1% of each run, Pallas kernels for 48% -> 42%
where the time goes in v6:
time: 84.8 us; the launch traced here: 84.5 us
  Pallas kernels  42.7 us (50%)
  waiting for transfers between devices  30 us (35%)
  starting transfers between devices  9.37 us (11%)
  between operations  1.63 us (2%)
    ppermute x9, waiting for transfers between devices, swap(): return lax.ppermute(a, 'tp', [(i, i ^ bit) for i in range(ntp)])  30 us
    pallas_call x1, Pallas kernels, _dw(): pl.pallas_call(functools.partial(_dw_kernel, lo, nz, -(-nz // steps)), ou...  13.2 us
    pallas_call x1, Pallas kernels, _acc(): pl.pallas_call(functools.partial(_acc_kernel, lo, n), out_shape=(jax.Shap...  8.96 us
    ppermute x9, starting transfers between devices, swap(): return lax.ppermute(a, 'tp', [(i, i ^ bit) for i in range(ntp)])  7.8 us
    pallas_call x1, Pallas kernels, _u(): pl.pallas_call(_u_kernel, out_shape=(jax.ShapeDtypeStruct((nk, ntok // nk...  7.29 us
    pallas_call x1, Pallas kernels, _index_call(): pl.pallas_call(functools.partial(_index_kernel, vs, ntp, first), out_shap...  4.95 us
    pallas_call x1, Pallas kernels, _p_terms(): pl.pallas_call(functools.partial(_p_kernel, ts), out_shape=(jax.ShapeDtyp...  3.94 us
    pallas_call x1, Pallas kernels, _write(): pl.pallas_call(_write_kernel, out_shape=(jax.ShapeDtypeStruct((vs, d), F3...  1.99 us
  transfers between devices with their start and end apart: 10, of which 3 were waited for; matrix products, arithmetic and copies ran while one was open for 1% of the time, Pallas kernels for 42%

profile of v6, /device:TPU:0, one launch (start us, length us, event | category | flops | bytes accessed | tf_op | source)
XLA Modules:
  0.0 84.5 jit_solution(14982169891280938784)
XLA Ops:
  0.6 0.0 copy-start.4
  0.6 0.0 copy-start.3
  0.7 5.0 %index_gather.4 = (bf16[64,2304]{1,0:T(8,128)(2,1)S(1)}, f32[512,1]{1,0:T(8,128)S(1)}, f32[1,512]{1,0:T(1,128)}, s32[1,512]{1,0:T(1,128)S(1)}, s32[1,128]{1,0:T(...) custom-call(s32[2,256]{1,0:T(2,128)} %refs_0_.1, bf16[8192,2304]{1,0:T(8,128)(2,1)} %refs_1_.1), custom_call_target="tpu_custom_call" | custom-call | flops 48000000000 | bytes 1000000 | tf_op jit(solution)/shard_map/index_gather/pallas_call | solution.py:231
  5.6 3.2 %collective-permute-start.13 = (bf16[64,2304]{1,0:T(8,128)(2,1)S(1)}, bf16[64,2304]{1,0:T(8,128)(2,1)S(1)}, u32[]{:S(2)}, u32[]{:S(2)}) collective-permute-start(bf16[64,2304]{1,0:T(8,128)(2,1)S(1)} %get-tuple-element.158.refs_1_), channel_id=1, source_target_pairs={{0,2},{1,3},{2,0},{3,1},{4,6},{5,7},{6,4},{7,5}} | collective-permute-start | bytes 884744 | tf_op jit(solution)/shard_map/ppermute | solution.py:622
  8.8 0.0 collective-permute-start.12
  8.8 1.6 %collective-permute-start.11 = (s32[1,128]{1,0:T(1,128)S(1)}, s32[1,128]{1,0:T(1,128)S(1)}, u32[]{:S(2)}, u32[]{:S(2)}) collective-permute-start(s32[1,128]{1,0:T(1,128)S(1)} %get-tuple-element.154.cnt_ref), channel_id=1, source_target_pairs={{0,4},{4,0},{1,5},{5,1},{2,6},{6,2},{3,7},{7,3}} | collective-permute-start | bytes 1544 | tf_op jit(solution)/shard_map/ppermute | solution.py:650
  10.4 5.5 %collective-permute-done.13.refs_3_ = bf16[64,2304]{1,0:T(8,128)(2,1)S(1)} collective-permute-done((bf16[64,2304]{1,0:T(8,128)(2,1)S(1)}, bf16[64,2304]{1,0:T(8,128)(2,1)S(1)}, u32[]{:S(2)}, u32[]{:S(2)}) %collective-permute-start.13) | collective-permute-done | bytes 294944 | tf_op jit(solution)/shard_map/ppermute | solution.py:622
  15.9 0.0 collective-permute-start.14
  15.9 3.9 %p_terms.3 = (bf16[128,2304]{1,0:T(8,128)(2,1)S(1)}, bf16[128,2304]{1,0:T(8,128)(2,1)S(1)}, bf16[128,2304]{1,0:T(8,128)(2,1)S(1)}, bf16[128,2304]{1,0:T(8,128)(2,1)S(1)}, f32[8192,2304]{1,0:T(8,128)}) custom-call(bf16[2,256,1024]{2,1,0:T(8,128)(2,1)S(1)} %copy-done.4, bf16[2304,1024]{1,0:T(8,128)(2,1)S(1)} %copy-done.3), custom_call_target="tpu_custom_call" | custom-call | flops 20000000000 | bytes 1000000 | tf_op jit(solution)/shard_map/p_terms/pallas_call | solution.py:316
  19.8 0.5 collective-permute-start.15
  20.4 1.8 %collective-permute-start.16 = (bf16[128,2304]{1,0:T(8,128)(2,1)S(1)}, bf16[128,2304]{1,0:T(8,128)(2,1)S(1)}, u32[]{:S(2)}, u32[]{:S(2)}) collective-permute-start(bf16[128,2304]{1,0:T(8,128)(2,1)S(1)} %get-tuple-element.162), channel_id=1, source_target_pairs={{0,2},{1,3},{2,0},{3,1},{4,6},{5,7},{6,4},{7,5}} | collective-permute-start | bytes 1769480 | tf_op jit(solution)/shard_map/ppermute | solution.py:622
  22.1 0.0 collective-permute-done.12.refs_2_
  22.1 0.0 collective-permute-start.17
  22.1 0.0 collective-permute-done.14.refs_4_
  22.1 0.0 copy-start.6
  22.1 0.9 %expand.2 = (bf16[512,2304]{1,0:T(8,128)(2,1)S(1)}, bf16[2,64,2304]{2,1,0:T(8,128)(2,1)S(1)}) custom-call(f32[512,1]{1,0:T(8,128)S(1)} %get-tuple-element.157.refs_0_, bf16[64,2304]{1,0:T(8,128)(2,1)S(1)} %get-tuple-element.158.refs_1_, bf16[64,2304]{1,0:T(8,128)(2,1)S(1)} %collective-permute-done.12.refs_2_, ...), custom_call_target="tpu_custom_call" | custom-call | flops 12000000000 | bytes 1000000 | tf_op jit(solution)/shard_map/expand/pallas_call | solution.py:279
  23.1 0.0 copy-start.10
  23.1 13.5 %collective-permute-done.16.p2 = bf16[128,2304]{1,0:T(8,128)(2,1)S(1)} collective-permute-done((bf16[128,2304]{1,0:T(8,128)(2,1)S(1)}, bf16[128,2304]{1,0:T(8,128)(2,1)S(1)}, u32[]{:S(2)}, u32[]{:S(2)}) %collective-permute-start.16) | collective-permute-done | bytes 589856 | tf_op jit(solution)/shard_map/ppermute | solution.py:622
  36.6 11.0 %collective-permute-done.17.p3 = bf16[128,2304]{1,0:T(8,128)(2,1)S(1)} collective-permute-done((bf16[128,2304]{1,0:T(8,128)(2,1)S(1)}, bf16[128,2304]{1,0:T(8,128)(2,1)S(1)}, u32[]{:S(2)}, u32[]{:S(2)}) %collective-permute-start.17) | collective-permute-done | bytes 589856 | tf_op jit(solution)/shard_map/ppermute | solution.py:622
  47.5 1.2 %dx_form.3 = (bf16[128,2304]{1,0:T(8,128)(2,1)S(1)}, f32[1,2304]{1,0:T(1,128)S(1)}) custom-call(bf16[128,2304]{1,0:T(8,128)(2,1)S(1)} %bitcast.12, bf16[128,2304]{1,0:T(8,128)(2,1)S(1)} %get-tuple-element.160.p0, bf16[128,2304]{1,0:T(8,128)(2,1)S(1)} %collective-permute-done.15.p1, bf16[128,2304]{1,0:T(8,128)(2,1)S(1)} %collective-permute-done.16.p2, ...), custom_call_target="tpu_custom_call" | custom-call | flops 8000000000 | bytes 1000000 | tf_op jit(solution)/shard_map/dx_form/pallas_call | solution.py:370
  48.7 0.6 collective-permute-start.19
  49.3 0.0 collective-permute-start.18
  49.4 7.3 %u_terms.3 = (bf16[2,256,1024]{2,1,0:T(8,128)(2,1)}, bf16[512,2304]{1,0:T(8,128)(2,1)S(1)}, f32[8192,2304]{1,0:T(8,128)}) custom-call(bf16[512,2304]{1,0:T(8,128)(2,1)S(1)} %get-tuple-element.165.x_ref, bf16[1,2304]{1,0:T(2,128)(2,1)S(1)} %reshape.35.g.g_ref, bf16[2304,1024]{1,0:T(8,128)(2,1)S(1)} %copy-done.3, ...), custom_call_target="tpu_custom_call", output_to_operand_aliasing={{2}: (3, {})} | custom-call | flops 40000000000 | bytes 1000000 | tf_op jit(solution)/shard_map/u_terms/pallas_call | solution.py:429
  56.7 13.2 %dw_terms.3 = (f32[2304,1024]{1,0:T(8,128)}, f32[8192,2304]{1,0:T(8,128)}) custom-call(bf16[512,2304]{1,0:T(8,128)(2,1)S(1)} %get-tuple-element.167.n_ref, bf16[2,256,1024]{2,1,0:T(8,128)(2,1)S(1)} %copy-done.4, f32[8192,2304]{1,0:T(8,128)} %get-tuple-element.168.de_in), custom_call_target="tpu_custom_call", output_to_operand_aliasing={{1}: (2, {})} | custom-call | flops 40000000000 | bytes 1000000 | tf_op jit(solution)/shard_map/dw_terms/pallas_call | solution.py:469
  69.9 0.0 collective-permute-done.19.dg1
  69.9 0.3 dx_sums.1.mine_ref
  70.2 1.7 %collective-permute-start.20 = (f32[32,2304]{1,0:T(8,128)S(1)}, f32[32,2304]{1,0:T(8,128)S(1)}, u32[]{:S(2)}, u32[]{:S(2)}) collective-permute-start(f32[32,2304]{1,0:T(8,128)S(1)} %dx_sums.1.mine_ref), channel_id=1, source_target_pairs={{0,2},{1,3},{2,0},{3,1},{4,6},{5,7},{6,4},{7,5}} | collective-permute-start | bytes 884744 | tf_op jit(solution)/shard_map/ppermute | solution.py:622
  71.9 9.0 %fill_acc.1 = (f32[8192,2304]{1,0:T(8,128)}, f32[64,2304]{1,0:T(8,128)S(1)}, s32[1,4]{1,0:T(1,128)S(1)}) custom-call(s32[1,128]{1,0:T(1,128)S(1)} %get-tuple-element.154.cnt_ref, s32[1,128]{1,0:T(1,128)S(1)} %collective-permute-done.11.oth_ref, s32[1,512]{1,0:T(1,128)S(1)} %get-tuple-element.155.list_ref, ...), custom_call_target="tpu_custom_call", output_to_operand_aliasing={{0}: (6, {})} | custom-call | flops 25500000256 | bytes 1000000 | tf_op jit(solution)/shard_map/fill_acc/pallas_call | solution.py:567
  80.9 0.6 slice.6
  82.2 0.0 copy-start.8
  82.2 2.0 %write_rows.1 = (f32[8192,2304]{1,0:T(8,128)}, f32[2304]{0:T(1024)}) custom-call(s32[1,256]{1,0:T(1,128)S(1)} %get-tuple-element.172.map_ref, f32[64,2304]{1,0:T(8,128)S(1)} %get-tuple-element.173.acc, f32[32,2304]{1,0:T(8,128)S(1)} %dx_sums.1.mine_ref, f32[32,2304]{1,0:T(8,128)S(1)} %collective-permute-done.20.got_ref, ...), custom_call_target="tpu_custom_call", output_to_operand_aliasing={{0}: (4, {})} | custom-call | flops 12000000000 | bytes 1000000 | tf_op jit(solution)/shard_map/write_rows/pallas_call | solution.py:604
  84.2 0.2 while.28
  (16 shorter events, 0.0 us)
Async XLA Ops:
  0.6 15.2 %copy-start.4 = (bf16[2,256,1024]{2,1,0:T(8,128)(2,1)S(1)}, bf16[2,256,1024]{2,1,0:T(8,128)(2,1)}, u32[]{:S(2)}) copy-start(bf16[2,256,1024]{2,1,0:T(8,128)(2,1)} %du_ref.3) | copy-start | bytes 3145732
  0.6 15.2 %copy-start.3 = (bf16[2304,1024]{1,0:T(8,128)(2,1)S(1)}, bf16[2304,1024]{1,0:T(8,128)(2,1)}, u32[]{:S(2)}) copy-start(bf16[2304,1024]{1,0:T(8,128)(2,1)} %w_ref.3) | copy-start | bytes 14155780
  5.6 10.3 %collective-permute-start.13 = (bf16[64,2304]{1,0:T(8,128)(2,1)S(1)}, bf16[64,2304]{1,0:T(8,128)(2,1)S(1)}, u32[]{:S(2)}, u32[]{:S(2)}) collective-permute-start(bf16[64,2304]{1,0:T(8,128)(2,1)S(1)} %get-tuple-element.158.refs_1_), channel_id=1, source_target_pairs={{0,2},{1,3},{2,0},{3,1},{4,6},{5,7},{6,4},{7,5}} | collective-permute-start | bytes 884744 | tf_op jit(solution)/shard_map/ppermute | solution.py:622
  8.8 13.3 %collective-permute-start.12 = (bf16[64,2304]{1,0:T(8,128)(2,1)S(1)}, bf16[64,2304]{1,0:T(8,128)(2,1)S(1)}, u32[]{:S(2)}, u32[]{:S(2)}) collective-permute-start(bf16[64,2304]{1,0:T(8,128)(2,1)S(1)} %get-tuple-element.158.refs_1_), channel_id=1, source_target_pairs={{0,1},{1,0},{2,3},{3,2},{4,5},{5,4},{6,7},{7,6}} | collective-permute-start | bytes 884744 | tf_op jit(solution)/shard_map/ppermute | solution.py:622
  8.8 11.5 %copy-start.2 = (bf16[2304]{0:T(1024)(128)(2,1)S(1)}, bf16[2304]{0:T(1024)(128)(2,1)}, u32[]{:S(2)}) copy-start(bf16[2304]{0:T(1024)(128)(2,1)} %param.12) | copy-start | bytes 13828
  8.8 63.2 %collective-permute-start.11 = (s32[1,128]{1,0:T(1,128)S(1)}, s32[1,128]{1,0:T(1,128)S(1)}, u32[]{:S(2)}, u32[]{:S(2)}) collective-permute-start(s32[1,128]{1,0:T(1,128)S(1)} %get-tuple-element.154.cnt_ref), channel_id=1, source_target_pairs={{0,4},{4,0},{1,5},{5,1},{2,6},{6,2},{3,7},{7,3}} | collective-permute-start | bytes 1544 | tf_op jit(solution)/shard_map/ppermute | solution.py:650
  15.9 6.3 %collective-permute-start.14 = (bf16[64,2304]{1,0:T(8,128)(2,1)S(1)}, bf16[64,2304]{1,0:T(8,128)(2,1)S(1)}, u32[]{:S(2)}, u32[]{:S(2)}) collective-permute-start(bf16[64,2304]{1,0:T(8,128)(2,1)S(1)} %collective-permute-done.13.refs_3_), channel_id=1, source_target_pairs={{0,1},{1,0},{2,3},{3,2},{4,5},{5,4},{6,7},{7,6}} | collective-permute-start | bytes 884744 | tf_op jit(solution)/shard_map/ppermute | solution.py:622
  19.8 3.2 %collective-permute-start.15 = (bf16[128,2304]{1,0:T(8,128)(2,1)S(1)}, bf16[128,2304]{1,0:T(8,128)(2,1)S(1)}, u32[]{:S(2)}, u32[]{:S(2)}) collective-permute-start(bf16[128,2304]{1,0:T(8,128)(2,1)S(1)} %get-tuple-element.161), channel_id=1, source_target_pairs={{0,1},{1,0},{2,3},{3,2},{4,5},{5,4},{6,7},{7,6}} | collective-permute-start | bytes 1769480 | tf_op jit(solution)/shard_map/ppermute | solution.py:622
  20.3 29.0 %copy-start = (bf16[1,2304]{1,0:T(2,128)(2,1)}, bf16[1,2304]{1,0:T(2,128)(2,1)S(1)}, u32[]{:S(2)}) copy-start(bf16[1,2304]{1,0:T(2,128)(2,1)S(1)} %reshape.35.g.g_ref) | copy-start | bytes 13828
  20.4 16.2 %collective-permute-start.16 = (bf16[128,2304]{1,0:T(8,128)(2,1)S(1)}, bf16[128,2304]{1,0:T(8,128)(2,1)S(1)}, u32[]{:S(2)}, u32[]{:S(2)}) collective-permute-start(bf16[128,2304]{1,0:T(8,128)(2,1)S(1)} %get-tuple-element.162), channel_id=1, source_target_pairs={{0,2},{1,3},{2,0},{3,1},{4,6},{5,7},{6,4},{7,5}} | collective-permute-start | bytes 1769480 | tf_op jit(solution)/shard_map/ppermute | solution.py:622
  22.1 25.4 %collective-permute-start.17 = (bf16[128,2304]{1,0:T(8,128)(2,1)S(1)}, bf16[128,2304]{1,0:T(8,128)(2,1)S(1)}, u32[]{:S(2)}, u32[]{:S(2)}) collective-permute-start(bf16[128,2304]{1,0:T(8,128)(2,1)S(1)} %get-tuple-element.163), channel_id=1, source_target_pairs={{0,3},{1,2},{2,1},{3,0},{4,7},{5,6},{6,5},{7,4}} | collective-permute-start | bytes 1769480 | tf_op jit(solution)/shard_map/ppermute | solution.py:622
  22.1 25.4 %copy-start.6 = (bf16[2,64,2304]{2,1,0:T(8,128)(2,1)S(1)}, bf16[2,64,2304]{2,1,0:T(8,128)(2,1)}, u32[]{:S(2)}) copy-start(bf16[2,64,2304]{2,1,0:T(8,128)(2,1)} %param.15) | copy-start | bytes 1769476
  23.1 25.7 %copy-start.10 = (bf16[2,64,2304]{2,1,0:T(8,128)(2,1)}, bf16[2,64,2304]{2,1,0:T(8,128)(2,1)S(1)}, u32[]{:S(2)}) copy-start(bf16[2,64,2304]{2,1,0:T(8,128)(2,1)S(1)} %get-tuple-element.302) | copy-start | bytes 1769476
  48.7 21.2 %collective-permute-start.19 = (f32[1,2304]{1,0:T(1,128)S(1)}, f32[1,2304]{1,0:T(1,128)S(1)}, u32[]{:S(2)}, u32[]{:S(2)}) collective-permute-start(f32[1,2304]{1,0:T(1,128)S(1)} %get-tuple-element.174.dg0), channel_id=1, source_target_pairs={{0,1},{1,0},{2,3},{3,2},{4,5},{5,4},{6,7},{7,6}} | collective-permute-start | bytes 27656 | tf_op jit(solution)/shard_map/ppermute | solution.py:622
  49.3 20.6 %collective-permute-start.18 = (bf16[128,2304]{1,0:T(8,128)(2,1)S(1)}, bf16[128,2304]{1,0:T(8,128)(2,1)S(1)}, u32[]{:S(2)}, u32[]{:S(2)}) collective-permute-start(bf16[128,2304]{1,0:T(8,128)(2,1)S(1)} %get-tuple-element.164.dx0), channel_id=1, source_target_pairs={{0,1},{1,0},{2,3},{3,2},{4,5},{5,4},{6,7},{7,6}} | collective-permute-start | bytes 1769480 | tf_op jit(solution)/shard_map/ppermute | solution.py:622
  70.2 12.0 %collective-permute-start.20 = (f32[32,2304]{1,0:T(8,128)S(1)}, f32[32,2304]{1,0:T(8,128)S(1)}, u32[]{:S(2)}, u32[]{:S(2)}) collective-permute-start(f32[32,2304]{1,0:T(8,128)S(1)} %dx_sums.1.mine_ref), channel_id=1, source_target_pairs={{0,2},{1,3},{2,0},{3,1},{4,6},{5,7},{6,4},{7,5}} | collective-permute-start | bytes 884744 | tf_op jit(solution)/shard_map/ppermute | solution.py:622
  80.9 3.3 %copy-start.12 = (s32[1,4]{1,0:T(1,128)}, s32[1,4]{1,0:T(1,128)S(1)}, u32[]{:S(2)}) copy-start(s32[1,4]{1,0:T(1,128)S(1)} %get-tuple-element.312) | copy-start | bytes 52
  82.2 2.0 %copy-start.8 = (s32[2,256]{1,0:T(2,128)S(1)}, s32[2,256]{1,0:T(2,128)}, u32[]{:S(2)}) copy-start(s32[2,256]{1,0:T(2,128)} %refs_0_.1) | copy-start | bytes 6148

commit v7 on v6

--- a/solution.py
+++ b/solution.py
@@ -15,8 +15,8 @@
 C2 = 32
 CB = 256
 ZR = 128
-ZP, ZU, ZW = 8, 15, 24
-AT_U, AT_W, AT_R = ZP, ZP + ZU, ZP + ZU + ZW
+ZP, ZA, ZU, ZW, ZB = 8, 4, 15, 21, 3
+AT_A, AT_U, AT_W, AT_B, AT_R = ZP, ZP + ZA, ZP + ZA + ZU, ZP + ZA + ZU + ZW, ZP + ZA + ZU + ZW + ZB
 TB = 64
 
 F32 = jnp.float32
@@ -203,16 +203,13 @@
     far = (part // 2).astype(F32) != jnp.floor(me * 0.5)
     got_r = jnp.where(far & (own_r == me), slot2_r, -1.0)
     acc2 = jnp.zeros((TB, 128), F32)
-    acc3 = jnp.zeros((TB, 128), F32)
     slot_j = _iota((TB, 128), 1)
     for b in range(nb):
-        hit = column(got_r, b) == slot_j
-        acc2 = jnp.maximum(acc2, jnp.where(hit, mys[b], 0.0))
-        acc3 = jnp.maximum(acc3, jnp.where(hit, idcs[b] - lo, 0.0))
+        acc2 = jnp.maximum(acc2, jnp.where(column(got_r, b) == slot_j, mys[b], 0.0))
     slots = jnp.minimum(jnp.max(acc2, axis=0, keepdims=True), C - 1.0)
-    local = jnp.max(acc3, axis=0, keepdims=True)
     many = jnp.where(lane1 == 127, cnt2, slots)
-    map_ref[...] = jnp.concatenate([many, local], axis=1).astype(jnp.int32)
+    mine = jnp.where(lane1 == 127, cnt, jnp.max(full, axis=0, keepdims=True)[:, :128])
+    map_ref[...] = jnp.concatenate([many, mine], axis=1).astype(jnp.int32)
     hit = jnp.where(my_r == _iota((C, ntok), 0) + base, idr - lo, 0.0)
     want = jnp.max(hit, axis=1, keepdims=True)
     want = want - jnp.floor(want * (1.0 / G)) * G
@@ -344,7 +341,6 @@
         input_output_aliases={0: 0},
         compiler_params=_params(4),
         cost_estimate=_cost(n * 0.375),
-        name="zero_fill",
     )(de)
 
 
@@ -534,7 +530,7 @@
     )(cnts, rows, srow, *pieces, de)
 
 
-def _acc_kernel(lo, n, cnt_ref, oth_ref, list_ref, slot_ref, dx0, dx1, de_in, de, acc, flag, z, sems, sem):
+def _acc_kernel(lo, n, cnt_ref, oth_ref, slot_ref, dx0, dx1, de_in, de, acc, flag, z, sems):
     z[...] = jnp.zeros_like(z)
     _fill(z, de, sems, lo, 0, n, False)
     for i in (0, 2):
@@ -547,21 +543,9 @@
         tot = jnp.dot(ohs[0], dx0[:, s], preferred_element_type=F32)
         acc[:, s] = tot + jnp.dot(ohs[1], dx1[:, s], preferred_element_type=F32)
     _fill(z, de, sems, lo, 0, n, True)
-    here = jnp.minimum(cnt_ref[0, 1], C)
-
-    def put(j, carry):
-        pltpu.make_async_copy(acc.at[pl.ds(j, 1)], de.at[pl.ds(list_ref[0, j], 1)], sem).start()
-        return carry
-
-    def done(j, carry):
-        pltpu.make_async_copy(acc.at[pl.ds(j, 1)], de.at[pl.ds(0, 1)], sem).wait()
-        return carry
-
-    lax.fori_loop(0, here, put, 0)
-    lax.fori_loop(0, here, done, 0)
-
-
-def _acc(cnts, other, rows, slots, dx0, dx1, de, lo):
+
+
+def _acc(cnts, other, slots, dx0, dx1, de, lo):
     vs, d = de.shape
     n = vs // ZR - lo
     return pl.pallas_call(
@@ -571,26 +555,33 @@
             jax.ShapeDtypeStruct((C, d), F32),
             jax.ShapeDtypeStruct((1, 4), jnp.int32),
         ),
-        in_specs=[_sm(), _sm(), _sm()] + [_vm()] * 3 + [_any()],
+        in_specs=[_sm(), _sm()] + [_vm()] * 3 + [_any()],
         out_specs=(_any(), _vm(), _sm()),
-        scratch_shapes=_zscratch(d, n) + [pltpu.SemaphoreType.DMA],
-        input_output_aliases={6: 0},
+        scratch_shapes=_zscratch(d, n),
+        input_output_aliases={5: 0},
         compiler_params=_params(8),
         cost_estimate=_cost(n * 0.375),
         name="fill_acc",
-    )(cnts, other, rows, slots, dx0, dx1, de)
-
-
-def _write_kernel(map_ref, acc, mine_ref, got_ref, de_in, de, dg_out, out, sem):
-    n = jnp.minimum(map_ref[0, 127], C2 - 1)
+    )(cnts, other, slots, dx0, dx1, de)
+
+
+def _write_kernel(map_ref, acc_in, mine_ref, got_ref, de_in, de, dg_out, acc, sem):
+    acc[...] = acc_in[...]
+
+    def add(j, carry):
+        at = pl.ds(map_ref[0, j], 1)
+        acc[at, :] = acc[at, :] + got_ref[pl.ds(j, 1), :]
+        return carry
+
+    lax.fori_loop(0, jnp.minimum(map_ref[0, 127], C2 - 1), add, 0)
+    n = jnp.minimum(map_ref[0, 255], C)
 
     def put(j, carry):
-        out[pl.ds(j, 1), :] = acc[pl.ds(map_ref[0, j], 1), :] + got_ref[pl.ds(j, 1), :]
-        pltpu.make_async_copy(out.at[pl.ds(j, 1)], de.at[pl.ds(map_ref[0, 128 + j], 1)], sem).start()
+        pltpu.make_async_copy(acc.at[pl.ds(j, 1)], de.at[pl.ds(map_ref[0, 128 + j], 1)], sem).start()
         return carry
 
     def done(j, carry):
-        pltpu.make_async_copy(out.at[pl.ds(j, 1)], de.at[pl.ds(0, 1)], sem).wait()
+        pltpu.make_async_copy(acc.at[pl.ds(j, 1)], de.at[pl.ds(0, 1)], sem).wait()
         return carry
 
     lax.fori_loop(0, n, put, 0)
@@ -606,7 +597,7 @@
         out_shape=(jax.ShapeDtypeStruct((vs, d), F32), jax.ShapeDtypeStruct((d,), F32)),
         in_specs=[_sm()] + [_vm()] * 3 + [_any()],
         out_specs=(_any(), _vm()),
-        scratch_shapes=[VMEM((C2, d), F32), pltpu.SemaphoreType.DMA],
+        scratch_shapes=[VMEM((C, d), F32), pltpu.SemaphoreType.DMA],
         input_output_aliases={4: 0},
         compiler_params=_params(6),
         cost_estimate=_cost(3),
@@ -637,18 +628,20 @@
         m = nk * ts
         g2 = g.reshape(1, d)
 
-        tab, pos, _, rows, cnts, slots, where = _index_call(None, ids, E, ntp)
+        tab, pos, _, _, cnts, slots, where = _index_call(None, ids, E, ntp)
         tabs = share(tab)
         de, ps = p_terms(du, W, ts, vs)
+        de = _zeros(de, AT_A, ZA)
         x, xl = _expand(pos, tabs, ts)
         u, n, de = _u(x, g2, W, nk, de)
         dW, de = _dw(n, du, de, AT_W, ZW)
         dx, dg = _dx(xl.reshape(m, d), ps, dres.reshape(m, d), g2)
         dx1, dg1 = swap(dx, 1), swap(dg, 1)
+        de = _zeros(de, AT_B, ZB)
         mine = _sums(slots, dx, dx1, dg, dg1)
         got = swap(mine, 2)
         other = lax.ppermute(cnts, "dp", [(i, (i + 1) % ndp) for i in range(ndp)])
-        de, acc, flags = _acc(cnts, other, rows, slots, dx, dx1, de, AT_R)
+        de, acc, flags = _acc(cnts, other, slots, dx, dx1, de, AT_R)
         dE, dg = _write(where, acc, mine, got, de)
         outs = u, xl, dE, dW, dg
 
@@ -668,12 +661,12 @@
             _, x, xl = lax.while_loop(lambda q: q[0] < rounds, more, (i0, *zeros))
             _, _, srow, rows, cs, _, _ = _index_call(i0, ids, E, ntp)
             de, ps = p_terms(du, W, ts, vs)
-            u, n, de = _u(x, g2, W, nk, de)
+            u, n, de = _u(x, g2, W, nk, _zeros(de, AT_A, ZA))
             dW, de = _dw(n, du, de, AT_W, ZW)
             dx, dg = _dx(xl.reshape(m, d), ps, dres.reshape(m, d), g2)
             dg2 = dg + swap(dg, 1)
             dg = (dg2 + swap(dg2, 2)).reshape(d)
-            dE = _scatter(cs, rows, srow, share(dx), _zeros(de, AT_R, vs // ZR - AT_R), ts, nk)
+            dE = _scatter(cs, rows, srow, share(dx), _zeros(de, AT_B, vs // ZR - AT_B), ts, nk)
             return i0, (u, xl, dE, dW, dg)
 
         _, outs = lax.while_loop(lambda c: c[0] > 0, again, (jnp.minimum(flags[0, 2], 1), outs))

time: 84.8 us -> 82.2 us (0.969)
  waiting for transfers between devices: 30 us -> 26.4 us
  Pallas kernels: 42.7 us -> 44 us
    pallas_call x0 -> x2, Pallas kernels: none -> 4.19 us  [_zeros(): pl.pallas_call(functools.partial(_zero_kernel, lo, n), out_shape=jax.Shap...]
    ppermute x9, waiting for transfers between devices: 30 us -> 26.4 us  [swap(): return lax.ppermute(a, 'tp', [(i, i ^ bit) for i in range(ntp)])]
    pallas_call x1, Pallas kernels: 8.96 us -> 6.86 us  [_acc(): pl.pallas_call(functools.partial(_acc_kernel, lo, n), out_shape=(jax.Shap...]
    pallas_call x1, Pallas kernels: 13.2 us -> 12.1 us  [_dw(): pl.pallas_call(functools.partial(_dw_kernel, lo, nz, -(-nz // steps)), ou...]
  transfers between devices with their start and end apart: 10 -> 10, of which waited for: 3 -> 3; matrix products, arithmetic and copies ran while one was open for 1% -> 1% of each run, Pallas kernels for 42% -> 45%
where the time goes in v7:
time: 82.2 us; the launch traced here: 82 us
  Pallas kernels  44 us (54%)
  waiting for transfers between devices  26.4 us (32%)
  starting transfers between devices  9.2 us (11%)
  between operations  1.61 us (2%)
    ppermute x9, waiting for transfers between devices, swap(): return lax.ppermute(a, 'tp', [(i, i ^ bit) for i in range(ntp)])  26.4 us
    pallas_call x1, Pallas kernels, _dw(): pl.pallas_call(functools.partial(_dw_kernel, lo, nz, -(-nz // steps)), ou...  12.1 us
    ppermute x9, starting transfers between devices, swap(): return lax.ppermute(a, 'tp', [(i, i ^ bit) for i in range(ntp)])  7.62 us
    pallas_call x1, Pallas kernels, _u(): pl.pallas_call(_u_kernel, out_shape=(jax.ShapeDtypeStruct((nk, ntok // nk...  7.29 us
    pallas_call x1, Pallas kernels, _acc(): pl.pallas_call(functools.partial(_acc_kernel, lo, n), out_shape=(jax.Shap...  6.86 us
    pallas_call x1, Pallas kernels, _index_call(): pl.pallas_call(functools.partial(_index_kernel, vs, ntp, first), out_shap...  4.96 us
    pallas_call x2, Pallas kernels, _zeros(): pl.pallas_call(functools.partial(_zero_kernel, lo, n), out_shape=jax.Shap...  4.19 us
    pallas_call x1, Pallas kernels, _p_terms(): pl.pallas_call(functools.partial(_p_kernel, ts), out_shape=(jax.ShapeDtyp...  3.91 us
  transfers between devices with their start and end apart: 10, of which 3 were waited for; matrix products, arithmetic and copies ran while one was open for 1% of the time, Pallas kernels for 45%

profile of v7, /device:TPU:0, one launch (start us, length us, event | category | flops | bytes accessed | tf_op | source)
XLA Modules:
  0.0 82.0 jit_solution(3946336596201783705)
XLA Ops:
  0.6 0.0 copy-start.5
  0.6 0.0 copy-start.4
  0.7 5.0 %index_gather.4 = (bf16[64,2304]{1,0:T(8,128)(2,1)S(1)}, f32[512,1]{1,0:T(8,128)S(1)}, f32[1,512]{1,0:T(1,128)}, s32[1,512]{1,0:T(1,128)}, s32[1,128]{1,0:T(1,12...) custom-call(s32[2,256]{1,0:T(2,128)} %refs_0_.1, bf16[8192,2304]{1,0:T(8,128)(2,1)} %refs_1_.1), custom_call_target="tpu_custom_call" | custom-call | flops 48000000000 | bytes 1000000 | tf_op jit(solution)/shard_map/index_gather/pallas_call | solution.py:228
  5.6 3.2 %collective-permute-start.13 = (bf16[64,2304]{1,0:T(8,128)(2,1)S(1)}, bf16[64,2304]{1,0:T(8,128)(2,1)S(1)}, u32[]{:S(2)}, u32[]{:S(2)}) collective-permute-start(bf16[64,2304]{1,0:T(8,128)(2,1)S(1)} %get-tuple-element.156.refs_1_), channel_id=1, source_target_pairs={{0,2},{1,3},{2,0},{3,1},{4,6},{5,7},{6,4},{7,5}} | collective-permute-start | bytes 884744 | tf_op jit(solution)/shard_map/ppermute | solution.py:613
  8.8 1.6 %collective-permute-start.11 = (s32[1,128]{1,0:T(1,128)}, s32[1,128]{1,0:T(1,128)}, u32[]{:S(2)}, u32[]{:S(2)}) collective-permute-start(s32[1,128]{1,0:T(1,128)} %get-tuple-element.153.cnt_ref), channel_id=1, source_target_pairs={{0,4},{4,0},{1,5},{5,1},{2,6},{6,2},{3,7},{7,3}} | collective-permute-start | bytes 1544 | tf_op jit(solution)/shard_map/ppermute | solution.py:643
  10.4 3.9 %p_terms.3 = (bf16[128,2304]{1,0:T(8,128)(2,1)S(1)}, bf16[128,2304]{1,0:T(8,128)(2,1)S(1)}, bf16[128,2304]{1,0:T(8,128)(2,1)S(1)}, bf16[128,2304]{1,0:T(8,128)(2,1)S(1)}, f32[8192,2304]{1,0:T(8,128)}) custom-call(bf16[2,256,1024]{2,1,0:T(8,128)(2,1)S(1)} %copy-done.5, bf16[2304,1024]{1,0:T(8,128)(2,1)S(1)} %copy-done.4), custom_call_target="tpu_custom_call" | custom-call | flops 20000000000 | bytes 1000000 | tf_op jit(solution)/shard_map/p_terms/pallas_call | solution.py:313
  14.3 0.2 collective-permute-start.15
  14.6 1.3 %collective-permute-done.13.refs_3_ = bf16[64,2304]{1,0:T(8,128)(2,1)S(1)} collective-permute-done((bf16[64,2304]{1,0:T(8,128)(2,1)S(1)}, bf16[64,2304]{1,0:T(8,128)(2,1)S(1)}, u32[]{:S(2)}, u32[]{:S(2)}) %collective-permute-start.13) | collective-permute-done | bytes 294944 | tf_op jit(solution)/shard_map/ppermute | solution.py:613
  15.9 0.0 collective-permute-start.14
  15.9 2.3 %shard_map.101.de_in = f32[8192,2304]{1,0:T(8,128)} custom-call(f32[8192,2304]{1,0:T(8,128)} %get-tuple-element.164.de_in), custom_call_target="tpu_custom_call", output_to_operand_aliasing={{}: (0, {})} | custom-call | flops 6000000000 | bytes 1000000 | tf_op jit(solution)/shard_map/pallas_call | solution.py:335
  18.2 1.8 %collective-permute-start.16 = (bf16[128,2304]{1,0:T(8,128)(2,1)S(1)}, bf16[128,2304]{1,0:T(8,128)(2,1)S(1)}, u32[]{:S(2)}, u32[]{:S(2)}) collective-permute-start(bf16[128,2304]{1,0:T(8,128)(2,1)S(1)} %get-tuple-element.160), channel_id=1, source_target_pairs={{0,2},{1,3},{2,0},{3,1},{4,6},{5,7},{6,4},{7,5}} | collective-permute-start | bytes 1769480 | tf_op jit(solution)/shard_map/ppermute | solution.py:613
  20.0 0.0 collective-permute-done.12.refs_2_
  20.0 0.2 collective-permute-start.17
  20.1 0.9 %expand.2 = (bf16[512,2304]{1,0:T(8,128)(2,1)S(1)}, bf16[2,64,2304]{2,1,0:T(8,128)(2,1)S(1)}) custom-call(f32[512,1]{1,0:T(8,128)S(1)} %get-tuple-element.155.refs_0_, bf16[64,2304]{1,0:T(8,128)(2,1)S(1)} %get-tuple-element.156.refs_1_, bf16[64,2304]{1,0:T(8,128)(2,1)S(1)} %collective-permute-done.12.refs_2_, ...), custom_call_target="tpu_custom_call" | custom-call | flops 12000000000 | bytes 1000000 | tf_op jit(solution)/shard_map/expand/pallas_call | solution.py:276
  21.0 0.0 copy-start.13
  21.0 0.0 collective-permute-done.15.p1
  21.1 13.4 %collective-permute-done.16.p2 = bf16[128,2304]{1,0:T(8,128)(2,1)S(1)} collective-permute-done((bf16[128,2304]{1,0:T(8,128)(2,1)S(1)}, bf16[128,2304]{1,0:T(8,128)(2,1)S(1)}, u32[]{:S(2)}, u32[]{:S(2)}) %collective-permute-start.16) | collective-permute-done | bytes 589856 | tf_op jit(solution)/shard_map/ppermute | solution.py:613
  34.4 11.7 %collective-permute-done.17.p3 = bf16[128,2304]{1,0:T(8,128)(2,1)S(1)} collective-permute-done((bf16[128,2304]{1,0:T(8,128)(2,1)S(1)}, bf16[128,2304]{1,0:T(8,128)(2,1)S(1)}, u32[]{:S(2)}, u32[]{:S(2)}) %collective-permute-start.17) | collective-permute-done | bytes 589856 | tf_op jit(solution)/shard_map/ppermute | solution.py:613
  46.1 1.2 %dx_form.3 = (bf16[128,2304]{1,0:T(8,128)(2,1)S(1)}, f32[1,2304]{1,0:T(1,128)S(1)}) custom-call(bf16[128,2304]{1,0:T(8,128)(2,1)S(1)} %bitcast.14, bf16[128,2304]{1,0:T(8,128)(2,1)S(1)} %get-tuple-element.158.p0, bf16[128,2304]{1,0:T(8,128)(2,1)S(1)} %collective-permute-done.15.p1, bf16[128,2304]{1,0:T(8,128)(2,1)S(1)} %collective-permute-done.16.p2, ...), custom_call_target="tpu_custom_call" | custom-call | flops 8000000000 | bytes 1000000 | tf_op jit(solution)/shard_map/dx_form/pallas_call | solution.py:366
  47.3 0.3 collective-permute-start.19
  47.6 0.2 collective-permute-start.18
  47.9 7.3 %u_terms.3 = (bf16[2,256,1024]{2,1,0:T(8,128)(2,1)}, bf16[512,2304]{1,0:T(8,128)(2,1)S(1)}, f32[8192,2304]{1,0:T(8,128)}) custom-call(bf16[512,2304]{1,0:T(8,128)(2,1)S(1)} %get-tuple-element.163.x_ref, bf16[1,2304]{1,0:T(2,128)(2,1)S(1)} %reshape.35.g.g_ref, bf16[2304,1024]{1,0:T(8,128)(2,1)S(1)} %copy-done.4, ...), custom_call_target="tpu_custom_call", output_to_operand_aliasing={{2}: (3, {})} | custom-call | flops 40000000000 | bytes 1000000 | tf_op jit(solution)/shard_map/u_terms/pallas_call | solution.py:425
  55.2 12.1 %dw_terms.3 = (f32[2304,1024]{1,0:T(8,128)}, f32[8192,2304]{1,0:T(8,128)}) custom-call(bf16[512,2304]{1,0:T(8,128)(2,1)S(1)} %get-tuple-element.165.n_ref, bf16[2,256,1024]{2,1,0:T(8,128)(2,1)S(1)} %copy-done.5, f32[8192,2304]{1,0:T(8,128)} %get-tuple-element.166.de_in), custom_call_target="tpu_custom_call", output_to_operand_aliasing={{1}: (2, {})} | custom-call | flops 40000000000 | bytes 1000000 | tf_op jit(solution)/shard_map/dw_terms/pallas_call | solution.py:465
  67.3 1.9 %shard_map.102.de_in = f32[8192,2304]{1,0:T(8,128)} custom-call(f32[8192,2304]{1,0:T(8,128)} %get-tuple-element.167.de_in), custom_call_target="tpu_custom_call", output_to_operand_aliasing={{}: (0, {})} | custom-call | flops 4499999744 | bytes 1000000 | tf_op jit(solution)/shard_map/pallas_call | solution.py:335
  69.2 0.0 collective-permute-done.19.dg1
  69.2 0.3 dx_sums.1.mine_ref
  69.5 1.8 %collective-permute-start.20 = (f32[32,2304]{1,0:T(8,128)S(1)}, f32[32,2304]{1,0:T(8,128)S(1)}, u32[]{:S(2)}, u32[]{:S(2)}) collective-permute-start(f32[32,2304]{1,0:T(8,128)S(1)} %dx_sums.1.mine_ref), channel_id=1, source_target_pairs={{0,2},{1,3},{2,0},{3,1},{4,6},{5,7},{6,4},{7,5}} | collective-permute-start | bytes 884744 | tf_op jit(solution)/shard_map/ppermute | solution.py:613
  71.3 6.9 %fill_acc.1 = (f32[8192,2304]{1,0:T(8,128)}, f32[64,2304]{1,0:T(8,128)S(1)}, s32[1,4]{1,0:T(1,128)S(1)}) custom-call(s32[1,128]{1,0:T(1,128)} %get-tuple-element.153.cnt_ref, s32[1,128]{1,0:T(1,128)} %collective-permute-done.11.oth_ref, f32[4,128]{1,0:T(4,128)S(1)} %get-tuple-element.154.slot_ref, ...), custom_call_target="tpu_custom_call", output_to_operand_aliasing={{0}: (5, {})} | custom-call | flops 19499999232 | bytes 1000000 | tf_op jit(solution)/shard_map/fill_acc/pallas_call | solution.py:551
  78.2 0.6 slice.6
  79.4 0.0 collective-permute-done.20.got_ref
  79.4 2.3 %write_rows.1 = (f32[8192,2304]{1,0:T(8,128)}, f32[2304]{0:T(1024)}) custom-call(s32[1,256]{1,0:T(1,128)S(1)} %get-tuple-element.170.map_ref, f32[64,2304]{1,0:T(8,128)S(1)} %get-tuple-element.171.acc_in, f32[32,2304]{1,0:T(8,128)S(1)} %dx_sums.1.mine_ref, f32[32,2304]{1,0:T(8,128)S(1)} %collective-permute-done.20.got_ref, ...), custom_call_target="tpu_custom_call", output_to_operand_aliasing={{0}: (4, {})} | custom-call | flops 12000000000 | bytes 1000000 | tf_op jit(solution)/shard_map/write_rows/pallas_call | solution.py:595
  81.7 0.2 while.28
  (16 shorter events, 0.0 us)
Async XLA Ops:
  0.6 9.8 %copy-start.5 = (bf16[2,256,1024]{2,1,0:T(8,128)(2,1)S(1)}, bf16[2,256,1024]{2,1,0:T(8,128)(2,1)}, u32[]{:S(2)}) copy-start(bf16[2,256,1024]{2,1,0:T(8,128)(2,1)} %du_ref.3) | copy-start | bytes 3145732
  0.6 9.7 %copy-start.4 = (bf16[2304,1024]{1,0:T(8,128)(2,1)S(1)}, bf16[2304,1024]{1,0:T(8,128)(2,1)}, u32[]{:S(2)}) copy-start(bf16[2304,1024]{1,0:T(8,128)(2,1)} %w_ref.3) | copy-start | bytes 14155780
  0.7 13.9 %copy-start.2 = (bf16[2304]{0:T(1024)(128)(2,1)S(1)}, bf16[2304]{0:T(1024)(128)(2,1)}, u32[]{:S(2)}) copy-start(bf16[2304]{0:T(1024)(128)(2,1)} %param.12) | copy-start | bytes 13828
  5.6 10.3 %collective-permute-start.13 = (bf16[64,2304]{1,0:T(8,128)(2,1)S(1)}, bf16[64,2304]{1,0:T(8,128)(2,1)S(1)}, u32[]{:S(2)}, u32[]{:S(2)}) collective-permute-start(bf16[64,2304]{1,0:T(8,128)(2,1)S(1)} %get-tuple-element.156.refs_1_), channel_id=1, source_target_pairs={{0,2},{1,3},{2,0},{3,1},{4,6},{5,7},{6,4},{7,5}} | collective-permute-start | bytes 884744 | tf_op jit(solution)/shard_map/ppermute | solution.py:613
  8.8 11.2 %collective-permute-start.12 = (bf16[64,2304]{1,0:T(8,128)(2,1)S(1)}, bf16[64,2304]{1,0:T(8,128)(2,1)S(1)}, u32[]{:S(2)}, u32[]{:S(2)}) collective-permute-start(bf16[64,2304]{1,0:T(8,128)(2,1)S(1)} %get-tuple-element.156.refs_1_), channel_id=1, source_target_pairs={{0,1},{1,0},{2,3},{3,2},{4,5},{5,4},{6,7},{7,6}} | collective-permute-start | bytes 884744 | tf_op jit(solution)/shard_map/ppermute | solution.py:613
  8.8 62.5 %collective-permute-start.11 = (s32[1,128]{1,0:T(1,128)}, s32[1,128]{1,0:T(1,128)}, u32[]{:S(2)}, u32[]{:S(2)}) collective-permute-start(s32[1,128]{1,0:T(1,128)} %get-tuple-element.153.cnt_ref), channel_id=1, source_target_pairs={{0,4},{4,0},{1,5},{5,1},{2,6},{6,2},{3,7},{7,3}} | collective-permute-start | bytes 1544 | tf_op jit(solution)/shard_map/ppermute | solution.py:643
  14.3 6.7 %collective-permute-start.15 = (bf16[128,2304]{1,0:T(8,128)(2,1)S(1)}, bf16[128,2304]{1,0:T(8,128)(2,1)S(1)}, u32[]{:S(2)}, u32[]{:S(2)}) collective-permute-start(bf16[128,2304]{1,0:T(8,128)(2,1)S(1)} %get-tuple-element.159), channel_id=1, source_target_pairs={{0,1},{1,0},{2,3},{3,2},{4,5},{5,4},{6,7},{7,6}} | collective-permute-start | bytes 1769480 | tf_op jit(solution)/shard_map/ppermute | solution.py:613
  14.6 33.3 %copy-start = (bf16[1,2304]{1,0:T(2,128)(2,1)}, bf16[1,2304]{1,0:T(2,128)(2,1)S(1)}, u32[]{:S(2)}) copy-start(bf16[1,2304]{1,0:T(2,128)(2,1)S(1)} %reshape.35.g.g_ref) | copy-start | bytes 13828
  15.9 4.2 %collective-permute-start.14 = (bf16[64,2304]{1,0:T(8,128)(2,1)S(1)}, bf16[64,2304]{1,0:T(8,128)(2,1)S(1)}, u32[]{:S(2)}, u32[]{:S(2)}) collective-permute-start(bf16[64,2304]{1,0:T(8,128)(2,1)S(1)} %collective-permute-done.13.refs_3_), channel_id=1, source_target_pairs={{0,1},{1,0},{2,3},{3,2},{4,5},{5,4},{6,7},{7,6}} | collective-permute-start | bytes 884744 | tf_op jit(solution)/shard_map/ppermute | solution.py:613
  15.9 30.2 %copy-start.7 = (bf16[2,64,2304]{2,1,0:T(8,128)(2,1)S(1)}, bf16[2,64,2304]{2,1,0:T(8,128)(2,1)}, u32[]{:S(2)}) copy-start(bf16[2,64,2304]{2,1,0:T(8,128)(2,1)} %param.15) | copy-start | bytes 1769476
  18.2 16.2 %collective-permute-start.16 = (bf16[128,2304]{1,0:T(8,128)(2,1)S(1)}, bf16[128,2304]{1,0:T(8,128)(2,1)S(1)}, u32[]{:S(2)}, u32[]{:S(2)}) collective-permute-start(bf16[128,2304]{1,0:T(8,128)(2,1)S(1)} %get-tuple-element.160), channel_id=1, source_target_pairs={{0,2},{1,3},{2,0},{3,1},{4,6},{5,7},{6,4},{7,5}} | collective-permute-start | bytes 1769480 | tf_op jit(solution)/shard_map/ppermute | solution.py:613
  20.0 26.2 %collective-permute-start.17 = (bf16[128,2304]{1,0:T(8,128)(2,1)S(1)}, bf16[128,2304]{1,0:T(8,128)(2,1)S(1)}, u32[]{:S(2)}, u32[]{:S(2)}) collective-permute-start(bf16[128,2304]{1,0:T(8,128)(2,1)S(1)} %get-tuple-element.161), channel_id=1, source_target_pairs={{0,3},{1,2},{2,1},{3,0},{4,7},{5,6},{6,5},{7,4}} | collective-permute-start | bytes 1769480 | tf_op jit(solution)/shard_map/ppermute | solution.py:613
  21.0 26.8 %copy-start.13 = (bf16[2,64,2304]{2,1,0:T(8,128)(2,1)}, bf16[2,64,2304]{2,1,0:T(8,128)(2,1)S(1)}, u32[]{:S(2)}) copy-start(bf16[2,64,2304]{2,1,0:T(8,128)(2,1)S(1)} %get-tuple-element.300) | copy-start | bytes 1769476
  47.3 21.9 %collective-permute-start.19 = (f32[1,2304]{1,0:T(1,128)S(1)}, f32[1,2304]{1,0:T(1,128)S(1)}, u32[]{:S(2)}, u32[]{:S(2)}) collective-permute-start(f32[1,2304]{1,0:T(1,128)S(1)} %get-tuple-element.172.dg0), channel_id=1, source_target_pairs={{0,1},{1,0},{2,3},{3,2},{4,5},{5,4},{6,7},{7,6}} | collective-permute-start | bytes 27656 | tf_op jit(solution)/shard_map/ppermute | solution.py:613
  47.6 21.6 %collective-permute-start.18 = (bf16[128,2304]{1,0:T(8,128)(2,1)S(1)}, bf16[128,2304]{1,0:T(8,128)(2,1)S(1)}, u32[]{:S(2)}, u32[]{:S(2)}) collective-permute-start(bf16[128,2304]{1,0:T(8,128)(2,1)S(1)} %get-tuple-element.162.dx0), channel_id=1, source_target_pairs={{0,1},{1,0},{2,3},{3,2},{4,5},{5,4},{6,7},{7,6}} | collective-permute-start | bytes 1769480 | tf_op jit(solution)/shard_map/ppermute | solution.py:613
  69.5 12.1 %copy-start.9 = (s32[2,256]{1,0:T(2,128)S(1)}, s32[2,256]{1,0:T(2,128)}, u32[]{:S(2)}) copy-start(s32[2,256]{1,0:T(2,128)} %refs_0_.1) | copy-start | bytes 6148
  69.5 9.9 %collective-permute-start.20 = (f32[32,2304]{1,0:T(8,128)S(1)}, f32[32,2304]{1,0:T(8,128)S(1)}, u32[]{:S(2)}, u32[]{:S(2)}) collective-permute-start(f32[32,2304]{1,0:T(8,128)S(1)} %dx_sums.1.mine_ref), channel_id=1, source_target_pairs={{0,2},{1,3},{2,0},{3,1},{4,6},{5,7},{6,4},{7,5}} | collective-permute-start | bytes 884744 | tf_op jit(solution)/shard_map/ppermute | solution.py:613

commit v8 on v7

--- a/solution.py
+++ b/solution.py
@@ -11,12 +11,11 @@
 EPS = 1e-6
 C = 64
 G = 2
-GS = 64
 C2 = 32
 CB = 256
 ZR = 128
-ZP, ZA, ZU, ZW, ZB = 8, 4, 15, 21, 3
-AT_A, AT_U, AT_W, AT_B, AT_R = ZP, ZP + ZA, ZP + ZA + ZU, ZP + ZA + ZU + ZW, ZP + ZA + ZU + ZW + ZB
+ZP, ZA, ZU, ZW, ZB = 8, 6, 14, 20, 3
+AT_A, AT_U, AT_B, AT_R = ZP, ZP + ZA, ZP + ZA + ZU + ZW, ZP + ZA + ZU + ZW + ZB
 TB = 64
 
 F32 = jnp.float32
@@ -66,101 +65,144 @@
     return [VMEM((ZR, d), F32), pltpu.SemaphoreType.DMA((n,))]
 
 
+def _column(row, b):
+    w = (b * TB) // 128 * 128
+    part = jnp.broadcast_to(row[:, w:w + 128], (TB, 128))
+    hit = _iota((TB, 128), 1) == _iota((TB, 128), 0) + float(b * TB - w)
+    return jnp.sum(jnp.where(hit, part, 0.0), axis=1, keepdims=True)
+
+
+def _fold(a):
+    return sum(a[8 * q:8 * q + 8] for q in range(1, TB // 8)) + a[:8]
+
+
+def _ids_row(ids_ref):
+    idsf = ids_ref[...].astype(F32)
+    return jnp.concatenate([idsf[k:k + 1] for k in range(ids_ref.shape[0])], axis=1)
+
+
+def _ranks(idr, idcs, vs, ntp, masks):
+    ntok = idr.shape[1]
+    lane = _iota((TB, ntok), 1)
+    thr = _iota((TB, 128), 1) * float(vs)
+    rank8 = jnp.zeros((8, ntok), F32)
+    below8 = [jnp.zeros((8, 128), F32) for _ in masks]
+    for b, idc in enumerate(idcs):
+        i = [i for i, (_, blocks) in enumerate(masks) if blocks[b]][0]
+        mask = masks[i][0]
+        dup = (jnp.broadcast_to(idc, (TB, ntok)) == idr) & (lane < _iota((TB, ntok), 0) + float(b * TB))
+        seen = jnp.max(jnp.where(dup, mask, 0.0), axis=1, keepdims=True)
+        key = jnp.where(seen > 0.5, float(vs * ntp), idc)
+        rank8 = rank8 + _fold(jnp.where(jnp.broadcast_to(key, (TB, ntok)) < idr, mask, 0.0))
+        below8[i] = below8[i] + _fold(jnp.where(jnp.broadcast_to(key, (TB, 128)) < thr, 1.0, 0.0))
+    return jnp.sum(rank8, axis=0, keepdims=True), [jnp.sum(b8, axis=0, keepdims=True) for b8 in below8]
+
+
+def _table_slots(idr, idcs, vs, ntp):
+    rank, (below,) = _ranks(idr, idcs, vs, ntp, [(jnp.ones_like(idr), [True] * len(idcs))])
+    own_r = jnp.floor(idr * (1.0 / vs))
+    start = jnp.zeros_like(rank)
+    for d in range(ntp):
+        start = jnp.where(own_r == float(d), below[:, d:d + 1], start)
+    return own_r, rank - start, below
+
+
 def _index_kernel(vs, ntp, first, *refs):
     if first:
-        ids_ref, e_ref, tab_ref, pos_ref, srow_ref, list_ref, cnt_ref, slot_ref, map_ref, buf, glv, gls, gsem, sems = refs
+        ids_ref, e_ref, tab_ref, buf, glv, gls, gsem, sem = refs
         base = 0.0
     else:
-        c_ref, ids_ref, e_ref, tab_ref, pos_ref, srow_ref, list_ref, cnt_ref, slot_ref, map_ref, buf, glv, gls, gsem, sems = refs
+        c_ref, ids_ref, e_ref, tab_ref, buf, glv, gls, gsem, sem = refs
         base = (c_ref[0] * C).astype(F32)
+    me = _me().astype(F32)
+    lo = me * vs
+    idr = _ids_row(ids_ref)
+    ntok = idr.shape[1]
+    idcs = [_column(idr, b) for b in range(ntok // TB)]
+    own_r, slot_r, _ = _table_slots(idr, idcs, vs, ntp)
+    my_r = jnp.where(own_r == me, slot_r, -1.0)
+    slot_l = _iota((TB, 128), 1) + base
+    acc = jnp.zeros((TB, 128), F32)
+    for b, idc in enumerate(idcs):
+        acc = jnp.maximum(acc, jnp.where(_column(my_r, b) == slot_l, idc - lo, 0.0))
+    glv[...] = jnp.broadcast_to(jnp.max(acc, axis=0, keepdims=True), (8, 128)).astype(jnp.int32)
+    cp = pltpu.make_async_copy(glv, gls, gsem)
+    cp.start()
+    cp.wait()
+
+    def fetch(j, carry):
+        g = pl.multiple_of((gls[0, j] >> 1) << 1, G)
+        at = pl.multiple_of(j * G, G)
+        pltpu.make_async_copy(e_ref.at[pl.ds(g, G)], buf.at[pl.ds(at, G)], sem).start()
+        return carry
+
+    lax.fori_loop(0, C, fetch, 0, unroll=8)
+    hit = jnp.where(my_r == _iota((C, ntok), 0) + base, idr - lo, 0.0)
+    want = jnp.max(hit, axis=1, keepdims=True)
+    want = want - jnp.floor(want * (1.0 / G)) * G + _iota((C, 1), 0) * G
+    sel = jnp.where(_iota((C, C * G), 1) == want, 1.0, 0.0).astype(BF16)
+    pltpu.make_async_copy(e_ref.at[pl.ds(0, C * G)], buf, sem).wait()
+    tab_ref[...] = jnp.dot(sel, buf[...], preferred_element_type=F32).astype(BF16)
+
+
+def _index_call(chunk, ids, E, ntp):
+    vs, d = E.shape
+    first = chunk is None
+    return pl.pallas_call(
+        functools.partial(_index_kernel, vs, ntp, first),
+        out_shape=jax.ShapeDtypeStruct((C, d), BF16),
+        in_specs=([] if first else [_sm()]) + [_vm(), pl.BlockSpec(memory_space=pltpu.HBM)],
+        out_specs=_vm(),
+        scratch_shapes=[
+            VMEM((C * G, d), BF16),
+            VMEM((8, 128), jnp.int32),
+            pltpu.SMEM((8, 128), jnp.int32),
+            pltpu.SemaphoreType.DMA,
+            pltpu.SemaphoreType.DMA,
+        ],
+        compiler_params=_params(8),
+        cost_estimate=_cost(12),
+        name="index_gather",
+    )(*([] if first else [chunk.reshape(1)]), ids, E)
+
+
+def _slots_kernel(vs, ntp, c_ref, ids_ref, de_in, pos_ref, srow_ref, list_ref, cnt_ref, slot_ref, map_ref, de, z, sems):
+    z[...] = jnp.zeros_like(z)
+    _fill(z, de, sems, AT_A, 0, ZA, False)
+    base = (c_ref[0] * C).astype(F32)
     mei = _me()
     me = mei.astype(F32)
     lo = me * vs
     nk, t = ids_ref.shape
     ntok = nk * t
     nb = ntok // TB
-    idsf = ids_ref[...].astype(F32)
-    idr = jnp.concatenate([idsf[k:k + 1] for k in range(nk)], axis=1)
-
-    def column(row, b):
-        w = (b * TB) // 128 * 128
-        part = jnp.broadcast_to(row[:, w:w + 128], (TB, 128))
-        hit = _iota((TB, 128), 1) == _iota((TB, 128), 0) + float(b * TB - w)
-        return jnp.sum(jnp.where(hit, part, 0.0), axis=1, keepdims=True)
-
-    def fold(a):
-        return sum(a[8 * q:8 * q + 8] for q in range(1, TB // 8)) + a[:8]
-
-    lane = _iota((TB, ntok), 1)
-    thr = _iota((TB, 128), 1) * float(vs)
-    rank8 = jnp.zeros((8, ntok), F32)
-    below8 = jnp.zeros((8, 128), F32)
-    idcs = []
-    for b in range(nb):
-        idc = column(idr, b)
-        idcs.append(idc)
-        idb = jnp.broadcast_to(idc, (TB, ntok))
-        dup = (idb == idr) & (lane < _iota((TB, ntok), 0) + float(b * TB))
-        seen = jnp.max(jnp.where(dup, 1.0, 0.0), axis=1, keepdims=True)
-        key = jnp.where(seen > 0.5, float(vs * ntp), idc)
-        rank8 = rank8 + fold(jnp.where(jnp.broadcast_to(key, (TB, ntok)) < idr, 1.0, 0.0))
-        below8 = below8 + fold(jnp.where(jnp.broadcast_to(key, (TB, 128)) < thr, 1.0, 0.0))
-    rank = jnp.sum(rank8, axis=0, keepdims=True)
-    below = jnp.sum(below8, axis=0, keepdims=True)
-    own_r = jnp.floor(idr * (1.0 / vs))
-    start = jnp.zeros_like(rank)
+    ts = t // ntp
+    idr = _ids_row(ids_ref)
+    idcs = [_column(idr, b) for b in range(nb)]
+    own_r, slot_r, below = _table_slots(idr, idcs, vs, ntp)
+    my_r = jnp.where(own_r == me, slot_r, -1.0)
     cnt = jnp.zeros((1, 1), F32)
     mx = jnp.zeros((1, 1), F32)
     for d in range(ntp):
-        ld = below[:, d:d + 1]
-        nd = below[:, d + 1:d + 2] - ld
-        start = jnp.where(own_r == float(d), ld, start)
+        nd = below[:, d + 1:d + 2] - below[:, d:d + 1]
         cnt = jnp.where(me == float(d), nd, cnt)
         mx = jnp.maximum(mx, nd)
-    slot_r = rank - start
-    my_r = jnp.where(own_r == me, slot_r, -1.0)
-
-    slot_l = _iota((TB, 128), 1) + base
-    acc = jnp.zeros((TB, 128), F32)
-    mys = []
+    srow_ref[...] = my_r
+    rel = (own_r.astype(jnp.int32) ^ mei).astype(F32)
+    pos = jnp.where((slot_r >= base) & (slot_r < base + C), rel * C + slot_r - base, -1.0)
     for b in range(nb):
-        my_c = column(my_r, b)
-        mys.append(my_c)
-        acc = jnp.maximum(acc, jnp.where(my_c == slot_l, idcs[b] - lo, 0.0))
-    glv[...] = jnp.broadcast_to(jnp.max(acc, axis=0, keepdims=True), (8, 128)).astype(jnp.int32)
-    cp = pltpu.make_async_copy(glv, gls, gsem)
-    cp.start()
-    cp.wait()
-
-    def fetch(q, j, carry):
-        j = q * GS + j
-        g = pl.multiple_of((gls[0, j] >> 1) << 1, G)
-        at = pl.multiple_of(j * G, G)
-        pltpu.make_async_copy(e_ref.at[pl.ds(g, G)], buf.at[pl.ds(at, G)], sems.at[q]).start()
-        return carry
-
-    for q in range(C // GS):
-        lax.fori_loop(0, GS, functools.partial(fetch, q), 0, unroll=8)
-
-    ts = t // ntp
+        pos_ref[b * TB:(b + 1) * TB, :] = _column(pos, b)
+
     part = lax.broadcasted_iota(jnp.int32, (1, ntok), 1) // ts % ntp
-    chips = [jnp.where(part // 2 == c, 1.0, 0.0) for c in range(ntp // 2)]
-    rank28 = jnp.zeros((8, ntok), F32)
-    below28 = [jnp.zeros((8, 128), F32) for _ in chips]
-    for b in range(nb):
-        idc = idcs[b]
-        dup = (jnp.broadcast_to(idc, (TB, ntok)) == idr) & (lane < _iota((TB, ntok), 0) + float(b * TB))
-        c = b * TB // ts % ntp // 2
-        seen = jnp.max(jnp.where(dup, chips[c], 0.0), axis=1, keepdims=True)
-        key = jnp.where(seen > 0.5, float(vs * ntp), idc)
-        rank28 = rank28 + fold(jnp.where(jnp.broadcast_to(key, (TB, ntok)) < idr, chips[c], 0.0))
-        below28[c] = below28[c] + fold(jnp.where(jnp.broadcast_to(key, (TB, 128)) < thr, 1.0, 0.0))
-    rank2 = jnp.sum(rank28, axis=0, keepdims=True)
-    below2 = [jnp.sum(b8, axis=0, keepdims=True) for b8 in below28]
-    start2 = jnp.zeros_like(rank)
+    chips = [
+        (jnp.where(part // 2 == c, 1.0, 0.0), [b * TB // ts % ntp // 2 == c for b in range(nb)])
+        for c in range(ntp // 2)
+    ]
+    rank2, below2 = _ranks(idr, idcs, vs, ntp, chips)
+    start2 = jnp.zeros_like(rank2)
     cnt2 = jnp.zeros((1, 1), F32)
     mx2 = jnp.zeros((1, 1), F32)
-    for c, chip in enumerate(chips):
+    for c, (chip, _) in enumerate(chips):
         for d in range(ntp):
             ld = below2[c][:, d:d + 1]
             nd = below2[c][:, d + 1:d + 2] - ld
@@ -169,18 +211,6 @@
                 cnt2 = jnp.where(me == float(d), nd, cnt2)
                 mx2 = jnp.maximum(mx2, nd)
     slot2_r = rank2 - start2
-    srow_ref[...] = my_r
-    full = jnp.zeros((8, ntok), F32)
-    lane8 = _iota((8, ntok), 1)
-    for b in range(nb):
-        for q in range(TB // 8):
-            s = slice(8 * q, 8 * q + 8)
-            full = jnp.maximum(full, jnp.where(mys[b][s] == lane8, idcs[b][s] - lo, 0.0))
-    list_ref[...] = jnp.max(full, axis=0, keepdims=True).astype(jnp.int32)
-    rel = (own_r.astype(jnp.int32) ^ mei).astype(F32)
-    pos = jnp.where((slot_r >= base) & (slot_r < base + C), rel * C + slot_r - base, -1.0)
-    for b in range(nb):
-        pos_ref[b * TB:(b + 1) * TB, :] = column(pos, b)
     lane1 = lax.broadcasted_iota(jnp.int32, (1, 128), 1)
     over = jnp.where((mx > C) | (mx2 > C2 - 1), 1.0, 0.0)
     rounds = jnp.floor((mx + C - 1.0) * (1.0 / C))
@@ -204,51 +234,45 @@
     got_r = jnp.where(far & (own_r == me), slot2_r, -1.0)
     acc2 = jnp.zeros((TB, 128), F32)
     slot_j = _iota((TB, 128), 1)
+    full = jnp.zeros((8, ntok), F32)
+    lane8 = _iota((8, ntok), 1)
     for b in range(nb):
-        acc2 = jnp.maximum(acc2, jnp.where(column(got_r, b) == slot_j, mys[b], 0.0))
+        my_c = _column(my_r, b)
+        acc2 = jnp.maximum(acc2, jnp.where(_column(got_r, b) == slot_j, my_c, 0.0))
+        for q in range(TB // 8):
+            s = slice(8 * q, 8 * q + 8)
+            full = jnp.maximum(full, jnp.where(my_c[s] == lane8, idcs[b][s] - lo, 0.0))
+    full = jnp.max(full, axis=0, keepdims=True)
+    list_ref[...] = full.astype(jnp.int32)
     slots = jnp.minimum(jnp.max(acc2, axis=0, keepdims=True), C - 1.0)
     many = jnp.where(lane1 == 127, cnt2, slots)
-    mine = jnp.where(lane1 == 127, cnt, jnp.max(full, axis=0, keepdims=True)[:, :128])
+    mine = jnp.where(lane1 == 127, cnt, full[:, :128])
     map_ref[...] = jnp.concatenate([many, mine], axis=1).astype(jnp.int32)
-    hit = jnp.where(my_r == _iota((C, ntok), 0) + base, idr - lo, 0.0)
-    want = jnp.max(hit, axis=1, keepdims=True)
-    want = want - jnp.floor(want * (1.0 / G)) * G
-    for q in range(C // GS):
-        r = slice(q * GS * G, (q + 1) * GS * G)
-        mine = want[q * GS:(q + 1) * GS] + _iota((GS, 1), 0) * G
-        sel = jnp.where(_iota((GS, GS * G), 1) == mine, 1.0, 0.0).astype(BF16)
-        pltpu.make_async_copy(e_ref.at[pl.ds(0, GS * G)], buf.at[r], sems.at[q]).wait()
-        tab_ref[q * GS:(q + 1) * GS, :] = jnp.dot(sel, buf[r, :], preferred_element_type=F32).astype(BF16)
-
-
-def _index_call(chunk, ids, E, ntp):
-    vs, d = E.shape
+    _fill(z, de, sems, AT_A, 0, ZA, True)
+
+
+def _slots(chunk, ids, ntp, de):
+    vs, d = de.shape
     ntok = ids.shape[0] * ids.shape[1]
-    first = chunk is None
-    return pl.pallas_call(
-        functools.partial(_index_kernel, vs, ntp, first),
+    return pl.pallas_call(
+        functools.partial(_slots_kernel, vs, ntp),
         out_shape=(
-            jax.ShapeDtypeStruct((C, d), BF16),
             jax.ShapeDtypeStruct((ntok, 1), F32),
             jax.ShapeDtypeStruct((1, ntok), F32),
             jax.ShapeDtypeStruct((1, ntok), jnp.int32),
             jax.ShapeDtypeStruct((1, 128), jnp.int32),
             jax.ShapeDtypeStruct((4, ntok // ntp), F32),
             jax.ShapeDtypeStruct((1, 256), jnp.int32),
+            jax.ShapeDtypeStruct(de.shape, F32),
         ),
-        in_specs=([] if first else [_sm()]) + [_vm(), pl.BlockSpec(memory_space=pltpu.HBM)],
-        out_specs=(_vm(),) * 7,
-        scratch_shapes=[
-            VMEM((C * G, d), BF16),
-            VMEM((8, 128), jnp.int32),
-            pltpu.SMEM((8, 128), jnp.int32),
-            pltpu.SemaphoreType.DMA,
-            pltpu.SemaphoreType.DMA((C // GS,)),
-        ],
-        compiler_params=_params(8),
-        cost_estimate=_cost(12),
-        name="index_gather",
-    )(*([] if first else [chunk.reshape(1)]), ids, E)
+        in_specs=[_sm(), _vm(), _any()],
+        out_specs=(_vm(),) * 6 + (_any(),),
+        scratch_shapes=_zscratch(d, ZA),
+        input_output_aliases={2: 6},
+        compiler_params=_params(6),
+        cost_estimate=_cost(3),
+        name="slots",
+    )(chunk.reshape(1), ids, de)
 
 
 def _expand_kernel(ts, acc, *refs):
@@ -401,83 +425,59 @@
     )(slots, dx0, dx1, dg0, dg1)
 
 
-def _u_kernel(x_ref, g_ref, w_ref, de_in, u_ref, n_ref, de, z, sems):
-    z[...] = jnp.zeros_like(z)
-    _fill(z, de, sems, AT_U, 0, ZU, False)
-    rows = 64
-    for b in range(n_ref.shape[0] // rows):
-        s = slice(b * rows, (b + 1) * rows)
-        xf = x_ref[s].astype(F32)
-        rs = lax.rsqrt(jnp.mean(xf * xf, axis=-1, keepdims=True) + EPS)
-        n_ref[s] = (xf * rs * g_ref[...].astype(F32)).astype(BF16)
-    nk, t, f = u_ref.shape
-    for c in range(f // CB):
-        s = slice(c * CB, (c + 1) * CB)
-        out = jnp.dot(n_ref[...], w_ref[:, s], preferred_element_type=F32).astype(BF16)
-        for k in range(nk):
-            u_ref[k, :, s] = out[k * t:(k + 1) * t]
-    _fill(z, de, sems, AT_U, 0, ZU, True)
-
-
-def _u(x, g, W, nk, de):
-    ntok, d = x.shape
-    f = W.shape[1]
-    return pl.pallas_call(
-        _u_kernel,
-        out_shape=(
-            jax.ShapeDtypeStruct((nk, ntok // nk, f), BF16),
-            jax.ShapeDtypeStruct((ntok, d), BF16),
-            jax.ShapeDtypeStruct(de.shape, F32),
-        ),
-        in_specs=[_vm(), _vm(), _vm(), _any()],
-        out_specs=(_vm(), _vm(), _any()),
-        scratch_shapes=_zscratch(d, ZU),
-        input_output_aliases={3: 2},
-        compiler_params=_params(20),
-        cost_estimate=_cost(10),
-        name="u_terms",
-    )(x, g, W, de)
-
-
-def _dw_kernel(lo, n, per, n_ref, du_ref, de_in, dw_ref, de, z, sems):
+def _udw_kernel(per, x_ref, g_ref, w_ref, du_ref, de_in, u_ref, dw_ref, de, n, z, sems):
     i = pl.program_id(0)
     nk, t, f = du_ref.shape
+    cb = dw_ref.shape[0]
 
     @pl.when(i == 0)
     def _():
         z[...] = jnp.zeros_like(z)
-
-    _fill(z, de, sems, lo, i * per, jnp.minimum(per, n - i * per), False)
+        _fill(z, de, sems, AT_U, 0, ZU, False)
+        rows = 64
+        for b in range(n.shape[0] // rows):
+            s = slice(b * rows, (b + 1) * rows)
+            xf = x_ref[s].astype(F32)
+            rs = lax.rsqrt(jnp.mean(xf * xf, axis=-1, keepdims=True) + EPS)
+            n[s] = (xf * rs * g_ref[...].astype(F32)).astype(BF16)
+        for c in range(f // CB):
+            s = slice(c * CB, (c + 1) * CB)
+            out = jnp.dot(n[...], w_ref[:, s], preferred_element_type=F32).astype(BF16)
+            for k in range(nk):
+                u_ref[k, :, s] = out[k * t:(k + 1) * t]
+
+    _fill(z, de, sems, AT_U, ZU + i * per, jnp.minimum(per, ZW - i * per), False)
+    blk = n[:, pl.ds(pl.multiple_of(i * cb, 128), cb)]
     dw_ref[...] = lax.dot_general(
-        n_ref[...], du_ref[...].reshape(nk * t, f), (((0,), (0,)), ((), ())), preferred_element_type=F32
+        blk, du_ref[...].reshape(nk * t, f), (((0,), (0,)), ((), ())), preferred_element_type=F32
     )
 
     @pl.when(i == pl.num_programs(0) - 1)
     def _():
-        _fill(z, de, sems, lo, 0, n, True)
-
-
-def _dw(n, du, de, lo, nz):
+        _fill(z, de, sems, AT_U, 0, ZU + ZW, True)
+
+
+def _udw(x, g, W, du, de):
     nk, t, f = du.shape
-    ntok, d = n.shape
+    ntok, d = x.shape
     cb = d // 6
     steps = d // cb
     return pl.pallas_call(
-        functools.partial(_dw_kernel, lo, nz, -(-nz // steps)),
-        out_shape=(jax.ShapeDtypeStruct((d, f), F32), jax.ShapeDtypeStruct(de.shape, F32)),
+        functools.partial(_udw_kernel, -(-ZW // steps)),
+        out_shape=(
+            jax.ShapeDtypeStruct((nk, t, f), BF16),
+            jax.ShapeDtypeStruct((d, f), F32),
+            jax.ShapeDtypeStruct(de.shape, F32),
+        ),
         grid=(steps,),
-        in_specs=[
-            pl.BlockSpec((ntok, cb), lambda i: (0, i)),
-            pl.BlockSpec((nk, t, f), lambda i: (0, 0, 0)),
-            _any(),
-        ],
-        out_specs=(pl.BlockSpec((cb, f), lambda i: (i, 0)), _any()),
-        scratch_shapes=_zscratch(d, nz),
-        input_output_aliases={2: 1},
+        in_specs=[_vm(), _vm(), _vm(), _vm(), _any()],
+        out_specs=(pl.BlockSpec((nk, t, f), lambda i: (0, 0, 0)), pl.BlockSpec((cb, f), lambda i: (i, 0)), _any()),
+        scratch_shapes=[VMEM((ntok, d), BF16)] + _zscratch(d, ZU + ZW),
+        input_output_aliases={4: 2},
         compiler_params=_params(20),
-        cost_estimate=_cost(10),
-        name="dw_terms",
-    )(n, du, de)
+        cost_estimate=_cost(20),
+        name="u_dw",
+    )(x, g, W, du, de)
 
 
 def _scatter_kernel(ts, nk, cnt_ref, list_ref, srow_ref, *refs):
@@ -628,13 +628,11 @@
         m = nk * ts
         g2 = g.reshape(1, d)
 
-        tab, pos, _, _, cnts, slots, where = _index_call(None, ids, E, ntp)
-        tabs = share(tab)
+        tabs = share(_index_call(None, ids, E, ntp))
         de, ps = p_terms(du, W, ts, vs)
-        de = _zeros(de, AT_A, ZA)
+        pos, _, _, cnts, slots, where, de = _slots(jnp.int32(0), ids, ntp, de)
         x, xl = _expand(pos, tabs, ts)
-        u, n, de = _u(x, g2, W, nk, de)
-        dW, de = _dw(n, du, de, AT_W, ZW)
+        u, dW, de = _udw(x, g2, W, du, de)
         dx, dg = _dx(xl.reshape(m, d), ps, dres.reshape(m, d), g2)
         dx1, dg1 = swap(dx, 1), swap(dg, 1)
         de = _zeros(de, AT_B, ZB)
@@ -653,16 +651,15 @@
             i0 = left - left
 
             def more(q):
-                i, x, _ = q
-                tab, pos, *_ = _index_call(i, ids, E, ntp)
-                return i + 1, *_expand(pos, share(tab), ts, x)
+                i, x, _, de = q
+                pos, *_, de = _slots(i, ids, ntp, de)
+                return i + 1, *_expand(pos, share(_index_call(i, ids, E, ntp)), ts, x), de
 
             zeros = jnp.zeros((nk * t, d), BF16), jnp.zeros((nk, ts, d), BF16)
-            _, x, xl = lax.while_loop(lambda q: q[0] < rounds, more, (i0, *zeros))
-            _, _, srow, rows, cs, _, _ = _index_call(i0, ids, E, ntp)
             de, ps = p_terms(du, W, ts, vs)
-            u, n, de = _u(x, g2, W, nk, _zeros(de, AT_A, ZA))
-            dW, de = _dw(n, du, de, AT_W, ZW)
+            _, x, xl, de = lax.while_loop(lambda q: q[0] < rounds, more, (i0, *zeros, de))
+            _, srow, rows, cs, _, _, de = _slots(i0, ids, ntp, de)
+            u, dW, de = _udw(x, g2, W, du, de)
             dx, dg = _dx(xl.reshape(m, d), ps, dres.reshape(m, d), g2)
             dg2 = dg + swap(dg, 1)
             dg = (dg2 + swap(dg2, 2)).reshape(d)

time: 82.2 us -> 81.5 us (level)
  Pallas kernels: 44 us -> 41.8 us
  waiting for transfers between devices: 26.4 us -> 28 us
    pallas_call x2 -> x1, Pallas kernels: 4.19 us -> 1.9 us  [_zeros(): pl.pallas_call(functools.partial(_zero_kernel, lo, n), out_shape=jax.Shap...]
    ppermute x9, waiting for transfers between devices: 26.4 us -> 28 us  [swap(): return lax.ppermute(a, 'tp', [(i, i ^ bit) for i in range(ntp)])]
  transfers between devices with their start and end apart: 10 -> 10, of which waited for: 3 -> 3; matrix products, arithmetic and copies ran while one was open for 1% -> 1% of each run, Pallas kernels for 45% -> 43%
where the time goes in v8:
time: 81.5 us; the launch traced here: 81.3 us
  Pallas kernels  41.8 us (51%)
  waiting for transfers between devices  28 us (34%)
  starting transfers between devices  9.03 us (11%)
  between operations  1.63 us (2%)
    ppermute x9, waiting for transfers between devices, swap(): return lax.ppermute(a, 'tp', [(i, i ^ bit) for i in range(ntp)])  28 us
    pallas_call x1, Pallas kernels, _udw(): pl.pallas_call(functools.partial(_udw_kernel, -(-ZW // steps)), out_shape...  16.6 us
    ppermute x9, starting transfers between devices, swap(): return lax.ppermute(a, 'tp', [(i, i ^ bit) for i in range(ntp)])  7.08 us
    pallas_call x1, Pallas kernels, _acc(): pl.pallas_call(functools.partial(_acc_kernel, lo, n), out_shape=(jax.Shap...  6.73 us
    pallas_call x1, Pallas kernels, _index_call(): pl.pallas_call(functools.partial(_index_kernel, vs, ntp, first), out_shap...  4.41 us
    pallas_call x1, Pallas kernels, _p_terms(): pl.pallas_call(functools.partial(_p_kernel, ts), out_shape=(jax.ShapeDtyp...  3.94 us
    pallas_call x1, Pallas kernels, _slots(): pl.pallas_call(functools.partial(_slots_kernel, vs, ntp), out_shape=(jax....  3.63 us
    pallas_call x1, Pallas kernels, _write(): pl.pallas_call(_write_kernel, out_shape=(jax.ShapeDtypeStruct((vs, d), F3...  2.26 us
  transfers between devices with their start and end apart: 10, of which 3 were waited for; matrix products, arithmetic and copies ran while one was open for 1% of the time, Pallas kernels for 43%

profile of v8, /device:TPU:0, one launch (start us, length us, event | category | flops | bytes accessed | tf_op | source)
XLA Modules:
  0.0 81.3 jit_solution(11497753522068654586)
XLA Ops:
  0.6 0.0 copy-start.1
  0.6 0.0 copy-start.8
  0.7 0.0 copy-start.7
  0.7 4.4 %index_gather.2.refs_1_ = bf16[64,2304]{1,0:T(8,128)(2,1)S(1)} custom-call(s32[2,256]{1,0:T(2,128)} %refs_0_.1, bf16[8192,2304]{1,0:T(8,128)(2,1)} %refs_1_.1), custom_call_target="tpu_custom_call" | custom-call | flops 48000000000 | bytes 1000000 | tf_op jit(solution)/shard_map/index_gather/pallas_call | solution.py:151
  5.1 0.0 copy-start.6
  5.1 3.2 %collective-permute-start.13 = (bf16[64,2304]{1,0:T(8,128)(2,1)S(1)}, bf16[64,2304]{1,0:T(8,128)(2,1)S(1)}, u32[]{:S(2)}, u32[]{:S(2)}) collective-permute-start(bf16[64,2304]{1,0:T(8,128)(2,1)S(1)} %index_gather.2.refs_1_), channel_id=1, source_target_pairs={{0,2},{1,3},{2,0},{3,1},{4,6},{5,7},{6,4},{7,5}} | collective-permute-start | bytes 884744 | tf_op jit(solution)/shard_map/ppermute | solution.py:613
  8.3 3.9 %p_terms.3 = (bf16[128,2304]{1,0:T(8,128)(2,1)S(1)}, bf16[128,2304]{1,0:T(8,128)(2,1)S(1)}, bf16[128,2304]{1,0:T(8,128)(2,1)S(1)}, bf16[128,2304]{1,0:T(8,128)(2,1)S(1)}, f32[8192,2304]{1,0:T(8,128)}) custom-call(bf16[2,256,1024]{2,1,0:T(8,128)(2,1)S(1)} %copy-done.8, bf16[2304,1024]{1,0:T(8,128)(2,1)S(1)} %copy-done.7), custom_call_target="tpu_custom_call" | custom-call | flops 20000000000 | bytes 1000000 | tf_op jit(solution)/shard_map/p_terms/pallas_call | solution.py:337
  12.2 0.0 copy-start.10
  12.2 3.1 %collective-permute-done.13.refs_3_ = bf16[64,2304]{1,0:T(8,128)(2,1)S(1)} collective-permute-done((bf16[64,2304]{1,0:T(8,128)(2,1)S(1)}, bf16[64,2304]{1,0:T(8,128)(2,1)S(1)}, u32[]{:S(2)}, u32[]{:S(2)}) %collective-permute-start.13) | collective-permute-done | bytes 294944 | tf_op jit(solution)/shard_map/ppermute | solution.py:613
  15.3 0.0 collective-permute-start.14
  15.4 3.6 %slots.4 = (f32[512,1]{1,0:T(8,128)S(1)}, f32[1,512]{1,0:T(1,128)}, s32[1,512]{1,0:T(1,128)}, s32[1,128]{1,0:T(1,128)S(1)}, f32[4,128]{1,0:T(4,128)S(1)}, /*index=5*/s32[1,256]{1,0:T(1,128)S(1)}, f32[8192,2304]{1,0:T(8,128)}) custom-call(s32[1]{0:T(128)} %constant.12.clone.1.c_ref, s32[2,256]{1,0:T(2,128)S(1)} %copy-done.1, ...), custom_call_target="tpu_custom_call", output_to_operand_aliasing={{6}: (2, {})} | custom-call | flops 12000000000 | bytes 1000000 | tf_op jit(solution)/shard_map/slots/pallas_call | solution.py:257
  19.0 1.9 %collective-permute-start.11 = (s32[1,128]{1,0:T(1,128)S(1)}, s32[1,128]{1,0:T(1,128)S(1)}, u32[]{:S(2)}, u32[]{:S(2)}) collective-permute-start(s32[1,128]{1,0:T(1,128)S(1)} %get-tuple-element.157.cnt_ref), channel_id=1, source_target_pairs={{0,4},{4,0},{1,5},{5,1},{2,6},{6,2},{3,7},{7,3}} | collective-permute-start | bytes 1544 | tf_op jit(solution)/shard_map/ppermute | solution.py:641
  20.9 0.2 collective-permute-start.15
  21.2 1.5 %collective-permute-start.16 = (bf16[128,2304]{1,0:T(8,128)(2,1)S(1)}, bf16[128,2304]{1,0:T(8,128)(2,1)S(1)}, u32[]{:S(2)}, u32[]{:S(2)}) collective-permute-start(bf16[128,2304]{1,0:T(8,128)(2,1)S(1)} %get-tuple-element.163), channel_id=1, source_target_pairs={{0,2},{1,3},{2,0},{3,1},{4,6},{5,7},{6,4},{7,5}} | collective-permute-start | bytes 1769480 | tf_op jit(solution)/shard_map/ppermute | solution.py:613
  22.7 0.2 collective-permute-start.17
  22.9 0.9 %expand.2 = (bf16[512,2304]{1,0:T(8,128)(2,1)S(1)}, bf16[2,64,2304]{2,1,0:T(8,128)(2,1)S(1)}) custom-call(f32[512,1]{1,0:T(8,128)S(1)} %get-tuple-element.159.refs_0_, bf16[64,2304]{1,0:T(8,128)(2,1)S(1)} %index_gather.2.refs_1_, bf16[64,2304]{1,0:T(8,128)(2,1)S(1)} %collective-permute-done.12.refs_2_, bf16[64,2304]{1,0:T(8,128)(2,1)S(1)} %collective-permute-done.13.refs_3_, ...), custom_call_target="tpu_custom_call" | custom-call | flops 12000000000 | bytes 1000000 | tf_op jit(solution)/shard_map/expand/pallas_call | solution.py:300
  23.8 0.0 copy-start.14
  23.8 0.0 collective-permute-done.15.p1
  23.8 13.6 %collective-permute-done.16.p2 = bf16[128,2304]{1,0:T(8,128)(2,1)S(1)} collective-permute-done((bf16[128,2304]{1,0:T(8,128)(2,1)S(1)}, bf16[128,2304]{1,0:T(8,128)(2,1)S(1)}, u32[]{:S(2)}, u32[]{:S(2)}) %collective-permute-start.16) | collective-permute-done | bytes 589856 | tf_op jit(solution)/shard_map/ppermute | solution.py:613
  37.4 11.3 %collective-permute-done.17.p3 = bf16[128,2304]{1,0:T(8,128)(2,1)S(1)} collective-permute-done((bf16[128,2304]{1,0:T(8,128)(2,1)S(1)}, bf16[128,2304]{1,0:T(8,128)(2,1)S(1)}, u32[]{:S(2)}, u32[]{:S(2)}) %collective-permute-start.17) | collective-permute-done | bytes 589856 | tf_op jit(solution)/shard_map/ppermute | solution.py:613
  48.7 1.2 %dx_form.3 = (bf16[128,2304]{1,0:T(8,128)(2,1)S(1)}, f32[1,2304]{1,0:T(1,128)S(1)}) custom-call(bf16[128,2304]{1,0:T(8,128)(2,1)S(1)} %bitcast.16, bf16[128,2304]{1,0:T(8,128)(2,1)S(1)} %get-tuple-element.161.p0, bf16[128,2304]{1,0:T(8,128)(2,1)S(1)} %collective-permute-done.15.p1, bf16[128,2304]{1,0:T(8,128)(2,1)S(1)} %collective-permute-done.16.p2, ...), custom_call_target="tpu_custom_call" | custom-call | flops 8000000000 | bytes 1000000 | tf_op jit(solution)/shard_map/dx_form/pallas_call | solution.py:390
  49.9 0.5 collective-permute-start.19
  50.4 0.0 collective-permute-start.18
  50.5 16.6 %u_dw.3 = (bf16[2,256,1024]{2,1,0:T(8,128)(2,1)}, f32[2304,1024]{1,0:T(8,128)}, f32[8192,2304]{1,0:T(8,128)}) custom-call(bf16[512,2304]{1,0:T(8,128)(2,1)S(1)} %get-tuple-element.166.x_ref, bf16[1,2304]{1,0:T(2,128)(2,1)S(1)} %reshape.36.g.g_ref, bf16[2304,1024]{1,0:T(8,128)(2,1)S(1)} %copy-done.7, ...), custom_call_target="tpu_custom_call", output_to_operand_aliasing={{2}: (4, {})} | custom-call | flops 80000000000 | bytes 1000000 | tf_op jit(solution)/shard_map/u_dw/pallas_call | solution.py:465
  67.1 1.9 %shard_map.101.de_in = f32[8192,2304]{1,0:T(8,128)} custom-call(f32[8192,2304]{1,0:T(8,128)} %get-tuple-element.168.de_in), custom_call_target="tpu_custom_call", output_to_operand_aliasing={{}: (0, {})} | custom-call | flops 4499999744 | bytes 1000000 | tf_op jit(solution)/shard_map/pallas_call | solution.py:359
  69.0 0.0 collective-permute-done.19.dg1
  69.0 0.3 dx_sums.1.mine_ref
  69.3 1.5 %collective-permute-start.20 = (f32[32,2304]{1,0:T(8,128)S(1)}, f32[32,2304]{1,0:T(8,128)S(1)}, u32[]{:S(2)}, u32[]{:S(2)}) collective-permute-start(f32[32,2304]{1,0:T(8,128)S(1)} %dx_sums.1.mine_ref), channel_id=1, source_target_pairs={{0,2},{1,3},{2,0},{3,1},{4,6},{5,7},{6,4},{7,5}} | collective-permute-start | bytes 884744 | tf_op jit(solution)/shard_map/ppermute | solution.py:613
  70.7 6.7 %fill_acc.1 = (f32[8192,2304]{1,0:T(8,128)}, f32[64,2304]{1,0:T(8,128)S(1)}, s32[1,4]{1,0:T(1,128)S(1)}) custom-call(s32[1,128]{1,0:T(1,128)S(1)} %get-tuple-element.157.cnt_ref, s32[1,128]{1,0:T(1,128)S(1)} %collective-permute-done.11.oth_ref, f32[4,128]{1,0:T(4,128)S(1)} %get-tuple-element.158.slot_ref, ...), custom_call_target="tpu_custom_call", output_to_operand_aliasing={{0}: (5, {})} | custom-call | flops 19499999232 | bytes 1000000 | tf_op jit(solution)/shard_map/fill_acc/pallas_call | solution.py:551
  77.5 0.6 slice.6
  78.7 2.3 %write_rows.1 = (f32[8192,2304]{1,0:T(8,128)}, f32[2304]{0:T(1024)}) custom-call(s32[1,256]{1,0:T(1,128)S(1)} %get-tuple-element.171.map_ref, f32[64,2304]{1,0:T(8,128)S(1)} %get-tuple-element.172.acc_in, f32[32,2304]{1,0:T(8,128)S(1)} %dx_sums.1.mine_ref, f32[32,2304]{1,0:T(8,128)S(1)} %collective-permute-done.20.got_ref, ...), custom_call_target="tpu_custom_call", output_to_operand_aliasing={{0}: (4, {})} | custom-call | flops 12000000000 | bytes 1000000 | tf_op jit(solution)/shard_map/write_rows/pallas_call | solution.py:595
  81.0 0.2 while.30
  (17 shorter events, 0.0 us)
Async XLA Ops:
  0.6 14.7 %copy-start.1 = (s32[2,256]{1,0:T(2,128)S(1)}, s32[2,256]{1,0:T(2,128)}, u32[]{:S(2)}) copy-start(s32[2,256]{1,0:T(2,128)} %refs_0_.1) | copy-start | bytes 6148
  0.6 7.6 %copy-start.8 = (bf16[2,256,1024]{2,1,0:T(8,128)(2,1)S(1)}, bf16[2,256,1024]{2,1,0:T(8,128)(2,1)}, u32[]{:S(2)}) copy-start(bf16[2,256,1024]{2,1,0:T(8,128)(2,1)} %du_ref.3) | copy-start | bytes 3145732
  0.7 7.6 %copy-start.7 = (bf16[2304,1024]{1,0:T(8,128)(2,1)S(1)}, bf16[2304,1024]{1,0:T(8,128)(2,1)}, u32[]{:S(2)}) copy-start(bf16[2304,1024]{1,0:T(8,128)(2,1)} %w_ref.3) | copy-start | bytes 14155780
  5.1 16.1 %copy-start.6 = (bf16[2304]{0:T(1024)(128)(2,1)S(1)}, bf16[2304]{0:T(1024)(128)(2,1)}, u32[]{:S(2)}) copy-start(bf16[2304]{0:T(1024)(128)(2,1)} %param.12) | copy-start | bytes 13828
  5.1 10.3 %collective-permute-start.13 = (bf16[64,2304]{1,0:T(8,128)(2,1)S(1)}, bf16[64,2304]{1,0:T(8,128)(2,1)S(1)}, u32[]{:S(2)}, u32[]{:S(2)}) collective-permute-start(bf16[64,2304]{1,0:T(8,128)(2,1)S(1)} %index_gather.2.refs_1_), channel_id=1, source_target_pairs={{0,2},{1,3},{2,0},{3,1},{4,6},{5,7},{6,4},{7,5}} | collective-permute-start | bytes 884744 | tf_op jit(solution)/shard_map/ppermute | solution.py:613
  8.3 14.4 %collective-permute-start.12 = (bf16[64,2304]{1,0:T(8,128)(2,1)S(1)}, bf16[64,2304]{1,0:T(8,128)(2,1)S(1)}, u32[]{:S(2)}, u32[]{:S(2)}) collective-permute-start(bf16[64,2304]{1,0:T(8,128)(2,1)S(1)} %index_gather.2.refs_1_), channel_id=1, source_target_pairs={{0,1},{1,0},{2,3},{3,2},{4,5},{5,4},{6,7},{7,6}} | collective-permute-start | bytes 884744 | tf_op jit(solution)/shard_map/ppermute | solution.py:613
  12.2 36.5 %copy-start.10 = (bf16[2,64,2304]{2,1,0:T(8,128)(2,1)S(1)}, bf16[2,64,2304]{2,1,0:T(8,128)(2,1)}, u32[]{:S(2)}) copy-start(bf16[2,64,2304]{2,1,0:T(8,128)(2,1)} %param.15) | copy-start | bytes 1769476
  15.3 7.5 %collective-permute-start.14 = (bf16[64,2304]{1,0:T(8,128)(2,1)S(1)}, bf16[64,2304]{1,0:T(8,128)(2,1)S(1)}, u32[]{:S(2)}, u32[]{:S(2)}) collective-permute-start(bf16[64,2304]{1,0:T(8,128)(2,1)S(1)} %collective-permute-done.13.refs_3_), channel_id=1, source_target_pairs={{0,1},{1,0},{2,3},{3,2},{4,5},{5,4},{6,7},{7,6}} | collective-permute-start | bytes 884744 | tf_op jit(solution)/shard_map/ppermute | solution.py:613
  19.0 51.7 %collective-permute-start.11 = (s32[1,128]{1,0:T(1,128)S(1)}, s32[1,128]{1,0:T(1,128)S(1)}, u32[]{:S(2)}, u32[]{:S(2)}) collective-permute-start(s32[1,128]{1,0:T(1,128)S(1)} %get-tuple-element.157.cnt_ref), channel_id=1, source_target_pairs={{0,4},{4,0},{1,5},{5,1},{2,6},{6,2},{3,7},{7,3}} | collective-permute-start | bytes 1544 | tf_op jit(solution)/shard_map/ppermute | solution.py:641
  20.9 2.8 %collective-permute-start.15 = (bf16[128,2304]{1,0:T(8,128)(2,1)S(1)}, bf16[128,2304]{1,0:T(8,128)(2,1)S(1)}, u32[]{:S(2)}, u32[]{:S(2)}) collective-permute-start(bf16[128,2304]{1,0:T(8,128)(2,1)S(1)} %get-tuple-element.162), channel_id=1, source_target_pairs={{0,1},{1,0},{2,3},{3,2},{4,5},{5,4},{6,7},{7,6}} | collective-permute-start | bytes 1769480 | tf_op jit(solution)/shard_map/ppermute | solution.py:613
  21.2 45.9 %copy-start.4 = (bf16[1,2304]{1,0:T(2,128)(2,1)}, bf16[1,2304]{1,0:T(2,128)(2,1)S(1)}, u32[]{:S(2)}) copy-start(bf16[1,2304]{1,0:T(2,128)(2,1)S(1)} %reshape.36.g.g_ref) | copy-start | bytes 13828
  21.2 16.2 %collective-permute-start.16 = (bf16[128,2304]{1,0:T(8,128)(2,1)S(1)}, bf16[128,2304]{1,0:T(8,128)(2,1)S(1)}, u32[]{:S(2)}, u32[]{:S(2)}) collective-permute-start(bf16[128,2304]{1,0:T(8,128)(2,1)S(1)} %get-tuple-element.163), channel_id=1, source_target_pairs={{0,2},{1,3},{2,0},{3,1},{4,6},{5,7},{6,4},{7,5}} | collective-permute-start | bytes 1769480 | tf_op jit(solution)/shard_map/ppermute | solution.py:613
  22.7 26.0 %collective-permute-start.17 = (bf16[128,2304]{1,0:T(8,128)(2,1)S(1)}, bf16[128,2304]{1,0:T(8,128)(2,1)S(1)}, u32[]{:S(2)}, u32[]{:S(2)}) collective-permute-start(bf16[128,2304]{1,0:T(8,128)(2,1)S(1)} %get-tuple-element.164), channel_id=1, source_target_pairs={{0,3},{1,2},{2,1},{3,0},{4,7},{5,6},{6,5},{7,4}} | collective-permute-start | bytes 1769480 | tf_op jit(solution)/shard_map/ppermute | solution.py:613
  23.8 26.6 %copy-start.14 = (bf16[2,64,2304]{2,1,0:T(8,128)(2,1)}, bf16[2,64,2304]{2,1,0:T(8,128)(2,1)S(1)}, u32[]{:S(2)}) copy-start(bf16[2,64,2304]{2,1,0:T(8,128)(2,1)S(1)} %get-tuple-element.312) | copy-start | bytes 1769476
  49.9 19.1 %collective-permute-start.19 = (f32[1,2304]{1,0:T(1,128)S(1)}, f32[1,2304]{1,0:T(1,128)S(1)}, u32[]{:S(2)}, u32[]{:S(2)}) collective-permute-start(f32[1,2304]{1,0:T(1,128)S(1)} %get-tuple-element.173.dg0), channel_id=1, source_target_pairs={{0,1},{1,0},{2,3},{3,2},{4,5},{5,4},{6,7},{7,6}} | collective-permute-start | bytes 27656 | tf_op jit(solution)/shard_map/ppermute | solution.py:613
  50.4 18.6 %collective-permute-start.18 = (bf16[128,2304]{1,0:T(8,128)(2,1)S(1)}, bf16[128,2304]{1,0:T(8,128)(2,1)S(1)}, u32[]{:S(2)}, u32[]{:S(2)}) collective-permute-start(bf16[128,2304]{1,0:T(8,128)(2,1)S(1)} %get-tuple-element.165.dx0), channel_id=1, source_target_pairs={{0,1},{1,0},{2,3},{3,2},{4,5},{5,4},{6,7},{7,6}} | collective-permute-start | bytes 1769480 | tf_op jit(solution)/shard_map/ppermute | solution.py:613
  69.3 11.7 %copy-start.2 = (s32[2,256]{1,0:T(2,128)S(1)}, s32[2,256]{1,0:T(2,128)}, u32[]{:S(2)}) copy-start(s32[2,256]{1,0:T(2,128)} %refs_0_.1) | copy-start | bytes 6148
  69.3 9.4 %collective-permute-start.20 = (f32[32,2304]{1,0:T(8,128)S(1)}, f32[32,2304]{1,0:T(8,128)S(1)}, u32[]{:S(2)}, u32[]{:S(2)}) collective-permute-start(f32[32,2304]{1,0:T(8,128)S(1)} %dx_sums.1.mine_ref), channel_id=1, source_target_pairs={{0,2},{1,3},{2,0},{3,1},{4,6},{5,7},{6,4},{7,5}} | collective-permute-start | bytes 884744 | tf_op jit(solution)/shard_map/ppermute | solution.py:613

commit v9 on v8

--- a/solution.py
+++ b/solution.py
@@ -9,13 +9,13 @@
 
 
 EPS = 1e-6
-C = 64
+C = 56
 G = 2
 C2 = 32
 CB = 256
 ZR = 128
-ZP, ZA, ZU, ZW, ZB = 8, 6, 14, 20, 3
-AT_A, AT_U, AT_B, AT_R = ZP, ZP + ZA, ZP + ZA + ZU + ZW, ZP + ZA + ZU + ZW + ZB
+ZP, ZA, ZU, ZW = 8, 6, 15, 22
+AT_A, AT_U, AT_R = ZP, ZP + ZA, ZP + ZA + ZU + ZW
 TB = 64
 
 F32 = jnp.float32
@@ -635,7 +635,6 @@
         u, dW, de = _udw(x, g2, W, du, de)
         dx, dg = _dx(xl.reshape(m, d), ps, dres.reshape(m, d), g2)
         dx1, dg1 = swap(dx, 1), swap(dg, 1)
-        de = _zeros(de, AT_B, ZB)
         mine = _sums(slots, dx, dx1, dg, dg1)
         got = swap(mine, 2)
         other = lax.ppermute(cnts, "dp", [(i, (i + 1) % ndp) for i in range(ndp)])
@@ -663,7 +662,7 @@
             dx, dg = _dx(xl.reshape(m, d), ps, dres.reshape(m, d), g2)
             dg2 = dg + swap(dg, 1)
             dg = (dg2 + swap(dg2, 2)).reshape(d)
-            dE = _scatter(cs, rows, srow, share(dx), _zeros(de, AT_B, vs // ZR - AT_B), ts, nk)
+            dE = _scatter(cs, rows, srow, share(dx), _zeros(de, AT_R, vs // ZR - AT_R), ts, nk)
             return i0, (u, xl, dE, dW, dg)
 
         _, outs = lax.while_loop(lambda c: c[0] > 0, again, (jnp.minimum(flags[0, 2], 1), outs))

time: 81.5 us -> 80.1 us (0.983)
    pallas_call x1 -> x0, Pallas kernels: 1.9 us -> none  [_zeros(): pl.pallas_call(functools.partial(_zero_kernel, lo, n), out_shape=jax.Shap...]
    pallas_call x1, Pallas kernels: 16.6 us -> 18.2 us  [_udw(): pl.pallas_call(functools.partial(_udw_kernel, -(-ZW // steps)), out_shape...]
  transfers between devices with their start and end apart: 10 -> 10, of which waited for: 3 -> 3; matrix products, arithmetic and copies ran while one was open for 1% -> 1% of each run, Pallas kernels for 43% -> 44%
where the time goes in v9:
time: 80.1 us; the launch traced here: 79.9 us
  Pallas kernels  41.2 us (51%)
  waiting for transfers between devices  27.3 us (34%)
  starting transfers between devices  9.01 us (11%)
  between operations  1.62 us (2%)
    ppermute x9, waiting for transfers between devices, swap(): return lax.ppermute(a, 'tp', [(i, i ^ bit) for i in range(ntp)])  27.3 us
    pallas_call x1, Pallas kernels, _udw(): pl.pallas_call(functools.partial(_udw_kernel, -(-ZW // steps)), out_shape...  18.2 us
    ppermute x9, starting transfers between devices, swap(): return lax.ppermute(a, 'tp', [(i, i ^ bit) for i in range(ntp)])  7.05 us
    pallas_call x1, Pallas kernels, _acc(): pl.pallas_call(functools.partial(_acc_kernel, lo, n), out_shape=(jax.Shap...  6.73 us
    pallas_call x1, Pallas kernels, _index_call(): pl.pallas_call(functools.partial(_index_kernel, vs, ntp, first), out_shap...  4.12 us
    pallas_call x1, Pallas kernels, _p_terms(): pl.pallas_call(functools.partial(_p_kernel, ts), out_shape=(jax.ShapeDtyp...  3.94 us
    pallas_call x1, Pallas kernels, _slots(): pl.pallas_call(functools.partial(_slots_kernel, vs, ntp), out_shape=(jax....  3.63 us
    pallas_call x1, Pallas kernels, _write(): pl.pallas_call(_write_kernel, out_shape=(jax.ShapeDtypeStruct((vs, d), F3...  2.25 us
  transfers between devices with their start and end apart: 10, of which 3 were waited for; matrix products, arithmetic and copies ran while one was open for 1% of the time, Pallas kernels for 44%

profile of v9, /device:TPU:0, one launch (start us, length us, event | category | flops | bytes accessed | tf_op | source)
XLA Modules:
  0.0 79.9 jit_solution(15623089455693265809)
XLA Ops:
  0.6 0.0 copy-start.1
  0.6 0.0 copy-start.8
  0.7 0.0 copy-start.7
  0.7 4.1 %index_gather.2.refs_1_ = bf16[56,2304]{1,0:T(8,128)(2,1)S(1)} custom-call(s32[2,256]{1,0:T(2,128)} %refs_0_.1, bf16[8192,2304]{1,0:T(8,128)(2,1)} %refs_1_.1), custom_call_target="tpu_custom_call" | custom-call | flops 48000000000 | bytes 1000000 | tf_op jit(solution)/shard_map/index_gather/pallas_call | solution.py:151
  4.8 0.0 copy-start.6
  4.8 3.2 %collective-permute-start.13 = (bf16[56,2304]{1,0:T(8,128)(2,1)S(1)}, bf16[56,2304]{1,0:T(8,128)(2,1)S(1)}, u32[]{:S(2)}, u32[]{:S(2)}) collective-permute-start(bf16[56,2304]{1,0:T(8,128)(2,1)S(1)} %index_gather.2.refs_1_), channel_id=1, source_target_pairs={{0,2},{1,3},{2,0},{3,1},{4,6},{5,7},{6,4},{7,5}} | collective-permute-start | bytes 774152 | tf_op jit(solution)/shard_map/ppermute | solution.py:613
  8.0 0.0 collective-permute-start.12
  8.0 3.9 %p_terms.3 = (bf16[128,2304]{1,0:T(8,128)(2,1)S(1)}, bf16[128,2304]{1,0:T(8,128)(2,1)S(1)}, bf16[128,2304]{1,0:T(8,128)(2,1)S(1)}, bf16[128,2304]{1,0:T(8,128)(2,1)S(1)}, f32[8192,2304]{1,0:T(8,128)}) custom-call(bf16[2,256,1024]{2,1,0:T(8,128)(2,1)S(1)} %copy-done.8, bf16[2304,1024]{1,0:T(8,128)(2,1)S(1)} %copy-done.7), custom_call_target="tpu_custom_call" | custom-call | flops 20000000000 | bytes 1000000 | tf_op jit(solution)/shard_map/p_terms/pallas_call | solution.py:337
  11.9 0.0 copy-start.10
  11.9 2.3 %collective-permute-done.13.refs_3_ = bf16[56,2304]{1,0:T(8,128)(2,1)S(1)} collective-permute-done((bf16[56,2304]{1,0:T(8,128)(2,1)S(1)}, bf16[56,2304]{1,0:T(8,128)(2,1)S(1)}, u32[]{:S(2)}, u32[]{:S(2)}) %collective-permute-start.13) | collective-permute-done | bytes 258080 | tf_op jit(solution)/shard_map/ppermute | solution.py:613
  14.3 0.0 collective-permute-start.14
  14.3 3.6 %slots.4 = (f32[512,1]{1,0:T(8,128)S(1)}, f32[1,512]{1,0:T(1,128)}, s32[1,512]{1,0:T(1,128)}, s32[1,128]{1,0:T(1,128)S(1)}, f32[4,128]{1,0:T(4,128)S(1)}, /*index=5*/s32[1,256]{1,0:T(1,128)S(1)}, f32[8192,2304]{1,0:T(8,128)}) custom-call(s32[1]{0:T(128)} %constant.12.clone.1.c_ref, s32[2,256]{1,0:T(2,128)S(1)} %copy-done.1, ...), custom_call_target="tpu_custom_call", output_to_operand_aliasing={{6}: (2, {})} | custom-call | flops 12000000000 | bytes 1000000 | tf_op jit(solution)/shard_map/slots/pallas_call | solution.py:257
  17.9 2.0 %collective-permute-start.11 = (s32[1,128]{1,0:T(1,128)S(1)}, s32[1,128]{1,0:T(1,128)S(1)}, u32[]{:S(2)}, u32[]{:S(2)}) collective-permute-start(s32[1,128]{1,0:T(1,128)S(1)} %get-tuple-element.157.cnt_ref), channel_id=1, source_target_pairs={{0,4},{4,0},{1,5},{5,1},{2,6},{6,2},{3,7},{7,3}} | collective-permute-start | bytes 1544 | tf_op jit(solution)/shard_map/ppermute | solution.py:640
  19.9 0.2 collective-permute-start.15
  20.1 1.4 %collective-permute-start.16 = (bf16[128,2304]{1,0:T(8,128)(2,1)S(1)}, bf16[128,2304]{1,0:T(8,128)(2,1)S(1)}, u32[]{:S(2)}, u32[]{:S(2)}) collective-permute-start(bf16[128,2304]{1,0:T(8,128)(2,1)S(1)} %get-tuple-element.163), channel_id=1, source_target_pairs={{0,2},{1,3},{2,0},{3,1},{4,6},{5,7},{6,4},{7,5}} | collective-permute-start | bytes 1769480 | tf_op jit(solution)/shard_map/ppermute | solution.py:613
  21.6 0.0 collective-permute-done.12.refs_2_
  21.6 0.2 collective-permute-start.17
  21.8 0.0 collective-permute-done.14.refs_4_
  21.8 0.9 %expand.2 = (bf16[512,2304]{1,0:T(8,128)(2,1)S(1)}, bf16[2,64,2304]{2,1,0:T(8,128)(2,1)S(1)}) custom-call(f32[512,1]{1,0:T(8,128)S(1)} %get-tuple-element.159.refs_0_, bf16[56,2304]{1,0:T(8,128)(2,1)S(1)} %index_gather.2.refs_1_, bf16[56,2304]{1,0:T(8,128)(2,1)S(1)} %collective-permute-done.12.refs_2_, bf16[56,2304]{1,0:T(8,128)(2,1)S(1)} %collective-permute-done.13.refs_3_, ...), custom_call_target="tpu_custom_call" | custom-call | flops 12000000000 | bytes 1000000 | tf_op jit(solution)/shard_map/expand/pallas_call | solution.py:300
  22.7 0.0 copy-start.14
  22.7 13.6 %collective-permute-done.16.p2 = bf16[128,2304]{1,0:T(8,128)(2,1)S(1)} collective-permute-done((bf16[128,2304]{1,0:T(8,128)(2,1)S(1)}, bf16[128,2304]{1,0:T(8,128)(2,1)S(1)}, u32[]{:S(2)}, u32[]{:S(2)}) %collective-permute-start.16) | collective-permute-done | bytes 589856 | tf_op jit(solution)/shard_map/ppermute | solution.py:613
  36.3 11.3 %collective-permute-done.17.p3 = bf16[128,2304]{1,0:T(8,128)(2,1)S(1)} collective-permute-done((bf16[128,2304]{1,0:T(8,128)(2,1)S(1)}, bf16[128,2304]{1,0:T(8,128)(2,1)S(1)}, u32[]{:S(2)}, u32[]{:S(2)}) %collective-permute-start.17) | collective-permute-done | bytes 589856 | tf_op jit(solution)/shard_map/ppermute | solution.py:613
  47.6 1.2 %dx_form.3 = (bf16[128,2304]{1,0:T(8,128)(2,1)S(1)}, f32[1,2304]{1,0:T(1,128)S(1)}) custom-call(bf16[128,2304]{1,0:T(8,128)(2,1)S(1)} %bitcast.16, bf16[128,2304]{1,0:T(8,128)(2,1)S(1)} %get-tuple-element.161.p0, bf16[128,2304]{1,0:T(8,128)(2,1)S(1)} %collective-permute-done.15.p1, bf16[128,2304]{1,0:T(8,128)(2,1)S(1)} %collective-permute-done.16.p2, ...), custom_call_target="tpu_custom_call" | custom-call | flops 8000000000 | bytes 1000000 | tf_op jit(solution)/shard_map/dx_form/pallas_call | solution.py:390
  48.8 0.5 collective-permute-start.19
  49.3 0.0 collective-permute-start.18
  49.4 18.2 %u_dw.3 = (bf16[2,256,1024]{2,1,0:T(8,128)(2,1)}, f32[2304,1024]{1,0:T(8,128)}, f32[8192,2304]{1,0:T(8,128)}) custom-call(bf16[512,2304]{1,0:T(8,128)(2,1)S(1)} %get-tuple-element.166.x_ref, bf16[1,2304]{1,0:T(2,128)(2,1)S(1)} %reshape.36.g.g_ref, bf16[2304,1024]{1,0:T(8,128)(2,1)S(1)} %copy-done.7, ...), custom_call_target="tpu_custom_call", output_to_operand_aliasing={{2}: (4, {})} | custom-call | flops 80000000000 | bytes 1000000 | tf_op jit(solution)/shard_map/u_dw/pallas_call | solution.py:465
  67.6 0.3 dx_sums.1.mine_ref
  67.9 1.4 %collective-permute-start.20 = (f32[32,2304]{1,0:T(8,128)S(1)}, f32[32,2304]{1,0:T(8,128)S(1)}, u32[]{:S(2)}, u32[]{:S(2)}) collective-permute-start(f32[32,2304]{1,0:T(8,128)S(1)} %dx_sums.1.mine_ref), channel_id=1, source_target_pairs={{0,2},{1,3},{2,0},{3,1},{4,6},{5,7},{6,4},{7,5}} | collective-permute-start | bytes 884744 | tf_op jit(solution)/shard_map/ppermute | solution.py:613
  69.3 6.7 %fill_acc.1 = (f32[8192,2304]{1,0:T(8,128)}, f32[56,2304]{1,0:T(8,128)S(1)}, s32[1,4]{1,0:T(1,128)S(1)}) custom-call(s32[1,128]{1,0:T(1,128)S(1)} %get-tuple-element.157.cnt_ref, s32[1,128]{1,0:T(1,128)S(1)} %collective-permute-done.11.oth_ref, f32[4,128]{1,0:T(4,128)S(1)} %get-tuple-element.158.slot_ref, ...), custom_call_target="tpu_custom_call", output_to_operand_aliasing={{0}: (5, {})} | custom-call | flops 19499999232 | bytes 1000000 | tf_op jit(solution)/shard_map/fill_acc/pallas_call | solution.py:551
  76.1 0.6 slice.6
  77.3 2.3 %write_rows.1 = (f32[8192,2304]{1,0:T(8,128)}, f32[2304]{0:T(1024)}) custom-call(s32[1,256]{1,0:T(1,128)S(1)} %get-tuple-element.171.map_ref, f32[56,2304]{1,0:T(8,128)S(1)} %get-tuple-element.172.acc_in, f32[32,2304]{1,0:T(8,128)S(1)} %dx_sums.1.mine_ref, f32[32,2304]{1,0:T(8,128)S(1)} %collective-permute-done.20.got_ref, ...), custom_call_target="tpu_custom_call", output_to_operand_aliasing={{0}: (4, {})} | custom-call | flops 12000000000 | bytes 1000000 | tf_op jit(solution)/shard_map/write_rows/pallas_call | solution.py:595
  79.6 0.2 while.30
  (16 shorter events, 0.0 us)
Async XLA Ops:
  0.6 13.6 %copy-start.1 = (s32[2,256]{1,0:T(2,128)S(1)}, s32[2,256]{1,0:T(2,128)}, u32[]{:S(2)}) copy-start(s32[2,256]{1,0:T(2,128)} %refs_0_.1) | copy-start | bytes 6148
  0.6 7.3 %copy-start.8 = (bf16[2,256,1024]{2,1,0:T(8,128)(2,1)S(1)}, bf16[2,256,1024]{2,1,0:T(8,128)(2,1)}, u32[]{:S(2)}) copy-start(bf16[2,256,1024]{2,1,0:T(8,128)(2,1)} %du_ref.3) | copy-start | bytes 3145732
  0.7 7.3 %copy-start.7 = (bf16[2304,1024]{1,0:T(8,128)(2,1)S(1)}, bf16[2304,1024]{1,0:T(8,128)(2,1)}, u32[]{:S(2)}) copy-start(bf16[2304,1024]{1,0:T(8,128)(2,1)} %w_ref.3) | copy-start | bytes 14155780
  4.8 15.3 %copy-start.6 = (bf16[2304]{0:T(1024)(128)(2,1)S(1)}, bf16[2304]{0:T(1024)(128)(2,1)}, u32[]{:S(2)}) copy-start(bf16[2304]{0:T(1024)(128)(2,1)} %param.12) | copy-start | bytes 13828
  4.8 9.5 %collective-permute-start.13 = (bf16[56,2304]{1,0:T(8,128)(2,1)S(1)}, bf16[56,2304]{1,0:T(8,128)(2,1)S(1)}, u32[]{:S(2)}, u32[]{:S(2)}) collective-permute-start(bf16[56,2304]{1,0:T(8,128)(2,1)S(1)} %index_gather.2.refs_1_), channel_id=1, source_target_pairs={{0,2},{1,3},{2,0},{3,1},{4,6},{5,7},{6,4},{7,5}} | collective-permute-start | bytes 774152 | tf_op jit(solution)/shard_map/ppermute | solution.py:613
  8.0 13.6 %collective-permute-start.12 = (bf16[56,2304]{1,0:T(8,128)(2,1)S(1)}, bf16[56,2304]{1,0:T(8,128)(2,1)S(1)}, u32[]{:S(2)}, u32[]{:S(2)}) collective-permute-start(bf16[56,2304]{1,0:T(8,128)(2,1)S(1)} %index_gather.2.refs_1_), channel_id=1, source_target_pairs={{0,1},{1,0},{2,3},{3,2},{4,5},{5,4},{6,7},{7,6}} | collective-permute-start | bytes 774152 | tf_op jit(solution)/shard_map/ppermute | solution.py:613
  11.9 35.7 %copy-start.10 = (bf16[2,64,2304]{2,1,0:T(8,128)(2,1)S(1)}, bf16[2,64,2304]{2,1,0:T(8,128)(2,1)}, u32[]{:S(2)}) copy-start(bf16[2,64,2304]{2,1,0:T(8,128)(2,1)} %param.15) | copy-start | bytes 1769476
  14.3 7.5 %collective-permute-start.14 = (bf16[56,2304]{1,0:T(8,128)(2,1)S(1)}, bf16[56,2304]{1,0:T(8,128)(2,1)S(1)}, u32[]{:S(2)}, u32[]{:S(2)}) collective-permute-start(bf16[56,2304]{1,0:T(8,128)(2,1)S(1)} %collective-permute-done.13.refs_3_), channel_id=1, source_target_pairs={{0,1},{1,0},{2,3},{3,2},{4,5},{5,4},{6,7},{7,6}} | collective-permute-start | bytes 774152 | tf_op jit(solution)/shard_map/ppermute | solution.py:613
  17.9 51.4 %collective-permute-start.11 = (s32[1,128]{1,0:T(1,128)S(1)}, s32[1,128]{1,0:T(1,128)S(1)}, u32[]{:S(2)}, u32[]{:S(2)}) collective-permute-start(s32[1,128]{1,0:T(1,128)S(1)} %get-tuple-element.157.cnt_ref), channel_id=1, source_target_pairs={{0,4},{4,0},{1,5},{5,1},{2,6},{6,2},{3,7},{7,3}} | collective-permute-start | bytes 1544 | tf_op jit(solution)/shard_map/ppermute | solution.py:640
  19.9 2.8 %collective-permute-start.15 = (bf16[128,2304]{1,0:T(8,128)(2,1)S(1)}, bf16[128,2304]{1,0:T(8,128)(2,1)S(1)}, u32[]{:S(2)}, u32[]{:S(2)}) collective-permute-start(bf16[128,2304]{1,0:T(8,128)(2,1)S(1)} %get-tuple-element.162), channel_id=1, source_target_pairs={{0,1},{1,0},{2,3},{3,2},{4,5},{5,4},{6,7},{7,6}} | collective-permute-start | bytes 1769480 | tf_op jit(solution)/shard_map/ppermute | solution.py:613
  20.1 47.5 %copy-start.4 = (bf16[1,2304]{1,0:T(2,128)(2,1)}, bf16[1,2304]{1,0:T(2,128)(2,1)S(1)}, u32[]{:S(2)}) copy-start(bf16[1,2304]{1,0:T(2,128)(2,1)S(1)} %reshape.36.g.g_ref) | copy-start | bytes 13828
  20.1 16.2 %collective-permute-start.16 = (bf16[128,2304]{1,0:T(8,128)(2,1)S(1)}, bf16[128,2304]{1,0:T(8,128)(2,1)S(1)}, u32[]{:S(2)}, u32[]{:S(2)}) collective-permute-start(bf16[128,2304]{1,0:T(8,128)(2,1)S(1)} %get-tuple-element.163), channel_id=1, source_target_pairs={{0,2},{1,3},{2,0},{3,1},{4,6},{5,7},{6,4},{7,5}} | collective-permute-start | bytes 1769480 | tf_op jit(solution)/shard_map/ppermute | solution.py:613
  21.6 26.0 %collective-permute-start.17 = (bf16[128,2304]{1,0:T(8,128)(2,1)S(1)}, bf16[128,2304]{1,0:T(8,128)(2,1)S(1)}, u32[]{:S(2)}, u32[]{:S(2)}) collective-permute-start(bf16[128,2304]{1,0:T(8,128)(2,1)S(1)} %get-tuple-element.164), channel_id=1, source_target_pairs={{0,3},{1,2},{2,1},{3,0},{4,7},{5,6},{6,5},{7,4}} | collective-permute-start | bytes 1769480 | tf_op jit(solution)/shard_map/ppermute | solution.py:613
  22.7 26.7 %copy-start.14 = (bf16[2,64,2304]{2,1,0:T(8,128)(2,1)}, bf16[2,64,2304]{2,1,0:T(8,128)(2,1)S(1)}, u32[]{:S(2)}) copy-start(bf16[2,64,2304]{2,1,0:T(8,128)(2,1)S(1)} %get-tuple-element.312) | copy-start | bytes 1769476
  48.8 18.8 %collective-permute-start.19 = (f32[1,2304]{1,0:T(1,128)S(1)}, f32[1,2304]{1,0:T(1,128)S(1)}, u32[]{:S(2)}, u32[]{:S(2)}) collective-permute-start(f32[1,2304]{1,0:T(1,128)S(1)} %get-tuple-element.173.dg0), channel_id=1, source_target_pairs={{0,1},{1,0},{2,3},{3,2},{4,5},{5,4},{6,7},{7,6}} | collective-permute-start | bytes 27656 | tf_op jit(solution)/shard_map/ppermute | solution.py:613
  49.3 18.2 %collective-permute-start.18 = (bf16[128,2304]{1,0:T(8,128)(2,1)S(1)}, bf16[128,2304]{1,0:T(8,128)(2,1)S(1)}, u32[]{:S(2)}, u32[]{:S(2)}) collective-permute-start(bf16[128,2304]{1,0:T(8,128)(2,1)S(1)} %get-tuple-element.165.dx0), channel_id=1, source_target_pairs={{0,1},{1,0},{2,3},{3,2},{4,5},{5,4},{6,7},{7,6}} | collective-permute-start | bytes 1769480 | tf_op jit(solution)/shard_map/ppermute | solution.py:613
  67.9 9.4 %collective-permute-start.20 = (f32[32,2304]{1,0:T(8,128)S(1)}, f32[32,2304]{1,0:T(8,128)S(1)}, u32[]{:S(2)}, u32[]{:S(2)}) collective-permute-start(f32[32,2304]{1,0:T(8,128)S(1)} %dx_sums.1.mine_ref), channel_id=1, source_target_pairs={{0,2},{1,3},{2,0},{3,1},{4,6},{5,7},{6,4},{7,5}} | collective-permute-start | bytes 884744 | tf_op jit(solution)/shard_map/ppermute | solution.py:613
  69.3 10.2 %copy-start.2 = (s32[2,256]{1,0:T(2,128)S(1)}, s32[2,256]{1,0:T(2,128)}, u32[]{:S(2)}) copy-start(s32[2,256]{1,0:T(2,128)} %refs_0_.1) | copy-start | bytes 6148

commit v10 on v8

--- a/solution.py
+++ b/solution.py
@@ -9,12 +9,12 @@
 
 
 EPS = 1e-6
-C = 64
+C = 56
 G = 2
 C2 = 32
 CB = 256
 ZR = 128
-ZP, ZA, ZU, ZW, ZB = 8, 6, 14, 20, 3
+ZP, ZA, ZU, ZW, ZB = 8, 6, 15, 22, 4
 AT_A, AT_U, AT_B, AT_R = ZP, ZP + ZA, ZP + ZA + ZU + ZW, ZP + ZA + ZU + ZW + ZB
 TB = 64
 
@@ -216,17 +216,16 @@
     rounds = jnp.floor((mx + C - 1.0) * (1.0 / C))
     cnts = jnp.where(lane1 == 0, rounds, jnp.where(lane1 == 1, cnt, jnp.where(lane1 == 2, over, cnt2)))
     cnt_ref[...] = cnts.astype(jnp.int32)
-    facing = (mei ^ 2).astype(F32)
-    sums_r = jnp.where(own_r == facing, slot2_r, -1.0)
+    sums_r = [jnp.where(own_r == (mei ^ o).astype(F32), slot2_r, -1.0) for o in (2, 3)]
     rows = [jnp.zeros((1, nk * ts), F32)] * 4
     for q in range(ntp):
         at = [slice(k * t + q * ts, k * t + (q + 1) * ts) for k in range(nk)]
         mine = jnp.concatenate([my_r[:, w] for w in at], axis=1)
-        sums = jnp.concatenate([sums_r[:, w] for w in at], axis=1)
+        sums = [jnp.concatenate([r[:, w] for w in at], axis=1) for r in sums_r]
         own, sib = me == float(q), me == float(q ^ 1)
         rows = [
             jnp.where(own, mine, rows[0]), jnp.where(sib, mine, rows[1]),
-            jnp.where(own, sums, rows[2]), jnp.where(sib, sums, rows[3]),
+            jnp.where(own, sums[0], rows[2]), jnp.where(own, sums[1], rows[3]),
         ]
     for j, r in enumerate(rows):
         slot_ref[j:j + 1, :] = r
@@ -368,7 +367,7 @@
     )(de)
 
 
-def _dx_kernel(x, p0, p1, p2, p3, dres, g, dx, dg):
+def _dx_rows(x, p0, p1, p2, p3, dres, g, dx):
     rows = 32
     tot = None
     for b in range(dx.shape[0] // rows):
@@ -382,7 +381,11 @@
         dx[s] = out.astype(BF16)
         part = jnp.sum(dn * nh, axis=0, keepdims=True)
         tot = part if tot is None else tot + part
-    dg[...] = tot
+    return tot
+
+
+def _dx_kernel(*refs):
+    refs[-1][...] = _dx_rows(*refs[:-1])
 
 
 def _dx(x, ps, dres, g):
@@ -401,28 +404,44 @@
     )(x, *ps, dres, g)
 
 
-def _sums_kernel(slot_ref, dx0, dx1, dg0, dg1, out):
-    m = dx0.shape[0]
-    j = _iota((C2, m), 0)
-    ohs = [jnp.where(slot_ref[i:i + 1, :] == j, 1.0, 0.0).astype(BF16) for i in (2, 3)]
+def _dx_sums_kernel(x, p0, p1, p2, p3, dres, g, slot_ref, dx, mine, out, got, send, recv):
+    sib = _me() ^ 1
+    barrier = pltpu.get_barrier_semaphore()
+    pl.semaphore_signal(barrier, inc=1, device_id={"tp": sib}, device_id_type=pl.DeviceIdType.MESH)
+    dg = _dx_rows(x, p0, p1, p2, p3, dres, g, dx)
+    j = _iota((C2, dx.shape[0]), 0)
     last = lax.broadcasted_iota(jnp.int32, (C2, CB), 0) == C2 - 1
-    for c in range(out.shape[1] // CB):
-        s = slice(c * CB, (c + 1) * CB)
-        tot = jnp.dot(ohs[0], dx0[:, s], preferred_element_type=F32)
-        tot = tot + jnp.dot(ohs[1], dx1[:, s], preferred_element_type=F32)
-        out[:, s] = jnp.where(last, dg0[:, s] + dg1[:, s], tot)
-
-
-def _sums(slots, dx0, dx1, dg0, dg1):
-    return pl.pallas_call(
-        _sums_kernel,
-        out_shape=jax.ShapeDtypeStruct((C2, dx0.shape[1]), F32),
-        in_specs=[_vm()] * 5,
-        out_specs=_vm(),
-        compiler_params=_params(6),
-        cost_estimate=_cost(1),
+
+    def sums(i, to):
+        oh = jnp.where(slot_ref[i:i + 1, :] == j, 1.0, 0.0).astype(BF16)
+        for c in range(to.shape[1] // CB):
+            s = slice(c * CB, (c + 1) * CB)
+            to[:, s] = jnp.where(last, dg[:, s], jnp.dot(oh, dx[:, s], preferred_element_type=F32))
+
+    sums(3, out)
+    pl.semaphore_wait(barrier, 1)
+    copy = pltpu.make_async_remote_copy(
+        src_ref=out, dst_ref=got, send_sem=send, recv_sem=recv,
+        device_id={"tp": sib}, device_id_type=pl.DeviceIdType.MESH,
+    )
+    copy.start()
+    sums(2, mine)
+    copy.wait()
+    mine[...] = mine[...] + got[...]
+
+
+def _dx_sums(x, ps, dres, g, slots):
+    m, d = x.shape
+    return pl.pallas_call(
+        _dx_sums_kernel,
+        out_shape=(jax.ShapeDtypeStruct((m, d), BF16), jax.ShapeDtypeStruct((C2, d), F32)),
+        in_specs=[_vm()] * 8,
+        out_specs=(_vm(), _vm()),
+        scratch_shapes=[VMEM((C2, d), F32), VMEM((C2, d), F32), pltpu.SemaphoreType.DMA, pltpu.SemaphoreType.DMA],
+        compiler_params=pltpu.CompilerParams(vmem_limit_bytes=12 << 20, collective_id=0, has_side_effects=True),
+        cost_estimate=_cost(3),
         name="dx_sums",
-    )(slots, dx0, dx1, dg0, dg1)
+    )(x, *ps, dres, g, slots)
 
 
 def _udw_kernel(per, x_ref, g_ref, w_ref, du_ref, de_in, u_ref, dw_ref, de, n, z, sems):
@@ -633,11 +652,10 @@
         pos, _, _, cnts, slots, where, de = _slots(jnp.int32(0), ids, ntp, de)
         x, xl = _expand(pos, tabs, ts)
         u, dW, de = _udw(x, g2, W, du, de)
-        dx, dg = _dx(xl.reshape(m, d), ps, dres.reshape(m, d), g2)
-        dx1, dg1 = swap(dx, 1), swap(dg, 1)
+        dx, mine = _dx_sums(xl.reshape(m, d), ps, dres.reshape(m, d), g2, slots)
+        got = swap(mine, 2)
+        dx1 = swap(dx, 1)
         de = _zeros(de, AT_B, ZB)
-        mine = _sums(slots, dx, dx1, dg, dg1)
-        got = swap(mine, 2)
         other = lax.ppermute(cnts, "dp", [(i, (i + 1) % ndp) for i in range(ndp)])
         de, acc, flags = _acc(cnts, other, slots, dx, dx1, de, AT_R)
         dE, dg = _write(where, acc, mine, got, de)

time: 81.5 us -> 83.1 us (1.020)
  Pallas kernels: 41.8 us -> 43.3 us
    pallas_call x1, Pallas kernels: 16.6 us -> 18.2 us  [_udw(): pl.pallas_call(functools.partial(_udw_kernel, -(-ZW // steps)), out_shape...]
    pallas_call x1, Pallas kernels: 6.73 us -> 5.28 us  [_acc(): pl.pallas_call(functools.partial(_acc_kernel, lo, n), out_shape=(jax.Shap...]
    pallas_call x2 -> x1, Pallas kernels: 1.47 us -> 2.75 us  [_dx_sums(): pl.pallas_call(_dx_sums_kernel, out_shape=(jax.ShapeDtypeStruct((m, d), B...]
    ppermute x9 -> x8, waiting for transfers between devices: 28 us -> 28.6 us  [swap(): return lax.ppermute(a, 'tp', [(i, i ^ bit) for i in range(ntp)])]
    ppermute x9 -> x8, starting transfers between devices: 7.08 us -> 6.66 us  [swap(): return lax.ppermute(a, 'tp', [(i, i ^ bit) for i in range(ntp)])]
  transfers between devices with their start and end apart: 10 -> 9, of which waited for: 3 -> 4; matrix products, arithmetic and copies ran while one was open for 1% -> 1% of each run, Pallas kernels for 43% -> 45%
where the time goes in v10:
time: 83.1 us; the launch traced here: 83 us
  Pallas kernels  43.3 us (52%)
  waiting for transfers between devices  28.6 us (34%)
  starting transfers between devices  8.61 us (10%)
  between operations  1.63 us (2%)
    ppermute x8, waiting for transfers between devices, swap(): return lax.ppermute(a, 'tp', [(i, i ^ bit) for i in range(ntp)])  28.6 us
    pallas_call x1, Pallas kernels, _udw(): pl.pallas_call(functools.partial(_udw_kernel, -(-ZW // steps)), out_shape...  18.2 us
    ppermute x8, starting transfers between devices, swap(): return lax.ppermute(a, 'tp', [(i, i ^ bit) for i in range(ntp)])  6.66 us
    pallas_call x1, Pallas kernels, _acc(): pl.pallas_call(functools.partial(_acc_kernel, lo, n), out_shape=(jax.Shap...  5.28 us
    pallas_call x1, Pallas kernels, _index_call(): pl.pallas_call(functools.partial(_index_kernel, vs, ntp, first), out_shap...  4.12 us
    pallas_call x1, Pallas kernels, _p_terms(): pl.pallas_call(functools.partial(_p_kernel, ts), out_shape=(jax.ShapeDtyp...  3.94 us
    pallas_call x1, Pallas kernels, _slots(): pl.pallas_call(functools.partial(_slots_kernel, vs, ntp), out_shape=(jax....  3.63 us
    pallas_call x1, Pallas kernels, _dx_sums(): pl.pallas_call(_dx_sums_kernel, out_shape=(jax.ShapeDtypeStruct((m, d), B...  2.75 us
  transfers between devices with their start and end apart: 9, of which 4 were waited for; matrix products, arithmetic and copies ran while one was open for 1% of the time, Pallas kernels for 45%

profile of v10, /device:TPU:0, one launch (start us, length us, event | category | flops | bytes accessed | tf_op | source)
XLA Modules:
  0.0 83.0 jit_solution(6205248294736948511)
XLA Ops:
  0.6 0.0 copy-start.1
  0.6 0.0 copy-start.8
  0.7 0.0 copy-start.7
  0.7 4.1 %index_gather.2.refs_1_ = bf16[56,2304]{1,0:T(8,128)(2,1)S(1)} custom-call(s32[2,256]{1,0:T(2,128)} %refs_0_.1, bf16[8192,2304]{1,0:T(8,128)(2,1)} %refs_1_.1), custom_call_target="tpu_custom_call" | custom-call | flops 48000000000 | bytes 1000000 | tf_op jit(solution)/shard_map/index_gather/pallas_call | solution.py:151
  4.8 0.0 copy-start.6
  4.8 3.2 %collective-permute-start.13 = (bf16[56,2304]{1,0:T(8,128)(2,1)S(1)}, bf16[56,2304]{1,0:T(8,128)(2,1)S(1)}, u32[]{:S(2)}, u32[]{:S(2)}) collective-permute-start(bf16[56,2304]{1,0:T(8,128)(2,1)S(1)} %index_gather.2.refs_1_), channel_id=1, source_target_pairs={{0,2},{1,3},{2,0},{3,1},{4,6},{5,7},{6,4},{7,5}} | collective-permute-start | bytes 774152 | tf_op jit(solution)/shard_map/ppermute | solution.py:632
  8.0 0.0 collective-permute-start.12
  8.0 3.9 %p_terms.3 = (bf16[128,2304]{1,0:T(8,128)(2,1)S(1)}, bf16[128,2304]{1,0:T(8,128)(2,1)S(1)}, bf16[128,2304]{1,0:T(8,128)(2,1)S(1)}, bf16[128,2304]{1,0:T(8,128)(2,1)S(1)}, f32[8192,2304]{1,0:T(8,128)}) custom-call(bf16[2,256,1024]{2,1,0:T(8,128)(2,1)S(1)} %copy-done.8, bf16[2304,1024]{1,0:T(8,128)(2,1)S(1)} %copy-done.7), custom_call_target="tpu_custom_call" | custom-call | flops 20000000000 | bytes 1000000 | tf_op jit(solution)/shard_map/p_terms/pallas_call | solution.py:336
  11.9 0.0 copy-start.10
  11.9 2.3 %collective-permute-done.13.refs_3_ = bf16[56,2304]{1,0:T(8,128)(2,1)S(1)} collective-permute-done((bf16[56,2304]{1,0:T(8,128)(2,1)S(1)}, bf16[56,2304]{1,0:T(8,128)(2,1)S(1)}, u32[]{:S(2)}, u32[]{:S(2)}) %collective-permute-start.13) | collective-permute-done | bytes 258080 | tf_op jit(solution)/shard_map/ppermute | solution.py:632
  14.3 0.0 collective-permute-start.14
  14.3 3.6 %slots.4 = (f32[512,1]{1,0:T(8,128)S(1)}, f32[1,512]{1,0:T(1,128)}, s32[1,512]{1,0:T(1,128)}, s32[1,128]{1,0:T(1,128)S(1)}, f32[4,128]{1,0:T(4,128)S(1)}, /*index=5*/s32[1,256]{1,0:T(1,128)S(1)}, f32[8192,2304]{1,0:T(8,128)}) custom-call(s32[1]{0:T(128)} %constant.12.clone.1.c_ref, s32[2,256]{1,0:T(2,128)S(1)} %copy-done.1, ...), custom_call_target="tpu_custom_call", output_to_operand_aliasing={{6}: (2, {})} | custom-call | flops 12000000000 | bytes 1000000 | tf_op jit(solution)/shard_map/slots/pallas_call | solution.py:256
  17.9 2.0 %collective-permute-start.11 = (s32[1,128]{1,0:T(1,128)S(1)}, s32[1,128]{1,0:T(1,128)S(1)}, u32[]{:S(2)}, u32[]{:S(2)}) collective-permute-start(s32[1,128]{1,0:T(1,128)S(1)} %get-tuple-element.157.cnt_ref), channel_id=1, source_target_pairs={{0,4},{4,0},{1,5},{5,1},{2,6},{6,2},{3,7},{7,3}} | collective-permute-start | bytes 1544 | tf_op jit(solution)/shard_map/ppermute | solution.py:659
  19.9 0.2 collective-permute-start.15
  20.1 1.4 %collective-permute-start.16 = (bf16[128,2304]{1,0:T(8,128)(2,1)S(1)}, bf16[128,2304]{1,0:T(8,128)(2,1)S(1)}, u32[]{:S(2)}, u32[]{:S(2)}) collective-permute-start(bf16[128,2304]{1,0:T(8,128)(2,1)S(1)} %get-tuple-element.163), channel_id=1, source_target_pairs={{0,2},{1,3},{2,0},{3,1},{4,6},{5,7},{6,4},{7,5}} | collective-permute-start | bytes 1769480 | tf_op jit(solution)/shard_map/ppermute | solution.py:632
  21.6 0.0 collective-permute-done.12.refs_2_
  21.6 0.2 collective-permute-start.17
  21.8 0.9 %expand.2 = (bf16[512,2304]{1,0:T(8,128)(2,1)S(1)}, bf16[2,64,2304]{2,1,0:T(8,128)(2,1)S(1)}) custom-call(f32[512,1]{1,0:T(8,128)S(1)} %get-tuple-element.159.refs_0_, bf16[56,2304]{1,0:T(8,128)(2,1)S(1)} %index_gather.2.refs_1_, bf16[56,2304]{1,0:T(8,128)(2,1)S(1)} %collective-permute-done.12.refs_2_, bf16[56,2304]{1,0:T(8,128)(2,1)S(1)} %collective-permute-done.13.refs_3_, ...), custom_call_target="tpu_custom_call" | custom-call | flops 12000000000 | bytes 1000000 | tf_op jit(solution)/shard_map/expand/pallas_call | solution.py:299
  22.7 0.0 copy-start.14
  22.7 13.6 %collective-permute-done.16.p2 = bf16[128,2304]{1,0:T(8,128)(2,1)S(1)} collective-permute-done((bf16[128,2304]{1,0:T(8,128)(2,1)S(1)}, bf16[128,2304]{1,0:T(8,128)(2,1)S(1)}, u32[]{:S(2)}, u32[]{:S(2)}) %collective-permute-start.16) | collective-permute-done | bytes 589856 | tf_op jit(solution)/shard_map/ppermute | solution.py:632
  36.3 11.3 %collective-permute-done.17.p3 = bf16[128,2304]{1,0:T(8,128)(2,1)S(1)} collective-permute-done((bf16[128,2304]{1,0:T(8,128)(2,1)S(1)}, bf16[128,2304]{1,0:T(8,128)(2,1)S(1)}, u32[]{:S(2)}, u32[]{:S(2)}) %collective-permute-start.17) | collective-permute-done | bytes 589856 | tf_op jit(solution)/shard_map/ppermute | solution.py:632
  47.6 2.7 %dx_sums.1 = (bf16[128,2304]{1,0:T(8,128)(2,1)S(1)}, f32[32,2304]{1,0:T(8,128)S(1)}) custom-call(bf16[128,2304]{1,0:T(8,128)(2,1)S(1)} %bitcast.16, bf16[128,2304]{1,0:T(8,128)(2,1)S(1)} %get-tuple-element.161.p0, bf16[128,2304]{1,0:T(8,128)(2,1)S(1)} %collective-permute-done.15.p1, bf16[128,2304]{1,0:T(8,128)(2,1)S(1)} %collective-permute-done.16.p2, ...), custom_call_target="tpu_custom_call" | custom-call | flops 12000000000 | bytes 1000000 | tf_op jit(solution)/shard_map/dx_sums/pallas_call | solution.py:435
  50.4 0.2 collective-permute-start.18
  50.5 18.2 %u_dw.3 = (bf16[2,256,1024]{2,1,0:T(8,128)(2,1)}, f32[2304,1024]{1,0:T(8,128)}, f32[8192,2304]{1,0:T(8,128)}) custom-call(bf16[512,2304]{1,0:T(8,128)(2,1)S(1)} %get-tuple-element.166.x_ref, bf16[1,2304]{1,0:T(2,128)(2,1)S(1)} %reshape.36.g.g_ref, bf16[2304,1024]{1,0:T(8,128)(2,1)S(1)} %copy-done.7, ...), custom_call_target="tpu_custom_call", output_to_operand_aliasing={{2}: (4, {})} | custom-call | flops 80000000000 | bytes 1000000 | tf_op jit(solution)/shard_map/u_dw/pallas_call | solution.py:484
  68.7 2.3 %shard_map.101.de_in = f32[8192,2304]{1,0:T(8,128)} custom-call(f32[8192,2304]{1,0:T(8,128)} %get-tuple-element.168.de_in), custom_call_target="tpu_custom_call", output_to_operand_aliasing={{}: (0, {})} | custom-call | flops 6000000000 | bytes 1000000 | tf_op jit(solution)/shard_map/pallas_call | solution.py:358
  71.0 0.0 copy-start.2
  71.0 1.4 %collective-permute-start.19 = (f32[32,2304]{1,0:T(8,128)S(1)}, f32[32,2304]{1,0:T(8,128)S(1)}, u32[]{:S(2)}, u32[]{:S(2)}) collective-permute-start(f32[32,2304]{1,0:T(8,128)S(1)} %get-tuple-element.173.mine_ref), channel_id=1, source_target_pairs={{0,2},{1,3},{2,0},{3,1},{4,6},{5,7},{6,4},{7,5}} | collective-permute-start | bytes 884744 | tf_op jit(solution)/shard_map/ppermute | solution.py:632
  72.5 5.3 %fill_acc.1 = (f32[8192,2304]{1,0:T(8,128)}, f32[56,2304]{1,0:T(8,128)S(1)}, s32[1,4]{1,0:T(1,128)S(1)}) custom-call(s32[1,128]{1,0:T(1,128)S(1)} %get-tuple-element.157.cnt_ref, s32[1,128]{1,0:T(1,128)S(1)} %collective-permute-done.11.oth_ref, f32[4,128]{1,0:T(4,128)S(1)} %get-tuple-element.158.slot_ref, ...), custom_call_target="tpu_custom_call", output_to_operand_aliasing={{0}: (5, {})} | custom-call | flops 13500000256 | bytes 1000000 | tf_op jit(solution)/shard_map/fill_acc/pallas_call | solution.py:570
  77.8 0.6 slice.6
  79.0 1.3 %collective-permute-done.19.got_ref = f32[32,2304]{1,0:T(8,128)S(1)} collective-permute-done((f32[32,2304]{1,0:T(8,128)S(1)}, f32[32,2304]{1,0:T(8,128)S(1)}, u32[]{:S(2)}, u32[]{:S(2)}) %collective-permute-start.19) | collective-permute-done | bytes 294944 | tf_op jit(solution)/shard_map/ppermute | solution.py:632
  80.3 2.2 %write_rows.1 = (f32[8192,2304]{1,0:T(8,128)}, f32[2304]{0:T(1024)}) custom-call(s32[1,256]{1,0:T(1,128)S(1)} %get-tuple-element.171.map_ref, f32[56,2304]{1,0:T(8,128)S(1)} %get-tuple-element.172.acc_in, f32[32,2304]{1,0:T(8,128)S(1)} %get-tuple-element.173.mine_ref, ...), custom_call_target="tpu_custom_call", output_to_operand_aliasing={{0}: (4, {})} | custom-call | flops 12000000000 | bytes 1000000 | tf_op jit(solution)/shard_map/write_rows/pallas_call | solution.py:614
  82.6 0.2 while.30
  (14 shorter events, 0.0 us)
Async XLA Ops:
  0.6 13.6 %copy-start.1 = (s32[2,256]{1,0:T(2,128)S(1)}, s32[2,256]{1,0:T(2,128)}, u32[]{:S(2)}) copy-start(s32[2,256]{1,0:T(2,128)} %refs_0_.1) | copy-start | bytes 6148
  0.6 7.3 %copy-start.8 = (bf16[2,256,1024]{2,1,0:T(8,128)(2,1)S(1)}, bf16[2,256,1024]{2,1,0:T(8,128)(2,1)}, u32[]{:S(2)}) copy-start(bf16[2,256,1024]{2,1,0:T(8,128)(2,1)} %du_ref.3) | copy-start | bytes 3145732
  0.7 7.3 %copy-start.7 = (bf16[2304,1024]{1,0:T(8,128)(2,1)S(1)}, bf16[2304,1024]{1,0:T(8,128)(2,1)}, u32[]{:S(2)}) copy-start(bf16[2304,1024]{1,0:T(8,128)(2,1)} %w_ref.3) | copy-start | bytes 14155780
  4.8 15.3 %copy-start.6 = (bf16[2304]{0:T(1024)(128)(2,1)S(1)}, bf16[2304]{0:T(1024)(128)(2,1)}, u32[]{:S(2)}) copy-start(bf16[2304]{0:T(1024)(128)(2,1)} %param.12) | copy-start | bytes 13828
  4.8 9.5 %collective-permute-start.13 = (bf16[56,2304]{1,0:T(8,128)(2,1)S(1)}, bf16[56,2304]{1,0:T(8,128)(2,1)S(1)}, u32[]{:S(2)}, u32[]{:S(2)}) collective-permute-start(bf16[56,2304]{1,0:T(8,128)(2,1)S(1)} %index_gather.2.refs_1_), channel_id=1, source_target_pairs={{0,2},{1,3},{2,0},{3,1},{4,6},{5,7},{6,4},{7,5}} | collective-permute-start | bytes 774152 | tf_op jit(solution)/shard_map/ppermute | solution.py:632
  8.0 13.6 %collective-permute-start.12 = (bf16[56,2304]{1,0:T(8,128)(2,1)S(1)}, bf16[56,2304]{1,0:T(8,128)(2,1)S(1)}, u32[]{:S(2)}, u32[]{:S(2)}) collective-permute-start(bf16[56,2304]{1,0:T(8,128)(2,1)S(1)} %index_gather.2.refs_1_), channel_id=1, source_target_pairs={{0,1},{1,0},{2,3},{3,2},{4,5},{5,4},{6,7},{7,6}} | collective-permute-start | bytes 774152 | tf_op jit(solution)/shard_map/ppermute | solution.py:632
  11.9 35.7 %copy-start.10 = (bf16[2,64,2304]{2,1,0:T(8,128)(2,1)S(1)}, bf16[2,64,2304]{2,1,0:T(8,128)(2,1)}, u32[]{:S(2)}) copy-start(bf16[2,64,2304]{2,1,0:T(8,128)(2,1)} %param.15) | copy-start | bytes 1769476
  14.3 7.5 %collective-permute-start.14 = (bf16[56,2304]{1,0:T(8,128)(2,1)S(1)}, bf16[56,2304]{1,0:T(8,128)(2,1)S(1)}, u32[]{:S(2)}, u32[]{:S(2)}) collective-permute-start(bf16[56,2304]{1,0:T(8,128)(2,1)S(1)} %collective-permute-done.13.refs_3_), channel_id=1, source_target_pairs={{0,1},{1,0},{2,3},{3,2},{4,5},{5,4},{6,7},{7,6}} | collective-permute-start | bytes 774152 | tf_op jit(solution)/shard_map/ppermute | solution.py:632
  17.9 54.6 %collective-permute-start.11 = (s32[1,128]{1,0:T(1,128)S(1)}, s32[1,128]{1,0:T(1,128)S(1)}, u32[]{:S(2)}, u32[]{:S(2)}) collective-permute-start(s32[1,128]{1,0:T(1,128)S(1)} %get-tuple-element.157.cnt_ref), channel_id=1, source_target_pairs={{0,4},{4,0},{1,5},{5,1},{2,6},{6,2},{3,7},{7,3}} | collective-permute-start | bytes 1544 | tf_op jit(solution)/shard_map/ppermute | solution.py:659
  19.9 2.8 %collective-permute-start.15 = (bf16[128,2304]{1,0:T(8,128)(2,1)S(1)}, bf16[128,2304]{1,0:T(8,128)(2,1)S(1)}, u32[]{:S(2)}, u32[]{:S(2)}) collective-permute-start(bf16[128,2304]{1,0:T(8,128)(2,1)S(1)} %get-tuple-element.162), channel_id=1, source_target_pairs={{0,1},{1,0},{2,3},{3,2},{4,5},{5,4},{6,7},{7,6}} | collective-permute-start | bytes 1769480 | tf_op jit(solution)/shard_map/ppermute | solution.py:632
  20.1 48.6 %copy-start.4 = (bf16[1,2304]{1,0:T(2,128)(2,1)}, bf16[1,2304]{1,0:T(2,128)(2,1)S(1)}, u32[]{:S(2)}) copy-start(bf16[1,2304]{1,0:T(2,128)(2,1)S(1)} %reshape.36.g.g_ref) | copy-start | bytes 13828
  20.1 16.2 %collective-permute-start.16 = (bf16[128,2304]{1,0:T(8,128)(2,1)S(1)}, bf16[128,2304]{1,0:T(8,128)(2,1)S(1)}, u32[]{:S(2)}, u32[]{:S(2)}) collective-permute-start(bf16[128,2304]{1,0:T(8,128)(2,1)S(1)} %get-tuple-element.163), channel_id=1, source_target_pairs={{0,2},{1,3},{2,0},{3,1},{4,6},{5,7},{6,4},{7,5}} | collective-permute-start | bytes 1769480 | tf_op jit(solution)/shard_map/ppermute | solution.py:632
  21.6 26.0 %collective-permute-start.17 = (bf16[128,2304]{1,0:T(8,128)(2,1)S(1)}, bf16[128,2304]{1,0:T(8,128)(2,1)S(1)}, u32[]{:S(2)}, u32[]{:S(2)}) collective-permute-start(bf16[128,2304]{1,0:T(8,128)(2,1)S(1)} %get-tuple-element.164), channel_id=1, source_target_pairs={{0,3},{1,2},{2,1},{3,0},{4,7},{5,6},{6,5},{7,4}} | collective-permute-start | bytes 1769480 | tf_op jit(solution)/shard_map/ppermute | solution.py:632
  22.7 27.7 %copy-start.14 = (bf16[2,64,2304]{2,1,0:T(8,128)(2,1)}, bf16[2,64,2304]{2,1,0:T(8,128)(2,1)S(1)}, u32[]{:S(2)}) copy-start(bf16[2,64,2304]{2,1,0:T(8,128)(2,1)S(1)} %get-tuple-element.312) | copy-start | bytes 1769476
  50.4 22.1 %collective-permute-start.18 = (bf16[128,2304]{1,0:T(8,128)(2,1)S(1)}, bf16[128,2304]{1,0:T(8,128)(2,1)S(1)}, u32[]{:S(2)}, u32[]{:S(2)}) collective-permute-start(bf16[128,2304]{1,0:T(8,128)(2,1)S(1)} %get-tuple-element.165.dx0), channel_id=1, source_target_pairs={{0,1},{1,0},{2,3},{3,2},{4,5},{5,4},{6,7},{7,6}} | collective-permute-start | bytes 1769480 | tf_op jit(solution)/shard_map/ppermute | solution.py:632
  71.0 11.6 %copy-start.2 = (s32[2,256]{1,0:T(2,128)S(1)}, s32[2,256]{1,0:T(2,128)}, u32[]{:S(2)}) copy-start(s32[2,256]{1,0:T(2,128)} %refs_0_.1) | copy-start | bytes 6148
  71.0 9.3 %collective-permute-start.19 = (f32[32,2304]{1,0:T(8,128)S(1)}, f32[32,2304]{1,0:T(8,128)S(1)}, u32[]{:S(2)}, u32[]{:S(2)}) collective-permute-start(f32[32,2304]{1,0:T(8,128)S(1)} %get-tuple-element.173.mine_ref), channel_id=1, source_target_pairs={{0,2},{1,3},{2,0},{3,1},{4,6},{5,7},{6,4},{7,5}} | collective-permute-start | bytes 884744 | tf_op jit(solution)/shard_map/ppermute | solution.py:632

commit v11 on v10

--- a/solution.py
+++ b/solution.py
@@ -14,7 +14,7 @@
 C2 = 32
 CB = 256
 ZR = 128
-ZP, ZA, ZU, ZW, ZB = 8, 6, 15, 22, 4
+ZP, ZA, ZU, ZW, ZB = 8, 4, 22, 20, 4
 AT_A, AT_U, AT_B, AT_R = ZP, ZP + ZA, ZP + ZA + ZU + ZW, ZP + ZA + ZU + ZW + ZB
 TB = 64
 
@@ -166,10 +166,37 @@
     )(*([] if first else [chunk.reshape(1)]), ids, E)
 
 
-def _slots_kernel(vs, ntp, c_ref, ids_ref, de_in, pos_ref, srow_ref, list_ref, cnt_ref, slot_ref, map_ref, de, z, sems):
+def _pos_kernel(vs, ntp, c_ref, ids_ref, de_in, pos_ref, de, z, sems):
     z[...] = jnp.zeros_like(z)
     _fill(z, de, sems, AT_A, 0, ZA, False)
     base = (c_ref[0] * C).astype(F32)
+    idr = _ids_row(ids_ref)
+    nb = idr.shape[1] // TB
+    own_r, slot_r, _ = _table_slots(idr, [_column(idr, b) for b in range(nb)], vs, ntp)
+    rel = (own_r.astype(jnp.int32) ^ _me()).astype(F32)
+    pos = jnp.where((slot_r >= base) & (slot_r < base + C), rel * C + slot_r - base, -1.0)
+    for b in range(nb):
+        pos_ref[b * TB:(b + 1) * TB, :] = _column(pos, b)
+    _fill(z, de, sems, AT_A, 0, ZA, True)
+
+
+def _pos(chunk, ids, ntp, de):
+    vs, d = de.shape
+    ntok = ids.shape[0] * ids.shape[1]
+    return pl.pallas_call(
+        functools.partial(_pos_kernel, vs, ntp),
+        out_shape=(jax.ShapeDtypeStruct((ntok, 1), F32), jax.ShapeDtypeStruct(de.shape, F32)),
+        in_specs=[_sm(), _vm(), _any()],
+        out_specs=(_vm(), _any()),
+        scratch_shapes=_zscratch(d, ZA),
+        input_output_aliases={2: 1},
+        compiler_params=_params(6),
+        cost_estimate=_cost(3),
+        name="positions",
+    )(chunk.reshape(1), ids, de)
+
+
+def _slots(vs, ntp, ids_ref, srow_ref, list_ref, cnt_ref, slot_ref, map_ref):
     mei = _me()
     me = mei.astype(F32)
     lo = me * vs
@@ -188,10 +215,6 @@
         cnt = jnp.where(me == float(d), nd, cnt)
         mx = jnp.maximum(mx, nd)
     srow_ref[...] = my_r
-    rel = (own_r.astype(jnp.int32) ^ mei).astype(F32)
-    pos = jnp.where((slot_r >= base) & (slot_r < base + C), rel * C + slot_r - base, -1.0)
-    for b in range(nb):
-        pos_ref[b * TB:(b + 1) * TB, :] = _column(pos, b)
 
     part = lax.broadcasted_iota(jnp.int32, (1, ntok), 1) // ts % ntp
     chips = [
@@ -247,31 +270,6 @@
     many = jnp.where(lane1 == 127, cnt2, slots)
     mine = jnp.where(lane1 == 127, cnt, full[:, :128])
     map_ref[...] = jnp.concatenate([many, mine], axis=1).astype(jnp.int32)
-    _fill(z, de, sems, AT_A, 0, ZA, True)
-
-
-def _slots(chunk, ids, ntp, de):
-    vs, d = de.shape
-    ntok = ids.shape[0] * ids.shape[1]
-    return pl.pallas_call(
-        functools.partial(_slots_kernel, vs, ntp),
-        out_shape=(
-            jax.ShapeDtypeStruct((ntok, 1), F32),
-            jax.ShapeDtypeStruct((1, ntok), F32),
-            jax.ShapeDtypeStruct((1, ntok), jnp.int32),
-            jax.ShapeDtypeStruct((1, 128), jnp.int32),
-            jax.ShapeDtypeStruct((4, ntok // ntp), F32),
-            jax.ShapeDtypeStruct((1, 256), jnp.int32),
-            jax.ShapeDtypeStruct(de.shape, F32),
-        ),
-        in_specs=[_sm(), _vm(), _any()],
-        out_specs=(_vm(),) * 6 + (_any(),),
-        scratch_shapes=_zscratch(d, ZA),
-        input_output_aliases={2: 6},
-        compiler_params=_params(6),
-        cost_estimate=_cost(3),
-        name="slots",
-    )(chunk.reshape(1), ids, de)
 
 
 def _expand_kernel(ts, acc, *refs):
@@ -444,7 +442,8 @@
     )(x, *ps, dres, g, slots)
 
 
-def _udw_kernel(per, x_ref, g_ref, w_ref, du_ref, de_in, u_ref, dw_ref, de, n, z, sems):
+def _udw_kernel(per, vs, ntp, x_ref, g_ref, w_ref, du_ref, ids_ref, de_in, *refs):
+    u_ref, dw_ref, *slot_refs, de, n, z, sems = refs
     i = pl.program_id(0)
     nk, t, f = du_ref.shape
     cb = dw_ref.shape[0]
@@ -453,6 +452,7 @@
     def _():
         z[...] = jnp.zeros_like(z)
         _fill(z, de, sems, AT_U, 0, ZU, False)
+        _slots(vs, ntp, ids_ref, *slot_refs)
         rows = 64
         for b in range(n.shape[0] // rows):
             s = slice(b * rows, (b + 1) * rows)
@@ -476,27 +476,35 @@
         _fill(z, de, sems, AT_U, 0, ZU + ZW, True)
 
 
-def _udw(x, g, W, du, de):
+def _udw(x, g, W, du, ids, ntp, de):
     nk, t, f = du.shape
     ntok, d = x.shape
     cb = d // 6
     steps = d // cb
     return pl.pallas_call(
-        functools.partial(_udw_kernel, -(-ZW // steps)),
+        functools.partial(_udw_kernel, -(-ZW // steps), de.shape[0], ntp),
         out_shape=(
             jax.ShapeDtypeStruct((nk, t, f), BF16),
             jax.ShapeDtypeStruct((d, f), F32),
+            jax.ShapeDtypeStruct((1, ntok), F32),
+            jax.ShapeDtypeStruct((1, ntok), jnp.int32),
+            jax.ShapeDtypeStruct((1, 128), jnp.int32),
+            jax.ShapeDtypeStruct((4, ntok // ntp), F32),
+            jax.ShapeDtypeStruct((1, 256), jnp.int32),
             jax.ShapeDtypeStruct(de.shape, F32),
         ),
         grid=(steps,),
-        in_specs=[_vm(), _vm(), _vm(), _vm(), _any()],
-        out_specs=(pl.BlockSpec((nk, t, f), lambda i: (0, 0, 0)), pl.BlockSpec((cb, f), lambda i: (i, 0)), _any()),
+        in_specs=[_vm()] * 5 + [_any()],
+        out_specs=(
+            pl.BlockSpec((nk, t, f), lambda i: (0, 0, 0)), pl.BlockSpec((cb, f), lambda i: (i, 0)),
+            *[_vm()] * 5, _any(),
+        ),
         scratch_shapes=[VMEM((ntok, d), BF16)] + _zscratch(d, ZU + ZW),
-        input_output_aliases={4: 2},
+        input_output_aliases={5: 7},
         compiler_params=_params(20),
         cost_estimate=_cost(20),
         name="u_dw",
-    )(x, g, W, du, de)
+    )(x, g, W, du, ids, de)
 
 
 def _scatter_kernel(ts, nk, cnt_ref, list_ref, srow_ref, *refs):
@@ -649,9 +657,9 @@
 
         tabs = share(_index_call(None, ids, E, ntp))
         de, ps = p_terms(du, W, ts, vs)
-        pos, _, _, cnts, slots, where, de = _slots(jnp.int32(0), ids, ntp, de)
+        pos, de = _pos(jnp.int32(0), ids, ntp, de)
         x, xl = _expand(pos, tabs, ts)
-        u, dW, de = _udw(x, g2, W, du, de)
+        u, dW, _, _, cnts, slots, where, de = _udw(x, g2, W, du, ids, ntp, de)
         dx, mine = _dx_sums(xl.reshape(m, d), ps, dres.reshape(m, d), g2, slots)
         got = swap(mine, 2)
         dx1 = swap(dx, 1)
@@ -670,14 +678,13 @@
 
             def more(q):
                 i, x, _, de = q
-                pos, *_, de = _slots(i, ids, ntp, de)
+                pos, de = _pos(i, ids, ntp, de)
                 return i + 1, *_expand(pos, share(_index_call(i, ids, E, ntp)), ts, x), de
 
             zeros = jnp.zeros((nk * t, d), BF16), jnp.zeros((nk, ts, d), BF16)
             de, ps = p_terms(du, W, ts, vs)
             _, x, xl, de = lax.while_loop(lambda q: q[0] < rounds, more, (i0, *zeros, de))
-            _, srow, rows, cs, _, _, de = _slots(i0, ids, ntp, de)
-            u, dW, de = _udw(x, g2, W, du, de)
+            u, dW, srow, rows, cs, _, _, de = _udw(x, g2, W, du, ids, ntp, de)
             dx, dg = _dx(xl.reshape(m, d), ps, dres.reshape(m, d), g2)
             dg2 = dg + swap(dg, 1)
             dg = (dg2 + swap(dg2, 2)).reshape(d)

time: 83.1 us -> 58.3 us (0.70)
  waiting for transfers between devices: 28.6 us -> 4.4 us
  Pallas kernels: 43.3 us -> 42.2 us
    ppermute x8, waiting for transfers between devices: 28.6 us -> 4.4 us  [swap(): return lax.ppermute(a, 'tp', [(i, i ^ bit) for i in range(ntp)])]
    pallas_call x1, Pallas kernels: 5.28 us -> 4.19 us  [_acc(): pl.pallas_call(functools.partial(_acc_kernel, lo, n), out_shape=(jax.Shap...]
  transfers between devices with their start and end apart: 9 -> 9, of which waited for: 4 -> 2; matrix products, arithmetic and copies ran while one was open for 1% -> 1% of each run, Pallas kernels for 45% -> 57%
where the time goes in v11:
time: 58.3 us; the launch traced here: 58.1 us
  Pallas kernels  42.2 us (72%)
  starting transfers between devices  9 us (15%)
  waiting for transfers between devices  4.4 us (8%)
  between operations  1.66 us (3%)
  local copies, waits for them, and re-layouts  0.64 us (1%)
    pallas_call x1, Pallas kernels, _udw(): pl.pallas_call(functools.partial(_udw_kernel, -(-ZW // steps), de.shape[0...  19.6 us
    ppermute x8, starting transfers between devices, swap(): return lax.ppermute(a, 'tp', [(i, i ^ bit) for i in range(ntp)])  7.42 us
    ppermute x8, waiting for transfers between devices, swap(): return lax.ppermute(a, 'tp', [(i, i ^ bit) for i in range(ntp)])  4.4 us
    pallas_call x1, Pallas kernels, _acc(): pl.pallas_call(functools.partial(_acc_kernel, lo, n), out_shape=(jax.Shap...  4.19 us
    pallas_call x1, Pallas kernels, _index_call(): pl.pallas_call(functools.partial(_index_kernel, vs, ntp, first), out_shap...  4.12 us
    pallas_call x1, Pallas kernels, _p_terms(): pl.pallas_call(functools.partial(_p_kernel, ts), out_shape=(jax.ShapeDtyp...  3.94 us
    pallas_call x1, Pallas kernels, _dx_sums(): pl.pallas_call(_dx_sums_kernel, out_shape=(jax.ShapeDtypeStruct((m, d), B...  2.67 us
    pallas_call x1, Pallas kernels, _pos(): pl.pallas_call(functools.partial(_pos_kernel, vs, ntp), out_shape=(jax.Sh...  2.29 us
  transfers between devices with their start and end apart: 9, of which 2 were waited for; matrix products, arithmetic and copies ran while one was open for 1% of the time, Pallas kernels for 57%

profile of v11, /device:TPU:0, one launch (start us, length us, event | category | flops | bytes accessed | tf_op | source)
XLA Modules:
  0.0 58.1 jit_solution(12960273683971866917)
XLA Ops:
  0.6 0.0 copy-start
  0.6 0.0 copy-start.6
  0.7 0.0 copy-start.5
  0.7 4.1 %index_gather.2.refs_1_ = bf16[56,2304]{1,0:T(8,128)(2,1)S(1)} custom-call(s32[2,256]{1,0:T(2,128)} %ids_ref.3, bf16[8192,2304]{1,0:T(8,128)(2,1)} %refs_1_.1), custom_call_target="tpu_custom_call" | custom-call | flops 48000000000 | bytes 1000000 | tf_op jit(solution)/shard_map/index_gather/pallas_call | solution.py:151
  4.8 0.0 copy-start.4
  4.8 3.2 %collective-permute-start.12 = (bf16[56,2304]{1,0:T(8,128)(2,1)S(1)}, bf16[56,2304]{1,0:T(8,128)(2,1)S(1)}, u32[]{:S(2)}, u32[]{:S(2)}) collective-permute-start(bf16[56,2304]{1,0:T(8,128)(2,1)S(1)} %index_gather.2.refs_1_), channel_id=1, source_target_pairs={{0,2},{1,3},{2,0},{3,1},{4,6},{5,7},{6,4},{7,5}} | collective-permute-start | bytes 774152 | tf_op jit(solution)/shard_map/ppermute | solution.py:640
  8.0 0.0 collective-permute-start.11
  8.0 3.9 %p_terms.3 = (bf16[128,2304]{1,0:T(8,128)(2,1)S(1)}, bf16[128,2304]{1,0:T(8,128)(2,1)S(1)}, bf16[128,2304]{1,0:T(8,128)(2,1)S(1)}, bf16[128,2304]{1,0:T(8,128)(2,1)S(1)}, f32[8192,2304]{1,0:T(8,128)}) custom-call(bf16[2,256,1024]{2,1,0:T(8,128)(2,1)S(1)} %copy-done.6, bf16[2304,1024]{1,0:T(8,128)(2,1)S(1)} %copy-done.5), custom_call_target="tpu_custom_call" | custom-call | flops 20000000000 | bytes 1000000 | tf_op jit(solution)/shard_map/p_terms/pallas_call | solution.py:334
  11.9 0.5 collective-permute-start.15
  12.4 0.0 collective-permute-start.16
  12.5 1.8 %collective-permute-done.12.refs_3_ = bf16[56,2304]{1,0:T(8,128)(2,1)S(1)} collective-permute-done((bf16[56,2304]{1,0:T(8,128)(2,1)S(1)}, bf16[56,2304]{1,0:T(8,128)(2,1)S(1)}, u32[]{:S(2)}, u32[]{:S(2)}) %collective-permute-start.12) | collective-permute-done | bytes 258080 | tf_op jit(solution)/shard_map/ppermute | solution.py:640
  14.3 0.0 collective-permute-start.13
  14.3 2.3 %positions.2 = (f32[512,1]{1,0:T(8,128)S(1)}, f32[8192,2304]{1,0:T(8,128)}) custom-call(s32[1]{0:T(128)} %constant.10.clone.1.c_ref, s32[2,256]{1,0:T(2,128)S(1)} %copy-done, f32[8192,2304]{1,0:T(8,128)} %get-tuple-element.155.de_in), custom_call_target="tpu_custom_call", output_to_operand_aliasing={{1}: (2, {})} | custom-call | flops 12000000000 | bytes 1000000 | tf_op jit(solution)/shard_map/positions/pallas_call | solution.py:186
  16.6 2.5 %collective-permute-start.17 = (bf16[128,2304]{1,0:T(8,128)(2,1)S(1)}, bf16[128,2304]{1,0:T(8,128)(2,1)S(1)}, u32[]{:S(2)}, u32[]{:S(2)}) collective-permute-start(bf16[128,2304]{1,0:T(8,128)(2,1)S(1)} %get-tuple-element.165), channel_id=1, source_target_pairs={{0,3},{1,2},{2,1},{3,0},{4,7},{5,6},{6,5},{7,4}} | collective-permute-start | bytes 1769480 | tf_op jit(solution)/shard_map/ppermute | solution.py:640
  19.2 0.0 collective-permute-done.11.refs_2_
  19.2 0.0 collective-permute-done.13.refs_4_
  19.2 0.9 %expand.2 = (bf16[512,2304]{1,0:T(8,128)(2,1)S(1)}, bf16[2,64,2304]{2,1,0:T(8,128)(2,1)S(1)}) custom-call(f32[512,1]{1,0:T(8,128)S(1)} %get-tuple-element.156.refs_0_, bf16[56,2304]{1,0:T(8,128)(2,1)S(1)} %index_gather.2.refs_1_, bf16[56,2304]{1,0:T(8,128)(2,1)S(1)} %collective-permute-done.11.refs_2_, bf16[56,2304]{1,0:T(8,128)(2,1)S(1)} %collective-permute-done.12.refs_3_, ...), custom_call_target="tpu_custom_call" | custom-call | flops 12000000000 | bytes 1000000 | tf_op jit(solution)/shard_map/expand/pallas_call | solution.py:297
  20.1 0.0 copy-start.12
  20.1 0.0 copy-start.8
  20.1 19.6 %u_dw.3 = (bf16[2,256,1024]{2,1,0:T(8,128)(2,1)}, f32[2304,1024]{1,0:T(8,128)}, f32[1,512]{1,0:T(1,128)}, s32[1,512]{1,0:T(1,128)}, s32[1,128]{1,0:T(1,128)S(1)}...) custom-call(bf16[512,2304]{1,0:T(8,128)(2,1)S(1)} %get-tuple-element.15, ...), custom_call_target="tpu_custom_call", output_to_operand_aliasing={{7}: (5, {})} | custom-call | flops 80000000000 | bytes 1000000 | tf_op jit(solution)/shard_map/u_dw/pallas_call | solution.py:484
  39.7 0.0 collective-permute-done.15.p1
  39.8 2.7 %dx_sums.1 = (bf16[128,2304]{1,0:T(8,128)(2,1)S(1)}, f32[32,2304]{1,0:T(8,128)S(1)}) custom-call(bf16[128,2304]{1,0:T(8,128)(2,1)S(1)} %bitcast.14, bf16[128,2304]{1,0:T(8,128)(2,1)S(1)} %get-tuple-element.162.p0, bf16[128,2304]{1,0:T(8,128)(2,1)S(1)} %collective-permute-done.15.p1, bf16[128,2304]{1,0:T(8,128)(2,1)S(1)} %collective-permute-done.16.p2, ...), custom_call_target="tpu_custom_call" | custom-call | flops 12000000000 | bytes 1000000 | tf_op jit(solution)/shard_map/dx_sums/pallas_call | solution.py:433
  42.4 0.2 collective-permute-start.18
  42.6 1.6 %collective-permute-start.14 = (s32[1,128]{1,0:T(1,128)S(1)}, s32[1,128]{1,0:T(1,128)S(1)}, u32[]{:S(2)}, u32[]{:S(2)}) collective-permute-start(s32[1,128]{1,0:T(1,128)S(1)} %get-tuple-element.159.cnt_ref), channel_id=1, source_target_pairs={{0,4},{4,0},{1,5},{5,1},{2,6},{6,2},{3,7},{7,3}} | collective-permute-start | bytes 1544 | tf_op jit(solution)/shard_map/ppermute | solution.py:667
  44.2 2.3 %shard_map.101.de_in = f32[8192,2304]{1,0:T(8,128)} custom-call(f32[8192,2304]{1,0:T(8,128)} %get-tuple-element.167.de_in), custom_call_target="tpu_custom_call", output_to_operand_aliasing={{}: (0, {})} | custom-call | flops 6000000000 | bytes 1000000 | tf_op jit(solution)/shard_map/pallas_call | solution.py:356
  46.5 0.0 copy-start.1
  46.5 1.0 %collective-permute-start.19 = (f32[32,2304]{1,0:T(8,128)S(1)}, f32[32,2304]{1,0:T(8,128)S(1)}, u32[]{:S(2)}, u32[]{:S(2)}) collective-permute-start(f32[32,2304]{1,0:T(8,128)S(1)} %get-tuple-element.172.mine_ref), channel_id=1, source_target_pairs={{0,2},{1,3},{2,0},{3,1},{4,6},{5,7},{6,4},{7,5}} | collective-permute-start | bytes 884744 | tf_op jit(solution)/shard_map/ppermute | solution.py:640
  47.5 4.2 %fill_acc.1 = (f32[8192,2304]{1,0:T(8,128)}, f32[56,2304]{1,0:T(8,128)S(1)}, s32[1,4]{1,0:T(1,128)S(1)}) custom-call(s32[1,128]{1,0:T(1,128)S(1)} %get-tuple-element.159.cnt_ref, s32[1,128]{1,0:T(1,128)S(1)} %collective-permute-done.14.oth_ref, f32[4,128]{1,0:T(4,128)S(1)} %get-tuple-element.160.slot_ref, ...), custom_call_target="tpu_custom_call", output_to_operand_aliasing={{0}: (5, {})} | custom-call | flops 8999999488 | bytes 1000000 | tf_op jit(solution)/shard_map/fill_acc/pallas_call | solution.py:578
  51.7 0.6 %slice.6 = s32[1,1]{1,0:T(1,128)} slice(s32[1,4]{1,0:T(1,128)S(1)} %get-tuple-element.321), slice={[0:1], [2:3]} | slice | bytes 8 | tf_op jit(solution)/shard_map/slice | solution.py:694
  52.9 2.6 %collective-permute-done.19.got_ref = f32[32,2304]{1,0:T(8,128)S(1)} collective-permute-done((f32[32,2304]{1,0:T(8,128)S(1)}, f32[32,2304]{1,0:T(8,128)S(1)}, u32[]{:S(2)}, u32[]{:S(2)}) %collective-permute-start.19) | collective-permute-done | bytes 294944 | tf_op jit(solution)/shard_map/ppermute | solution.py:640
  55.5 2.2 %write_rows.1 = (f32[8192,2304]{1,0:T(8,128)}, f32[2304]{0:T(1024)}) custom-call(s32[1,256]{1,0:T(1,128)S(1)} %get-tuple-element.170.map_ref, f32[56,2304]{1,0:T(8,128)S(1)} %get-tuple-element.171.acc_in, f32[32,2304]{1,0:T(8,128)S(1)} %get-tuple-element.172.mine_ref, ...), custom_call_target="tpu_custom_call", output_to_operand_aliasing={{0}: (4, {})} | custom-call | flops 12000000000 | bytes 1000000 | tf_op jit(solution)/shard_map/write_rows/pallas_call | solution.py:622
  57.8 0.2 while.30
  (14 shorter events, 0.0 us)
Async XLA Ops:
  0.6 13.6 %copy-start = (s32[2,256]{1,0:T(2,128)S(1)}, s32[2,256]{1,0:T(2,128)}, u32[]{:S(2)}) copy-start(s32[2,256]{1,0:T(2,128)} %ids_ref.3) | copy-start | bytes 6148
  0.6 7.3 %copy-start.6 = (bf16[2,256,1024]{2,1,0:T(8,128)(2,1)S(1)}, bf16[2,256,1024]{2,1,0:T(8,128)(2,1)}, u32[]{:S(2)}) copy-start(bf16[2,256,1024]{2,1,0:T(8,128)(2,1)} %du_ref.3) | copy-start | bytes 3145732
  0.7 7.3 %copy-start.5 = (bf16[2304,1024]{1,0:T(8,128)(2,1)S(1)}, bf16[2304,1024]{1,0:T(8,128)(2,1)}, u32[]{:S(2)}) copy-start(bf16[2304,1024]{1,0:T(8,128)(2,1)} %w_ref.3) | copy-start | bytes 14155780
  4.8 11.8 %copy-start.4 = (bf16[2304]{0:T(1024)(128)(2,1)S(1)}, bf16[2304]{0:T(1024)(128)(2,1)}, u32[]{:S(2)}) copy-start(bf16[2304]{0:T(1024)(128)(2,1)} %param.12) | copy-start | bytes 13828
  4.8 9.5 %collective-permute-start.12 = (bf16[56,2304]{1,0:T(8,128)(2,1)S(1)}, bf16[56,2304]{1,0:T(8,128)(2,1)S(1)}, u32[]{:S(2)}, u32[]{:S(2)}) collective-permute-start(bf16[56,2304]{1,0:T(8,128)(2,1)S(1)} %index_gather.2.refs_1_), channel_id=1, source_target_pairs={{0,2},{1,3},{2,0},{3,1},{4,6},{5,7},{6,4},{7,5}} | collective-permute-start | bytes 774152 | tf_op jit(solution)/shard_map/ppermute | solution.py:640
  8.0 11.2 %collective-permute-start.11 = (bf16[56,2304]{1,0:T(8,128)(2,1)S(1)}, bf16[56,2304]{1,0:T(8,128)(2,1)S(1)}, u32[]{:S(2)}, u32[]{:S(2)}) collective-permute-start(bf16[56,2304]{1,0:T(8,128)(2,1)S(1)} %index_gather.2.refs_1_), channel_id=1, source_target_pairs={{0,1},{1,0},{2,3},{3,2},{4,5},{5,4},{6,7},{7,6}} | collective-permute-start | bytes 774152 | tf_op jit(solution)/shard_map/ppermute | solution.py:640
  11.9 27.8 %collective-permute-start.15 = (bf16[128,2304]{1,0:T(8,128)(2,1)S(1)}, bf16[128,2304]{1,0:T(8,128)(2,1)S(1)}, u32[]{:S(2)}, u32[]{:S(2)}) collective-permute-start(bf16[128,2304]{1,0:T(8,128)(2,1)S(1)} %get-tuple-element.163), channel_id=1, source_target_pairs={{0,1},{1,0},{2,3},{3,2},{4,5},{5,4},{6,7},{7,6}} | collective-permute-start | bytes 1769480 | tf_op jit(solution)/shard_map/ppermute | solution.py:640
  12.4 27.3 %collective-permute-start.16 = (bf16[128,2304]{1,0:T(8,128)(2,1)S(1)}, bf16[128,2304]{1,0:T(8,128)(2,1)S(1)}, u32[]{:S(2)}, u32[]{:S(2)}) collective-permute-start(bf16[128,2304]{1,0:T(8,128)(2,1)S(1)} %get-tuple-element.164), channel_id=1, source_target_pairs={{0,2},{1,3},{2,0},{3,1},{4,6},{5,7},{6,4},{7,5}} | collective-permute-start | bytes 1769480 | tf_op jit(solution)/shard_map/ppermute | solution.py:640
  14.3 4.9 %collective-permute-start.13 = (bf16[56,2304]{1,0:T(8,128)(2,1)S(1)}, bf16[56,2304]{1,0:T(8,128)(2,1)S(1)}, u32[]{:S(2)}, u32[]{:S(2)}) collective-permute-start(bf16[56,2304]{1,0:T(8,128)(2,1)S(1)} %collective-permute-done.12.refs_3_), channel_id=1, source_target_pairs={{0,1},{1,0},{2,3},{3,2},{4,5},{5,4},{6,7},{7,6}} | collective-permute-start | bytes 774152 | tf_op jit(solution)/shard_map/ppermute | solution.py:640
  16.6 23.1 %copy-start.2 = (bf16[1,2304]{1,0:T(2,128)(2,1)}, bf16[1,2304]{1,0:T(2,128)(2,1)S(1)}, u32[]{:S(2)}) copy-start(bf16[1,2304]{1,0:T(2,128)(2,1)S(1)} %reshape.34.g_ref.g) | copy-start | bytes 13828
  16.6 23.1 %collective-permute-start.17 = (bf16[128,2304]{1,0:T(8,128)(2,1)S(1)}, bf16[128,2304]{1,0:T(8,128)(2,1)S(1)}, u32[]{:S(2)}, u32[]{:S(2)}) collective-permute-start(bf16[128,2304]{1,0:T(8,128)(2,1)S(1)} %get-tuple-element.165), channel_id=1, source_target_pairs={{0,3},{1,2},{2,1},{3,0},{4,7},{5,6},{6,5},{7,4}} | collective-permute-start | bytes 1769480 | tf_op jit(solution)/shard_map/ppermute | solution.py:640
  20.1 19.7 %copy-start.12 = (bf16[2,64,2304]{2,1,0:T(8,128)(2,1)}, bf16[2,64,2304]{2,1,0:T(8,128)(2,1)S(1)}, u32[]{:S(2)}) copy-start(bf16[2,64,2304]{2,1,0:T(8,128)(2,1)S(1)} %get-tuple-element.311) | copy-start | bytes 1769476
  20.1 19.7 %copy-start.8 = (bf16[2,64,2304]{2,1,0:T(8,128)(2,1)S(1)}, bf16[2,64,2304]{2,1,0:T(8,128)(2,1)}, u32[]{:S(2)}) copy-start(bf16[2,64,2304]{2,1,0:T(8,128)(2,1)} %param.15) | copy-start | bytes 1769476
  42.4 5.1 %collective-permute-start.18 = (bf16[128,2304]{1,0:T(8,128)(2,1)S(1)}, bf16[128,2304]{1,0:T(8,128)(2,1)S(1)}, u32[]{:S(2)}, u32[]{:S(2)}) collective-permute-start(bf16[128,2304]{1,0:T(8,128)(2,1)S(1)} %get-tuple-element.166.dx0), channel_id=1, source_target_pairs={{0,1},{1,0},{2,3},{3,2},{4,5},{5,4},{6,7},{7,6}} | collective-permute-start | bytes 1769480 | tf_op jit(solution)/shard_map/ppermute | solution.py:640
  42.6 4.9 %collective-permute-start.14 = (s32[1,128]{1,0:T(1,128)S(1)}, s32[1,128]{1,0:T(1,128)S(1)}, u32[]{:S(2)}, u32[]{:S(2)}) collective-permute-start(s32[1,128]{1,0:T(1,128)S(1)} %get-tuple-element.159.cnt_ref), channel_id=1, source_target_pairs={{0,4},{4,0},{1,5},{5,1},{2,6},{6,2},{3,7},{7,3}} | collective-permute-start | bytes 1544 | tf_op jit(solution)/shard_map/ppermute | solution.py:667
  46.5 11.3 %copy-start.1 = (s32[2,256]{1,0:T(2,128)S(1)}, s32[2,256]{1,0:T(2,128)}, u32[]{:S(2)}) copy-start(s32[2,256]{1,0:T(2,128)} %ids_ref.3) | copy-start | bytes 6148
  46.5 9.0 %collective-permute-start.19 = (f32[32,2304]{1,0:T(8,128)S(1)}, f32[32,2304]{1,0:T(8,128)S(1)}, u32[]{:S(2)}, u32[]{:S(2)}) collective-permute-start(f32[32,2304]{1,0:T(8,128)S(1)} %get-tuple-element.172.mine_ref), channel_id=1, source_target_pairs={{0,2},{1,3},{2,0},{3,1},{4,6},{5,7},{6,4},{7,5}} | collective-permute-start | bytes 884744 | tf_op jit(solution)/shard_map/ppermute | solution.py:640

commit v12 on v11

--- a/solution.py
+++ b/solution.py
@@ -14,7 +14,7 @@
 C2 = 32
 CB = 256
 ZR = 128
-ZP, ZA, ZU, ZW, ZB = 8, 4, 22, 20, 4
+ZP, ZA, ZU, ZW, ZB = 8, 4, 22, 17, 4
 AT_A, AT_U, AT_B, AT_R = ZP, ZP + ZA, ZP + ZA + ZU + ZW, ZP + ZA + ZU + ZW + ZB
 TB = 64
 
@@ -557,11 +557,11 @@
     )(cnts, rows, srow, *pieces, de)
 
 
-def _acc_kernel(lo, n, cnt_ref, oth_ref, slot_ref, dx0, dx1, de_in, de, acc, flag, z, sems):
+def _acc_kernel(lo, n, cnt_ref, oth_ref, slot_ref, dx0, dx1, de_in, de, acc, rounds, over, z, sems):
     z[...] = jnp.zeros_like(z)
     _fill(z, de, sems, lo, 0, n, False)
-    for i in (0, 2):
-        flag[0, i] = jnp.maximum(cnt_ref[0, i], oth_ref[0, i])
+    rounds[0] = jnp.maximum(cnt_ref[0, 0], oth_ref[0, 0])
+    over[0] = jnp.maximum(cnt_ref[0, 2], oth_ref[0, 2])
     m = dx0.shape[0]
     j = _iota((C, m), 0)
     ohs = [jnp.where(slot_ref[i:i + 1, :] == j, 1.0, 0.0).astype(BF16) for i in (0, 1)]
@@ -580,10 +580,11 @@
         out_shape=(
             jax.ShapeDtypeStruct((vs, d), F32),
             jax.ShapeDtypeStruct((C, d), F32),
-            jax.ShapeDtypeStruct((1, 4), jnp.int32),
+            jax.ShapeDtypeStruct((1,), jnp.int32),
+            jax.ShapeDtypeStruct((1,), jnp.int32),
         ),
         in_specs=[_sm(), _sm()] + [_vm()] * 3 + [_any()],
-        out_specs=(_any(), _vm(), _sm()),
+        out_specs=(_any(), _vm(), _sm(), _sm()),
         scratch_shapes=_zscratch(d, n),
         input_output_aliases={5: 0},
         compiler_params=_params(8),
@@ -665,15 +666,15 @@
         dx1 = swap(dx, 1)
         de = _zeros(de, AT_B, ZB)
         other = lax.ppermute(cnts, "dp", [(i, (i + 1) % ndp) for i in range(ndp)])
-        de, acc, flags = _acc(cnts, other, slots, dx, dx1, de, AT_R)
+        de, acc, rounds, over = _acc(cnts, other, slots, dx, dx1, de, AT_R)
         dE, dg = _write(where, acc, mine, got, de)
         outs = u, xl, dE, dW, dg
 
-        inputs = ids, E, W, du, dres, g2, flags
+        inputs = ids, E, W, du, dres, g2, rounds
 
         def again(c):
             ids, E, W, du, dres, g2, fl, left = lax.optimization_barrier((*inputs, c[0]))
-            rounds = fl[0, 0]
+            rounds = fl.reshape(())
             i0 = left - left
 
             def more(q):
@@ -691,7 +692,7 @@
             dE = _scatter(cs, rows, srow, share(dx), _zeros(de, AT_B, vs // ZR - AT_B), ts, nk)
             return i0, (u, xl, dE, dW, dg)
 
-        _, outs = lax.while_loop(lambda c: c[0] > 0, again, (jnp.minimum(flags[0, 2], 1), outs))
+        _, outs = lax.while_loop(lambda c: c[0] > 0, again, (jnp.minimum(over.reshape(()), 1), outs))
         return outs
 
     return jax.shard_map(

time: 58.3 us -> 58.3 us (level)
  Pallas kernels: 42.2 us -> 43 us
    pallas_call x1, Pallas kernels: 4.19 us -> 5.21 us  [_acc(): pl.pallas_call(functools.partial(_acc_kernel, lo, n), out_shape=(jax.Shap...]
    pallas_call x1, Pallas kernels: 19.6 us -> 19 us  [_udw(): pl.pallas_call(functools.partial(_udw_kernel, -(-ZW // steps), de.shape[0...]
  transfers between devices with their start and end apart: 9 -> 9, of which waited for: 2 -> 3; matrix products, arithmetic and copies ran while one was open for 1% -> 0% of each run, Pallas kernels for 57% -> 58%
where the time goes in v12:
time: 58.3 us; the launch traced here: 58.1 us
  Pallas kernels  43 us (74%)
  starting transfers between devices  9 us (15%)
  waiting for transfers between devices  4.24 us (7%)
  between operations  1.63 us (3%)
    pallas_call x1, Pallas kernels, _udw(): pl.pallas_call(functools.partial(_udw_kernel, -(-ZW // steps), de.shape[0...  19 us
    ppermute x8, starting transfers between devices, swap(): return lax.ppermute(a, 'tp', [(i, i ^ bit) for i in range(ntp)])  7.42 us
    pallas_call x1, Pallas kernels, _acc(): pl.pallas_call(functools.partial(_acc_kernel, lo, n), out_shape=(jax.Shap...  5.21 us
    ppermute x8, waiting for transfers between devices, swap(): return lax.ppermute(a, 'tp', [(i, i ^ bit) for i in range(ntp)])  4.24 us
    pallas_call x1, Pallas kernels, _index_call(): pl.pallas_call(functools.partial(_index_kernel, vs, ntp, first), out_shap...  4.12 us
    pallas_call x1, Pallas kernels, _p_terms(): pl.pallas_call(functools.partial(_p_kernel, ts), out_shape=(jax.ShapeDtyp...  3.94 us
    pallas_call x1, Pallas kernels, _dx_sums(): pl.pallas_call(_dx_sums_kernel, out_shape=(jax.ShapeDtypeStruct((m, d), B...  3 us
    pallas_call x1, Pallas kernels, _pos(): pl.pallas_call(functools.partial(_pos_kernel, vs, ntp), out_shape=(jax.Sh...  2.29 us
  transfers between devices with their start and end apart: 9, of which 3 were waited for; matrix products, arithmetic and copies ran while one was open for 0% of the time, Pallas kernels for 58%

profile of v12, /device:TPU:0, one launch (start us, length us, event | category | flops | bytes accessed | tf_op | source)
XLA Modules:
  0.0 58.1 jit_solution(5808246189878981050)
XLA Ops:
  0.6 0.0 copy-start
  0.6 0.0 copy-start.6
  0.7 0.0 copy-start.5
  0.7 4.1 %index_gather.2.refs_1_ = bf16[56,2304]{1,0:T(8,128)(2,1)S(1)} custom-call(s32[2,256]{1,0:T(2,128)} %ids_ref.3, bf16[8192,2304]{1,0:T(8,128)(2,1)} %refs_1_.1), custom_call_target="tpu_custom_call" | custom-call | flops 48000000000 | bytes 1000000 | tf_op jit(solution)/shard_map/index_gather/pallas_call | solution.py:151
  4.8 0.0 copy-start.4
  4.8 3.2 %collective-permute-start.12 = (bf16[56,2304]{1,0:T(8,128)(2,1)S(1)}, bf16[56,2304]{1,0:T(8,128)(2,1)S(1)}, u32[]{:S(2)}, u32[]{:S(2)}) collective-permute-start(bf16[56,2304]{1,0:T(8,128)(2,1)S(1)} %index_gather.2.refs_1_), channel_id=1, source_target_pairs={{0,2},{1,3},{2,0},{3,1},{4,6},{5,7},{6,4},{7,5}} | collective-permute-start | bytes 774152 | tf_op jit(solution)/shard_map/ppermute | solution.py:641
  8.0 0.0 collective-permute-start.11
  8.0 3.9 %p_terms.3 = (bf16[128,2304]{1,0:T(8,128)(2,1)S(1)}, bf16[128,2304]{1,0:T(8,128)(2,1)S(1)}, bf16[128,2304]{1,0:T(8,128)(2,1)S(1)}, bf16[128,2304]{1,0:T(8,128)(2,1)S(1)}, f32[8192,2304]{1,0:T(8,128)}) custom-call(bf16[2,256,1024]{2,1,0:T(8,128)(2,1)S(1)} %copy-done.6, bf16[2304,1024]{1,0:T(8,128)(2,1)S(1)} %copy-done.5), custom_call_target="tpu_custom_call" | custom-call | flops 20000000000 | bytes 1000000 | tf_op jit(solution)/shard_map/p_terms/pallas_call | solution.py:334
  11.9 0.5 collective-permute-start.15
  12.4 0.0 collective-permute-start.16
  12.5 1.8 %collective-permute-done.12.refs_3_ = bf16[56,2304]{1,0:T(8,128)(2,1)S(1)} collective-permute-done((bf16[56,2304]{1,0:T(8,128)(2,1)S(1)}, bf16[56,2304]{1,0:T(8,128)(2,1)S(1)}, u32[]{:S(2)}, u32[]{:S(2)}) %collective-permute-start.12) | collective-permute-done | bytes 258080 | tf_op jit(solution)/shard_map/ppermute | solution.py:641
  14.3 0.0 collective-permute-start.13
  14.3 2.3 %positions.2 = (f32[512,1]{1,0:T(8,128)S(1)}, f32[8192,2304]{1,0:T(8,128)}) custom-call(s32[1]{0:T(128)} %constant.10.clone.1.c_ref, s32[2,256]{1,0:T(2,128)S(1)} %copy-done, f32[8192,2304]{1,0:T(8,128)} %get-tuple-element.156.de_in), custom_call_target="tpu_custom_call", output_to_operand_aliasing={{1}: (2, {})} | custom-call | flops 12000000000 | bytes 1000000 | tf_op jit(solution)/shard_map/positions/pallas_call | solution.py:186
  16.6 2.5 %collective-permute-start.17 = (bf16[128,2304]{1,0:T(8,128)(2,1)S(1)}, bf16[128,2304]{1,0:T(8,128)(2,1)S(1)}, u32[]{:S(2)}, u32[]{:S(2)}) collective-permute-start(bf16[128,2304]{1,0:T(8,128)(2,1)S(1)} %get-tuple-element.166), channel_id=1, source_target_pairs={{0,3},{1,2},{2,1},{3,0},{4,7},{5,6},{6,5},{7,4}} | collective-permute-start | bytes 1769480 | tf_op jit(solution)/shard_map/ppermute | solution.py:641
  19.2 0.0 collective-permute-done.11.refs_2_
  19.2 0.0 collective-permute-done.13.refs_4_
  19.2 0.9 %expand.2 = (bf16[512,2304]{1,0:T(8,128)(2,1)S(1)}, bf16[2,64,2304]{2,1,0:T(8,128)(2,1)S(1)}) custom-call(f32[512,1]{1,0:T(8,128)S(1)} %get-tuple-element.157.refs_0_, bf16[56,2304]{1,0:T(8,128)(2,1)S(1)} %index_gather.2.refs_1_, bf16[56,2304]{1,0:T(8,128)(2,1)S(1)} %collective-permute-done.11.refs_2_, bf16[56,2304]{1,0:T(8,128)(2,1)S(1)} %collective-permute-done.12.refs_3_, ...), custom_call_target="tpu_custom_call" | custom-call | flops 12000000000 | bytes 1000000 | tf_op jit(solution)/shard_map/expand/pallas_call | solution.py:297
  20.1 0.0 copy-start.10
  20.1 0.0 copy-start.8
  20.1 19.0 %u_dw.3 = (bf16[2,256,1024]{2,1,0:T(8,128)(2,1)}, f32[2304,1024]{1,0:T(8,128)}, f32[1,512]{1,0:T(1,128)}, s32[1,512]{1,0:T(1,128)}, s32[1,128]{1,0:T(1,128)S(1)}...) custom-call(bf16[512,2304]{1,0:T(8,128)(2,1)S(1)} %get-tuple-element.15, ...), custom_call_target="tpu_custom_call", output_to_operand_aliasing={{7}: (5, {})} | custom-call | flops 80000000000 | bytes 1000000 | tf_op jit(solution)/shard_map/u_dw/pallas_call | solution.py:484
  39.1 0.0 collective-permute-done.15.p1
  39.1 0.3 collective-permute-done.17.p3
  39.4 3.0 %dx_sums.1 = (bf16[128,2304]{1,0:T(8,128)(2,1)S(1)}, f32[32,2304]{1,0:T(8,128)S(1)}) custom-call(bf16[128,2304]{1,0:T(8,128)(2,1)S(1)} %bitcast.11, bf16[128,2304]{1,0:T(8,128)(2,1)S(1)} %get-tuple-element.163.p0, bf16[128,2304]{1,0:T(8,128)(2,1)S(1)} %collective-permute-done.15.p1, bf16[128,2304]{1,0:T(8,128)(2,1)S(1)} %collective-permute-done.16.p2, ...), custom_call_target="tpu_custom_call" | custom-call | flops 12000000000 | bytes 1000000 | tf_op jit(solution)/shard_map/dx_sums/pallas_call | solution.py:433
  42.4 0.2 collective-permute-start.18
  42.6 1.6 %collective-permute-start.14 = (s32[1,128]{1,0:T(1,128)S(1)}, s32[1,128]{1,0:T(1,128)S(1)}, u32[]{:S(2)}, u32[]{:S(2)}) collective-permute-start(s32[1,128]{1,0:T(1,128)S(1)} %get-tuple-element.160.cnt_ref), channel_id=1, source_target_pairs={{0,4},{4,0},{1,5},{5,1},{2,6},{6,2},{3,7},{7,3}} | collective-permute-start | bytes 1544 | tf_op jit(solution)/shard_map/ppermute | solution.py:668
  44.2 2.3 %shard_map.101.de_in = f32[8192,2304]{1,0:T(8,128)} custom-call(f32[8192,2304]{1,0:T(8,128)} %get-tuple-element.168.de_in), custom_call_target="tpu_custom_call", output_to_operand_aliasing={{}: (0, {})} | custom-call | flops 6000000000 | bytes 1000000 | tf_op jit(solution)/shard_map/pallas_call | solution.py:356
  46.5 0.0 copy-start.1
  46.5 1.0 %collective-permute-start.19 = (f32[32,2304]{1,0:T(8,128)S(1)}, f32[32,2304]{1,0:T(8,128)S(1)}, u32[]{:S(2)}, u32[]{:S(2)}) collective-permute-start(f32[32,2304]{1,0:T(8,128)S(1)} %get-tuple-element.173.mine_ref), channel_id=1, source_target_pairs={{0,2},{1,3},{2,0},{3,1},{4,6},{5,7},{6,4},{7,5}} | collective-permute-start | bytes 884744 | tf_op jit(solution)/shard_map/ppermute | solution.py:641
  47.5 5.2 %fill_acc.1 = (f32[8192,2304]{1,0:T(8,128)}, f32[56,2304]{1,0:T(8,128)S(1)}, s32[1]{0:T(128)}, s32[1]{0:T(128)}) custom-call(s32[1,128]{1,0:T(1,128)S(1)} %get-tuple-element.160.cnt_ref, s32[1,128]{1,0:T(1,128)S(1)} %collective-permute-done.14.oth_ref, f32[4,128]{1,0:T(4,128)S(1)} %get-tuple-element.161.slot_ref, ...), custom_call_target="tpu_custom_call", output_to_operand_aliasing={{0}: (5, {})} | custom-call | flops 13500000256 | bytes 1000000 | tf_op jit(solution)/shard_map/fill_acc/pallas_call | solution.py:578
  53.4 2.1 %collective-permute-done.19.got_ref = f32[32,2304]{1,0:T(8,128)S(1)} collective-permute-done((f32[32,2304]{1,0:T(8,128)S(1)}, f32[32,2304]{1,0:T(8,128)S(1)}, u32[]{:S(2)}, u32[]{:S(2)}) %collective-permute-start.19) | collective-permute-done | bytes 294944 | tf_op jit(solution)/shard_map/ppermute | solution.py:641
  55.5 2.2 %write_rows.1 = (f32[8192,2304]{1,0:T(8,128)}, f32[2304]{0:T(1024)}) custom-call(s32[1,256]{1,0:T(1,128)S(1)} %get-tuple-element.171.map_ref, f32[56,2304]{1,0:T(8,128)S(1)} %get-tuple-element.172.acc_in, f32[32,2304]{1,0:T(8,128)S(1)} %get-tuple-element.173.mine_ref, ...), custom_call_target="tpu_custom_call", output_to_operand_aliasing={{0}: (4, {})} | custom-call | flops 12000000000 | bytes 1000000 | tf_op jit(solution)/shard_map/write_rows/pallas_call | solution.py:623
  57.8 0.2 while.30
  (13 shorter events, 0.0 us)
Async XLA Ops:
  0.6 13.6 %copy-start = (s32[2,256]{1,0:T(2,128)S(1)}, s32[2,256]{1,0:T(2,128)}, u32[]{:S(2)}) copy-start(s32[2,256]{1,0:T(2,128)} %ids_ref.3) | copy-start | bytes 6148
  0.6 7.3 %copy-start.6 = (bf16[2,256,1024]{2,1,0:T(8,128)(2,1)S(1)}, bf16[2,256,1024]{2,1,0:T(8,128)(2,1)}, u32[]{:S(2)}) copy-start(bf16[2,256,1024]{2,1,0:T(8,128)(2,1)} %du_ref.3) | copy-start | bytes 3145732
  0.7 7.3 %copy-start.5 = (bf16[2304,1024]{1,0:T(8,128)(2,1)S(1)}, bf16[2304,1024]{1,0:T(8,128)(2,1)}, u32[]{:S(2)}) copy-start(bf16[2304,1024]{1,0:T(8,128)(2,1)} %w_ref.3) | copy-start | bytes 14155780
  4.8 11.8 %copy-start.4 = (bf16[2304]{0:T(1024)(128)(2,1)S(1)}, bf16[2304]{0:T(1024)(128)(2,1)}, u32[]{:S(2)}) copy-start(bf16[2304]{0:T(1024)(128)(2,1)} %param.12) | copy-start | bytes 13828
  4.8 9.5 %collective-permute-start.12 = (bf16[56,2304]{1,0:T(8,128)(2,1)S(1)}, bf16[56,2304]{1,0:T(8,128)(2,1)S(1)}, u32[]{:S(2)}, u32[]{:S(2)}) collective-permute-start(bf16[56,2304]{1,0:T(8,128)(2,1)S(1)} %index_gather.2.refs_1_), channel_id=1, source_target_pairs={{0,2},{1,3},{2,0},{3,1},{4,6},{5,7},{6,4},{7,5}} | collective-permute-start | bytes 774152 | tf_op jit(solution)/shard_map/ppermute | solution.py:641
  8.0 11.2 %collective-permute-start.11 = (bf16[56,2304]{1,0:T(8,128)(2,1)S(1)}, bf16[56,2304]{1,0:T(8,128)(2,1)S(1)}, u32[]{:S(2)}, u32[]{:S(2)}) collective-permute-start(bf16[56,2304]{1,0:T(8,128)(2,1)S(1)} %index_gather.2.refs_1_), channel_id=1, source_target_pairs={{0,1},{1,0},{2,3},{3,2},{4,5},{5,4},{6,7},{7,6}} | collective-permute-start | bytes 774152 | tf_op jit(solution)/shard_map/ppermute | solution.py:641
  11.9 27.2 %collective-permute-start.15 = (bf16[128,2304]{1,0:T(8,128)(2,1)S(1)}, bf16[128,2304]{1,0:T(8,128)(2,1)S(1)}, u32[]{:S(2)}, u32[]{:S(2)}) collective-permute-start(bf16[128,2304]{1,0:T(8,128)(2,1)S(1)} %get-tuple-element.164), channel_id=1, source_target_pairs={{0,1},{1,0},{2,3},{3,2},{4,5},{5,4},{6,7},{7,6}} | collective-permute-start | bytes 1769480 | tf_op jit(solution)/shard_map/ppermute | solution.py:641
  12.4 26.7 %collective-permute-start.16 = (bf16[128,2304]{1,0:T(8,128)(2,1)S(1)}, bf16[128,2304]{1,0:T(8,128)(2,1)S(1)}, u32[]{:S(2)}, u32[]{:S(2)}) collective-permute-start(bf16[128,2304]{1,0:T(8,128)(2,1)S(1)} %get-tuple-element.165), channel_id=1, source_target_pairs={{0,2},{1,3},{2,0},{3,1},{4,6},{5,7},{6,4},{7,5}} | collective-permute-start | bytes 1769480 | tf_op jit(solution)/shard_map/ppermute | solution.py:641
  14.3 4.9 %collective-permute-start.13 = (bf16[56,2304]{1,0:T(8,128)(2,1)S(1)}, bf16[56,2304]{1,0:T(8,128)(2,1)S(1)}, u32[]{:S(2)}, u32[]{:S(2)}) collective-permute-start(bf16[56,2304]{1,0:T(8,128)(2,1)S(1)} %collective-permute-done.12.refs_3_), channel_id=1, source_target_pairs={{0,1},{1,0},{2,3},{3,2},{4,5},{5,4},{6,7},{7,6}} | collective-permute-start | bytes 774152 | tf_op jit(solution)/shard_map/ppermute | solution.py:641
  16.6 22.8 %copy-start.2 = (bf16[1,2304]{1,0:T(2,128)(2,1)}, bf16[1,2304]{1,0:T(2,128)(2,1)S(1)}, u32[]{:S(2)}) copy-start(bf16[1,2304]{1,0:T(2,128)(2,1)S(1)} %reshape.38.g_ref.g) | copy-start | bytes 13828
  16.6 22.8 %collective-permute-start.17 = (bf16[128,2304]{1,0:T(8,128)(2,1)S(1)}, bf16[128,2304]{1,0:T(8,128)(2,1)S(1)}, u32[]{:S(2)}, u32[]{:S(2)}) collective-permute-start(bf16[128,2304]{1,0:T(8,128)(2,1)S(1)} %get-tuple-element.166), channel_id=1, source_target_pairs={{0,3},{1,2},{2,1},{3,0},{4,7},{5,6},{6,5},{7,4}} | collective-permute-start | bytes 1769480 | tf_op jit(solution)/shard_map/ppermute | solution.py:641
  20.1 19.3 %copy-start.10 = (bf16[2,64,2304]{2,1,0:T(8,128)(2,1)}, bf16[2,64,2304]{2,1,0:T(8,128)(2,1)S(1)}, u32[]{:S(2)}) copy-start(bf16[2,64,2304]{2,1,0:T(8,128)(2,1)S(1)} %get-tuple-element.313) | copy-start | bytes 1769476
  20.1 19.3 %copy-start.8 = (bf16[2,64,2304]{2,1,0:T(8,128)(2,1)S(1)}, bf16[2,64,2304]{2,1,0:T(8,128)(2,1)}, u32[]{:S(2)}) copy-start(bf16[2,64,2304]{2,1,0:T(8,128)(2,1)} %param.15) | copy-start | bytes 1769476
  42.4 5.1 %collective-permute-start.18 = (bf16[128,2304]{1,0:T(8,128)(2,1)S(1)}, bf16[128,2304]{1,0:T(8,128)(2,1)S(1)}, u32[]{:S(2)}, u32[]{:S(2)}) collective-permute-start(bf16[128,2304]{1,0:T(8,128)(2,1)S(1)} %get-tuple-element.167.dx0), channel_id=1, source_target_pairs={{0,1},{1,0},{2,3},{3,2},{4,5},{5,4},{6,7},{7,6}} | collective-permute-start | bytes 1769480 | tf_op jit(solution)/shard_map/ppermute | solution.py:641
  42.6 4.9 %collective-permute-start.14 = (s32[1,128]{1,0:T(1,128)S(1)}, s32[1,128]{1,0:T(1,128)S(1)}, u32[]{:S(2)}, u32[]{:S(2)}) collective-permute-start(s32[1,128]{1,0:T(1,128)S(1)} %get-tuple-element.160.cnt_ref), channel_id=1, source_target_pairs={{0,4},{4,0},{1,5},{5,1},{2,6},{6,2},{3,7},{7,3}} | collective-permute-start | bytes 1544 | tf_op jit(solution)/shard_map/ppermute | solution.py:668
  46.5 11.3 %copy-start.1 = (s32[2,256]{1,0:T(2,128)S(1)}, s32[2,256]{1,0:T(2,128)}, u32[]{:S(2)}) copy-start(s32[2,256]{1,0:T(2,128)} %ids_ref.3) | copy-start | bytes 6148
  46.5 9.0 %collective-permute-start.19 = (f32[32,2304]{1,0:T(8,128)S(1)}, f32[32,2304]{1,0:T(8,128)S(1)}, u32[]{:S(2)}, u32[]{:S(2)}) collective-permute-start(f32[32,2304]{1,0:T(8,128)S(1)} %get-tuple-element.173.mine_ref), channel_id=1, source_target_pairs={{0,2},{1,3},{2,0},{3,1},{4,6},{5,7},{6,4},{7,5}} | collective-permute-start | bytes 884744 | tf_op jit(solution)/shard_map/ppermute | solution.py:641

commit v13 on v12

--- a/solution.py
+++ b/solution.py
@@ -14,7 +14,7 @@
 C2 = 32
 CB = 256
 ZR = 128
-ZP, ZA, ZU, ZW, ZB = 8, 4, 22, 17, 4
+ZP, ZA, ZU, ZW, ZB = 8, 4, 22, 19, 4
 AT_A, AT_U, AT_B, AT_R = ZP, ZP + ZA, ZP + ZA + ZU + ZW, ZP + ZA + ZU + ZW + ZB
 TB = 64
 
@@ -136,7 +136,7 @@
         pltpu.make_async_copy(e_ref.at[pl.ds(g, G)], buf.at[pl.ds(at, G)], sem).start()
         return carry
 
-    lax.fori_loop(0, C, fetch, 0, unroll=8)
+    lax.fori_loop(0, C, fetch, 0, unroll=True)
     hit = jnp.where(my_r == _iota((C, ntok), 0) + base, idr - lo, 0.0)
     want = jnp.max(hit, axis=1, keepdims=True)
     want = want - jnp.floor(want * (1.0 / G)) * G + _iota((C, 1), 0) * G
@@ -366,7 +366,7 @@
 
 
 def _dx_rows(x, p0, p1, p2, p3, dres, g, dx):
-    rows = 32
+    rows = 16
     tot = None
     for b in range(dx.shape[0] // rows):
         s = slice(b * rows, (b + 1) * rows)

time: 58.3 us -> 58.2 us (level)
  Pallas kernels: 43 us -> 42.4 us
    pallas_call x1, Pallas kernels: 5.21 us -> 4.48 us  [_acc(): pl.pallas_call(functools.partial(_acc_kernel, lo, n), out_shape=(jax.Shap...]
  transfers between devices with their start and end apart: 9 -> 9, of which waited for: 3 -> 2; matrix products, arithmetic and copies ran while one was open for 0% -> 0% of each run, Pallas kernels for 58% -> 57%
where the time goes in v13:
time: 58.2 us; the launch traced here: 58 us
  Pallas kernels  42.4 us (73%)
  starting transfers between devices  9.02 us (15%)
  waiting for transfers between devices  4.69 us (8%)
  between operations  1.64 us (3%)
    pallas_call x1, Pallas kernels, _udw(): pl.pallas_call(functools.partial(_udw_kernel, -(-ZW // steps), de.shape[0...  19.2 us
    ppermute x8, starting transfers between devices, swap(): return lax.ppermute(a, 'tp', [(i, i ^ bit) for i in range(ntp)])  7.43 us
    ppermute x8, waiting for transfers between devices, swap(): return lax.ppermute(a, 'tp', [(i, i ^ bit) for i in range(ntp)])  4.69 us
    pallas_call x1, Pallas kernels, _acc(): pl.pallas_call(functools.partial(_acc_kernel, lo, n), out_shape=(jax.Shap...  4.48 us
    pallas_call x1, Pallas kernels, _index_call(): pl.pallas_call(functools.partial(_index_kernel, vs, ntp, first), out_shap...  4 us
    pallas_call x1, Pallas kernels, _p_terms(): pl.pallas_call(functools.partial(_p_kernel, ts), out_shape=(jax.ShapeDtyp...  3.94 us
    pallas_call x1, Pallas kernels, _dx_sums(): pl.pallas_call(_dx_sums_kernel, out_shape=(jax.ShapeDtypeStruct((m, d), B...  3.05 us
    pallas_call x1, Pallas kernels, _pos(): pl.pallas_call(functools.partial(_pos_kernel, vs, ntp), out_shape=(jax.Sh...  2.29 us
  transfers between devices with their start and end apart: 9, of which 2 were waited for; matrix products, arithmetic and copies ran while one was open for 0% of the time, Pallas kernels for 57%

profile of v13, /device:TPU:0, one launch (start us, length us, event | category | flops | bytes accessed | tf_op | source)
XLA Modules:
  0.0 58.0 jit_solution(10857944041464662613)
XLA Ops:
  0.6 0.0 copy-start
  0.6 0.0 copy-start.6
  0.7 0.0 copy-start.5
  0.7 4.0 %index_gather.2.refs_1_ = bf16[56,2304]{1,0:T(8,128)(2,1)S(1)} custom-call(s32[2,256]{1,0:T(2,128)} %ids_ref.3, bf16[8192,2304]{1,0:T(8,128)(2,1)} %refs_1_.1), custom_call_target="tpu_custom_call" | custom-call | flops 48000000000 | bytes 1000000 | tf_op jit(solution)/shard_map/index_gather/pallas_call | solution.py:151
  4.7 0.0 copy-start.4
  4.7 3.1 %collective-permute-start.12 = (bf16[56,2304]{1,0:T(8,128)(2,1)S(1)}, bf16[56,2304]{1,0:T(8,128)(2,1)S(1)}, u32[]{:S(2)}, u32[]{:S(2)}) collective-permute-start(bf16[56,2304]{1,0:T(8,128)(2,1)S(1)} %index_gather.2.refs_1_), channel_id=1, source_target_pairs={{0,2},{1,3},{2,0},{3,1},{4,6},{5,7},{6,4},{7,5}} | collective-permute-start | bytes 774152 | tf_op jit(solution)/shard_map/ppermute | solution.py:641
  7.8 0.0 collective-permute-start.11
  7.8 3.9 %p_terms.3 = (bf16[128,2304]{1,0:T(8,128)(2,1)S(1)}, bf16[128,2304]{1,0:T(8,128)(2,1)S(1)}, bf16[128,2304]{1,0:T(8,128)(2,1)S(1)}, bf16[128,2304]{1,0:T(8,128)(2,1)S(1)}, f32[8192,2304]{1,0:T(8,128)}) custom-call(bf16[2,256,1024]{2,1,0:T(8,128)(2,1)S(1)} %copy-done.6, bf16[2304,1024]{1,0:T(8,128)(2,1)S(1)} %copy-done.5), custom_call_target="tpu_custom_call" | custom-call | flops 20000000000 | bytes 1000000 | tf_op jit(solution)/shard_map/p_terms/pallas_call | solution.py:334
  11.8 0.5 collective-permute-start.15
  12.3 0.0 collective-permute-start.16
  12.3 1.8 %collective-permute-done.12.refs_3_ = bf16[56,2304]{1,0:T(8,128)(2,1)S(1)} collective-permute-done((bf16[56,2304]{1,0:T(8,128)(2,1)S(1)}, bf16[56,2304]{1,0:T(8,128)(2,1)S(1)}, u32[]{:S(2)}, u32[]{:S(2)}) %collective-permute-start.12) | collective-permute-done | bytes 258080 | tf_op jit(solution)/shard_map/ppermute | solution.py:641
  14.1 0.0 collective-permute-start.13
  14.1 2.3 %positions.2 = (f32[512,1]{1,0:T(8,128)S(1)}, f32[8192,2304]{1,0:T(8,128)}) custom-call(s32[1]{0:T(128)} %constant.10.clone.1.c_ref, s32[2,256]{1,0:T(2,128)S(1)} %copy-done, f32[8192,2304]{1,0:T(8,128)} %get-tuple-element.156.de_in), custom_call_target="tpu_custom_call", output_to_operand_aliasing={{1}: (2, {})} | custom-call | flops 12000000000 | bytes 1000000 | tf_op jit(solution)/shard_map/positions/pallas_call | solution.py:186
  16.5 2.5 %collective-permute-start.17 = (bf16[128,2304]{1,0:T(8,128)(2,1)S(1)}, bf16[128,2304]{1,0:T(8,128)(2,1)S(1)}, u32[]{:S(2)}, u32[]{:S(2)}) collective-permute-start(bf16[128,2304]{1,0:T(8,128)(2,1)S(1)} %get-tuple-element.166), channel_id=1, source_target_pairs={{0,3},{1,2},{2,1},{3,0},{4,7},{5,6},{6,5},{7,4}} | collective-permute-start | bytes 1769480 | tf_op jit(solution)/shard_map/ppermute | solution.py:641
  19.0 0.0 collective-permute-done.11.refs_2_
  19.0 0.0 collective-permute-done.13.refs_4_
  19.0 0.9 %expand.2 = (bf16[512,2304]{1,0:T(8,128)(2,1)S(1)}, bf16[2,64,2304]{2,1,0:T(8,128)(2,1)S(1)}) custom-call(f32[512,1]{1,0:T(8,128)S(1)} %get-tuple-element.157.refs_0_, bf16[56,2304]{1,0:T(8,128)(2,1)S(1)} %index_gather.2.refs_1_, bf16[56,2304]{1,0:T(8,128)(2,1)S(1)} %collective-permute-done.11.refs_2_, bf16[56,2304]{1,0:T(8,128)(2,1)S(1)} %collective-permute-done.12.refs_3_, ...), custom_call_target="tpu_custom_call" | custom-call | flops 12000000000 | bytes 1000000 | tf_op jit(solution)/shard_map/expand/pallas_call | solution.py:297
  19.9 0.0 copy-start.10
  20.0 0.0 copy-start.8
  20.0 19.2 %u_dw.3 = (bf16[2,256,1024]{2,1,0:T(8,128)(2,1)}, f32[2304,1024]{1,0:T(8,128)}, f32[1,512]{1,0:T(1,128)}, s32[1,512]{1,0:T(1,128)}, s32[1,128]{1,0:T(1,128)S(1)}...) custom-call(bf16[512,2304]{1,0:T(8,128)(2,1)S(1)} %get-tuple-element.15, ...), custom_call_target="tpu_custom_call", output_to_operand_aliasing={{7}: (5, {})} | custom-call | flops 80000000000 | bytes 1000000 | tf_op jit(solution)/shard_map/u_dw/pallas_call | solution.py:484
  39.2 0.0 collective-permute-done.16.p2
  39.2 0.0 collective-permute-done.17.p3
  39.3 3.0 %dx_sums.1 = (bf16[128,2304]{1,0:T(8,128)(2,1)S(1)}, f32[32,2304]{1,0:T(8,128)S(1)}) custom-call(bf16[128,2304]{1,0:T(8,128)(2,1)S(1)} %bitcast.11, bf16[128,2304]{1,0:T(8,128)(2,1)S(1)} %get-tuple-element.163.p0, bf16[128,2304]{1,0:T(8,128)(2,1)S(1)} %collective-permute-done.15.p1, bf16[128,2304]{1,0:T(8,128)(2,1)S(1)} %collective-permute-done.16.p2, ...), custom_call_target="tpu_custom_call" | custom-call | flops 12000000000 | bytes 1000000 | tf_op jit(solution)/shard_map/dx_sums/pallas_call | solution.py:433
  42.3 0.2 collective-permute-start.18
  42.5 1.6 %collective-permute-start.14 = (s32[1,128]{1,0:T(1,128)S(1)}, s32[1,128]{1,0:T(1,128)S(1)}, u32[]{:S(2)}, u32[]{:S(2)}) collective-permute-start(s32[1,128]{1,0:T(1,128)S(1)} %get-tuple-element.160.cnt_ref), channel_id=1, source_target_pairs={{0,4},{4,0},{1,5},{5,1},{2,6},{6,2},{3,7},{7,3}} | collective-permute-start | bytes 1544 | tf_op jit(solution)/shard_map/ppermute | solution.py:668
  44.1 2.3 %shard_map.101.de_in = f32[8192,2304]{1,0:T(8,128)} custom-call(f32[8192,2304]{1,0:T(8,128)} %get-tuple-element.168.de_in), custom_call_target="tpu_custom_call", output_to_operand_aliasing={{}: (0, {})} | custom-call | flops 6000000000 | bytes 1000000 | tf_op jit(solution)/shard_map/pallas_call | solution.py:356
  46.4 0.0 copy-start.1
  46.4 1.0 %collective-permute-start.19 = (f32[32,2304]{1,0:T(8,128)S(1)}, f32[32,2304]{1,0:T(8,128)S(1)}, u32[]{:S(2)}, u32[]{:S(2)}) collective-permute-start(f32[32,2304]{1,0:T(8,128)S(1)} %get-tuple-element.173.mine_ref), channel_id=1, source_target_pairs={{0,2},{1,3},{2,0},{3,1},{4,6},{5,7},{6,4},{7,5}} | collective-permute-start | bytes 884744 | tf_op jit(solution)/shard_map/ppermute | solution.py:641
  47.4 4.5 %fill_acc.1 = (f32[8192,2304]{1,0:T(8,128)}, f32[56,2304]{1,0:T(8,128)S(1)}, s32[1]{0:T(128)}, s32[1]{0:T(128)}) custom-call(s32[1,128]{1,0:T(1,128)S(1)} %get-tuple-element.160.cnt_ref, s32[1,128]{1,0:T(1,128)S(1)} %collective-permute-done.14.oth_ref, f32[4,128]{1,0:T(4,128)S(1)} %get-tuple-element.161.slot_ref, ...), custom_call_target="tpu_custom_call", output_to_operand_aliasing={{0}: (5, {})} | custom-call | flops 10499999744 | bytes 1000000 | tf_op jit(solution)/shard_map/fill_acc/pallas_call | solution.py:578
  52.6 2.8 %collective-permute-done.19.got_ref = f32[32,2304]{1,0:T(8,128)S(1)} collective-permute-done((f32[32,2304]{1,0:T(8,128)S(1)}, f32[32,2304]{1,0:T(8,128)S(1)}, u32[]{:S(2)}, u32[]{:S(2)}) %collective-permute-start.19) | collective-permute-done | bytes 294944 | tf_op jit(solution)/shard_map/ppermute | solution.py:641
  55.4 2.2 %write_rows.1 = (f32[8192,2304]{1,0:T(8,128)}, f32[2304]{0:T(1024)}) custom-call(s32[1,256]{1,0:T(1,128)S(1)} %get-tuple-element.171.map_ref, f32[56,2304]{1,0:T(8,128)S(1)} %get-tuple-element.172.acc_in, f32[32,2304]{1,0:T(8,128)S(1)} %get-tuple-element.173.mine_ref, ...), custom_call_target="tpu_custom_call", output_to_operand_aliasing={{0}: (4, {})} | custom-call | flops 12000000000 | bytes 1000000 | tf_op jit(solution)/shard_map/write_rows/pallas_call | solution.py:623
  57.7 0.2 while.30
  (13 shorter events, 0.0 us)
Async XLA Ops:
  0.6 13.5 %copy-start = (s32[2,256]{1,0:T(2,128)S(1)}, s32[2,256]{1,0:T(2,128)}, u32[]{:S(2)}) copy-start(s32[2,256]{1,0:T(2,128)} %ids_ref.3) | copy-start | bytes 6148
  0.6 7.2 %copy-start.6 = (bf16[2,256,1024]{2,1,0:T(8,128)(2,1)S(1)}, bf16[2,256,1024]{2,1,0:T(8,128)(2,1)}, u32[]{:S(2)}) copy-start(bf16[2,256,1024]{2,1,0:T(8,128)(2,1)} %du_ref.3) | copy-start | bytes 3145732
  0.7 7.2 %copy-start.5 = (bf16[2304,1024]{1,0:T(8,128)(2,1)S(1)}, bf16[2304,1024]{1,0:T(8,128)(2,1)}, u32[]{:S(2)}) copy-start(bf16[2304,1024]{1,0:T(8,128)(2,1)} %w_ref.3) | copy-start | bytes 14155780
  4.7 11.8 %copy-start.4 = (bf16[2304]{0:T(1024)(128)(2,1)S(1)}, bf16[2304]{0:T(1024)(128)(2,1)}, u32[]{:S(2)}) copy-start(bf16[2304]{0:T(1024)(128)(2,1)} %param.12) | copy-start | bytes 13828
  4.7 9.4 %collective-permute-start.12 = (bf16[56,2304]{1,0:T(8,128)(2,1)S(1)}, bf16[56,2304]{1,0:T(8,128)(2,1)S(1)}, u32[]{:S(2)}, u32[]{:S(2)}) collective-permute-start(bf16[56,2304]{1,0:T(8,128)(2,1)S(1)} %index_gather.2.refs_1_), channel_id=1, source_target_pairs={{0,2},{1,3},{2,0},{3,1},{4,6},{5,7},{6,4},{7,5}} | collective-permute-start | bytes 774152 | tf_op jit(solution)/shard_map/ppermute | solution.py:641
  7.8 11.2 %collective-permute-start.11 = (bf16[56,2304]{1,0:T(8,128)(2,1)S(1)}, bf16[56,2304]{1,0:T(8,128)(2,1)S(1)}, u32[]{:S(2)}, u32[]{:S(2)}) collective-permute-start(bf16[56,2304]{1,0:T(8,128)(2,1)S(1)} %index_gather.2.refs_1_), channel_id=1, source_target_pairs={{0,1},{1,0},{2,3},{3,2},{4,5},{5,4},{6,7},{7,6}} | collective-permute-start | bytes 774152 | tf_op jit(solution)/shard_map/ppermute | solution.py:641
  11.8 27.4 %collective-permute-start.15 = (bf16[128,2304]{1,0:T(8,128)(2,1)S(1)}, bf16[128,2304]{1,0:T(8,128)(2,1)S(1)}, u32[]{:S(2)}, u32[]{:S(2)}) collective-permute-start(bf16[128,2304]{1,0:T(8,128)(2,1)S(1)} %get-tuple-element.164), channel_id=1, source_target_pairs={{0,1},{1,0},{2,3},{3,2},{4,5},{5,4},{6,7},{7,6}} | collective-permute-start | bytes 1769480 | tf_op jit(solution)/shard_map/ppermute | solution.py:641
  12.3 26.9 %collective-permute-start.16 = (bf16[128,2304]{1,0:T(8,128)(2,1)S(1)}, bf16[128,2304]{1,0:T(8,128)(2,1)S(1)}, u32[]{:S(2)}, u32[]{:S(2)}) collective-permute-start(bf16[128,2304]{1,0:T(8,128)(2,1)S(1)} %get-tuple-element.165), channel_id=1, source_target_pairs={{0,2},{1,3},{2,0},{3,1},{4,6},{5,7},{6,4},{7,5}} | collective-permute-start | bytes 1769480 | tf_op jit(solution)/shard_map/ppermute | solution.py:641
  14.1 4.9 %collective-permute-start.13 = (bf16[56,2304]{1,0:T(8,128)(2,1)S(1)}, bf16[56,2304]{1,0:T(8,128)(2,1)S(1)}, u32[]{:S(2)}, u32[]{:S(2)}) collective-permute-start(bf16[56,2304]{1,0:T(8,128)(2,1)S(1)} %collective-permute-done.12.refs_3_), channel_id=1, source_target_pairs={{0,1},{1,0},{2,3},{3,2},{4,5},{5,4},{6,7},{7,6}} | collective-permute-start | bytes 774152 | tf_op jit(solution)/shard_map/ppermute | solution.py:641
  16.5 22.8 %copy-start.2 = (bf16[1,2304]{1,0:T(2,128)(2,1)}, bf16[1,2304]{1,0:T(2,128)(2,1)S(1)}, u32[]{:S(2)}) copy-start(bf16[1,2304]{1,0:T(2,128)(2,1)S(1)} %reshape.38.g_ref.g) | copy-start | bytes 13828
  16.5 22.8 %collective-permute-start.17 = (bf16[128,2304]{1,0:T(8,128)(2,1)S(1)}, bf16[128,2304]{1,0:T(8,128)(2,1)S(1)}, u32[]{:S(2)}, u32[]{:S(2)}) collective-permute-start(bf16[128,2304]{1,0:T(8,128)(2,1)S(1)} %get-tuple-element.166), channel_id=1, source_target_pairs={{0,3},{1,2},{2,1},{3,0},{4,7},{5,6},{6,5},{7,4}} | collective-permute-start | bytes 1769480 | tf_op jit(solution)/shard_map/ppermute | solution.py:641
  19.9 19.3 %copy-start.10 = (bf16[2,64,2304]{2,1,0:T(8,128)(2,1)}, bf16[2,64,2304]{2,1,0:T(8,128)(2,1)S(1)}, u32[]{:S(2)}) copy-start(bf16[2,64,2304]{2,1,0:T(8,128)(2,1)S(1)} %get-tuple-element.313) | copy-start | bytes 1769476
  20.0 19.3 %copy-start.8 = (bf16[2,64,2304]{2,1,0:T(8,128)(2,1)S(1)}, bf16[2,64,2304]{2,1,0:T(8,128)(2,1)}, u32[]{:S(2)}) copy-start(bf16[2,64,2304]{2,1,0:T(8,128)(2,1)} %param.15) | copy-start | bytes 1769476
  42.3 5.1 %collective-permute-start.18 = (bf16[128,2304]{1,0:T(8,128)(2,1)S(1)}, bf16[128,2304]{1,0:T(8,128)(2,1)S(1)}, u32[]{:S(2)}, u32[]{:S(2)}) collective-permute-start(bf16[128,2304]{1,0:T(8,128)(2,1)S(1)} %get-tuple-element.167.dx0), channel_id=1, source_target_pairs={{0,1},{1,0},{2,3},{3,2},{4,5},{5,4},{6,7},{7,6}} | collective-permute-start | bytes 1769480 | tf_op jit(solution)/shard_map/ppermute | solution.py:641
  42.5 4.9 %collective-permute-start.14 = (s32[1,128]{1,0:T(1,128)S(1)}, s32[1,128]{1,0:T(1,128)S(1)}, u32[]{:S(2)}, u32[]{:S(2)}) collective-permute-start(s32[1,128]{1,0:T(1,128)S(1)} %get-tuple-element.160.cnt_ref), channel_id=1, source_target_pairs={{0,4},{4,0},{1,5},{5,1},{2,6},{6,2},{3,7},{7,3}} | collective-permute-start | bytes 1544 | tf_op jit(solution)/shard_map/ppermute | solution.py:668
  46.4 11.3 %copy-start.1 = (s32[2,256]{1,0:T(2,128)S(1)}, s32[2,256]{1,0:T(2,128)}, u32[]{:S(2)}) copy-start(s32[2,256]{1,0:T(2,128)} %ids_ref.3) | copy-start | bytes 6148
  46.4 9.0 %collective-permute-start.19 = (f32[32,2304]{1,0:T(8,128)S(1)}, f32[32,2304]{1,0:T(8,128)S(1)}, u32[]{:S(2)}, u32[]{:S(2)}) collective-permute-start(f32[32,2304]{1,0:T(8,128)S(1)} %get-tuple-element.173.mine_ref), channel_id=1, source_target_pairs={{0,2},{1,3},{2,0},{3,1},{4,6},{5,7},{6,4},{7,5}} | collective-permute-start | bytes 884744 | tf_op jit(solution)/shard_map/ppermute | solution.py:641
